TPU v7x, 32 devices: a whole 2x2x4 slice. The times are simulated.
32 devices in a mesh: gx: 2 (over y), gy: 4 (over z), gz: 4 (over x, core).
Axes of the slice: x: 2, y: 2, z: 4, core: 2. Of those that a mesh axis runs over, the one named last changes fastest.
Arguments:
- density: float32 [64, 64, 512], P('gx', 'gy', 'gz'), may hold values from -8 to 8
Outputs:
- potential: float32 [64, 64, 512], P('gx', 'gy', 'gz')
All inputs are finite; a program needn't handle non-finite values.
Results may differ from a plain program's by a relative error of at most 0.00002.
Values sent between devices are 32-bit elements; how exact they have to be, the bound alone decides.
No kernel may reach another device: no remote copies, remote signals or barrier semaphores. Data moves between devices by JAX's collectives and lax.ppermute only.
A program may use at most 128 MiB of HBM per device.

v0:
```python
import jax
import jax.numpy as jnp
from jax import lax
from jax.sharding import PartitionSpec as P

LEVELS = 7
CSWEEPS = 4


rsd_beta = 0.5
centre = 4.0 + 2.0 * (1.0 + rsd_beta)


def extended_2(value, sides, width):
    for axis, dim in sides:
        count, length = (lax.axis_size(axis), value.shape[dim])
        up = [(i, (i + 1) % count) for i in range(count - 1)]
        down = [(j, i) for i, j in up]
        last = lax.slice_in_dim(value, length - width, length, axis=dim)
        leading = lax.slice_in_dim(value, 0, width, axis=dim)
        before = lax.ppermute(last, axis, up)
        after = lax.ppermute(leading, axis, down)
        value = jnp.concatenate([before, value, after], axis=dim)
    return value


def stencil_sum(padded):
    plane = (
        padded[2:, 1:-1, 1:-1]
        + padded[:-2, 1:-1, 1:-1]
        + padded[1:-1, 2:, 1:-1]
        + padded[1:-1, :-2, 1:-1]
    )
    sight = padded[1:-1, 1:-1, 2:] + padded[1:-1, 1:-1, :-2]
    return plane + (1.0 + rsd_beta) * sight


def grid_index(shape, starts):
    return [lax.broadcasted_iota(jnp.int32, shape, which) + starts[which] for which in range(3)]


def parity_of(shape, starts):
    position = grid_index(shape, starts)
    return (position[0] + position[1] + position[2] + 6) % 2


def inside_grid(shape, starts, whole):
    position = grid_index(shape, starts)
    keep = (position[0] >= 0) & (position[0] < whole[0])
    for which in (1, 2):
        keep = keep & (position[which] >= 0) & (position[which] < whole[which])
    return keep


def half_sweep(field, source, scale, chosen):
    update = (source / scale + stencil_sum(jnp.pad(field, 1))) / centre
    return jnp.where(chosen, update, field)


def full_sweep(field, source, scale, parity):
    field = half_sweep(field, source, scale, parity == 0)
    return half_sweep(field, source, scale, parity == 1)


def restrict(residue):
    shape = residue.shape
    blocks = residue.reshape(shape[0] // 2, 2, shape[1] // 2, 2, shape[2] // 2, 2)
    return jnp.mean(blocks, axis=(1, 3, 5))


def prolong(coarse):
    return jnp.repeat(jnp.repeat(jnp.repeat(coarse, 2, 0), 2, 1), 2, 2)


def local_cycle(source, level):
    scale = 0.25**level
    parity = parity_of(source.shape, (0, 0, 0))
    field = jnp.zeros_like(source)
    if level == LEVELS - 1:
        for number in range(CSWEEPS):
            field = full_sweep(field, source, scale, parity)
        return field
    for number in range(2):
        field = full_sweep(field, source, scale, parity)
    residue = source - scale * (centre * field - stencil_sum(jnp.pad(field, 1)))
    field = field + prolong(local_cycle(restrict(residue), level + 1))
    for number in range(2):
        field = full_sweep(field, source, scale, parity)
    return field


def faces(field):
    return extended_2(field, (("gx", 0), ("gy", 1), ("gz", 2)), 1)


def wide(field):
    return extended_2(field, (("gx", 0), ("gy", 1), ("gz", 2)), 2)


def block_starts(shape, margin):
    return (
        lax.axis_index("gx") * shape[0] - margin,
        lax.axis_index("gy") * shape[1] - margin,
        lax.axis_index("gz") * shape[2] - margin,
    )


def padded_half(padded, source, scale, chosen):
    field = padded[1:-1, 1:-1, 1:-1]
    update = (source / scale + stencil_sum(padded)) / centre
    return jnp.where(chosen, update, field)


def wide_sweep(extended, wide_source, scale, red_wide, source, black):
    update = (wide_source / scale + stencil_sum(jnp.pad(extended, 1))) / centre
    extended = jnp.where(red_wide, update, extended)
    return padded_half(extended[1:-1, 1:-1, 1:-1], source, scale, black)


def coarse_level(source, level):
    shape = source.shape
    stack = lax.all_gather(source[None], ("gx", "gy", "gz"), axis=0, tiled=True)
    count_x, count_y, count_z = (lax.axis_size("gx"), lax.axis_size("gy"), lax.axis_size("gz"))
    whole = stack.reshape(count_x, count_y, count_z, shape[0], shape[1], shape[2])
    whole = whole.transpose(0, 3, 1, 4, 2, 5).reshape(
        count_x * shape[0], count_y * shape[1], count_z * shape[2]
    )
    solved = local_cycle(whole, level)
    starts = block_starts(shape, 0)
    return lax.dynamic_slice(solved, starts, shape)


def shared_cycle(source, level, top):
    if level == top:
        return coarse_level(source, level)
    scale = 0.25**level
    shape = source.shape
    whole = (
        shape[0] * lax.axis_size("gx"),
        shape[1] * lax.axis_size("gy"),
        shape[2] * lax.axis_size("gz"),
    )
    parity = parity_of(shape, block_starts(shape, 0))
    black = parity == 1
    wide_shape = (shape[0] + 4, shape[1] + 4, shape[2] + 4)
    wide_starts = block_starts(shape, 2)
    red_wide = (parity_of(wide_shape, wide_starts) == 0) & inside_grid(
        wide_shape, wide_starts, whole
    )
    wide_source = wide(source)
    field = wide_sweep(
        jnp.zeros(wide_shape, jnp.float32), wide_source, scale, red_wide, source, black
    )
    field = wide_sweep(wide(field), wide_source, scale, red_wide, source, black)
    residue = source - scale * (centre * field - stencil_sum(faces(field)))
    field = field + prolong(shared_cycle(restrict(residue), level + 1, top))
    for number in range(2):
        field = wide_sweep(wide(field), wide_source, scale, red_wide, source, black)
    return field


def on_device(density):
    top = 4
    return shared_cycle(density, 0, top)


def solution(mesh):
    return jax.shard_map(
        on_device,
        mesh=mesh,
        in_specs=(P("gx", "gy", "gz"),),
        out_specs=P("gx", "gy", "gz"),
        check_vma=False,
    )
```

profile of v0, /device:TPU:0, one launch (start us, length us, event | category | flops | bytes accessed | tf_op | source)
XLA Modules:
  0.0 588.2 jit_solution(11038459568714890345)
XLA Ops:
  0.8 4.9 collective-permute-start
  16.5 4.2 collective-permute-done.3
  49.0 5.5 collective-permute-start.10
  67.1 4.5 collective-permute-start.13
  83.7 6.4 %collective-permute-start.17 = (f32[34,18,1]{2,0,1:T(8,128)S(1)}, f32[34,18,1]{2,0,1:T(8,128)S(1)}, u32[]{:S(2)}, u32[]{:S(2)}) collective-permute-start(f32[34,18,1]{2,0,1:T(8,128)S(1)} %get-tuple-element.20), channel_id=1, source_target_pairs={{0,1},{1,2},{2,3},{4,5},{5,6},{6,7},{8,9},{9,10},{10,11},{12,13},{... | collective-permute-start | bytes 7352 | tf_op jit(solution)/shard_map/ppermute | solution.py:21
  92.2 18.1 %reshape.174 = f32[16,2,8,2,64,2]{5,4,3,2,1,0:T(8,128)} reshape(f32[32,16,128]{2,1,0:T(8,128)S(1)} %fusion.34) | data formatting | bytes 524288 | tf_op jit(solution)/shard_map/reshape | solution.py:67
  110.3 7.0 %reduce_sum.68 = f32[16,8,64]{2,1,0:T(8,128)S(1)} reduce(f32[16,2,8,2,64,2]{5,4,3,2,1,0:T(8,128)} %reshape.174, f32[]{:T(128)} %constant.315.clone.1), dimensions={1,3,5}, to_apply=%region_0.1 | reduce | flops 57344 | bytes 294916 | tf_op jit(solution)/shard_map/reduce_sum | solution.py:68
  122.6 4.2 collective-permute-done.19
  130.5 4.2 collective-permute-done.21
  134.8 4.6 collective-permute-start.22
  140.8 6.8 %collective-permute-done.23 = f32[20,12,2]{2,0,1:T(8,128)S(1)} collective-permute-done((f32[20,12,2]{2,0,1:T(8,128)S(1)}, f32[20,12,2]{2,0,1:T(8,128)S(1)}, u32[]{:S(2)}, u32[]{:S(2)}) %collective-permute-start.23) | collective-permute-done | bytes 1952 | tf_op jit(solution)/shard_map/ppermute | solution.py:22
  159.3 4.3 collective-permute-done.27
  174.0 4.5 collective-permute-start.31
  183.8 4.2 collective-permute-done.32
  203.6 4.2 collective-permute-done.37
  211.4 4.2 collective-permute-done.39
  219.4 6.6 %collective-permute-done.41 = f32[12,8,2]{2,1,0:T(8,128)S(1)} collective-permute-done((f32[12,8,2]{2,1,0:T(8,128)S(1)}, f32[12,8,2]{2,1,0:T(8,128)S(1)}, u32[]{:S(2)}, u32[]{:S(2)}) %collective-permute-start.41) | collective-permute-done | bytes 800 | tf_op jit(solution)/shard_map/ppermute | solution.py:22
  230.0 4.2 collective-permute-done.43
  237.5 4.2 collective-permute-done.45
  251.6 4.5 collective-permute-start.49
  258.7 4.5 collective-permute-start.51
  280.0 4.2 collective-permute-start.56
  285.5 4.2 collective-permute-done.57
  292.7 6.5 %collective-permute-done.59 = f32[8,6,2]{2,0,1:T(8,128)S(1)} collective-permute-done((f32[8,6,2]{2,0,1:T(8,128)S(1)}, f32[8,6,2]{2,0,1:T(8,128)S(1)}, u32[]{:S(2)}, u32[]{:S(2)}) %collective-permute-start.59) | collective-permute-done | bytes 416 | tf_op jit(solution)/shard_map/ppermute | solution.py:22
  302.3 4.2 collective-permute-done.61
  309.8 4.2 collective-permute-done.63
  322.8 4.5 collective-permute-start.67
  329.9 4.5 collective-permute-start.69
  341.3 43.0 %all-gather.1 = f32[32,2,8]{2,1,0:T(2,128)S(1)} all-gather(f32[1,2,8]{2,1,0:T(2,128)S(1)} %multiply_bitcast_fusion), channel_id=2, replica_groups=mesh['gx'=2,'gy'=4,'gz'=4] {'gx','gy','gz'}, dimensions={0}, use_global_device_ids=true | all-gather | bytes 2112 | tf_op jit(solution)/shard_map/all_gather | solution.py:122
  391.4 4.2 collective-permute-done.73
  398.2 4.2 collective-permute-done.75
  410.2 4.2 collective-permute-done.79
  418.2 4.2 collective-permute-done.81
  433.0 4.2 collective-permute-done.85
  442.6 4.2 collective-permute-done.87
  458.1 4.2 collective-permute-done.91
  465.6 4.2 collective-permute-done.93
  482.5 4.2 collective-permute-done.97
  490.2 4.3 collective-permute-done.99
  507.4 4.2 collective-permute-done.103
  515.0 4.2 collective-permute-done.105
  533.3 4.2 collective-permute-done.109
  541.1 4.2 collective-permute-done.111
  549.7 4.5 collective-permute-done.113
  560.6 4.2 collective-permute-done.115
  568.4 4.2 collective-permute-done.117
  572.9 5.5 collective-permute-start.118
  579.8 4.5 collective-permute-done.119
  (578 shorter events, 311.9 us)
Async XLA Ops:
  0.8 6.4 %collective-permute-start = (f32[2,16,128]{2,1,0:T(8,128)S(1)}, f32[2,16,128]{2,1,0:T(8,128)S(1)}, u32[]{:S(2)}, u32[]{:S(2)}) collective-permute-start(f32[2,16,128]{2,1,0:T(8,128)S(1)} %get-tuple-element.40), channel_id=1, source_target_pairs={{0,16},{1,17},{2,18},{3,19},{4,20},{5,21},{6,22},{7,23},{8,24},{9,... | collective-permute-start | bytes 49160 | tf_op jit(solution)/shard_map/ppermute | solution.py:21
  5.7 5.6 collective-permute-start.1
  14.8 5.9 collective-permute-start.3
  33.0 5.6 collective-permute-start.7
  42.2 5.9 collective-permute-start.9
  49.0 7.3 %collective-permute-start.10 = (f32[36,20,2]{2,1,0:T(8,128)S(1)}, f32[36,20,2]{2,1,0:T(8,128)S(1)}, u32[]{:S(2)}, u32[]{:S(2)}) collective-permute-start(f32[36,20,2]{2,1,0:T(8,128)S(1)} %get-tuple-element.13), channel_id=1, source_target_pairs={{0,1},{1,2},{2,3},{4,5},{5,6},{6,7},{8,9},{9,10},{10,11},{12,13},{... | collective-permute-start | bytes 17288 | tf_op jit(solution)/shard_map/ppermute | solution.py:21
  54.5 5.9 collective-permute-start.11
  65.8 5.9 collective-permute-start.12
  67.1 5.9 %collective-permute-start.13 = (f32[1,16,128]{2,1,0:T(8,128)S(1)}, f32[1,16,128]{2,1,0:T(8,128)S(1)}, u32[]{:S(2)}, u32[]{:S(2)}) collective-permute-start(f32[1,16,128]{2,1,0:T(8,128)S(1)} %get-tuple-element.35), channel_id=1, source_target_pairs={{0,16},{1,17},{2,18},{3,19},{4,20},{5,21},{6,22},{7,23},{8,24},{9,... | collective-permute-start | bytes 24584 | tf_op jit(solution)/shard_map/ppermute | solution.py:21
  76.6 5.6 collective-permute-start.14
  82.4 7.8 %collective-permute-start.16 = (f32[34,18,1]{2,0,1:T(8,128)S(1)}, f32[34,18,1]{2,0,1:T(8,128)S(1)}, u32[]{:S(2)}, u32[]{:S(2)}) collective-permute-start(f32[34,18,1]{2,0,1:T(8,128)S(1)} %get-tuple-element.19), channel_id=1, source_target_pairs={{1,0},{2,1},{3,2},{5,4},{6,5},{7,6},{9,8},{10,9},{11,10},{13,12},{... | collective-permute-start | bytes 7352 | tf_op jit(solution)/shard_map/ppermute | solution.py:22
  83.7 7.7 %collective-permute-start.17 = (f32[34,18,1]{2,0,1:T(8,128)S(1)}, f32[34,18,1]{2,0,1:T(8,128)S(1)}, u32[]{:S(2)}, u32[]{:S(2)}) collective-permute-start(f32[34,18,1]{2,0,1:T(8,128)S(1)} %get-tuple-element.20), channel_id=1, source_target_pairs={{0,1},{1,2},{2,3},{4,5},{5,6},{6,7},{8,9},{9,10},{10,11},{12,13},{... | collective-permute-start | bytes 7352 | tf_op jit(solution)/shard_map/ppermute | solution.py:21
  121.2 5.5 collective-permute-start.19
  129.0 5.7 collective-permute-start.21
  134.8 6.0 %collective-permute-start.22 = (f32[20,12,2]{2,0,1:T(8,128)S(1)}, f32[20,12,2]{2,0,1:T(8,128)S(1)}, u32[]{:S(2)}, u32[]{:S(2)}) collective-permute-start(f32[20,12,2]{2,0,1:T(8,128)S(1)} %get-tuple-element.47), channel_id=1, source_target_pairs={{0,1},{1,2},{2,3},{4,5},{5,6},{6,7},{8,9},{9,10},{10,11},{12,13},{... | collective-permute-start | bytes 5768 | tf_op jit(solution)/shard_map/ppermute | solution.py:21
  139.4 8.1 %collective-permute-start.23 = (f32[20,12,2]{2,0,1:T(8,128)S(1)}, f32[20,12,2]{2,0,1:T(8,128)S(1)}, u32[]{:S(2)}, u32[]{:S(2)}) collective-permute-start(f32[20,12,2]{2,0,1:T(8,128)S(1)} %get-tuple-element.48), channel_id=1, source_target_pairs={{1,0},{2,1},{3,2},{5,4},{6,5},{7,6},{9,8},{10,9},{11,10},{13,12},{... | collective-permute-start | bytes 5768 | tf_op jit(solution)/shard_map/ppermute | solution.py:22
  158.0 5.7 collective-permute-start.27
  172.7 6.4 %collective-permute-start.30 = (f32[1,8,64]{2,1,0:T(8,128)S(1)}, f32[1,8,64]{2,1,0:T(8,128)S(1)}, u32[]{:S(2)}, u32[]{:S(2)}) collective-permute-start(f32[1,8,64]{2,1,0:T(8,128)S(1)} %get-tuple-element.75), channel_id=1, source_target_pairs={{16,0},{17,1},{18,2},{19,3},{20,4},{21,5},{22,6},{23,7},{24,8},{25... | collective-permute-start | bytes 6152 | tf_op jit(solution)/shard_map/ppermute | solution.py:22
  174.0 5.9 collective-permute-start.31
  188.1 5.6 collective-permute-start.34
  210.0 5.6 collective-permute-start.39
  218.1 7.9 %collective-permute-start.41 = (f32[12,8,2]{2,1,0:T(8,128)S(1)}, f32[12,8,2]{2,1,0:T(8,128)S(1)}, u32[]{:S(2)}, u32[]{:S(2)}) collective-permute-start(f32[12,8,2]{2,1,0:T(8,128)S(1)} %get-tuple-element.87), channel_id=1, source_target_pairs={{1,0},{2,1},{3,2},{5,4},{6,5},{7,6},{9,8},{10,9},{11,10},{13,12},{... | collective-permute-start | bytes 2312 | tf_op jit(solution)/shard_map/ppermute | solution.py:22
  236.2 5.6 collective-permute-start.45
  250.3 5.9 collective-permute-start.48
  251.6 5.8 collective-permute-start.49
  257.4 5.9 collective-permute-start.50
  258.7 5.9 collective-permute-start.51
  284.2 5.5 collective-permute-start.57
  291.4 7.8 %collective-permute-start.59 = (f32[8,6,2]{2,0,1:T(8,128)S(1)}, f32[8,6,2]{2,0,1:T(8,128)S(1)}, u32[]{:S(2)}, u32[]{:S(2)}) collective-permute-start(f32[8,6,2]{2,0,1:T(8,128)S(1)} %get-tuple-element.101), channel_id=1, source_target_pairs={{1,0},{2,1},{3,2},{5,4},{6,5},{7,6},{9,8},{10,9},{11,10},{13,12},{... | collective-permute-start | bytes 1160 | tf_op jit(solution)/shard_map/ppermute | solution.py:22
  321.5 5.9 collective-permute-start.66
  322.8 5.8 collective-permute-start.67
  328.6 5.9 collective-permute-start.68
  329.9 5.9 collective-permute-start.69
  396.9 5.5 collective-permute-start.75
  416.9 5.5 collective-permute-start.81
  441.2 5.6 collective-permute-start.87
  464.2 5.6 collective-permute-start.93
  481.2 5.5 collective-permute-start.97
  488.7 5.8 collective-permute-start.99
  506.0 5.5 collective-permute-start.103
  513.5 5.7 collective-permute-start.105
  531.9 5.6 collective-permute-start.109
  539.5 5.9 collective-permute-start.111
  548.4 5.9 collective-permute-start.113
  559.2 5.6 collective-permute-start.115
  566.8 5.9 collective-permute-start.117
  572.9 6.9 %collective-permute-start.118 = (f32[36,20,2]{2,1,0:T(8,128)S(1)}, f32[36,20,2]{2,1,0:T(8,128)S(1)}, u32[]{:S(2)}, u32[]{:S(2)}) collective-permute-start(f32[36,20,2]{2,1,0:T(8,128)S(1)} %get-tuple-element.9), channel_id=1, source_target_pairs={{0,1},{1,2},{2,3},{4,5},{5,6},{6,7},{8,9},{9,10},{10,11},{12,13},{... | collective-permute-start | bytes 17288 | tf_op jit(solution)/shard_map/ppermute | solution.py:21
  578.4 5.9 collective-permute-start.119
  (123 other events, 6134.6 us)
where the time goes:
time: 598 us; the launch traced here: 588 us
  starting transfers between devices  244 us (41%)
  waiting for transfers between devices  223 us (37%)
  other arithmetic  45.3 us (8%)
  blocking collectives  43 us (7%)
  local copies, waits for them, and re-layouts  29 us (5%)
    ppermute x60, waiting for transfers between devices, extended_2(): after = lax.ppermute(leading, axis, down)  210 us
    ppermute x60, starting transfers between devices, extended_2(): before = lax.ppermute(last, axis, up)  166 us
    ppermute x60, starting transfers between devices, extended_2(): after = lax.ppermute(leading, axis, down)  77.9 us
    all_gather x1, blocking collectives, coarse_level(): stack = lax.all_gather(source[None], ('gx', 'gy', 'gz'), axis=0, tiled=True)  43 us
    reshape x4, local copies, waits for them, and re-layouts, restrict(): residue.reshape(shape[0] // 2, 2, shape[1] // 2, 2, shape[2] // 2, 2)  21.3 us
    select_n x16, other arithmetic, wide_sweep(): extended = jnp.where(red_wide, update, extended)  15.7 us
    ppermute x60, waiting for transfers between devices, extended_2(): before = lax.ppermute(last, axis, up)  13.2 us
  transfers between devices with their start and end apart: 120, of which 75 were waited for; matrix products, arithmetic and copies ran while one was open for 1% of the time, Pallas kernels for 0%

commit v1 on v0

--- a/solution.py
+++ b/solution.py
@@ -1,6 +1,10 @@
+import functools
+
 import jax
 import jax.numpy as jnp
 from jax import lax
+from jax.experimental import pallas as pl
+from jax.experimental.pallas import tpu as pltpu
 from jax.sharding import PartitionSpec as P
 
 LEVELS = 7
@@ -159,7 +163,465 @@
     return field
 
 
+def pairs(count, first):
+    swaps = []
+    for i in range(first, count - 1, 2):
+        swaps += [(i, i + 1), (i + 1, i)]
+    return swaps
+
+
+def flips(count, bit):
+    return [(i, i ^ bit) for i in range(count)]
+
+
+def lanes_of(shape):
+    return lax.broadcasted_iota(jnp.int32, shape, len(shape) - 1)
+
+
+def rows_of(shape):
+    return lax.broadcasted_iota(jnp.int32, shape, len(shape) - 2)
+
+
+def odd_of(shape):
+    return ((lanes_of(shape) + rows_of(shape)) & 1) == 1
+
+
+def beside(value, closed):
+    rows, lanes = value.shape
+    up = pltpu.roll(value, 1, 0)
+    down = pltpu.roll(value, rows - 1, 0)
+    left = pltpu.roll(value, 1, 1)
+    right = pltpu.roll(value, lanes - 1, 1)
+    if closed:
+        row, lane = rows_of(value.shape), lanes_of(value.shape)
+        up = jnp.where(row == 0, 0.0, up)
+        down = jnp.where(row == rows - 1, 0.0, down)
+        left = jnp.where(lane == 0, 0.0, left)
+        right = jnp.where(lane == lanes - 1, 0.0, right)
+    return value + (up + down) + (1.0 + rsd_beta) * (left + right)
+
+
+def red_sum(black, at, odd, closed, before, after):
+    return beside(black[at], closed) + jnp.where(odd, after(black, at), before(black, at))
+
+
+def black_sum(red, at, odd, closed, before, after):
+    return beside(red[at], closed) + jnp.where(odd, before(red, at), after(red, at))
+
+
+def open_before(ref, at):
+    return ref[at - 1] if at > 0 else 0.0
+
+
+def open_after(ref, at):
+    return ref[at + 1] if at + 1 < ref.shape[0] else 0.0
+
+
+def ring_steps(count, own, at_low, at_high):
+    def before(ref, at):
+        value = ref[(at - 1) % count]
+        return jnp.where(at_low, 0.0, value) if at == 0 else value
+
+    def after(ref, at):
+        value = ref[(at + 1) % count]
+        return jnp.where(at_high, 0.0, value) if at == own - 1 else value
+
+    return before, after
+
+
+def exact_dot(a, b):
+    return jnp.dot(a, b, precision=lax.Precision.HIGHEST, preferred_element_type=jnp.float32)
+
+
+def pack_kernel(halo, own_ref, xh_ref, ya_ref, yb_ref, za_ref, zb_ref):
+    even_y = lax.axis_index("gy") % 2 == 0
+    even_z = lax.axis_index("gz") % 2 == 0
+    nx, ny, nz = own_ref.shape
+    groups = nz // halo
+    shape = (ny + 2 * halo, nz)
+    group = lanes_of(shape) // halo
+    for j in range(za_ref.shape[0]):
+        last = jnp.zeros(shape, jnp.float32)
+        first = jnp.zeros(shape, jnp.float32)
+        for k in range(groups):
+            at = j * groups + k
+            if at >= nx + halo:
+                break
+            plane = block_plane(at, nx, own_ref, xh_ref, ya_ref, yb_ref, even_y)
+            last = jnp.where(group == k, pltpu.roll(plane, (halo * k + halo) % nz, 1), last)
+            first = jnp.where(group == k, pltpu.roll(plane, halo * k, 1), first)
+        za_ref[j] = jnp.where(even_z, last, first)
+        zb_ref[j] = jnp.where(even_z, first, last)
+
+
+def block_plane(at, nx, own_ref, xh_ref, ya_ref, yb_ref, even_y):
+    a, b = ya_ref[at], yb_ref[at]
+    middle = own_ref[at] if at < nx else xh_ref[at - nx]
+    low = jnp.where(even_y, b, a)
+    high = jnp.where(even_y, a, b)
+    return jnp.concatenate([low, middle, high], axis=0)
+
+
+def block_mask(own, halo, lanes):
+    ny, nz = own
+    shape = (ny + 2 * halo, lanes)
+    row = rows_of(shape) - halo + lax.axis_index("gy") * ny
+    lane = lanes_of(shape)
+    lane = jnp.where(lane < lanes - halo, lane, lane - lanes) + lax.axis_index("gz") * nz
+    inside = (row >= 0) & (row < ny * lax.axis_size("gy"))
+    inside = inside & (lane >= 0) & (lane < nz * lax.axis_size("gz"))
+    return jnp.where(inside, 1.0 / centre, 0.0)
+
+
+def pre_kernel(
+    halo, own_ref, xh_ref, ya_ref, yb_ref, za_ref, zb_ref,
+    gr_ref, gb_ref, black_ref, send_ref,
+    fr_ref, fb_ref, red_ref, rest_ref,
+):
+    even_y = lax.axis_index("gy") % 2 == 0
+    even_z = lax.axis_index("gz") % 2 == 0
+    nx, ny, nz = own_ref.shape
+    count, rows, lanes = black_ref.shape
+    own = nx // 2
+    groups = nz // halo
+    odd = odd_of((rows, lanes))
+    mask = block_mask((ny, nz), halo, lanes)
+    lane = lanes_of((rows, nz))
+    low, high = lane < halo, lane >= nz - halo
+
+    def plane(at):
+        j, k = at // groups, at % groups
+        a, b = za_ref[j], zb_ref[j]
+        left = jnp.where(even_z, b, a)
+        right = jnp.where(even_z, a, b)
+        right = pltpu.roll(right, (nz - halo * k) % nz, 1)
+        left = pltpu.roll(left, (2 * nz - halo - halo * k) % nz, 1)
+        sides = jnp.where(low, right, jnp.where(high, left, 0.0))
+        middle = block_plane(at, nx, own_ref, xh_ref, ya_ref, yb_ref, even_y)
+        return jnp.concatenate([middle, sides], axis=1)
+
+    for at in range(count):
+        p, q = plane(2 * at), plane(2 * at + 1)
+        red, black = jnp.where(odd, q, p), jnp.where(odd, p, q)
+        fr_ref[at], fb_ref[at] = red, black
+        gr_ref[at], gb_ref[at] = mask * red, mask * black
+    here = lax.axis_index("gx")
+    before, after = ring_steps(count, own, here == 0, here == lax.axis_size("gx") - 1)
+    for at in range(count):
+        black_ref[at] = gb_ref[at] + mask * black_sum(gr_ref, at, odd, False, before, after)
+    for at in range(count):
+        red_ref[at] = gr_ref[at] + mask * red_sum(black_ref, at, odd, False, before, after)
+    inner = slice(halo, halo + ny)
+    for at in range(count):
+        total = black_sum(red_ref, at, odd, False, before, after)
+        value = gb_ref[at] + mask * total
+        black_ref[at] = value
+        if at < own:
+            left_over = fb_ref[at] + total - centre * value
+            rest_ref[at] = left_over[inner, :nz]
+    for at in range(own):
+        total = red_sum(black_ref, at, odd, False, before, after)
+        left_over = fr_ref[at] + total - centre * red_ref[at]
+        rest_ref[at] = rest_ref[at] + left_over[inner, :nz]
+    half, narrow = ny // 2, nz // 2
+    pairs_y = rest_ref[:, pl.ds(0, half, stride=2), :] + rest_ref[:, pl.ds(1, half, stride=2), :]
+    weight = jnp.where(
+        rows_of((nz, nz)) // 2 == lanes_of((nz, nz)) % narrow, 0.5, 0.0
+    )
+    coarse = exact_dot(pairs_y.reshape(own * half, nz), weight).reshape(own, half, nz)
+    lane = lanes_of((half, nz))
+    pick = odd_of((half, nz)) ^ (lane >= narrow)
+    for at in range(own // 2):
+        packed = jnp.where(pick, coarse[2 * at + 1], coarse[2 * at])
+        for member in range(send_ref.shape[0]):
+            send_ref[member, at] = packed
+
+
+def level_shapes(whole):
+    shapes = []
+    for level in range(1, LEVELS):
+        nx, ny, nz = (size >> level for size in whole)
+        shapes.append((max(nx // 2, 1), max(ny, 8), max(nz, 128), ny, nz))
+    return shapes
+
+
+LANES = 128
+
+
+def split_put(ref, at, value):
+    for part in range(ref.shape[1]):
+        ref[at, part] = value[:, part * LANES : (part + 1) * LANES]
+
+
+def split_get(ref, at):
+    return jnp.concatenate([ref[at, part] for part in range(ref.shape[1])], axis=1)
+
+
+def twice_put(ref, at, value):
+    for part in range(ref.shape[1]):
+        column = value[:, part * LANES : (part + 1) * LANES]
+        for start in range(2):
+            ref[at, part, pl.ds(start, value.shape[0], stride=2), :] = column
+
+
+def restrict_plane(rest_ref, at, weight):
+    half = rest_ref.shape[2] // 2
+    columns = [
+        rest_ref[at, part, pl.ds(0, half, stride=2), :] + rest_ref[at, part, pl.ds(1, half, stride=2), :]
+        for part in range(rest_ref.shape[1])
+    ]
+    total = jnp.concatenate(columns, axis=1)
+    if half < 8:
+        total = jnp.concatenate([total, jnp.zeros((8 - half, total.shape[1]), jnp.float32)], axis=0)
+    return exact_dot(total, weight)
+
+
+def solve_kernel(halo, whole, *refs):
+    here_ref, flip_ref, next_ref, both_ref, gr_ref, gb_ref, black_ref, out_ref = refs[:8]
+    scratch = list(refs[8:])
+    shapes = level_shapes(whole)
+    fields = [[scratch.pop(0) for _ in range(5)] for _ in shapes]
+    full_ref, tall_ref, red_ref, work_ref, wide_ref = scratch
+    gx, gy, gz = (lax.axis_index(axis) for axis in ("gx", "gy", "gz"))
+    low_bit, high_bit = gz % 2 == 1, gz >= 2
+
+    fr, fb = fields[0][:2]
+    members, slots, block_rows, block_lanes = here_ref.shape
+    narrow = block_lanes // 2
+    count_y = lax.axis_size("gy")
+    left = lanes_of((block_rows, block_lanes)) < narrow
+    for member in range(members):
+        i, j = member // count_y, member % count_y
+        rows = slice(j * block_rows, (j + 1) * block_rows)
+        for at in range(slots):
+            mine = (here_ref[member, at], next_ref[member, at])
+            other = (flip_ref[member, at], both_ref[member, at])
+            for part in range(2):
+                near = high_bit if part else jnp.logical_not(high_bit)
+                p = jnp.where(near, mine[0], other[0])
+                q = jnp.where(near, mine[1], other[1])
+                first = jnp.where(low_bit, q, p)
+                second = jnp.where(low_bit, p, q)
+                lanes = slice(part * block_lanes, (part + 1) * block_lanes)
+                fr[i * slots + at, rows, lanes] = jnp.where(left, first, pltpu.roll(second, narrow, 1))
+                fb[i * slots + at, rows, lanes] = jnp.where(left, pltpu.roll(first, narrow, 1), second)
+
+    def mask_of(index):
+        _, rows, lanes, ny, nz = shapes[index]
+        inside = (rows_of((rows, lanes)) < ny) & (lanes_of((rows, lanes)) < nz)
+        return jnp.where(inside, 1.0 / centre, 0.0)
+
+    def sweeps(index, number, start):
+        fr, fb, red, black, _ = fields[index]
+        count, rows, lanes = red.shape
+        odd, mask = odd_of((rows, lanes)), mask_of(index)
+        for step in range(number):
+            for at in range(count):
+                if start and step == 0:
+                    red[at] = mask * fr[at]
+                else:
+                    total = red_sum(black, at, odd, True, open_before, open_after)
+                    red[at] = mask * (fr[at] + total)
+            for at in range(count):
+                total = black_sum(red, at, odd, True, open_before, open_after)
+                black[at] = mask * (fb[at] + total)
+
+    def descend(index):
+        fr, fb, red, black, rest = fields[index]
+        count, rows, lanes = red.shape
+        odd = odd_of((rows, lanes))
+        for at in range(count):
+            first = fb[at] + black_sum(red, at, odd, True, open_before, open_after)
+            second = fr[at] + red_sum(black, at, odd, True, open_before, open_after)
+            split_put(rest, at, (first - centre * black[at]) + (second - centre * red[at]))
+        _, next_rows, next_lanes, _, _ = shapes[index + 1]
+        weight = jnp.where(
+            rows_of((lanes, next_lanes)) // 2 == lanes_of((lanes, next_lanes)), 0.5, 0.0
+        )
+        planes = [restrict_plane(rest, at, weight) for at in range(count)]
+        next_fr, next_fb = fields[index + 1][:2]
+        if count == 1:
+            next_fr[0] = planes[0]
+            return
+        odd = odd_of((next_rows, next_lanes))
+        for at in range(count // 2):
+            p, q = planes[2 * at], planes[2 * at + 1]
+            next_fr[at], next_fb[at] = jnp.where(odd, q, p), jnp.where(odd, p, q)
+
+    def ascend(index):
+        _, _, red, black, rest = fields[index]
+        count, rows, lanes = red.shape
+        _, _, coarse_red, coarse_black, _ = fields[index + 1]
+        _, next_rows, next_lanes, _, _ = shapes[index + 1]
+        odd = odd_of((next_rows, next_lanes))
+        weight = jnp.where(
+            rows_of((next_lanes, lanes)) == lanes_of((next_lanes, lanes)) // 2, 1.0, 0.0
+        )
+        half = rows // 2
+        for at in range(count):
+            r, b = coarse_red[at // 2], coarse_black[at // 2]
+            if count == 1:
+                plane = r + b
+            else:
+                plane = jnp.where(odd, r, b) if at % 2 else jnp.where(odd, b, r)
+            twice_put(rest, at, exact_dot(plane, weight)[:half])
+            black[at] = black[at] + split_get(rest, at)
+
+    def coarsest(index):
+        source, _, red, black, _ = fields[index]
+        odd = (lanes_of(source.shape[1:]) & 1) == 1
+        mask = mask_of(index)
+        mask_red, mask_black = jnp.where(odd, 0.0, mask), jnp.where(odd, mask, 0.0)
+        value, dark = source[0], jnp.zeros(source.shape[1:], jnp.float32)
+
+        def along(field):
+            return (1.0 + rsd_beta) * (pltpu.roll(field, 1, 1) + pltpu.roll(field, field.shape[1] - 1, 1))
+
+        for step in range(CSWEEPS):
+            light = mask_red * (value + along(dark))
+            dark = mask_black * (value + along(light))
+        red[0], black[0] = light, dark
+
+    last = len(shapes) - 1
+    for index in range(last):
+        sweeps(index, 2, True)
+        descend(index)
+    coarsest(last)
+    for index in reversed(range(last)):
+        ascend(index)
+        sweeps(index, 2, False)
+
+    count, rows, lanes = black_ref.shape
+    nx, ny, nz = out_ref.shape
+    own, reach = nx // 2, halo // 2
+    _, _, red1, black1, _ = fields[0]
+    _, rows1, lanes1 = red1.shape
+    odd1 = odd_of((rows1, lanes1))
+    border = jnp.zeros((full_ref.shape[0], 8, lanes1), jnp.float32)
+    full_ref[:, :8, :] = border
+    full_ref[:, rows1 + 8 :, :] = border
+    for at in range(red1.shape[0]):
+        r, b = red1[at], black1[at]
+        full_ref[2 * at, 8 : rows1 + 8, :] = jnp.where(odd1, b, r)
+        full_ref[2 * at + 1, 8 : rows1 + 8, :] = jnp.where(odd1, r, b)
+    half, block = rows // 2, ny // 2
+    z = lanes_of((lanes1, lanes))
+    z = jnp.where(z < lanes - halo, z, z - lanes) + gz * nz
+    weight = jnp.where(rows_of((lanes1, lanes)) == lax.shift_right_arithmetic(z, 1), 1.0, 0.0)
+    skip = 8 - reach
+    for at in range(count):
+        if at < own:
+            x = gx * own + at
+        else:
+            x = jnp.where(gx == 0, own, own - (count - own)) + (at - own)
+        tall_ref[at] = full_ref[x, pl.ds(pl.multiple_of(gy * block, 8), block + 16), :][skip : skip + half]
+    spread = exact_dot(tall_ref[...].reshape(count * half, lanes1), weight).reshape(count, half, lanes)
+    for at in range(count):
+        twice_put(wide_ref, at, spread[at])
+    odd = odd_of((rows, lanes))
+    mask = block_mask((ny, nz), halo, lanes)
+    for at in range(count):
+        work_ref[at] = split_get(wide_ref, at) + black_ref[at]
+    before, after = ring_steps(count, own, gx == 0, gx == lax.axis_size("gx") - 1)
+    for step in range(2):
+        for at in range(count):
+            red_ref[at] = gr_ref[at] + mask * red_sum(work_ref, at, odd, False, before, after)
+        for at in range(count if step == 0 else own):
+            work_ref[at] = gb_ref[at] + mask * black_sum(red_ref, at, odd, False, before, after)
+    inner = slice(halo, halo + ny)
+    odd = odd_of((ny, nz))
+    for at in range(own):
+        r, b = red_ref[at, inner, :nz], work_ref[at, inner, :nz]
+        out_ref[2 * at] = jnp.where(odd, b, r)
+        out_ref[2 * at + 1] = jnp.where(odd, r, b)
+
+
+def vmem(number):
+    return [pl.BlockSpec(memory_space=pltpu.VMEM)] * number
+
+
+def struct(*shape):
+    return jax.ShapeDtypeStruct(shape, jnp.float32)
+
+
+def scratch(*shape):
+    return pltpu.VMEM(shape, jnp.float32)
+
+
+HALO = 8
+
+
+def block_cycle(density):
+    halo = HALO
+    nx, ny, nz = density.shape
+    count_x, count_y, count_z = (lax.axis_size(axis) for axis in ("gx", "gy", "gz"))
+    whole = (nx * count_x, ny * count_y, nz * count_z)
+    gx, gy = lax.axis_index("gx"), lax.axis_index("gy")
+    face = lax.dynamic_slice_in_dim(density, jnp.where(gx == 0, nx - halo, 0), halo, 0)
+    side = lax.ppermute(face, "gx", flips(count_x, 1))
+    tall = jnp.concatenate([density, side], axis=0)
+    even = gy % 2 == 0
+    ya = lax.dynamic_slice_in_dim(tall, jnp.where(even, ny - halo, 0), halo, 1)
+    yb = lax.dynamic_slice_in_dim(tall, jnp.where(even, 0, ny - halo), halo, 1)
+    ya = lax.ppermute(ya, "gy", pairs(count_y, 0))
+    yb = lax.ppermute(yb, "gy", pairs(count_y, 1))
+    rows, lanes = ny + 2 * halo, 2 * nz
+    planes = nx + halo
+    packs = -(-planes * halo // nz)
+    params = pltpu.CompilerParams(vmem_limit_bytes=56 * 1024 * 1024)
+    za, zb = pl.pallas_call(
+        functools.partial(pack_kernel, halo),
+        out_shape=[struct(packs, rows, nz)] * 2,
+        in_specs=vmem(4), out_specs=vmem(2), compiler_params=params,
+    )(density, side, ya, yb)
+    za = lax.ppermute(za, "gz", pairs(count_z, 0))
+    zb = lax.ppermute(zb, "gz", pairs(count_z, 1) + [(0, count_z - 1), (count_z - 1, 0)])
+    members = count_x * count_y
+    slots = (planes // 2, rows, lanes)
+    gr, gb, black, send = pl.pallas_call(
+        functools.partial(pre_kernel, halo),
+        out_shape=[struct(*slots)] * 3 + [struct(members, nx // 4, ny // 2, nz)],
+        in_specs=vmem(6), out_specs=vmem(4), compiler_params=params,
+        scratch_shapes=[scratch(*slots)] * 3 + [scratch(nx // 2, ny, nz)],
+    )(density, side, ya, yb, za, zb)
+    here = lax.all_to_all(send, ("gx", "gy"), 0, 0, tiled=True)
+    flip = lax.ppermute(here, "gz", flips(count_z, 2))
+    beside_here = lax.ppermute(here, "gz", flips(count_z, 1))
+    beside_flip = lax.ppermute(flip, "gz", flips(count_z, 1))
+    room = []
+    for count, high, wide_lanes, _, _ in level_shapes(whole):
+        room += [scratch(count, high, wide_lanes)] * 4
+        room += [scratch(count, wide_lanes // LANES, high, LANES)]
+    room += [
+        scratch(whole[0] // 2, whole[1] // 2 + 16, whole[2] // 2),
+        scratch(planes // 2, rows // 2, whole[2] // 2),
+        scratch(*slots),
+        scratch(*slots),
+        scratch(planes // 2, lanes // LANES, rows, LANES),
+    ]
+    return pl.pallas_call(
+        functools.partial(solve_kernel, halo, whole),
+        out_shape=struct(nx, ny, nz),
+        in_specs=vmem(7), out_specs=pl.BlockSpec(memory_space=pltpu.VMEM),
+        compiler_params=params, scratch_shapes=room,
+    )(here, flip, beside_here, beside_flip, gr, gb, black)
+
+
+def fits_block_cycle(shape):
+    nx, ny, nz = shape
+    count_x, count_y, count_z = (lax.axis_size(axis) for axis in ("gx", "gy", "gz"))
+    whole = (nx * count_x, ny * count_y, nz * count_z)
+    coarsest = [size >> (LEVELS - 1) for size in whole]
+    exact = all(c << (LEVELS - 1) == size for c, size in zip(coarsest, whole))
+    return (
+        exact and coarsest[0] == coarsest[1] == 1 and nz == 128 and ny == 16 and nx >= 16
+        and nx % 4 == 0 and count_x == 2 and count_z == 4 and count_y % 2 == 0
+    )
+
+
 def on_device(density):
+    if fits_block_cycle(density.shape):
+        return block_cycle(density)
     top = 4
     return shared_cycle(density, 0, top)
 

time: 598 us -> 64.4 us (0.11); the launches traced: 588 us -> 64 us
  starting transfers between devices: 244 us -> 11.7 us
  waiting for transfers between devices: 223 us -> 13.5 us
  other arithmetic: 45.3 us -> 0 us
  blocking collectives: 43 us -> 14.7 us
  local copies, waits for them, and re-layouts: 29 us -> 4.41 us
  Pallas kernels: 0 us -> 19.6 us
    ppermute x120 -> x8, starting transfers between devices: 244 us -> 11.7 us  [the longest x1 4.96 us: block_cycle(): ya = lax.ppermute(ya, 'gy', pairs(count_y, 0))]
    ppermute x120 -> x8, waiting for transfers between devices: 223 us -> 13.5 us  [the longest x1 5.29 us: block_cycle(): flip = lax.ppermute(here, 'gz', flips(count_z, 2))]
    all_gather x1 -> x0, blocking collectives: 43 us -> none  [coarse_level(): stack = lax.all_gather(source[None], ('gx', 'gy', 'gz'), axis=0, tiled=True)]
    select_n x54 -> x0, other arithmetic: 24.8 us -> none  [the longest x16 15.7 us: wide_sweep(): extended = jnp.where(red_wide, update, extended)]
    reshape x12 -> x0, local copies, waits for them, and re-layouts: 22.6 us -> none  [the longest x4 21.3 us: restrict(): residue.reshape(shape[0] // 2, 2, shape[1] // 2, 2, shape[2] // 2, 2)]
    pallas_call x0 -> x3, Pallas kernels: none -> 19.6 us  [the longest x1 13.7 us: block_cycle(): pl.pallas_call(functools.partial(solve_kernel, halo, whole), out_shape=st...]
    all_to_all x0 -> x1, blocking collectives: none -> 14.7 us  [block_cycle(): here = lax.all_to_all(send, ('gx', 'gy'), 0, 0, tiled=True)]
    reduce_sum x8 -> x0, other arithmetic: 7.85 us -> none  [restrict(): return jnp.mean(blocks, axis=(1, 3, 5))]
  transfers between devices with their start and end apart: 120 -> 8, of which waited for: 75 -> 5; matrix products, arithmetic and copies ran while one was open for 1% -> 2% of each run, Pallas kernels for 0% -> 0%
where the time goes in v1:
time: 64.4 us; the launch traced here: 64 us
  Pallas kernels  19.6 us (30%)
  blocking collectives  14.7 us (23%)
  waiting for transfers between devices  13.5 us (21%)
  starting transfers between devices  11.7 us (18%)
  local copies, waits for them, and re-layouts  4.41 us (7%)
    all_to_all x1, blocking collectives, block_cycle(): here = lax.all_to_all(send, ('gx', 'gy'), 0, 0, tiled=True)  14.7 us
    pallas_call x1, Pallas kernels, block_cycle(): pl.pallas_call(functools.partial(solve_kernel, halo, whole), out_shape=st...  13.7 us
    ppermute x1, waiting for transfers between devices, block_cycle(): flip = lax.ppermute(here, 'gz', flips(count_z, 2))  5.29 us
    ppermute x1, starting transfers between devices, block_cycle(): ya = lax.ppermute(ya, 'gy', pairs(count_y, 0))  4.96 us
    pallas_call x1, Pallas kernels, block_cycle(): pl.pallas_call(functools.partial(pre_kernel, halo), out_shape=[struct(*sl...  3.76 us
    unnamed x19, local copies, waits for them, and re-layouts  3.53 us
    ppermute x1, waiting for transfers between devices, block_cycle(): ya = lax.ppermute(ya, 'gy', pairs(count_y, 0))  3.29 us
    ppermute x1, starting transfers between devices, block_cycle(): side = lax.ppermute(face, 'gx', flips(count_x, 1))  3 us
  transfers between devices with their start and end apart: 8, of which 5 were waited for; matrix products, arithmetic and copies ran while one was open for 2% of the time, Pallas kernels for 0%

profile of v1, /device:TPU:0, one launch (start us, length us, event | category | flops | bytes accessed | tf_op | source)
XLA Modules:
  0.0 64.0 jit_solution(1055212679735823906)
XLA Ops:
  0.0 0.8 %constant_dynamic-slice_fusion.2 = f32[8,16,128]{2,1,0:T(8,128)S(1)} fusion(f32[32,16,128]{2,1,0:T(8,128)} %own_ref.3, s32[]{:T(128)S(6)} %select_n.20), kind=kLoop, calls=%fused_computation.4 | loop fusion | bytes 131076 | tf_op jit(solution)/shard_map/dynamic_slice | solution.py:560
  0.8 3.0 %collective-permute-start = (f32[8,16,128]{2,1,0:T(8,128)S(1)}, f32[8,16,128]{2,1,0:T(8,128)S(1)}, u32[]{:S(2)}, u32[]{:S(2)}) collective-permute-start(f32[8,16,128]{2,1,0:T(8,128)S(1)} %constant_dynamic-slice_fusion.2), channel_id=1, source_target_pairs={{0,16},{16,0},{1,17},{17,1},{2,18},{18,2},{3,19},{19,3},{4,20},{20... | collective-permute-start | bytes 196616 | tf_op jit(solution)/shard_map/ppermute | solution.py:561
  3.8 1.0 %constant_dynamic-update-slice_fusion.1 = f32[40,16,128]{2,1,0:T(8,128)S(1)} fusion(f32[32,16,128]{2,1,0:T(8,128)} %own_ref.3), kind=kLoop, calls=%fused_computation.1 | loop fusion | bytes 524288
  4.8 1.3 %collective-permute-done.xh_ref = f32[8,16,128]{2,1,0:T(8,128)S(1)} collective-permute-done((f32[8,16,128]{2,1,0:T(8,128)S(1)}, f32[8,16,128]{2,1,0:T(8,128)S(1)}, u32[]{:S(2)}, u32[]{:S(2)}) %collective-permute-start) | collective-permute-done | bytes 65568 | tf_op jit(solution)/shard_map/ppermute | solution.py:561
  6.1 0.0 copy-start.3
  6.1 0.6 copy-done.3
  6.7 0.7 %collective-permute-start.2 = (f32[40,8,128]{2,1,0:T(8,128)S(1)}, f32[40,8,128]{2,1,0:T(8,128)S(1)}, u32[]{:S(2)}, u32[]{:S(2)}) collective-permute-start(f32[40,8,128]{2,1,0:T(8,128)S(1)} %get-tuple-element.17), channel_id=1, source_target_pairs={{4,8},{8,4},{5,9},{9,5},{6,10},{10,6},{7,11},{11,7},{20,24},{24,20... | collective-permute-start | bytes 491528 | tf_op jit(solution)/shard_map/ppermute | solution.py:567
  7.4 5.0 %collective-permute-start.1 = (f32[40,8,128]{2,1,0:T(8,128)S(1)}, f32[40,8,128]{2,1,0:T(8,128)S(1)}, u32[]{:S(2)}, u32[]{:S(2)}) collective-permute-start(f32[40,8,128]{2,1,0:T(8,128)S(1)} %get-tuple-element.18), channel_id=1, source_target_pairs={{0,4},{4,0},{8,12},{12,8},{1,5},{5,1},{9,13},{13,9},{2,6},{6,2},{1... | collective-permute-start | bytes 491528 | tf_op jit(solution)/shard_map/ppermute | solution.py:566
  12.3 0.0 collective-permute-done.2.yb_ref
  12.3 0.0 copy-start.1
  12.3 3.3 %collective-permute-done.1.ya_ref = f32[40,8,128]{2,1,0:T(8,128)S(1)} collective-permute-done((f32[40,8,128]{2,1,0:T(8,128)S(1)}, f32[40,8,128]{2,1,0:T(8,128)S(1)}, u32[]{:S(2)}, u32[]{:S(2)}) %collective-permute-start.1) | collective-permute-done | bytes 163872 | tf_op jit(solution)/shard_map/ppermute | solution.py:566
  15.6 0.0 copy-done.1
  15.6 0.0 copy-start.2
  15.6 0.7 %copy-done.2 = f32[40,8,128]{2,1,0:T(8,128)} copy-done((f32[40,8,128]{2,1,0:T(8,128)}, f32[40,8,128]{2,1,0:T(8,128)S(1)}, u32[]{:S(2)}) %copy-start.2) | copy-done | bytes 163864
  16.3 2.1 %shard_map.17 = (f32[3,32,128]{2,1,0:T(8,128)}, f32[3,32,128]{2,1,0:T(8,128)}) custom-call(f32[32,16,128]{2,1,0:T(8,128)} %own_ref.3, f32[8,16,128]{2,1,0:T(8,128)} %copy-done.3, f32[40,8,128]{2,1,0:T(8,128)} %copy-done.2, f32[40,8,128]{2,1,0:T(8,128)} %copy-done.1), custom_call_target="tpu_custom_call" | custom-call | tf_op jit(solution)/shard_map/pallas_call | solution.py:572
  18.4 0.0 collective-permute-start.3
  18.4 1.6 %collective-permute-start.4 = (f32[3,32,128]{2,1,0:T(8,128)}, f32[3,32,128]{2,1,0:T(8,128)S(1)}, u32[]{:S(2)}, u32[]{:S(2)}) collective-permute-start(f32[3,32,128]{2,1,0:T(8,128)} %get-tuple-element.12), channel_id=1, source_target_pairs={{1,2},{2,1},{0,3},{3,0},{5,6},{6,5},{4,7},{7,4},{9,10},{10,9},{8,1... | collective-permute-start | bytes 147464 | tf_op jit(solution)/shard_map/ppermute | solution.py:578
  20.0 0.0 collective-permute-done.3.za_ref
  20.0 0.0 copy-start.7
  20.0 2.1 %collective-permute-done.4.zb_ref = f32[3,32,128]{2,1,0:T(8,128)S(1)} collective-permute-done((f32[3,32,128]{2,1,0:T(8,128)}, f32[3,32,128]{2,1,0:T(8,128)S(1)}, u32[]{:S(2)}, u32[]{:S(2)}) %collective-permute-start.4) | collective-permute-done | bytes 49184 | tf_op jit(solution)/shard_map/ppermute | solution.py:578
  22.1 0.0 copy-done.7
  22.1 0.0 copy-start.8
  22.1 0.6 copy-done.8
  22.8 3.8 %shard_map.18 = (f32[20,32,256]{2,1,0:T(8,128)}, f32[20,32,256]{2,1,0:T(8,128)}, f32[20,32,256]{2,1,0:T(8,128)}, f32[8,8,8,128]{3,2,1,0:T(8,128)}) custom-call(f32[32,16,128]{2,1,0:T(8,128)} %own_ref.3, f32[8,16,128]{2,1,0:T(8,128)} %copy-done.3, f32[40,8,128]{2,1,0:T(8,128)} %copy-done.2, f32[40,8,128]{2,1,0:T(8,128)} %copy-done.1, ...), custom_call_target="tpu_custom_call" | custom-call | tf_op jit(solution)/shard_map/pallas_call | solution.py:581
  26.5 14.7 %all_to_all.5.refs_0_ = f32[8,8,8,128]{3,2,1,0:T(8,128)S(1)} all-to-all(f32[8,8,8,128]{3,2,1,0:T(8,128)} %get-tuple-element.13), channel_id=1, replica_groups=mesh['gx'=2,'gy'=4,'gz'=4] {'gx','gy'}, dimensions={0} | all-to-all | bytes 524288 | tf_op jit(solution)/shard_map/all_to_all | solution.py:587
  41.2 0.0 copy-start
  41.2 1.5 %collective-permute-start.5 = (f32[8,8,8,128]{3,2,1,0:T(8,128)S(1)}, f32[8,8,8,128]{3,2,1,0:T(8,128)S(1)}, u32[]{:S(2)}, u32[]{:S(2)}) collective-permute-start(f32[8,8,8,128]{3,2,1,0:T(8,128)S(1)} %all_to_all.5.refs_0_), channel_id=1, source_target_pairs={{0,2},{1,3},{2,0},{3,1},{4,6},{5,7},{6,4},{7,5},{8,10},{9,11},{10,... | collective-permute-start | bytes 786440 | tf_op jit(solution)/shard_map/ppermute | solution.py:588
  42.7 0.0 collective-permute-start.6
  42.7 5.3 %collective-permute-done.5.refs_1_ = f32[8,8,8,128]{3,2,1,0:T(8,128)S(1)} collective-permute-done((f32[8,8,8,128]{3,2,1,0:T(8,128)S(1)}, f32[8,8,8,128]{3,2,1,0:T(8,128)S(1)}, u32[]{:S(2)}, u32[]{:S(2)}) %collective-permute-start.5) | collective-permute-done | bytes 262176 | tf_op jit(solution)/shard_map/ppermute | solution.py:588
  48.0 0.0 copy-start.4
  48.0 0.0 collective-permute-start.7
  48.0 0.0 collective-permute-done.6.refs_2_
  48.0 0.0 copy-start.5
  48.0 1.5 %collective-permute-done.7.refs_3_ = f32[8,8,8,128]{3,2,1,0:T(8,128)S(1)} collective-permute-done((f32[8,8,8,128]{3,2,1,0:T(8,128)S(1)}, f32[8,8,8,128]{3,2,1,0:T(8,128)S(1)}, u32[]{:S(2)}, u32[]{:S(2)}) %collective-permute-start.7) | collective-permute-done | bytes 262176 | tf_op jit(solution)/shard_map/ppermute | solution.py:590
  49.5 0.0 copy-start.6
  49.5 0.0 copy-done
  49.5 0.0 copy-done.4
  49.6 0.0 copy-done.5
  49.6 0.7 %copy-done.6 = f32[8,8,8,128]{3,2,1,0:T(8,128)} copy-done((f32[8,8,8,128]{3,2,1,0:T(8,128)}, f32[8,8,8,128]{3,2,1,0:T(8,128)S(1)}, u32[]{:S(2)}) %copy-start.6) | copy-done | bytes 262168
  50.3 13.7 %shard_map.19 = f32[32,16,128]{2,1,0:T(8,128)} custom-call(f32[8,8,8,128]{3,2,1,0:T(8,128)} %copy-done, f32[8,8,8,128]{3,2,1,0:T(8,128)} %copy-done.4, f32[8,8,8,128]{3,2,1,0:T(8,128)} %copy-done.5, f32[8,8,8,128]{3,2,1,0:T(8,128)} %copy-done.6, f32[20,32,256]{2,1,0:T(8,128)} %get-tuple-element.14.refs_4_, f32[20,32,256]{2,1,0:T(8,128)} %get-tuple-element.15.refs_5_, ...), custom_call_target="tpu_custom_call" | custom-call | tf_op jit(solution)/shard_map/pallas_call | solution.py:602
  (2 shorter events, 0.0 us)
Async XLA Ops:
  0.8 5.2 %collective-permute-start = (f32[8,16,128]{2,1,0:T(8,128)S(1)}, f32[8,16,128]{2,1,0:T(8,128)S(1)}, u32[]{:S(2)}, u32[]{:S(2)}) collective-permute-start(f32[8,16,128]{2,1,0:T(8,128)S(1)} %constant_dynamic-slice_fusion.2), channel_id=1, source_target_pairs={{0,16},{16,0},{1,17},{17,1},{2,18},{18,2},{3,19},{19,3},{4,20},{20... | collective-permute-start | bytes 196616 | tf_op jit(solution)/shard_map/ppermute | solution.py:561
  6.1 0.6 copy-start.3
  6.7 5.6 %collective-permute-start.2 = (f32[40,8,128]{2,1,0:T(8,128)S(1)}, f32[40,8,128]{2,1,0:T(8,128)S(1)}, u32[]{:S(2)}, u32[]{:S(2)}) collective-permute-start(f32[40,8,128]{2,1,0:T(8,128)S(1)} %get-tuple-element.17), channel_id=1, source_target_pairs={{4,8},{8,4},{5,9},{9,5},{6,10},{10,6},{7,11},{11,7},{20,24},{24,20... | collective-permute-start | bytes 491528 | tf_op jit(solution)/shard_map/ppermute | solution.py:567
  7.4 8.3 %collective-permute-start.1 = (f32[40,8,128]{2,1,0:T(8,128)S(1)}, f32[40,8,128]{2,1,0:T(8,128)S(1)}, u32[]{:S(2)}, u32[]{:S(2)}) collective-permute-start(f32[40,8,128]{2,1,0:T(8,128)S(1)} %get-tuple-element.18), channel_id=1, source_target_pairs={{0,4},{4,0},{8,12},{12,8},{1,5},{5,1},{9,13},{13,9},{2,6},{6,2},{1... | collective-permute-start | bytes 491528 | tf_op jit(solution)/shard_map/ppermute | solution.py:566
  12.3 3.3 %copy-start.1 = (f32[40,8,128]{2,1,0:T(8,128)}, f32[40,8,128]{2,1,0:T(8,128)S(1)}, u32[]{:S(2)}) copy-start(f32[40,8,128]{2,1,0:T(8,128)S(1)} %collective-permute-done.2.yb_ref) | copy-start | bytes 491524
  15.6 0.7 %copy-start.2 = (f32[40,8,128]{2,1,0:T(8,128)}, f32[40,8,128]{2,1,0:T(8,128)S(1)}, u32[]{:S(2)}) copy-start(f32[40,8,128]{2,1,0:T(8,128)S(1)} %collective-permute-done.1.ya_ref) | copy-start | bytes 491524
  18.4 1.6 %collective-permute-start.3 = (f32[3,32,128]{2,1,0:T(8,128)}, f32[3,32,128]{2,1,0:T(8,128)S(1)}, u32[]{:S(2)}, u32[]{:S(2)}) collective-permute-start(f32[3,32,128]{2,1,0:T(8,128)} %get-tuple-element.11), channel_id=1, source_target_pairs={{0,1},{1,0},{2,3},{3,2},{4,5},{5,4},{6,7},{7,6},{8,9},{9,8},{10,11... | collective-permute-start | bytes 147464 | tf_op jit(solution)/shard_map/ppermute | solution.py:577
  18.4 3.7 %collective-permute-start.4 = (f32[3,32,128]{2,1,0:T(8,128)}, f32[3,32,128]{2,1,0:T(8,128)S(1)}, u32[]{:S(2)}, u32[]{:S(2)}) collective-permute-start(f32[3,32,128]{2,1,0:T(8,128)} %get-tuple-element.12), channel_id=1, source_target_pairs={{1,2},{2,1},{0,3},{3,0},{5,6},{6,5},{4,7},{7,4},{9,10},{10,9},{8,1... | collective-permute-start | bytes 147464 | tf_op jit(solution)/shard_map/ppermute | solution.py:578
  20.0 2.1 %copy-start.7 = (f32[3,32,128]{2,1,0:T(8,128)}, f32[3,32,128]{2,1,0:T(8,128)S(1)}, u32[]{:S(2)}) copy-start(f32[3,32,128]{2,1,0:T(8,128)S(1)} %collective-permute-done.3.za_ref) | copy-start | bytes 147460
  22.1 0.6 copy-start.8
  41.2 8.3 %copy-start = (f32[8,8,8,128]{3,2,1,0:T(8,128)}, f32[8,8,8,128]{3,2,1,0:T(8,128)S(1)}, u32[]{:S(2)}) copy-start(f32[8,8,8,128]{3,2,1,0:T(8,128)S(1)} %all_to_all.5.refs_0_) | copy-start | bytes 786436
  41.2 6.8 %collective-permute-start.5 = (f32[8,8,8,128]{3,2,1,0:T(8,128)S(1)}, f32[8,8,8,128]{3,2,1,0:T(8,128)S(1)}, u32[]{:S(2)}, u32[]{:S(2)}) collective-permute-start(f32[8,8,8,128]{3,2,1,0:T(8,128)S(1)} %all_to_all.5.refs_0_), channel_id=1, source_target_pairs={{0,2},{1,3},{2,0},{3,1},{4,6},{5,7},{6,4},{7,5},{8,10},{9,11},{10,... | collective-permute-start | bytes 786440 | tf_op jit(solution)/shard_map/ppermute | solution.py:588
  42.7 5.3 %collective-permute-start.6 = (f32[8,8,8,128]{3,2,1,0:T(8,128)S(1)}, f32[8,8,8,128]{3,2,1,0:T(8,128)S(1)}, u32[]{:S(2)}, u32[]{:S(2)}) collective-permute-start(f32[8,8,8,128]{3,2,1,0:T(8,128)S(1)} %all_to_all.5.refs_0_), channel_id=1, source_target_pairs={{0,1},{1,0},{2,3},{3,2},{4,5},{5,4},{6,7},{7,6},{8,9},{9,8},{10,11... | collective-permute-start | bytes 786440 | tf_op jit(solution)/shard_map/ppermute | solution.py:589
  48.0 1.5 %copy-start.4 = (f32[8,8,8,128]{3,2,1,0:T(8,128)}, f32[8,8,8,128]{3,2,1,0:T(8,128)S(1)}, u32[]{:S(2)}) copy-start(f32[8,8,8,128]{3,2,1,0:T(8,128)S(1)} %collective-permute-done.5.refs_1_) | copy-start | bytes 786436
  48.0 1.5 %collective-permute-start.7 = (f32[8,8,8,128]{3,2,1,0:T(8,128)S(1)}, f32[8,8,8,128]{3,2,1,0:T(8,128)S(1)}, u32[]{:S(2)}, u32[]{:S(2)}) collective-permute-start(f32[8,8,8,128]{3,2,1,0:T(8,128)S(1)} %collective-permute-done.5.refs_1_), channel_id=1, source_target_pairs={{0,1},{1,0},{2,3},{3,2},{4,5},{5,4},{6,7},{7,6},{8,9},{9,8},{10,11... | collective-permute-start | bytes 786440 | tf_op jit(solution)/shard_map/ppermute | solution.py:590
  48.0 1.5 %copy-start.5 = (f32[8,8,8,128]{3,2,1,0:T(8,128)}, f32[8,8,8,128]{3,2,1,0:T(8,128)S(1)}, u32[]{:S(2)}) copy-start(f32[8,8,8,128]{3,2,1,0:T(8,128)S(1)} %collective-permute-done.6.refs_2_) | copy-start | bytes 786436
  49.5 0.7 %copy-start.6 = (f32[8,8,8,128]{3,2,1,0:T(8,128)}, f32[8,8,8,128]{3,2,1,0:T(8,128)S(1)}, u32[]{:S(2)}) copy-start(f32[8,8,8,128]{3,2,1,0:T(8,128)S(1)} %collective-permute-done.7.refs_3_) | copy-start | bytes 786436

commit v2 on v1

--- a/solution.py
+++ b/solution.py
@@ -568,11 +568,14 @@
     rows, lanes = ny + 2 * halo, 2 * nz
     planes = nx + halo
     packs = -(-planes * halo // nz)
-    params = pltpu.CompilerParams(vmem_limit_bytes=56 * 1024 * 1024)
+
+    def params(mib):
+        return pltpu.CompilerParams(vmem_limit_bytes=mib * 1024 * 1024)
+
     za, zb = pl.pallas_call(
         functools.partial(pack_kernel, halo),
         out_shape=[struct(packs, rows, nz)] * 2,
-        in_specs=vmem(4), out_specs=vmem(2), compiler_params=params,
+        in_specs=vmem(4), out_specs=vmem(2), compiler_params=params(4),
     )(density, side, ya, yb)
     za = lax.ppermute(za, "gz", pairs(count_z, 0))
     zb = lax.ppermute(zb, "gz", pairs(count_z, 1) + [(0, count_z - 1), (count_z - 1, 0)])
@@ -581,7 +584,7 @@
     gr, gb, black, send = pl.pallas_call(
         functools.partial(pre_kernel, halo),
         out_shape=[struct(*slots)] * 3 + [struct(members, nx // 4, ny // 2, nz)],
-        in_specs=vmem(6), out_specs=vmem(4), compiler_params=params,
+        in_specs=vmem(6), out_specs=vmem(4), compiler_params=params(10),
         scratch_shapes=[scratch(*slots)] * 3 + [scratch(nx // 2, ny, nz)],
     )(density, side, ya, yb, za, zb)
     here = lax.all_to_all(send, ("gx", "gy"), 0, 0, tiled=True)
@@ -603,7 +606,7 @@
         functools.partial(solve_kernel, halo, whole),
         out_shape=struct(nx, ny, nz),
         in_specs=vmem(7), out_specs=pl.BlockSpec(memory_space=pltpu.VMEM),
-        compiler_params=params, scratch_shapes=room,
+        compiler_params=params(16), scratch_shapes=room,
     )(here, flip, beside_here, beside_flip, gr, gb, black)
 
 

time: 64.4 us -> 55.9 us (0.87)
  Pallas kernels: 19.6 us -> 14.1 us
  local copies, waits for them, and re-layouts: 4.41 us -> 1.85 us
    unnamed x19 -> x3, local copies, waits for them, and re-layouts: 3.53 us -> 0.97 us
    pallas_call x1, Pallas kernels: 3.76 us -> 1.83 us  [block_cycle(): pl.pallas_call(functools.partial(pre_kernel, halo), out_shape=[struct(*sl...]
    pallas_call x1, Pallas kernels: 13.7 us -> 11.9 us  [block_cycle(): pl.pallas_call(functools.partial(solve_kernel, halo, whole), out_shape=st...]
    pallas_call x1, Pallas kernels: 2.14 us -> 0.39 us  [block_cycle(): pl.pallas_call(functools.partial(pack_kernel, halo), out_shape=[struct(pa...]
where the time goes in v2:
time: 55.9 us; the launch traced here: 55.7 us
  blocking collectives  14.4 us (26%)
  Pallas kernels  14.1 us (25%)
  waiting for transfers between devices  13.3 us (24%)
  starting transfers between devices  11.9 us (21%)
  local copies, waits for them, and re-layouts  1.85 us (3%)
    all_to_all x1, blocking collectives, block_cycle(): here = lax.all_to_all(send, ('gx', 'gy'), 0, 0, tiled=True)  14.4 us
    pallas_call x1, Pallas kernels, block_cycle(): pl.pallas_call(functools.partial(solve_kernel, halo, whole), out_shape=st...  11.9 us
    ppermute x1, waiting for transfers between devices, block_cycle(): flip = lax.ppermute(here, 'gz', flips(count_z, 2))  5.21 us
    ppermute x1, starting transfers between devices, block_cycle(): ya = lax.ppermute(ya, 'gy', pairs(count_y, 0))  4.96 us
    ppermute x1, waiting for transfers between devices, block_cycle(): ya = lax.ppermute(ya, 'gy', pairs(count_y, 0))  3.3 us
    ppermute x1, starting transfers between devices, block_cycle(): side = lax.ppermute(face, 'gx', flips(count_x, 1))  3 us
    ppermute x1, waiting for transfers between devices, block_cycle(): lax.ppermute(zb, 'gz', pairs(count_z, 1) + [(0, count_z - 1), (count_z -...  1.98 us
    pallas_call x1, Pallas kernels, block_cycle(): pl.pallas_call(functools.partial(pre_kernel, halo), out_shape=[struct(*sl...  1.83 us
  transfers between devices with their start and end apart: 8, of which 5 were waited for; matrix products, arithmetic and copies ran while one was open for 2% of the time, Pallas kernels for 0%

profile of v2, /device:TPU:0, one launch (start us, length us, event | category | flops | bytes accessed | tf_op | source)
XLA Modules:
  0.0 55.7 jit_solution(4822078187231506855)
XLA Ops:
  0.0 0.8 %constant_dynamic-slice_fusion.2 = f32[8,16,128]{2,1,0:T(8,128)S(1)} fusion(f32[32,16,128]{2,1,0:T(8,128)} %own_ref.3, s32[]{:T(128)S(6)} %select_n.20), kind=kLoop, calls=%fused_computation.4 | loop fusion | bytes 131076 | tf_op jit(solution)/shard_map/dynamic_slice | solution.py:560
  0.8 3.0 %collective-permute-start = (f32[8,16,128]{2,1,0:T(8,128)S(1)}, f32[8,16,128]{2,1,0:T(8,128)S(1)}, u32[]{:S(2)}, u32[]{:S(2)}) collective-permute-start(f32[8,16,128]{2,1,0:T(8,128)S(1)} %constant_dynamic-slice_fusion.2), channel_id=1, source_target_pairs={{0,16},{16,0},{1,17},{17,1},{2,18},{18,2},{3,19},{19,3},{4,20},{20... | collective-permute-start | bytes 196616 | tf_op jit(solution)/shard_map/ppermute | solution.py:561
  3.8 1.0 %constant_dynamic-update-slice_fusion.1 = f32[40,16,128]{2,1,0:T(8,128)S(1)} fusion(f32[32,16,128]{2,1,0:T(8,128)} %own_ref.3), kind=kLoop, calls=%fused_computation.1 | loop fusion | bytes 524288
  4.8 1.3 %collective-permute-done.xh_ref = f32[8,16,128]{2,1,0:T(8,128)S(1)} collective-permute-done((f32[8,16,128]{2,1,0:T(8,128)S(1)}, f32[8,16,128]{2,1,0:T(8,128)S(1)}, u32[]{:S(2)}, u32[]{:S(2)}) %collective-permute-start) | collective-permute-done | bytes 65568 | tf_op jit(solution)/shard_map/ppermute | solution.py:561
  6.1 0.0 copy-start
  6.1 0.8 %collective-permute-start.2 = (f32[40,8,128]{2,1,0:T(8,128)S(1)}, f32[40,8,128]{2,1,0:T(8,128)S(1)}, u32[]{:S(2)}, u32[]{:S(2)}) collective-permute-start(f32[40,8,128]{2,1,0:T(8,128)S(1)} %get-tuple-element.17), channel_id=1, source_target_pairs={{4,8},{8,4},{5,9},{9,5},{6,10},{10,6},{7,11},{11,7},{20,24},{24,20... | collective-permute-start | bytes 491528 | tf_op jit(solution)/shard_map/ppermute | solution.py:567
  6.9 5.0 %collective-permute-start.1 = (f32[40,8,128]{2,1,0:T(8,128)S(1)}, f32[40,8,128]{2,1,0:T(8,128)S(1)}, u32[]{:S(2)}, u32[]{:S(2)}) collective-permute-start(f32[40,8,128]{2,1,0:T(8,128)S(1)} %get-tuple-element.18), channel_id=1, source_target_pairs={{0,4},{4,0},{8,12},{12,8},{1,5},{5,1},{9,13},{13,9},{2,6},{6,2},{1... | collective-permute-start | bytes 491528 | tf_op jit(solution)/shard_map/ppermute | solution.py:566
  11.9 0.0 collective-permute-done.2.yb_ref
  11.9 3.3 %collective-permute-done.1.ya_ref = f32[40,8,128]{2,1,0:T(8,128)S(1)} collective-permute-done((f32[40,8,128]{2,1,0:T(8,128)S(1)}, f32[40,8,128]{2,1,0:T(8,128)S(1)}, u32[]{:S(2)}, u32[]{:S(2)}) %collective-permute-start.1) | collective-permute-done | bytes 163872 | tf_op jit(solution)/shard_map/ppermute | solution.py:566
  15.2 0.0 copy-done
  15.2 0.4 shard_map.17
  15.6 0.1 collective-permute-start.3
  15.7 1.6 %collective-permute-start.4 = (f32[3,32,128]{2,1,0:T(8,128)S(1)}, f32[3,32,128]{2,1,0:T(8,128)S(1)}, u32[]{:S(2)}, u32[]{:S(2)}) collective-permute-start(f32[3,32,128]{2,1,0:T(8,128)S(1)} %get-tuple-element.12), channel_id=1, source_target_pairs={{1,2},{2,1},{0,3},{3,0},{5,6},{6,5},{4,7},{7,4},{9,10},{10,9},{8,1... | collective-permute-start | bytes 147464 | tf_op jit(solution)/shard_map/ppermute | solution.py:581
  17.3 0.0 collective-permute-done.3.za_ref
  17.3 2.0 %collective-permute-done.4.zb_ref = f32[3,32,128]{2,1,0:T(8,128)S(1)} collective-permute-done((f32[3,32,128]{2,1,0:T(8,128)S(1)}, f32[3,32,128]{2,1,0:T(8,128)S(1)}, u32[]{:S(2)}, u32[]{:S(2)}) %collective-permute-start.4) | collective-permute-done | bytes 49184 | tf_op jit(solution)/shard_map/ppermute | solution.py:581
  19.3 1.8 %shard_map.18 = (f32[20,32,256]{2,1,0:T(8,128)S(1)}, f32[20,32,256]{2,1,0:T(8,128)S(1)}, f32[20,32,256]{2,1,0:T(8,128)S(1)}, f32[8,8,8,128]{3,2,1,0:T(8,128)S(1)}) custom-call(f32[32,16,128]{2,1,0:T(8,128)S(1)} %copy-done, f32[8,16,128]{2,1,0:T(8,128)S(1)} %collective-permute-done.xh_ref, f32[40,8,128]{2,1,0:T(8,128)S(1)} %collective-permute-done.1.ya_ref, ...), custom_call_target="tpu_custom_call" | custom-call | tf_op jit(solution)/shard_map/pallas_call | solution.py:584
  21.1 14.4 %all_to_all.5.refs_0_ = f32[8,8,8,128]{3,2,1,0:T(8,128)S(1)} all-to-all(f32[8,8,8,128]{3,2,1,0:T(8,128)S(1)} %get-tuple-element.13), channel_id=1, replica_groups=mesh['gx'=2,'gy'=4,'gz'=4] {'gx','gy'}, dimensions={0} | all-to-all | bytes 524288 | tf_op jit(solution)/shard_map/all_to_all | solution.py:590
  35.5 1.5 %collective-permute-start.5 = (f32[8,8,8,128]{3,2,1,0:T(8,128)S(1)}, f32[8,8,8,128]{3,2,1,0:T(8,128)S(1)}, u32[]{:S(2)}, u32[]{:S(2)}) collective-permute-start(f32[8,8,8,128]{3,2,1,0:T(8,128)S(1)} %all_to_all.5.refs_0_), channel_id=1, source_target_pairs={{0,2},{1,3},{2,0},{3,1},{4,6},{5,7},{6,4},{7,5},{8,10},{9,11},{10,... | collective-permute-start | bytes 786440 | tf_op jit(solution)/shard_map/ppermute | solution.py:591
  37.0 0.0 collective-permute-start.6
  37.0 5.2 %collective-permute-done.5.refs_1_ = f32[8,8,8,128]{3,2,1,0:T(8,128)S(1)} collective-permute-done((f32[8,8,8,128]{3,2,1,0:T(8,128)S(1)}, f32[8,8,8,128]{3,2,1,0:T(8,128)S(1)}, u32[]{:S(2)}, u32[]{:S(2)}) %collective-permute-start.5) | collective-permute-done | bytes 262176 | tf_op jit(solution)/shard_map/ppermute | solution.py:591
  42.2 0.0 collective-permute-start.7
  42.2 0.0 collective-permute-done.6.refs_2_
  42.2 1.5 %collective-permute-done.7.refs_3_ = f32[8,8,8,128]{3,2,1,0:T(8,128)S(1)} collective-permute-done((f32[8,8,8,128]{3,2,1,0:T(8,128)S(1)}, f32[8,8,8,128]{3,2,1,0:T(8,128)S(1)}, u32[]{:S(2)}, u32[]{:S(2)}) %collective-permute-start.7) | collective-permute-done | bytes 262176 | tf_op jit(solution)/shard_map/ppermute | solution.py:593
  43.8 11.9 %shard_map.19 = f32[32,16,128]{2,1,0:T(8,128)} custom-call(f32[8,8,8,128]{3,2,1,0:T(8,128)S(1)} %all_to_all.5.refs_0_, f32[8,8,8,128]{3,2,1,0:T(8,128)S(1)} %collective-permute-done.5.refs_1_, f32[8,8,8,128]{3,2,1,0:T(8,128)S(1)} %collective-permute-done.6.refs_2_, f32[8,8,8,128]{3,2,1,0:T(8,128)S(1)} %collective-permute-done.7.refs_3_, ...), custom_call_target="tpu_custom_call" | custom-call | tf_op jit(solution)/shard_map/pallas_call | solution.py:605
  (2 shorter events, 0.0 us)
Async XLA Ops:
  0.8 5.2 %collective-permute-start = (f32[8,16,128]{2,1,0:T(8,128)S(1)}, f32[8,16,128]{2,1,0:T(8,128)S(1)}, u32[]{:S(2)}, u32[]{:S(2)}) collective-permute-start(f32[8,16,128]{2,1,0:T(8,128)S(1)} %constant_dynamic-slice_fusion.2), channel_id=1, source_target_pairs={{0,16},{16,0},{1,17},{17,1},{2,18},{18,2},{3,19},{19,3},{4,20},{20... | collective-permute-start | bytes 196616 | tf_op jit(solution)/shard_map/ppermute | solution.py:561
  6.1 9.1 %copy-start = (f32[32,16,128]{2,1,0:T(8,128)S(1)}, f32[32,16,128]{2,1,0:T(8,128)}, u32[]{:S(2)}) copy-start(f32[32,16,128]{2,1,0:T(8,128)} %own_ref.3) | copy-start | bytes 786436
  6.1 5.8 %collective-permute-start.2 = (f32[40,8,128]{2,1,0:T(8,128)S(1)}, f32[40,8,128]{2,1,0:T(8,128)S(1)}, u32[]{:S(2)}, u32[]{:S(2)}) collective-permute-start(f32[40,8,128]{2,1,0:T(8,128)S(1)} %get-tuple-element.17), channel_id=1, source_target_pairs={{4,8},{8,4},{5,9},{9,5},{6,10},{10,6},{7,11},{11,7},{20,24},{24,20... | collective-permute-start | bytes 491528 | tf_op jit(solution)/shard_map/ppermute | solution.py:567
  6.9 8.3 %collective-permute-start.1 = (f32[40,8,128]{2,1,0:T(8,128)S(1)}, f32[40,8,128]{2,1,0:T(8,128)S(1)}, u32[]{:S(2)}, u32[]{:S(2)}) collective-permute-start(f32[40,8,128]{2,1,0:T(8,128)S(1)} %get-tuple-element.18), channel_id=1, source_target_pairs={{0,4},{4,0},{8,12},{12,8},{1,5},{5,1},{9,13},{13,9},{2,6},{6,2},{1... | collective-permute-start | bytes 491528 | tf_op jit(solution)/shard_map/ppermute | solution.py:566
  15.6 1.7 %collective-permute-start.3 = (f32[3,32,128]{2,1,0:T(8,128)S(1)}, f32[3,32,128]{2,1,0:T(8,128)S(1)}, u32[]{:S(2)}, u32[]{:S(2)}) collective-permute-start(f32[3,32,128]{2,1,0:T(8,128)S(1)} %get-tuple-element.11), channel_id=1, source_target_pairs={{0,1},{1,0},{2,3},{3,2},{4,5},{5,4},{6,7},{7,6},{8,9},{9,8},{10,11... | collective-permute-start | bytes 147464 | tf_op jit(solution)/shard_map/ppermute | solution.py:580
  15.7 3.6 %collective-permute-start.4 = (f32[3,32,128]{2,1,0:T(8,128)S(1)}, f32[3,32,128]{2,1,0:T(8,128)S(1)}, u32[]{:S(2)}, u32[]{:S(2)}) collective-permute-start(f32[3,32,128]{2,1,0:T(8,128)S(1)} %get-tuple-element.12), channel_id=1, source_target_pairs={{1,2},{2,1},{0,3},{3,0},{5,6},{6,5},{4,7},{7,4},{9,10},{10,9},{8,1... | collective-permute-start | bytes 147464 | tf_op jit(solution)/shard_map/ppermute | solution.py:581
  35.5 6.7 %collective-permute-start.5 = (f32[8,8,8,128]{3,2,1,0:T(8,128)S(1)}, f32[8,8,8,128]{3,2,1,0:T(8,128)S(1)}, u32[]{:S(2)}, u32[]{:S(2)}) collective-permute-start(f32[8,8,8,128]{3,2,1,0:T(8,128)S(1)} %all_to_all.5.refs_0_), channel_id=1, source_target_pairs={{0,2},{1,3},{2,0},{3,1},{4,6},{5,7},{6,4},{7,5},{8,10},{9,11},{10,... | collective-permute-start | bytes 786440 | tf_op jit(solution)/shard_map/ppermute | solution.py:591
  37.0 5.2 %collective-permute-start.6 = (f32[8,8,8,128]{3,2,1,0:T(8,128)S(1)}, f32[8,8,8,128]{3,2,1,0:T(8,128)S(1)}, u32[]{:S(2)}, u32[]{:S(2)}) collective-permute-start(f32[8,8,8,128]{3,2,1,0:T(8,128)S(1)} %all_to_all.5.refs_0_), channel_id=1, source_target_pairs={{0,1},{1,0},{2,3},{3,2},{4,5},{5,4},{6,7},{7,6},{8,9},{9,8},{10,11... | collective-permute-start | bytes 786440 | tf_op jit(solution)/shard_map/ppermute | solution.py:592
  42.2 1.5 %collective-permute-start.7 = (f32[8,8,8,128]{3,2,1,0:T(8,128)S(1)}, f32[8,8,8,128]{3,2,1,0:T(8,128)S(1)}, u32[]{:S(2)}, u32[]{:S(2)}) collective-permute-start(f32[8,8,8,128]{3,2,1,0:T(8,128)S(1)} %collective-permute-done.5.refs_1_), channel_id=1, source_target_pairs={{0,1},{1,0},{2,3},{3,2},{4,5},{5,4},{6,7},{7,6},{8,9},{9,8},{10,11... | collective-permute-start | bytes 786440 | tf_op jit(solution)/shard_map/ppermute | solution.py:593

commit v3 on v0

--- a/solution.py
+++ b/solution.py
@@ -1,6 +1,10 @@
+import functools
+
 import jax
 import jax.numpy as jnp
 from jax import lax
+from jax.experimental import pallas as pl
+from jax.experimental.pallas import tpu as pltpu
 from jax.sharding import PartitionSpec as P
 
 LEVELS = 7
@@ -159,7 +163,555 @@
     return field
 
 
+def pairs(count, first):
+    swaps = []
+    for i in range(first, count - 1, 2):
+        swaps += [(i, i + 1), (i + 1, i)]
+    return swaps
+
+
+def flips(count, bit):
+    return [(i, i ^ bit) for i in range(count)]
+
+
+def lanes_of(shape):
+    return lax.broadcasted_iota(jnp.int32, shape, len(shape) - 1)
+
+
+def rows_of(shape):
+    return lax.broadcasted_iota(jnp.int32, shape, len(shape) - 2)
+
+
+LANES = 128
+PAD = 8
+
+
+def odd_of(shape):
+    return ((lanes_of(shape) + rows_of(shape)) & 1) == 1
+
+
+def exact_dot(a, b):
+    return jnp.dot(a, b, precision=lax.Precision.HIGHEST, preferred_element_type=jnp.float32)
+
+
+def window(ref, at, column, count, start=0, shift=0):
+    if isinstance(start, int):
+        return ref[at, column, PAD + start + shift : PAD + start + shift + count, :]
+    first = start + (PAD + shift)
+    if shift == 0:
+        first = pl.multiple_of(first, 8)
+    return ref[at, column, pl.ds(first, count), :]
+
+
+def clear_pads(ref):
+    edge = jnp.zeros((PAD, LANES), jnp.float32)
+    for at in range(ref.shape[0]):
+        for column in range(ref.shape[1]):
+            ref[at, column, :PAD, :] = edge
+            ref[at, column, ref.shape[2] - PAD :, :] = edge
+
+
+def block_sums(ref, at, rows):
+    lane = lanes_of((rows, LANES))
+    values = [window(ref, at, column, rows) for column in range(2)]
+    lefts = [pltpu.roll(value, 1, 1) for value in values]
+    rights = [pltpu.roll(value, LANES - 1, 1) for value in values]
+    sums = []
+    for column in range(2):
+        left = jnp.where(lane == 0, lefts[1 - column], lefts[column])
+        right = jnp.where(lane == LANES - 1, rights[1 - column], rights[column])
+        sides = window(ref, at, column, rows, shift=-1) + window(ref, at, column, rows, shift=1)
+        sums.append(values[column] + sides + (1.0 + rsd_beta) * (left + right))
+    return sums
+
+
+def block_totals(ref, at, rows, own, odd, to_red, at_low, at_high):
+    slots = ref.shape[0]
+    totals = []
+    for column, total in enumerate(block_sums(ref, at, rows)):
+        before = window(ref, (at - 1) % slots, column, rows)
+        after = window(ref, (at + 1) % slots, column, rows)
+        if at == 0:
+            before = jnp.where(at_low, 0.0, before)
+        if at == own - 1:
+            after = jnp.where(at_high, 0.0, after)
+        totals.append(total + (jnp.where(odd, after, before) if to_red else jnp.where(odd, before, after)))
+    return totals
+
+
+def block_mask(own, halo):
+    ny, nz = own
+    shape = (ny + 2 * halo, LANES)
+    row = rows_of(shape) - halo + lax.axis_index("gy") * ny
+    inside_y = (row >= 0) & (row < ny * lax.axis_size("gy"))
+    masks = []
+    for column in range(2):
+        lane = lanes_of(shape)
+        if column:
+            lane = jnp.where(lane < halo, lane + LANES, lane - LANES)
+        lane = lane + lax.axis_index("gz") * nz
+        inside = inside_y & (lane >= 0) & (lane < nz * lax.axis_size("gz"))
+        masks.append(jnp.where(inside, 1.0 / centre, 0.0))
+    return masks
+
+
+def block_plane(at, nx, own_ref, xh_ref, ya_ref, yb_ref, even_y):
+    a, b = ya_ref[at], yb_ref[at]
+    middle = own_ref[at] if at < nx else xh_ref[at - nx]
+    low = jnp.where(even_y, b, a)
+    high = jnp.where(even_y, a, b)
+    return jnp.concatenate([low, middle, high], axis=0)
+
+
+def pack_kernel(halo, own_ref, xh_ref, ya_ref, yb_ref, za_ref, zb_ref):
+    even_y = lax.axis_index("gy") % 2 == 0
+    even_z = lax.axis_index("gz") % 2 == 0
+    nx, ny, nz = own_ref.shape
+    groups = nz // halo
+    shape = (ny + 2 * halo, nz)
+    group = lanes_of(shape) // halo
+    for j in range(za_ref.shape[0]):
+        last = jnp.zeros(shape, jnp.float32)
+        first = jnp.zeros(shape, jnp.float32)
+        for k in range(groups):
+            at = j * groups + k
+            if at >= nx + halo:
+                break
+            plane = block_plane(at, nx, own_ref, xh_ref, ya_ref, yb_ref, even_y)
+            last = jnp.where(group == k, pltpu.roll(plane, (halo * k + halo) % nz, 1), last)
+            first = jnp.where(group == k, pltpu.roll(plane, halo * k, 1), first)
+        za_ref[j] = jnp.where(even_z, last, first)
+        zb_ref[j] = jnp.where(even_z, first, last)
+
+
+def pre_kernel(
+    halo, own_ref, xh_ref, ya_ref, yb_ref, za_ref, zb_ref,
+    gr_ref, gb_ref, dark_ref, send_ref,
+    fr_ref, fb_ref, red_ref, black_ref, rest_ref,
+):
+    even_y = lax.axis_index("gy") % 2 == 0
+    even_z = lax.axis_index("gz") % 2 == 0
+    nx, ny, nz = own_ref.shape
+    count, _, rows, _ = gr_ref.shape
+    own = nx // 2
+    groups = nz // halo
+    shape = (rows, LANES)
+    odd = odd_of(shape)
+    masks = block_mask((ny, nz), halo)
+    lane = lanes_of(shape)
+    low, high = lane < halo, lane >= nz - halo
+    inner = slice(halo, halo + ny)
+    body = slice(PAD, PAD + rows)
+    here = lax.axis_index("gx")
+    ends = (here == 0, here == lax.axis_size("gx") - 1)
+    clear_pads(red_ref)
+    clear_pads(black_ref)
+
+    def columns(at):
+        j, k = at // groups, at % groups
+        a, b = za_ref[j], zb_ref[j]
+        left = jnp.where(even_z, b, a)
+        right = jnp.where(even_z, a, b)
+        right = pltpu.roll(right, (nz - halo * k) % nz, 1)
+        left = pltpu.roll(left, (2 * nz - halo - halo * k) % nz, 1)
+        sides = jnp.where(low, right, jnp.where(high, left, 0.0))
+        return block_plane(at, nx, own_ref, xh_ref, ya_ref, yb_ref, even_y), sides
+
+    for at in range(count):
+        first, second = columns(2 * at), columns(2 * at + 1)
+        for c in range(2):
+            red = jnp.where(odd, second[c], first[c])
+            black = jnp.where(odd, first[c], second[c])
+            if c == 0 and at < own:
+                fr_ref[at], fb_ref[at] = red[inner], black[inner]
+            red = masks[c] * red
+            gr_ref[at, c], gb_ref[at, c] = red, masks[c] * black
+            red_ref[at, c, body, :] = red
+    for at in range(count):
+        totals = block_totals(red_ref, at, rows, own, odd, False, *ends)
+        for c in range(2):
+            black_ref[at, c, body, :] = gb_ref[at, c] + masks[c] * totals[c]
+    for at in range(count):
+        totals = block_totals(black_ref, at, rows, own, odd, True, *ends)
+        for c in range(2):
+            red_ref[at, c, body, :] = gr_ref[at, c] + masks[c] * totals[c]
+    for at in range(count):
+        totals = block_totals(red_ref, at, rows, own, odd, False, *ends)
+        for c in range(2):
+            value = gb_ref[at, c] + masks[c] * totals[c]
+            black_ref[at, c, body, :] = value
+            dark_ref[at, c] = value
+            if c == 0 and at < own:
+                rest_ref[at] = fb_ref[at] + totals[c][inner] - centre * value[inner]
+    for at in range(own):
+        total = block_totals(black_ref, at, rows, own, odd, True, *ends)[0]
+        left_over = fr_ref[at] + total[inner] - centre * red_ref[at, 0, PAD + halo : PAD + halo + ny, :]
+        rest_ref[at] = rest_ref[at] + left_over
+    half, quarter = ny // 2, nz // 4
+    pairs_y = rest_ref[:, pl.ds(0, half, stride=2), :] + rest_ref[:, pl.ds(1, half, stride=2), :]
+    column = lanes_of((nz, nz))
+    target = 2 * (column % quarter) + (column // quarter) % 2
+    weight = jnp.where(rows_of((nz, nz)) // 2 == target, 0.5, 0.0)
+    coarse = exact_dot(pairs_y.reshape(own * half, nz), weight).reshape(own, half, nz)
+    part = lanes_of((half, nz)) // quarter
+    pick = (((rows_of((half, nz)) + part) & 1) == 1) ^ (part >= 2)
+    for at in range(own // 2):
+        packed = jnp.where(pick, coarse[2 * at + 1], coarse[2 * at])
+        for member in range(send_ref.shape[0]):
+            send_ref[member, at] = packed
+
+
+def small_shapes(whole):
+    return [max(whole[0] >> (level + 1), 1) for level in range(2, LEVELS)]
+
+
+def solve_kernel(halo, whole, *refs):
+    here_ref, flip_ref, next_ref, both_ref, gr_ref, gb_ref, dark_ref, out_ref = refs[:8]
+    fr1, fb1, red1, black1, rest1, tall_ref, red_ref, work_ref = refs[8:16]
+    small = [refs[16 + 4 * i : 20 + 4 * i] for i in range(LEVELS - 2)]
+    gx, gy, gz = (lax.axis_index(axis) for axis in ("gx", "gy", "gz"))
+    weight_z = 1.0 + rsd_beta
+    share = 1.0 / centre
+    for ref in (red1, black1, red_ref, work_ref):
+        clear_pads(ref)
+    for level in small:
+        for ref in level[2:]:
+            clear_pads(ref)
+
+    members, slots, block_rows, _ = here_ref.shape
+    count_y = lax.axis_size("gy")
+    count1, _, rows1, _ = fr1.shape
+    quarter = LANES // 4
+    sources = [
+        (ref, jnp.bitwise_xor(gz, bits))
+        for ref, bits in ((here_ref, 0), (flip_ref, 2), (next_ref, 1), (both_ref, 3))
+    ]
+    group = lanes_of((block_rows, LANES)) // quarter
+    theirs = [group == which for _, which in sources]
+    for part, target in enumerate((fr1, fr1, fb1, fb1)):
+        turns = [quarter * jnp.bitwise_and(which - part, 3) for _, which in sources]
+        for member in range(members):
+            i, j = member // count_y, member % count_y
+            for at in range(slots):
+                value = None
+                for (ref, _), mine, turn in zip(sources, theirs, turns):
+                    moved = pltpu.roll(ref[member, at], turn, 1)
+                    value = moved if value is None else jnp.where(mine, moved, value)
+                rows = slice(j * block_rows, (j + 1) * block_rows)
+                target[i * slots + at, part % 2, rows, :] = value
+
+    def fold_total(ref, at, e, start, count, low, high, odds, to_red):
+        lane = lanes_of((count, LANES))
+        value, other = window(ref, at, e, count, start), window(ref, at, 1 - e, count, start)
+        sides = window(ref, at, e, count, start, -1) + window(ref, at, e, count, start, 1)
+        if e == 0:
+            near = jnp.where(lane == 0, 0.0, pltpu.roll(other, 1, 1))
+        else:
+            near = jnp.where(lane == LANES - 1, 0.0, pltpu.roll(other, LANES - 1, 1))
+        before = 0.0 if low is True else window(ref, at - 1, e, count, start)
+        after = 0.0 if high is True else window(ref, at + 1, e, count, start)
+        if not isinstance(low, bool):
+            before = jnp.where(low, 0.0, window(ref, jnp.maximum(at - 1, 0), e, count, start))
+        if not isinstance(high, bool):
+            after = jnp.where(high, 0.0, window(ref, jnp.minimum(at + 1, count1 - 1), e, count, start))
+        beside = jnp.where(odds[e], after, before) if to_red else jnp.where(odds[e], before, after)
+        return value + sides + beside + weight_z * (other + near)
+
+    def fold_odds(count):
+        row = rows_of((count, LANES))
+        return [((row + e) & 1) == 1 for e in range(2)]
+
+    odds = fold_odds(rows1)
+    body1 = slice(PAD, PAD + rows1)
+
+    def down_total(ref, at, e, to_red):
+        return fold_total(ref, at, e, 0, rows1, at == 0, at == count1 - 1, odds, to_red)
+
+    for at in range(count1):
+        for e in range(2):
+            red1[at, e, body1, :] = share * fr1[at, e]
+    for at in range(count1):
+        for e in range(2):
+            black1[at, e, body1, :] = share * (fb1[at, e] + down_total(red1, at, e, False))
+    for at in range(count1):
+        for e in range(2):
+            red1[at, e, body1, :] = share * (fr1[at, e] + down_total(black1, at, e, True))
+    for at in range(count1):
+        left_over = None
+        for e in range(2):
+            total = fb1[at, e] + down_total(red1, at, e, False)
+            value = share * total
+            black1[at, e, body1, :] = value
+            term = total - centre * value
+            left_over = term if left_over is None else left_over + term
+        rest1[at] = left_over
+    for at in range(count1):
+        left_over = rest1[at]
+        for e in range(2):
+            total = fr1[at, e] + down_total(black1, at, e, True)
+            left_over = left_over + (total - centre * window(red1, at, e, rows1))
+        rest1[at] = left_over
+    rows2 = rows1 // 2
+    shape2 = (rows2, LANES)
+    row2, lane2 = rows_of(shape2), lanes_of(shape2)
+    odd2 = odd_of(shape2)
+    planes = [
+        0.5 * (rest1[at, pl.ds(0, rows2, stride=2), :] + rest1[at, pl.ds(1, rows2, stride=2), :])
+        for at in range(count1)
+    ]
+
+    body2 = slice(PAD, PAD + rows2)
+
+    def grid_of(index):
+        step = 1 << index
+        return ((row2 & (step - 1)) == 0) & ((lane2 & (step - 1)) == 0)
+
+    def odd_at(index):
+        return (((row2 >> index) + (lane2 >> index)) & 1) == 1
+
+    def along(value, step):
+        left = jnp.where(lane2 < step, 0.0, pltpu.roll(value, step, 1))
+        right = jnp.where(lane2 >= LANES - step, 0.0, pltpu.roll(value, LANES - step, 1))
+        return weight_z * (left + right)
+
+    def small_total(index, ref, at, odd, to_red):
+        step = 1 << index
+        value = ref[at, 0, body2, :]
+        total = value + along(value, step)
+        total = total + (
+            ref[at, 0, PAD - step : PAD - step + rows2, :] + ref[at, 0, PAD + step : PAD + step + rows2, :]
+        )
+        slots = ref.shape[0]
+        if slots == 1:
+            return total
+        before = ref[at - 1, 0, body2, :] if at > 0 else 0.0
+        after = ref[at + 1, 0, body2, :] if at < slots - 1 else 0.0
+        return total + (jnp.where(odd, after, before) if to_red else jnp.where(odd, before, after))
+
+    def small_sweeps(index, start):
+        fr, fb, red, black = small[index]
+        mask, odd = jnp.where(grid_of(index), share, 0.0), odd_at(index)
+        slots = fr.shape[0]
+        for step in range(2):
+            for at in range(slots):
+                source = fr[at]
+                if not (start and step == 0):
+                    source = source + small_total(index, black, at, odd, True)
+                red[at, 0, body2, :] = mask * source
+            for at in range(slots):
+                black[at, 0, body2, :] = mask * (fb[at] + small_total(index, red, at, odd, False))
+
+    last = len(small) - 1
+    for index in range(last):
+        fr, fb, red, black = small[index]
+        slots, odd, step = fr.shape[0], odd_at(index), 1 << index
+        if len(planes) == 2 * slots:
+            for at in range(slots):
+                p, q = planes[2 * at], planes[2 * at + 1]
+                fr[at], fb[at] = jnp.where(odd, q, p), jnp.where(odd, p, q)
+        small_sweeps(index, True)
+        planes = []
+        for at in range(slots):
+            first = fb[at] + small_total(index, red, at, odd, False) - centre * black[at, 0, body2, :]
+            second = fr[at] + small_total(index, black, at, odd, True) - centre * red[at, 0, body2, :]
+            total = first + second
+            total = total + pltpu.roll(total, rows2 - step, 0)
+            planes.append(0.5 * (total + pltpu.roll(total, LANES - step, 1)))
+
+    step = 1 << last
+    grid = grid_of(last) & (row2 == 0)
+    odd = ((lane2 >> last) & 1) == 1
+    mask_red = jnp.where(grid & jnp.logical_not(odd), share, 0.0)
+    mask_black = jnp.where(grid & odd, share, 0.0)
+    source = planes[0]
+    light, dark = None, None
+    for sweep in range(CSWEEPS):
+        light = mask_red * (source if dark is None else source + along(dark, step))
+        dark = mask_black * (source + along(light, step))
+    fields = [light + dark]
+
+    for index in reversed(range(last)):
+        _, _, red, black = small[index]
+        slots, odd, step = red.shape[0], odd_at(index), 1 << index
+        for at in range(slots):
+            spread = fields[at] + pltpu.roll(fields[at], step, 1)
+            spread = spread + pltpu.roll(spread, step, 0)
+            black[at, 0, body2, :] = black[at, 0, body2, :] + spread
+        small_sweeps(index, False)
+        fields = []
+        for at in range(slots):
+            r, b = red[at, 0, body2, :], black[at, 0, body2, :]
+            fields += [jnp.where(odd, b, r), jnp.where(odd, r, b)]
+
+    for at in range(count1):
+        for start in range(2):
+            rest1[at, pl.ds(start, rows2, stride=2), :] = fields[at]
+    for at in range(count1):
+        for e in range(2):
+            black1[at, e, body1, :] = window(black1, at, e, rows1) + rest1[at]
+    nx, ny, nz = out_ref.shape
+    own = nx // 2
+    part_slots = min(own // 2 + 3, count1)
+    part_rows = min(ny // 2 + 16, rows1)
+    slot0 = jnp.where(gx == 0, 0, count1 - part_slots)
+    row0 = pl.multiple_of(jnp.clip(gy * (ny // 2) - 8, 0, rows1 - part_rows), 8)
+    odds = fold_odds(part_rows)
+
+    def up_total(ref, at, e, to_red):
+        low = gx == 0 if at == 0 else False
+        high = gx != 0 if at == part_slots - 1 else False
+        return fold_total(ref, slot0 + at, e, row0, part_rows, low, high, odds, to_red)
+
+    def up_half(target, other, sources, to_red):
+        for at in range(part_slots):
+            for e in range(2):
+                source = sources[slot0 + at, e, pl.ds(row0, part_rows), :]
+                value = share * (source + up_total(other, at, e, to_red))
+                target[slot0 + at, e, pl.ds(pl.multiple_of(row0 + PAD, 8), part_rows), :] = value
+
+    for sweep in range(2):
+        up_half(red1, black1, fr1, True)
+        up_half(black1, red1, fb1, False)
+
+    count, _, rows, _ = dark_ref.shape
+    half = rows // 2
+    odds = fold_odds(half)
+    row = gy * (ny // 2) + (PAD - halo // 2)
+    for at in range(count):
+        if at < own:
+            slot = gx * (own // 2) + at // 2
+        else:
+            slot = jnp.where(gx == 0, own // 2, own // 2 - (count - own) // 2) + (at - own) // 2
+        for e in range(2):
+            r, b = red1[slot, e, pl.ds(row, half), :], black1[slot, e, pl.ds(row, half), :]
+            plane = jnp.where(odds[e], r, b) if at % 2 else jnp.where(odds[e], b, r)
+            tall_ref[at, :, e * LANES : (e + 1) * LANES] = plane
+    shape = (2 * LANES, 2 * LANES)
+    z = lanes_of(shape)
+    z = jnp.where(z < 2 * LANES - halo, z, z - 2 * LANES) + gz * nz
+    line = rows_of(shape)
+    line = jnp.where(line < LANES, 2 * line, 2 * (line - LANES) + 1)
+    weight = jnp.where(line == lax.shift_right_arithmetic(z, 1), 1.0, 0.0)
+    spread = exact_dot(tall_ref[...].reshape(count * half, 2 * LANES), weight)
+    spread = spread.reshape(count, half, 2 * LANES)
+    for at in range(count):
+        for c in range(2):
+            value = spread[at, :, c * LANES : (c + 1) * LANES]
+            for start in range(2):
+                work_ref[at, c, pl.ds(PAD + start, half, stride=2), :] = value
+    body = slice(PAD, PAD + rows)
+    for at in range(count):
+        for c in range(2):
+            work_ref[at, c, body, :] = work_ref[at, c, body, :] + dark_ref[at, c]
+    odd = odd_of((rows, LANES))
+    masks = block_mask((ny, nz), halo)
+    ends = (gx == 0, gx == lax.axis_size("gx") - 1)
+    for sweep in range(2):
+        for at in range(count):
+            totals = block_totals(work_ref, at, rows, own, odd, True, *ends)
+            for c in range(2):
+                red_ref[at, c, body, :] = gr_ref[at, c] + masks[c] * totals[c]
+        for at in range(count if sweep == 0 else own):
+            totals = block_totals(red_ref, at, rows, own, odd, False, *ends)
+            for c in range(2 if sweep == 0 else 1):
+                work_ref[at, c, body, :] = gb_ref[at, c] + masks[c] * totals[c]
+    inner = slice(PAD + halo, PAD + halo + ny)
+    odd = odd_of((ny, nz))
+    for at in range(own):
+        r, b = red_ref[at, 0, inner, :], work_ref[at, 0, inner, :]
+        out_ref[2 * at] = jnp.where(odd, b, r)
+        out_ref[2 * at + 1] = jnp.where(odd, r, b)
+
+
+def vmem(number):
+    return [pl.BlockSpec(memory_space=pltpu.VMEM)] * number
+
+
+def struct(*shape):
+    return jax.ShapeDtypeStruct(shape, jnp.float32)
+
+
+def scratch(*shape):
+    return pltpu.VMEM(shape, jnp.float32)
+
+
+HALO = 8
+
+
+def block_cycle(density):
+    halo = HALO
+    nx, ny, nz = density.shape
+    count_x, count_y, count_z = (lax.axis_size(axis) for axis in ("gx", "gy", "gz"))
+    whole = (nx * count_x, ny * count_y, nz * count_z)
+    gx, gy = lax.axis_index("gx"), lax.axis_index("gy")
+    face = lax.dynamic_slice_in_dim(density, jnp.where(gx == 0, nx - halo, 0), halo, 0)
+    side = lax.ppermute(face, "gx", flips(count_x, 1))
+    tall = jnp.concatenate([density, side], axis=0)
+    even = gy % 2 == 0
+    ya = lax.dynamic_slice_in_dim(tall, jnp.where(even, ny - halo, 0), halo, 1)
+    yb = lax.dynamic_slice_in_dim(tall, jnp.where(even, 0, ny - halo), halo, 1)
+    ya = lax.ppermute(ya, "gy", pairs(count_y, 0))
+    yb = lax.ppermute(yb, "gy", pairs(count_y, 1))
+    rows = ny + 2 * halo
+    planes = nx + halo
+    packs = -(-planes * halo // nz)
+
+    def params(mib):
+        return pltpu.CompilerParams(vmem_limit_bytes=mib * 1024 * 1024)
+
+    za, zb = pl.pallas_call(
+        functools.partial(pack_kernel, halo),
+        out_shape=[struct(packs, rows, nz)] * 2,
+        in_specs=vmem(4), out_specs=vmem(2), compiler_params=params(4),
+    )(density, side, ya, yb)
+    za = lax.ppermute(za, "gz", pairs(count_z, 0))
+    zb = lax.ppermute(zb, "gz", pairs(count_z, 1) + [(0, count_z - 1), (count_z - 1, 0)])
+    members = count_x * count_y
+    slots = (planes // 2, 2, rows, LANES)
+    padded = (planes // 2, 2, rows + 2 * PAD, LANES)
+    gr, gb, black, send = pl.pallas_call(
+        functools.partial(pre_kernel, halo),
+        out_shape=[struct(*slots)] * 3 + [struct(members, nx // 4, ny // 2, nz)],
+        in_specs=vmem(6), out_specs=vmem(4), compiler_params=params(10),
+        scratch_shapes=[scratch(nx // 2, ny, nz)] * 2
+        + [scratch(*padded)] * 2
+        + [scratch(nx // 2, ny, nz)],
+    )(density, side, ya, yb, za, zb)
+    here = lax.all_to_all(send, ("gx", "gy"), 0, 0, tiled=True)
+    flip = lax.ppermute(here, "gz", flips(count_z, 2))
+    beside_here = lax.ppermute(here, "gz", flips(count_z, 1))
+    beside_flip = lax.ppermute(flip, "gz", flips(count_z, 1))
+    count1, rows1, rows2 = whole[0] // 4, whole[1] // 2, whole[1] // 4
+    room = [scratch(count1, 2, rows1, LANES)] * 2
+    room += [scratch(count1, 2, rows1 + 2 * PAD, LANES)] * 2
+    room += [scratch(count1, rows1, LANES), scratch(planes // 2, rows // 2, 2 * LANES)]
+    room += [scratch(*padded)] * 2
+    for count in small_shapes(whole):
+        room += [scratch(count, rows2, LANES)] * 2
+        room += [scratch(count, 1, rows2 + 2 * PAD, LANES)] * 2
+    return pl.pallas_call(
+        functools.partial(solve_kernel, halo, whole),
+        out_shape=struct(nx, ny, nz),
+        in_specs=vmem(7), out_specs=pl.BlockSpec(memory_space=pltpu.VMEM),
+        compiler_params=params(16), scratch_shapes=room,
+    )(here, flip, beside_here, beside_flip, gr, gb, black)
+
+
+def fits_block_cycle(shape):
+    nx, ny, nz = shape
+    count_x, count_y, count_z = (lax.axis_size(axis) for axis in ("gx", "gy", "gz"))
+    whole = (nx * count_x, ny * count_y, nz * count_z)
+    coarsest = [size >> (LEVELS - 1) for size in whole]
+    exact = all(c << (LEVELS - 1) == size for c, size in zip(coarsest, whole))
+    return (
+        exact and coarsest[0] == coarsest[1] == 1 and nz == LANES and ny == 2 * HALO
+        and count_x == 2 and count_z == 4 and count_y % 2 == 0
+    )
+
+
 def on_device(density):
+    if fits_block_cycle(density.shape):
+        return block_cycle(density)
     top = 4
     return shared_cycle(density, 0, top)
 

time: 598 us -> 52.6 us (0.09); the launches traced: 588 us -> 52.3 us
  starting transfers between devices: 244 us -> 11.9 us
  waiting for transfers between devices: 223 us -> 13.3 us
  other arithmetic: 45.3 us -> 0 us
  blocking collectives: 43 us -> 14.4 us
  local copies, waits for them, and re-layouts: 29 us -> 1.85 us
  Pallas kernels: 0 us -> 10.8 us
    ppermute x120 -> x8, starting transfers between devices: 244 us -> 11.9 us  [the longest x1 4.96 us: block_cycle(): ya = lax.ppermute(ya, 'gy', pairs(count_y, 0))]
    ppermute x120 -> x8, waiting for transfers between devices: 223 us -> 13.3 us  [the longest x1 5.21 us: block_cycle(): flip = lax.ppermute(here, 'gz', flips(count_z, 2))]
    all_gather x1 -> x0, blocking collectives: 43 us -> none  [coarse_level(): stack = lax.all_gather(source[None], ('gx', 'gy', 'gz'), axis=0, tiled=True)]
    select_n x54 -> x0, other arithmetic: 24.8 us -> none  [the longest x16 15.7 us: wide_sweep(): extended = jnp.where(red_wide, update, extended)]
    reshape x12 -> x0, local copies, waits for them, and re-layouts: 22.6 us -> none  [the longest x4 21.3 us: restrict(): residue.reshape(shape[0] // 2, 2, shape[1] // 2, 2, shape[2] // 2, 2)]
    all_to_all x0 -> x1, blocking collectives: none -> 14.4 us  [block_cycle(): here = lax.all_to_all(send, ('gx', 'gy'), 0, 0, tiled=True)]
    pallas_call x0 -> x3, Pallas kernels: none -> 10.8 us  [the longest x1 8.71 us: block_cycle(): pl.pallas_call(functools.partial(solve_kernel, halo, whole), out_shape=st...]
    reduce_sum x8 -> x0, other arithmetic: 7.85 us -> none  [restrict(): return jnp.mean(blocks, axis=(1, 3, 5))]
  transfers between devices with their start and end apart: 120 -> 8, of which waited for: 75 -> 5; matrix products, arithmetic and copies ran while one was open for 1% -> 2% of each run, Pallas kernels for 0% -> 0%
where the time goes in v3:
time: 52.6 us; the launch traced here: 52.3 us
  blocking collectives  14.4 us (27%)
  waiting for transfers between devices  13.3 us (25%)
  starting transfers between devices  11.9 us (23%)
  Pallas kernels  10.8 us (21%)
  local copies, waits for them, and re-layouts  1.85 us (4%)
    all_to_all x1, blocking collectives, block_cycle(): here = lax.all_to_all(send, ('gx', 'gy'), 0, 0, tiled=True)  14.4 us
    pallas_call x1, Pallas kernels, block_cycle(): pl.pallas_call(functools.partial(solve_kernel, halo, whole), out_shape=st...  8.71 us
    ppermute x1, waiting for transfers between devices, block_cycle(): flip = lax.ppermute(here, 'gz', flips(count_z, 2))  5.21 us
    ppermute x1, starting transfers between devices, block_cycle(): ya = lax.ppermute(ya, 'gy', pairs(count_y, 0))  4.96 us
    ppermute x1, waiting for transfers between devices, block_cycle(): ya = lax.ppermute(ya, 'gy', pairs(count_y, 0))  3.3 us
    ppermute x1, starting transfers between devices, block_cycle(): side = lax.ppermute(face, 'gx', flips(count_x, 1))  3 us
    ppermute x1, waiting for transfers between devices, block_cycle(): lax.ppermute(zb, 'gz', pairs(count_z, 1) + [(0, count_z - 1), (count_z -...  1.98 us
    pallas_call x1, Pallas kernels, block_cycle(): pl.pallas_call(functools.partial(pre_kernel, halo), out_shape=[struct(*sl...  1.72 us
  transfers between devices with their start and end apart: 8, of which 5 were waited for; matrix products, arithmetic and copies ran while one was open for 2% of the time, Pallas kernels for 0%

profile of v3, /device:TPU:0, one launch (start us, length us, event | category | flops | bytes accessed | tf_op | source)
XLA Modules:
  0.0 52.3 jit_solution(1613154901041881498)
XLA Ops:
  0.0 0.8 %constant_dynamic-slice_fusion.2 = f32[8,16,128]{2,1,0:T(8,128)S(1)} fusion(f32[32,16,128]{2,1,0:T(8,128)} %own_ref.3, s32[]{:T(128)S(6)} %select_n.20), kind=kLoop, calls=%fused_computation.4 | loop fusion | bytes 131076 | tf_op jit(solution)/shard_map/dynamic_slice | solution.py:647
  0.8 3.0 %collective-permute-start = (f32[8,16,128]{2,1,0:T(8,128)S(1)}, f32[8,16,128]{2,1,0:T(8,128)S(1)}, u32[]{:S(2)}, u32[]{:S(2)}) collective-permute-start(f32[8,16,128]{2,1,0:T(8,128)S(1)} %constant_dynamic-slice_fusion.2), channel_id=1, source_target_pairs={{0,16},{16,0},{1,17},{17,1},{2,18},{18,2},{3,19},{19,3},{4,20},{20... | collective-permute-start | bytes 196616 | tf_op jit(solution)/shard_map/ppermute | solution.py:648
  3.8 1.0 %constant_dynamic-update-slice_fusion.1 = f32[40,16,128]{2,1,0:T(8,128)S(1)} fusion(f32[32,16,128]{2,1,0:T(8,128)} %own_ref.3), kind=kLoop, calls=%fused_computation.1 | loop fusion | bytes 524288
  4.8 1.3 %collective-permute-done.xh_ref = f32[8,16,128]{2,1,0:T(8,128)S(1)} collective-permute-done((f32[8,16,128]{2,1,0:T(8,128)S(1)}, f32[8,16,128]{2,1,0:T(8,128)S(1)}, u32[]{:S(2)}, u32[]{:S(2)}) %collective-permute-start) | collective-permute-done | bytes 65568 | tf_op jit(solution)/shard_map/ppermute | solution.py:648
  6.1 0.0 copy-start
  6.1 0.8 %collective-permute-start.2 = (f32[40,8,128]{2,1,0:T(8,128)S(1)}, f32[40,8,128]{2,1,0:T(8,128)S(1)}, u32[]{:S(2)}, u32[]{:S(2)}) collective-permute-start(f32[40,8,128]{2,1,0:T(8,128)S(1)} %get-tuple-element.17), channel_id=1, source_target_pairs={{4,8},{8,4},{5,9},{9,5},{6,10},{10,6},{7,11},{11,7},{20,24},{24,20... | collective-permute-start | bytes 491528 | tf_op jit(solution)/shard_map/ppermute | solution.py:654
  6.9 5.0 %collective-permute-start.1 = (f32[40,8,128]{2,1,0:T(8,128)S(1)}, f32[40,8,128]{2,1,0:T(8,128)S(1)}, u32[]{:S(2)}, u32[]{:S(2)}) collective-permute-start(f32[40,8,128]{2,1,0:T(8,128)S(1)} %get-tuple-element.18), channel_id=1, source_target_pairs={{0,4},{4,0},{8,12},{12,8},{1,5},{5,1},{9,13},{13,9},{2,6},{6,2},{1... | collective-permute-start | bytes 491528 | tf_op jit(solution)/shard_map/ppermute | solution.py:653
  11.9 0.0 collective-permute-done.2.yb_ref
  11.9 3.3 %collective-permute-done.1.ya_ref = f32[40,8,128]{2,1,0:T(8,128)S(1)} collective-permute-done((f32[40,8,128]{2,1,0:T(8,128)S(1)}, f32[40,8,128]{2,1,0:T(8,128)S(1)}, u32[]{:S(2)}, u32[]{:S(2)}) %collective-permute-start.1) | collective-permute-done | bytes 163872 | tf_op jit(solution)/shard_map/ppermute | solution.py:653
  15.2 0.0 copy-done
  15.2 0.4 shard_map.17
  15.6 0.1 collective-permute-start.3
  15.7 1.6 %collective-permute-start.4 = (f32[3,32,128]{2,1,0:T(8,128)S(1)}, f32[3,32,128]{2,1,0:T(8,128)S(1)}, u32[]{:S(2)}, u32[]{:S(2)}) collective-permute-start(f32[3,32,128]{2,1,0:T(8,128)S(1)} %get-tuple-element.12), channel_id=1, source_target_pairs={{1,2},{2,1},{0,3},{3,0},{5,6},{6,5},{4,7},{7,4},{9,10},{10,9},{8,1... | collective-permute-start | bytes 147464 | tf_op jit(solution)/shard_map/ppermute | solution.py:668
  17.3 0.0 collective-permute-done.3.za_ref
  17.3 2.0 %collective-permute-done.4.zb_ref = f32[3,32,128]{2,1,0:T(8,128)S(1)} collective-permute-done((f32[3,32,128]{2,1,0:T(8,128)S(1)}, f32[3,32,128]{2,1,0:T(8,128)S(1)}, u32[]{:S(2)}, u32[]{:S(2)}) %collective-permute-start.4) | collective-permute-done | bytes 49184 | tf_op jit(solution)/shard_map/ppermute | solution.py:668
  19.3 1.7 %shard_map.18 = (f32[20,2,32,128]{3,2,1,0:T(8,128)S(1)}, f32[20,2,32,128]{3,2,1,0:T(8,128)S(1)}, f32[20,2,32,128]{3,2,1,0:T(8,128)S(1)}, f32[8,8,8,128]{3,2,1,0:T(8,128)S(1)}) custom-call(f32[32,16,128]{2,1,0:T(8,128)S(1)} %copy-done, f32[8,16,128]{2,1,0:T(8,128)S(1)} %collective-permute-done.xh_ref, f32[40,8,128]{2,1,0:T(8,128)S(1)} %collective-permute-done.1.ya_ref, ...), custom_call_target="tpu_custom_call" | custom-call | tf_op jit(solution)/shard_map/pallas_call | solution.py:672
  21.0 14.4 %all_to_all.5.refs_0_ = f32[8,8,8,128]{3,2,1,0:T(8,128)S(1)} all-to-all(f32[8,8,8,128]{3,2,1,0:T(8,128)S(1)} %get-tuple-element.13), channel_id=1, replica_groups=mesh['gx'=2,'gy'=4,'gz'=4] {'gx','gy'}, dimensions={0} | all-to-all | bytes 524288 | tf_op jit(solution)/shard_map/all_to_all | solution.py:680
  35.4 1.5 %collective-permute-start.5 = (f32[8,8,8,128]{3,2,1,0:T(8,128)S(1)}, f32[8,8,8,128]{3,2,1,0:T(8,128)S(1)}, u32[]{:S(2)}, u32[]{:S(2)}) collective-permute-start(f32[8,8,8,128]{3,2,1,0:T(8,128)S(1)} %all_to_all.5.refs_0_), channel_id=1, source_target_pairs={{0,2},{1,3},{2,0},{3,1},{4,6},{5,7},{6,4},{7,5},{8,10},{9,11},{10,... | collective-permute-start | bytes 786440 | tf_op jit(solution)/shard_map/ppermute | solution.py:681
  36.9 0.0 collective-permute-start.6
  36.9 5.2 %collective-permute-done.5.refs_1_ = f32[8,8,8,128]{3,2,1,0:T(8,128)S(1)} collective-permute-done((f32[8,8,8,128]{3,2,1,0:T(8,128)S(1)}, f32[8,8,8,128]{3,2,1,0:T(8,128)S(1)}, u32[]{:S(2)}, u32[]{:S(2)}) %collective-permute-start.5) | collective-permute-done | bytes 262176 | tf_op jit(solution)/shard_map/ppermute | solution.py:681
  42.1 0.0 collective-permute-start.7
  42.1 0.0 collective-permute-done.6.refs_2_
  42.1 1.5 %collective-permute-done.7.refs_3_ = f32[8,8,8,128]{3,2,1,0:T(8,128)S(1)} collective-permute-done((f32[8,8,8,128]{3,2,1,0:T(8,128)S(1)}, f32[8,8,8,128]{3,2,1,0:T(8,128)S(1)}, u32[]{:S(2)}, u32[]{:S(2)}) %collective-permute-start.7) | collective-permute-done | bytes 262176 | tf_op jit(solution)/shard_map/ppermute | solution.py:683
  43.6 8.7 %shard_map.19 = f32[32,16,128]{2,1,0:T(8,128)} custom-call(f32[8,8,8,128]{3,2,1,0:T(8,128)S(1)} %all_to_all.5.refs_0_, f32[8,8,8,128]{3,2,1,0:T(8,128)S(1)} %collective-permute-done.5.refs_1_, f32[8,8,8,128]{3,2,1,0:T(8,128)S(1)} %collective-permute-done.6.refs_2_, f32[8,8,8,128]{3,2,1,0:T(8,128)S(1)} %collective-permute-done.7.refs_3_, ...), custom_call_target="tpu_custom_call" | custom-call | tf_op jit(solution)/shard_map/pallas_call | solution.py:692
  (2 shorter events, 0.0 us)
Async XLA Ops:
  0.8 5.2 %collective-permute-start = (f32[8,16,128]{2,1,0:T(8,128)S(1)}, f32[8,16,128]{2,1,0:T(8,128)S(1)}, u32[]{:S(2)}, u32[]{:S(2)}) collective-permute-start(f32[8,16,128]{2,1,0:T(8,128)S(1)} %constant_dynamic-slice_fusion.2), channel_id=1, source_target_pairs={{0,16},{16,0},{1,17},{17,1},{2,18},{18,2},{3,19},{19,3},{4,20},{20... | collective-permute-start | bytes 196616 | tf_op jit(solution)/shard_map/ppermute | solution.py:648
  6.1 9.1 %copy-start = (f32[32,16,128]{2,1,0:T(8,128)S(1)}, f32[32,16,128]{2,1,0:T(8,128)}, u32[]{:S(2)}) copy-start(f32[32,16,128]{2,1,0:T(8,128)} %own_ref.3) | copy-start | bytes 786436
  6.1 5.8 %collective-permute-start.2 = (f32[40,8,128]{2,1,0:T(8,128)S(1)}, f32[40,8,128]{2,1,0:T(8,128)S(1)}, u32[]{:S(2)}, u32[]{:S(2)}) collective-permute-start(f32[40,8,128]{2,1,0:T(8,128)S(1)} %get-tuple-element.17), channel_id=1, source_target_pairs={{4,8},{8,4},{5,9},{9,5},{6,10},{10,6},{7,11},{11,7},{20,24},{24,20... | collective-permute-start | bytes 491528 | tf_op jit(solution)/shard_map/ppermute | solution.py:654
  6.9 8.3 %collective-permute-start.1 = (f32[40,8,128]{2,1,0:T(8,128)S(1)}, f32[40,8,128]{2,1,0:T(8,128)S(1)}, u32[]{:S(2)}, u32[]{:S(2)}) collective-permute-start(f32[40,8,128]{2,1,0:T(8,128)S(1)} %get-tuple-element.18), channel_id=1, source_target_pairs={{0,4},{4,0},{8,12},{12,8},{1,5},{5,1},{9,13},{13,9},{2,6},{6,2},{1... | collective-permute-start | bytes 491528 | tf_op jit(solution)/shard_map/ppermute | solution.py:653
  15.6 1.7 %collective-permute-start.3 = (f32[3,32,128]{2,1,0:T(8,128)S(1)}, f32[3,32,128]{2,1,0:T(8,128)S(1)}, u32[]{:S(2)}, u32[]{:S(2)}) collective-permute-start(f32[3,32,128]{2,1,0:T(8,128)S(1)} %get-tuple-element.11), channel_id=1, source_target_pairs={{0,1},{1,0},{2,3},{3,2},{4,5},{5,4},{6,7},{7,6},{8,9},{9,8},{10,11... | collective-permute-start | bytes 147464 | tf_op jit(solution)/shard_map/ppermute | solution.py:667
  15.7 3.6 %collective-permute-start.4 = (f32[3,32,128]{2,1,0:T(8,128)S(1)}, f32[3,32,128]{2,1,0:T(8,128)S(1)}, u32[]{:S(2)}, u32[]{:S(2)}) collective-permute-start(f32[3,32,128]{2,1,0:T(8,128)S(1)} %get-tuple-element.12), channel_id=1, source_target_pairs={{1,2},{2,1},{0,3},{3,0},{5,6},{6,5},{4,7},{7,4},{9,10},{10,9},{8,1... | collective-permute-start | bytes 147464 | tf_op jit(solution)/shard_map/ppermute | solution.py:668
  35.4 6.7 %collective-permute-start.5 = (f32[8,8,8,128]{3,2,1,0:T(8,128)S(1)}, f32[8,8,8,128]{3,2,1,0:T(8,128)S(1)}, u32[]{:S(2)}, u32[]{:S(2)}) collective-permute-start(f32[8,8,8,128]{3,2,1,0:T(8,128)S(1)} %all_to_all.5.refs_0_), channel_id=1, source_target_pairs={{0,2},{1,3},{2,0},{3,1},{4,6},{5,7},{6,4},{7,5},{8,10},{9,11},{10,... | collective-permute-start | bytes 786440 | tf_op jit(solution)/shard_map/ppermute | solution.py:681
  36.9 5.2 %collective-permute-start.6 = (f32[8,8,8,128]{3,2,1,0:T(8,128)S(1)}, f32[8,8,8,128]{3,2,1,0:T(8,128)S(1)}, u32[]{:S(2)}, u32[]{:S(2)}) collective-permute-start(f32[8,8,8,128]{3,2,1,0:T(8,128)S(1)} %all_to_all.5.refs_0_), channel_id=1, source_target_pairs={{0,1},{1,0},{2,3},{3,2},{4,5},{5,4},{6,7},{7,6},{8,9},{9,8},{10,11... | collective-permute-start | bytes 786440 | tf_op jit(solution)/shard_map/ppermute | solution.py:682
  42.1 1.5 %collective-permute-start.7 = (f32[8,8,8,128]{3,2,1,0:T(8,128)S(1)}, f32[8,8,8,128]{3,2,1,0:T(8,128)S(1)}, u32[]{:S(2)}, u32[]{:S(2)}) collective-permute-start(f32[8,8,8,128]{3,2,1,0:T(8,128)S(1)} %collective-permute-done.5.refs_1_), channel_id=1, source_target_pairs={{0,1},{1,0},{2,3},{3,2},{4,5},{5,4},{6,7},{7,6},{8,9},{9,8},{10,11... | collective-permute-start | bytes 786440 | tf_op jit(solution)/shard_map/ppermute | solution.py:683

commit v4 on v3

--- a/solution.py
+++ b/solution.py
@@ -2,6 +2,7 @@
 
 import jax
 import jax.numpy as jnp
+import numpy as np
 from jax import lax
 from jax.experimental import pallas as pl
 from jax.experimental.pallas import tpu as pltpu
@@ -355,24 +356,64 @@
     coarse = exact_dot(pairs_y.reshape(own * half, nz), weight).reshape(own, half, nz)
     part = lanes_of((half, nz)) // quarter
     pick = (((rows_of((half, nz)) + part) & 1) == 1) ^ (part >= 2)
+    turn = quarter * lax.axis_index("gz")
     for at in range(own // 2):
-        packed = jnp.where(pick, coarse[2 * at + 1], coarse[2 * at])
+        packed = pltpu.roll(jnp.where(pick, coarse[2 * at + 1], coarse[2 * at]), turn, 1)
         for member in range(send_ref.shape[0]):
             send_ref[member, at] = packed
 
 
 def small_shapes(whole):
-    return [max(whole[0] >> (level + 1), 1) for level in range(2, LEVELS)]
+    return [whole[0] >> (level + 1) for level in range(2, LEVELS - 2)]
+
+
+def plain_sum(field):
+    padded = np.pad(field, ((0, 0), (1, 1), (1, 1), (1, 1)))
+    inner = slice(1, -1)
+    plane = padded[:, 2:, inner, inner] + padded[:, :-2, inner, inner]
+    plane = plane + padded[:, inner, 2:, inner] + padded[:, inner, :-2, inner]
+    return plane + (1.0 + rsd_beta) * (padded[:, inner, inner, 2:] + padded[:, inner, inner, :-2])
+
+
+def plain_cycle(source, level):
+    parity = np.indices(source.shape[1:]).sum(axis=0) % 2
+    field = np.zeros_like(source)
+
+    def sweeps(field, number):
+        for step in range(2 * number):
+            field = np.where(parity == step % 2, (source + plain_sum(field)) / centre, field)
+        return field
+
+    if level == LEVELS - 1:
+        return sweeps(field, CSWEEPS)
+    field = sweeps(field, 2)
+    rest = source - centre * field + plain_sum(field)
+    nx, ny, nz = source.shape[1:]
+    rest = rest.reshape(-1, nx // 2, 2, ny // 2, 2, nz // 2, 2).sum(axis=(2, 4, 6)) / 2.0
+    coarse = plain_cycle(rest, level + 1)
+    for axis in (1, 2, 3):
+        coarse = np.repeat(coarse, 2, axis)
+    return sweeps(field + coarse, 2)
+
+
+def cycle_matrix(whole):
+    level = LEVELS - 2
+    nx, ny, nz = (size >> level for size in whole)
+    size = nx * ny * 2 * nz
+    unit = np.eye(size).reshape(size, 2 * nz, nx, ny).transpose(0, 2, 3, 1)
+    source = unit.reshape(size, nx, ny, nz, 2).sum(axis=-1) / 2.0
+    result = np.repeat(plain_cycle(source, level), 2, axis=3)
+    return jnp.asarray(result.transpose(0, 3, 1, 2).reshape(size, size), jnp.float32)
 
 
 def solve_kernel(halo, whole, *refs):
-    here_ref, flip_ref, next_ref, both_ref, gr_ref, gb_ref, dark_ref, out_ref = refs[:8]
-    fr1, fb1, red1, black1, rest1, tall_ref, red_ref, work_ref = refs[8:16]
-    small = [refs[16 + 4 * i : 20 + 4 * i] for i in range(LEVELS - 2)]
+    here_ref, flip_ref, next_ref, both_ref, gr_ref, gb_ref, dark_ref, matrix_ref, out_ref = refs[:9]
+    fr1, fb1, red1, black1, rest1, tall_ref, red_ref, work_ref, passing = refs[9:18]
+    small = [refs[18 + 4 * i : 22 + 4 * i] for i in range(LEVELS - 4)]
     gx, gy, gz = (lax.axis_index(axis) for axis in ("gx", "gy", "gz"))
     weight_z = 1.0 + rsd_beta
     share = 1.0 / centre
-    for ref in (red1, black1, red_ref, work_ref):
+    for ref in (red1, black1, red_ref, work_ref, passing):
         clear_pads(ref)
     for level in small:
         for ref in level[2:]:
@@ -387,18 +428,18 @@
         for ref, bits in ((here_ref, 0), (flip_ref, 2), (next_ref, 1), (both_ref, 3))
     ]
     group = lanes_of((block_rows, LANES)) // quarter
-    theirs = [group == which for _, which in sources]
+    held = [jnp.bitwise_and(group - which, 3) for _, which in sources]
     for part, target in enumerate((fr1, fr1, fb1, fb1)):
-        turns = [quarter * jnp.bitwise_and(which - part, 3) for _, which in sources]
+        theirs = [kind == part for kind in held]
         for member in range(members):
             i, j = member // count_y, member % count_y
             for at in range(slots):
-                value = None
-                for (ref, _), mine, turn in zip(sources, theirs, turns):
-                    moved = pltpu.roll(ref[member, at], turn, 1)
-                    value = moved if value is None else jnp.where(mine, moved, value)
+                value = sources[0][0][member, at]
+                for (ref, _), mine in zip(sources[1:], theirs[1:]):
+                    value = jnp.where(mine, ref[member, at], value)
                 rows = slice(j * block_rows, (j + 1) * block_rows)
-                target[i * slots + at, part % 2, rows, :] = value
+                turned = pltpu.roll(value, LANES - quarter * part, 1) if part else value
+                target[i * slots + at, part % 2, rows, :] = turned
 
     def fold_total(ref, at, e, start, count, low, high, odds, to_red):
         lane = lanes_of((count, LANES))
@@ -501,42 +542,59 @@
             for at in range(slots):
                 black[at, 0, body2, :] = mask * (fb[at] + small_total(index, red, at, odd, False))
 
+    def spread_rows(value, step, ref, at):
+        ref[at, 0, body2, :] = value
+        return value + ref[at, 0, PAD - step : PAD - step + rows2, :]
+
     last = len(small) - 1
-    for index in range(last):
+    for index in range(len(small)):
         fr, fb, red, black = small[index]
         slots, odd, step = fr.shape[0], odd_at(index), 1 << index
-        if len(planes) == 2 * slots:
-            for at in range(slots):
-                p, q = planes[2 * at], planes[2 * at + 1]
-                fr[at], fb[at] = jnp.where(odd, q, p), jnp.where(odd, p, q)
+        for at in range(slots):
+            p, q = planes[2 * at], planes[2 * at + 1]
+            fr[at], fb[at] = jnp.where(odd, q, p), jnp.where(odd, p, q)
         small_sweeps(index, True)
-        planes = []
+        totals = []
         for at in range(slots):
             first = fb[at] + small_total(index, red, at, odd, False) - centre * black[at, 0, body2, :]
             second = fr[at] + small_total(index, black, at, odd, True) - centre * red[at, 0, body2, :]
-            total = first + second
-            total = total + pltpu.roll(total, rows2 - step, 0)
-            planes.append(0.5 * (total + pltpu.roll(total, LANES - step, 1)))
-
-    step = 1 << last
-    grid = grid_of(last) & (row2 == 0)
-    odd = ((lane2 >> last) & 1) == 1
-    mask_red = jnp.where(grid & jnp.logical_not(odd), share, 0.0)
-    mask_black = jnp.where(grid & odd, share, 0.0)
-    source = planes[0]
-    light, dark = None, None
-    for sweep in range(CSWEEPS):
-        light = mask_red * (source if dark is None else source + along(dark, step))
-        dark = mask_black * (source + along(light, step))
-    fields = [light + dark]
-
-    for index in reversed(range(last)):
+            totals.append(first + second)
+        for at in range(slots):
+            passing[at, 0, body2, :] = totals[at]
+        lower = [passing[at, 0, PAD + step : PAD + step + rows2, :] for at in range(slots)]
+        if index < last:
+            totals = [total + below for total, below in zip(totals, lower)]
+            planes = [0.5 * (total + pltpu.roll(total, LANES - step, 1)) for total in totals]
+
+    half_rows = rows2 // 2
+    upper = [passing[at, 0, PAD - step : PAD - step + rows2, :] for at in range(slots)]
+    odd_line = (row2 & step) != 0
+    summed = [
+        total + jnp.where(odd_line, above, below) for total, above, below in zip(totals, upper, lower)
+    ]
+    lines = [total[start : start + half_rows] for total in summed for start in (0, half_rows)]
+    place = lanes_of((half_rows, LANES)) & (len(lines) - 1)
+    joined = lines[0]
+    for q in range(1, len(lines)):
+        joined = jnp.where(place == q, pltpu.roll(lines[q], q, 1), joined)
+    answer = exact_dot(joined, matrix_ref[...])
+    grid = (place == 0) & ((rows_of((half_rows, LANES)) & (step - 1)) == 0)
+    parts = []
+    for q in range(len(lines)):
+        part = pltpu.roll(answer, LANES - q, 1) if q else answer
+        parts.append(jnp.where(grid, part, 0.0))
+    spreads = [jnp.concatenate(parts[2 * at : 2 * at + 2], axis=0) for at in range(slots)]
+
+    for index in reversed(range(len(small))):
         _, _, red, black = small[index]
         slots, odd, step = red.shape[0], odd_at(index), 1 << index
+        if index < last:
+            spreads = [
+                spread_rows(field + pltpu.roll(field, step, 1), step, passing, at)
+                for at, field in enumerate(fields)
+            ]
         for at in range(slots):
-            spread = fields[at] + pltpu.roll(fields[at], step, 1)
-            spread = spread + pltpu.roll(spread, step, 0)
-            black[at, 0, body2, :] = black[at, 0, body2, :] + spread
+            black[at, 0, body2, :] = black[at, 0, body2, :] + spreads[at]
         small_sweeps(index, False)
         fields = []
         for at in range(slots):
@@ -685,16 +743,16 @@
     room = [scratch(count1, 2, rows1, LANES)] * 2
     room += [scratch(count1, 2, rows1 + 2 * PAD, LANES)] * 2
     room += [scratch(count1, rows1, LANES), scratch(planes // 2, rows // 2, 2 * LANES)]
-    room += [scratch(*padded)] * 2
+    room += [scratch(*padded)] * 2 + [scratch(count1 // 2, 1, rows2 + 2 * PAD, LANES)]
     for count in small_shapes(whole):
         room += [scratch(count, rows2, LANES)] * 2
         room += [scratch(count, 1, rows2 + 2 * PAD, LANES)] * 2
     return pl.pallas_call(
         functools.partial(solve_kernel, halo, whole),
         out_shape=struct(nx, ny, nz),
-        in_specs=vmem(7), out_specs=pl.BlockSpec(memory_space=pltpu.VMEM),
+        in_specs=vmem(8), out_specs=pl.BlockSpec(memory_space=pltpu.VMEM),
         compiler_params=params(16), scratch_shapes=room,
-    )(here, flip, beside_here, beside_flip, gr, gb, black)
+    )(here, flip, beside_here, beside_flip, gr, gb, black, cycle_matrix(whole))
 
 
 def fits_block_cycle(shape):

time: 52.6 us -> 51 us (0.970)
  Pallas kernels: 10.8 us -> 9.04 us
    pallas_call x1, Pallas kernels: 8.71 us -> 6.87 us  [block_cycle(): pl.pallas_call(functools.partial(solve_kernel, halo, whole), out_shape=st...]
where the time goes in v4:
time: 51 us; the launch traced here: 50.7 us
  blocking collectives  14.5 us (28%)
  waiting for transfers between devices  13.3 us (26%)
  starting transfers between devices  11.9 us (23%)
  Pallas kernels  9.04 us (18%)
  local copies, waits for them, and re-layouts  1.86 us (4%)
    all_to_all x1, blocking collectives, block_cycle(): here = lax.all_to_all(send, ('gx', 'gy'), 0, 0, tiled=True)  14.5 us
    pallas_call x1, Pallas kernels, block_cycle(): pl.pallas_call(functools.partial(solve_kernel, halo, whole), out_shape=st...  6.87 us
    ppermute x1, waiting for transfers between devices, block_cycle(): flip = lax.ppermute(here, 'gz', flips(count_z, 2))  5.21 us
    ppermute x1, starting transfers between devices, block_cycle(): ya = lax.ppermute(ya, 'gy', pairs(count_y, 0))  4.96 us
    ppermute x1, waiting for transfers between devices, block_cycle(): ya = lax.ppermute(ya, 'gy', pairs(count_y, 0))  3.3 us
    ppermute x1, starting transfers between devices, block_cycle(): side = lax.ppermute(face, 'gx', flips(count_x, 1))  3 us
    ppermute x1, waiting for transfers between devices, block_cycle(): lax.ppermute(zb, 'gz', pairs(count_z, 1) + [(0, count_z - 1), (count_z -...  1.98 us
    pallas_call x1, Pallas kernels, block_cycle(): pl.pallas_call(functools.partial(pre_kernel, halo), out_shape=[struct(*sl...  1.79 us
  transfers between devices with their start and end apart: 8, of which 5 were waited for; matrix products, arithmetic and copies ran while one was open for 2% of the time, Pallas kernels for 0%

profile of v4, /device:TPU:0, one launch (start us, length us, event | category | flops | bytes accessed | tf_op | source)
XLA Modules:
  0.0 50.7 jit_solution(2369963856952210557)
XLA Ops:
  0.0 0.8 %constant_dynamic-slice_fusion.2 = f32[8,16,128]{2,1,0:T(8,128)S(1)} fusion(f32[32,16,128]{2,1,0:T(8,128)} %own_ref.3, s32[]{:T(128)S(6)} %select_n.20), kind=kLoop, calls=%fused_computation.4 | loop fusion | bytes 131076 | tf_op jit(solution)/shard_map/dynamic_slice | solution.py:705
  0.8 3.0 %collective-permute-start = (f32[8,16,128]{2,1,0:T(8,128)S(1)}, f32[8,16,128]{2,1,0:T(8,128)S(1)}, u32[]{:S(2)}, u32[]{:S(2)}) collective-permute-start(f32[8,16,128]{2,1,0:T(8,128)S(1)} %constant_dynamic-slice_fusion.2), channel_id=1, source_target_pairs={{0,16},{16,0},{1,17},{17,1},{2,18},{18,2},{3,19},{19,3},{4,20},{20... | collective-permute-start | bytes 196616 | tf_op jit(solution)/shard_map/ppermute | solution.py:706
  3.8 1.0 %constant_dynamic-update-slice_fusion.1 = f32[40,16,128]{2,1,0:T(8,128)S(1)} fusion(f32[32,16,128]{2,1,0:T(8,128)} %own_ref.3), kind=kLoop, calls=%fused_computation.1 | loop fusion | bytes 524288
  4.8 1.3 %collective-permute-done.xh_ref = f32[8,16,128]{2,1,0:T(8,128)S(1)} collective-permute-done((f32[8,16,128]{2,1,0:T(8,128)S(1)}, f32[8,16,128]{2,1,0:T(8,128)S(1)}, u32[]{:S(2)}, u32[]{:S(2)}) %collective-permute-start) | collective-permute-done | bytes 65568 | tf_op jit(solution)/shard_map/ppermute | solution.py:706
  6.1 0.0 copy-start
  6.1 0.8 %collective-permute-start.2 = (f32[40,8,128]{2,1,0:T(8,128)S(1)}, f32[40,8,128]{2,1,0:T(8,128)S(1)}, u32[]{:S(2)}, u32[]{:S(2)}) collective-permute-start(f32[40,8,128]{2,1,0:T(8,128)S(1)} %get-tuple-element.17), channel_id=1, source_target_pairs={{4,8},{8,4},{5,9},{9,5},{6,10},{10,6},{7,11},{11,7},{20,24},{24,20... | collective-permute-start | bytes 491528 | tf_op jit(solution)/shard_map/ppermute | solution.py:712
  6.9 5.0 %collective-permute-start.1 = (f32[40,8,128]{2,1,0:T(8,128)S(1)}, f32[40,8,128]{2,1,0:T(8,128)S(1)}, u32[]{:S(2)}, u32[]{:S(2)}) collective-permute-start(f32[40,8,128]{2,1,0:T(8,128)S(1)} %get-tuple-element.18), channel_id=1, source_target_pairs={{0,4},{4,0},{8,12},{12,8},{1,5},{5,1},{9,13},{13,9},{2,6},{6,2},{1... | collective-permute-start | bytes 491528 | tf_op jit(solution)/shard_map/ppermute | solution.py:711
  11.9 0.0 collective-permute-done.2.yb_ref
  11.9 3.3 %collective-permute-done.1.ya_ref = f32[40,8,128]{2,1,0:T(8,128)S(1)} collective-permute-done((f32[40,8,128]{2,1,0:T(8,128)S(1)}, f32[40,8,128]{2,1,0:T(8,128)S(1)}, u32[]{:S(2)}, u32[]{:S(2)}) %collective-permute-start.1) | collective-permute-done | bytes 163872 | tf_op jit(solution)/shard_map/ppermute | solution.py:711
  15.2 0.0 copy-done
  15.2 0.4 shard_map.28
  15.6 0.1 collective-permute-start.3
  15.7 1.6 %collective-permute-start.4 = (f32[3,32,128]{2,1,0:T(8,128)S(1)}, f32[3,32,128]{2,1,0:T(8,128)S(1)}, u32[]{:S(2)}, u32[]{:S(2)}) collective-permute-start(f32[3,32,128]{2,1,0:T(8,128)S(1)} %get-tuple-element.12), channel_id=1, source_target_pairs={{1,2},{2,1},{0,3},{3,0},{5,6},{6,5},{4,7},{7,4},{9,10},{10,9},{8,1... | collective-permute-start | bytes 147464 | tf_op jit(solution)/shard_map/ppermute | solution.py:726
  17.3 0.0 collective-permute-done.3.za_ref
  17.3 2.0 %collective-permute-done.4.zb_ref = f32[3,32,128]{2,1,0:T(8,128)S(1)} collective-permute-done((f32[3,32,128]{2,1,0:T(8,128)S(1)}, f32[3,32,128]{2,1,0:T(8,128)S(1)}, u32[]{:S(2)}, u32[]{:S(2)}) %collective-permute-start.4) | collective-permute-done | bytes 49184 | tf_op jit(solution)/shard_map/ppermute | solution.py:726
  19.3 1.8 %shard_map.29 = (f32[20,2,32,128]{3,2,1,0:T(8,128)S(1)}, f32[20,2,32,128]{3,2,1,0:T(8,128)S(1)}, f32[20,2,32,128]{3,2,1,0:T(8,128)S(1)}, f32[8,8,8,128]{3,2,1,0:T(8,128)S(1)}) custom-call(f32[32,16,128]{2,1,0:T(8,128)S(1)} %copy-done, f32[8,16,128]{2,1,0:T(8,128)S(1)} %collective-permute-done.xh_ref, f32[40,8,128]{2,1,0:T(8,128)S(1)} %collective-permute-done.1.ya_ref, ...), custom_call_target="tpu_custom_call" | custom-call | tf_op jit(solution)/shard_map/pallas_call | solution.py:730
  21.1 0.0 copy-start.1
  21.1 14.5 %all_to_all.5.refs_0_ = f32[8,8,8,128]{3,2,1,0:T(8,128)S(1)} all-to-all(f32[8,8,8,128]{3,2,1,0:T(8,128)S(1)} %get-tuple-element.13), channel_id=1, replica_groups=mesh['gx'=2,'gy'=4,'gz'=4] {'gx','gy'}, dimensions={0} | all-to-all | bytes 524288 | tf_op jit(solution)/shard_map/all_to_all | solution.py:738
  35.6 1.5 %collective-permute-start.5 = (f32[8,8,8,128]{3,2,1,0:T(8,128)S(1)}, f32[8,8,8,128]{3,2,1,0:T(8,128)S(1)}, u32[]{:S(2)}, u32[]{:S(2)}) collective-permute-start(f32[8,8,8,128]{3,2,1,0:T(8,128)S(1)} %all_to_all.5.refs_0_), channel_id=1, source_target_pairs={{0,2},{1,3},{2,0},{3,1},{4,6},{5,7},{6,4},{7,5},{8,10},{9,11},{10,... | collective-permute-start | bytes 786440 | tf_op jit(solution)/shard_map/ppermute | solution.py:739
  37.1 0.0 collective-permute-start.6
  37.1 5.2 %collective-permute-done.5.refs_1_ = f32[8,8,8,128]{3,2,1,0:T(8,128)S(1)} collective-permute-done((f32[8,8,8,128]{3,2,1,0:T(8,128)S(1)}, f32[8,8,8,128]{3,2,1,0:T(8,128)S(1)}, u32[]{:S(2)}, u32[]{:S(2)}) %collective-permute-start.5) | collective-permute-done | bytes 262176 | tf_op jit(solution)/shard_map/ppermute | solution.py:739
  42.3 0.0 collective-permute-start.7
  42.3 0.0 collective-permute-done.6.refs_2_
  42.3 1.5 %collective-permute-done.7.refs_3_ = f32[8,8,8,128]{3,2,1,0:T(8,128)S(1)} collective-permute-done((f32[8,8,8,128]{3,2,1,0:T(8,128)S(1)}, f32[8,8,8,128]{3,2,1,0:T(8,128)S(1)}, u32[]{:S(2)}, u32[]{:S(2)}) %collective-permute-start.7) | collective-permute-done | bytes 262176 | tf_op jit(solution)/shard_map/ppermute | solution.py:741
  43.9 0.0 copy-done.1
  43.9 6.9 %shard_map.30 = f32[32,16,128]{2,1,0:T(8,128)} custom-call(f32[8,8,8,128]{3,2,1,0:T(8,128)S(1)} %all_to_all.5.refs_0_, f32[8,8,8,128]{3,2,1,0:T(8,128)S(1)} %collective-permute-done.5.refs_1_, f32[8,8,8,128]{3,2,1,0:T(8,128)S(1)} %collective-permute-done.6.refs_2_, f32[8,8,8,128]{3,2,1,0:T(8,128)S(1)} %collective-permute-done.7.refs_3_, ...), custom_call_target="tpu_custom_call" | custom-call | tf_op jit(solution)/shard_map/pallas_call | solution.py:750
  (2 shorter events, 0.0 us)
Async XLA Ops:
  0.8 5.2 %collective-permute-start = (f32[8,16,128]{2,1,0:T(8,128)S(1)}, f32[8,16,128]{2,1,0:T(8,128)S(1)}, u32[]{:S(2)}, u32[]{:S(2)}) collective-permute-start(f32[8,16,128]{2,1,0:T(8,128)S(1)} %constant_dynamic-slice_fusion.2), channel_id=1, source_target_pairs={{0,16},{16,0},{1,17},{17,1},{2,18},{18,2},{3,19},{19,3},{4,20},{20... | collective-permute-start | bytes 196616 | tf_op jit(solution)/shard_map/ppermute | solution.py:706
  6.1 9.1 %copy-start = (f32[32,16,128]{2,1,0:T(8,128)S(1)}, f32[32,16,128]{2,1,0:T(8,128)}, u32[]{:S(2)}) copy-start(f32[32,16,128]{2,1,0:T(8,128)} %own_ref.3) | copy-start | bytes 786436
  6.1 5.8 %collective-permute-start.2 = (f32[40,8,128]{2,1,0:T(8,128)S(1)}, f32[40,8,128]{2,1,0:T(8,128)S(1)}, u32[]{:S(2)}, u32[]{:S(2)}) collective-permute-start(f32[40,8,128]{2,1,0:T(8,128)S(1)} %get-tuple-element.17), channel_id=1, source_target_pairs={{4,8},{8,4},{5,9},{9,5},{6,10},{10,6},{7,11},{11,7},{20,24},{24,20... | collective-permute-start | bytes 491528 | tf_op jit(solution)/shard_map/ppermute | solution.py:712
  6.9 8.3 %collective-permute-start.1 = (f32[40,8,128]{2,1,0:T(8,128)S(1)}, f32[40,8,128]{2,1,0:T(8,128)S(1)}, u32[]{:S(2)}, u32[]{:S(2)}) collective-permute-start(f32[40,8,128]{2,1,0:T(8,128)S(1)} %get-tuple-element.18), channel_id=1, source_target_pairs={{0,4},{4,0},{8,12},{12,8},{1,5},{5,1},{9,13},{13,9},{2,6},{6,2},{1... | collective-permute-start | bytes 491528 | tf_op jit(solution)/shard_map/ppermute | solution.py:711
  15.6 1.7 %collective-permute-start.3 = (f32[3,32,128]{2,1,0:T(8,128)S(1)}, f32[3,32,128]{2,1,0:T(8,128)S(1)}, u32[]{:S(2)}, u32[]{:S(2)}) collective-permute-start(f32[3,32,128]{2,1,0:T(8,128)S(1)} %get-tuple-element.11), channel_id=1, source_target_pairs={{0,1},{1,0},{2,3},{3,2},{4,5},{5,4},{6,7},{7,6},{8,9},{9,8},{10,11... | collective-permute-start | bytes 147464 | tf_op jit(solution)/shard_map/ppermute | solution.py:725
  15.7 3.6 %collective-permute-start.4 = (f32[3,32,128]{2,1,0:T(8,128)S(1)}, f32[3,32,128]{2,1,0:T(8,128)S(1)}, u32[]{:S(2)}, u32[]{:S(2)}) collective-permute-start(f32[3,32,128]{2,1,0:T(8,128)S(1)} %get-tuple-element.12), channel_id=1, source_target_pairs={{1,2},{2,1},{0,3},{3,0},{5,6},{6,5},{4,7},{7,4},{9,10},{10,9},{8,1... | collective-permute-start | bytes 147464 | tf_op jit(solution)/shard_map/ppermute | solution.py:726
  21.1 22.8 %copy-start.1 = (f32[128,128]{1,0:T(8,128)S(1)}, f32[128,128]{1,0:T(8,128)}, u32[]{:S(2)}) copy-start(f32[128,128]{1,0:T(8,128)} %constant.36.clone.refs_7_) | copy-start | bytes 196612
  35.6 6.7 %collective-permute-start.5 = (f32[8,8,8,128]{3,2,1,0:T(8,128)S(1)}, f32[8,8,8,128]{3,2,1,0:T(8,128)S(1)}, u32[]{:S(2)}, u32[]{:S(2)}) collective-permute-start(f32[8,8,8,128]{3,2,1,0:T(8,128)S(1)} %all_to_all.5.refs_0_), channel_id=1, source_target_pairs={{0,2},{1,3},{2,0},{3,1},{4,6},{5,7},{6,4},{7,5},{8,10},{9,11},{10,... | collective-permute-start | bytes 786440 | tf_op jit(solution)/shard_map/ppermute | solution.py:739
  37.1 5.2 %collective-permute-start.6 = (f32[8,8,8,128]{3,2,1,0:T(8,128)S(1)}, f32[8,8,8,128]{3,2,1,0:T(8,128)S(1)}, u32[]{:S(2)}, u32[]{:S(2)}) collective-permute-start(f32[8,8,8,128]{3,2,1,0:T(8,128)S(1)} %all_to_all.5.refs_0_), channel_id=1, source_target_pairs={{0,1},{1,0},{2,3},{3,2},{4,5},{5,4},{6,7},{7,6},{8,9},{9,8},{10,11... | collective-permute-start | bytes 786440 | tf_op jit(solution)/shard_map/ppermute | solution.py:740
  42.3 1.5 %collective-permute-start.7 = (f32[8,8,8,128]{3,2,1,0:T(8,128)S(1)}, f32[8,8,8,128]{3,2,1,0:T(8,128)S(1)}, u32[]{:S(2)}, u32[]{:S(2)}) collective-permute-start(f32[8,8,8,128]{3,2,1,0:T(8,128)S(1)} %collective-permute-done.5.refs_1_), channel_id=1, source_target_pairs={{0,1},{1,0},{2,3},{3,2},{4,5},{5,4},{6,7},{7,6},{8,9},{9,8},{10,11... | collective-permute-start | bytes 786440 | tf_op jit(solution)/shard_map/ppermute | solution.py:741

commit v5 on v4

--- a/solution.py
+++ b/solution.py
@@ -168,6 +168,14 @@
     swaps = []
     for i in range(first, count - 1, 2):
         swaps += [(i, i + 1), (i + 1, i)]
+    return swaps
+
+
+def inner_pairs(count_x, count):
+    swaps = []
+    for x in range(count_x):
+        swaps += [(x * count + i, x * count + j) for i, j in pairs(count, 1)]
+        swaps += [(x * count + i, (x ^ 1) * count + i) for i in (0, count - 1)]
     return swaps
 
 
@@ -709,7 +717,7 @@
     ya = lax.dynamic_slice_in_dim(tall, jnp.where(even, ny - halo, 0), halo, 1)
     yb = lax.dynamic_slice_in_dim(tall, jnp.where(even, 0, ny - halo), halo, 1)
     ya = lax.ppermute(ya, "gy", pairs(count_y, 0))
-    yb = lax.ppermute(yb, "gy", pairs(count_y, 1))
+    yb = lax.ppermute(yb, ("gx", "gy"), inner_pairs(count_x, count_y))
     rows = ny + 2 * halo
     planes = nx + halo
     packs = -(-planes * halo // nz)

time: 51 us -> 49.9 us (0.978)
  starting transfers between devices: 11.9 us -> 9.88 us
  blocking collectives: 14.5 us -> 15.2 us
    ppermute x1, starting transfers between devices: 4.96 us -> 1.63 us  [block_cycle(): ya = lax.ppermute(ya, 'gy', pairs(count_y, 0))]
    ppermute x1, waiting for transfers between devices: 0.01 us -> 1.66 us  [block_cycle(): yb = lax.ppermute(yb, ('gx', 'gy'), inner_pairs(count_x, count_y))]
    ppermute x1, starting transfers between devices: 0.8 us -> 2.09 us  [block_cycle(): yb = lax.ppermute(yb, ('gx', 'gy'), inner_pairs(count_x, count_y))]
    ppermute x1, waiting for transfers between devices: 3.3 us -> 2.02 us  [block_cycle(): ya = lax.ppermute(ya, 'gy', pairs(count_y, 0))]
    all_to_all x1, blocking collectives: 14.5 us -> 15.2 us  [block_cycle(): here = lax.all_to_all(send, ('gx', 'gy'), 0, 0, tiled=True)]
  transfers between devices with their start and end apart: 8 -> 8, of which waited for: 5 -> 6; matrix products, arithmetic and copies ran while one was open for 2% -> 2% of each run, Pallas kernels for 0% -> 0%
where the time goes in v5:
time: 49.9 us; the launch traced here: 49.7 us
  blocking collectives  15.2 us (30%)
  waiting for transfers between devices  13.7 us (27%)
  starting transfers between devices  9.88 us (20%)
  Pallas kernels  9.04 us (18%)
  local copies, waits for them, and re-layouts  1.86 us (4%)
    all_to_all x1, blocking collectives, block_cycle(): here = lax.all_to_all(send, ('gx', 'gy'), 0, 0, tiled=True)  15.2 us
    pallas_call x1, Pallas kernels, block_cycle(): pl.pallas_call(functools.partial(solve_kernel, halo, whole), out_shape=st...  6.87 us
    ppermute x1, waiting for transfers between devices, block_cycle(): flip = lax.ppermute(here, 'gz', flips(count_z, 2))  5.21 us
    ppermute x1, starting transfers between devices, block_cycle(): side = lax.ppermute(face, 'gx', flips(count_x, 1))  3 us
    ppermute x1, starting transfers between devices, block_cycle(): yb = lax.ppermute(yb, ('gx', 'gy'), inner_pairs(count_x, count_y))  2.09 us
    ppermute x1, waiting for transfers between devices, block_cycle(): ya = lax.ppermute(ya, 'gy', pairs(count_y, 0))  2.02 us
    ppermute x1, waiting for transfers between devices, block_cycle(): lax.ppermute(zb, 'gz', pairs(count_z, 1) + [(0, count_z - 1), (count_z -...  1.98 us
    pallas_call x1, Pallas kernels, block_cycle(): pl.pallas_call(functools.partial(pre_kernel, halo), out_shape=[struct(*sl...  1.79 us
  transfers between devices with their start and end apart: 8, of which 6 were waited for; matrix products, arithmetic and copies ran while one was open for 2% of the time, Pallas kernels for 0%

profile of v5, /device:TPU:0, one launch (start us, length us, event | category | flops | bytes accessed | tf_op | source)
XLA Modules:
  0.0 49.7 jit_solution(2599257590608926418)
XLA Ops:
  0.0 0.8 %constant_dynamic-slice_fusion.2 = f32[8,16,128]{2,1,0:T(8,128)S(1)} fusion(f32[32,16,128]{2,1,0:T(8,128)} %own_ref.3, s32[]{:T(128)S(6)} %select_n.20), kind=kLoop, calls=%fused_computation.4 | loop fusion | bytes 131076 | tf_op jit(solution)/shard_map/dynamic_slice | solution.py:713
  0.8 3.0 %collective-permute-start = (f32[8,16,128]{2,1,0:T(8,128)S(1)}, f32[8,16,128]{2,1,0:T(8,128)S(1)}, u32[]{:S(2)}, u32[]{:S(2)}) collective-permute-start(f32[8,16,128]{2,1,0:T(8,128)S(1)} %constant_dynamic-slice_fusion.2), channel_id=1, source_target_pairs={{0,16},{16,0},{1,17},{17,1},{2,18},{18,2},{3,19},{19,3},{4,20},{20... | collective-permute-start | bytes 196616 | tf_op jit(solution)/shard_map/ppermute | solution.py:714
  3.8 1.0 %constant_dynamic-update-slice_fusion.1 = f32[40,16,128]{2,1,0:T(8,128)S(1)} fusion(f32[32,16,128]{2,1,0:T(8,128)} %own_ref.3), kind=kLoop, calls=%fused_computation.1 | loop fusion | bytes 524288
  4.8 1.3 %collective-permute-done.xh_ref = f32[8,16,128]{2,1,0:T(8,128)S(1)} collective-permute-done((f32[8,16,128]{2,1,0:T(8,128)S(1)}, f32[8,16,128]{2,1,0:T(8,128)S(1)}, u32[]{:S(2)}, u32[]{:S(2)}) %collective-permute-start) | collective-permute-done | bytes 65568 | tf_op jit(solution)/shard_map/ppermute | solution.py:714
  6.1 0.0 copy-start
  6.1 2.1 %collective-permute-start.2 = (f32[40,8,128]{2,1,0:T(8,128)S(1)}, f32[40,8,128]{2,1,0:T(8,128)S(1)}, u32[]{:S(2)}, u32[]{:S(2)}) collective-permute-start(f32[40,8,128]{2,1,0:T(8,128)S(1)} %get-tuple-element.17), channel_id=1, source_target_pairs={{4,8},{8,4},{0,16},{12,28},{20,24},{24,20},{16,0},{28,12},{5,9},{9... | collective-permute-start | bytes 491528 | tf_op jit(solution)/shard_map/ppermute | solution.py:720
  8.2 1.6 %collective-permute-start.1 = (f32[40,8,128]{2,1,0:T(8,128)S(1)}, f32[40,8,128]{2,1,0:T(8,128)S(1)}, u32[]{:S(2)}, u32[]{:S(2)}) collective-permute-start(f32[40,8,128]{2,1,0:T(8,128)S(1)} %get-tuple-element.18), channel_id=1, source_target_pairs={{0,4},{4,0},{8,12},{12,8},{1,5},{5,1},{9,13},{13,9},{2,6},{6,2},{1... | collective-permute-start | bytes 491528 | tf_op jit(solution)/shard_map/ppermute | solution.py:719
  9.9 1.7 %collective-permute-done.2.yb_ref = f32[40,8,128]{2,1,0:T(8,128)S(1)} collective-permute-done((f32[40,8,128]{2,1,0:T(8,128)S(1)}, f32[40,8,128]{2,1,0:T(8,128)S(1)}, u32[]{:S(2)}, u32[]{:S(2)}) %collective-permute-start.2) | collective-permute-done | bytes 163872 | tf_op jit(solution)/shard_map/ppermute | solution.py:720
  11.5 2.0 %collective-permute-done.1.ya_ref = f32[40,8,128]{2,1,0:T(8,128)S(1)} collective-permute-done((f32[40,8,128]{2,1,0:T(8,128)S(1)}, f32[40,8,128]{2,1,0:T(8,128)S(1)}, u32[]{:S(2)}, u32[]{:S(2)}) %collective-permute-start.1) | collective-permute-done | bytes 163872 | tf_op jit(solution)/shard_map/ppermute | solution.py:719
  13.5 0.0 copy-done
  13.5 0.4 shard_map.28
  13.9 0.1 collective-permute-start.3
  14.0 1.6 %collective-permute-start.4 = (f32[3,32,128]{2,1,0:T(8,128)S(1)}, f32[3,32,128]{2,1,0:T(8,128)S(1)}, u32[]{:S(2)}, u32[]{:S(2)}) collective-permute-start(f32[3,32,128]{2,1,0:T(8,128)S(1)} %get-tuple-element.12), channel_id=1, source_target_pairs={{1,2},{2,1},{0,3},{3,0},{5,6},{6,5},{4,7},{7,4},{9,10},{10,9},{8,1... | collective-permute-start | bytes 147464 | tf_op jit(solution)/shard_map/ppermute | solution.py:734
  15.6 0.0 collective-permute-done.3.za_ref
  15.6 2.0 %collective-permute-done.4.zb_ref = f32[3,32,128]{2,1,0:T(8,128)S(1)} collective-permute-done((f32[3,32,128]{2,1,0:T(8,128)S(1)}, f32[3,32,128]{2,1,0:T(8,128)S(1)}, u32[]{:S(2)}, u32[]{:S(2)}) %collective-permute-start.4) | collective-permute-done | bytes 49184 | tf_op jit(solution)/shard_map/ppermute | solution.py:734
  17.6 1.8 %shard_map.29 = (f32[20,2,32,128]{3,2,1,0:T(8,128)S(1)}, f32[20,2,32,128]{3,2,1,0:T(8,128)S(1)}, f32[20,2,32,128]{3,2,1,0:T(8,128)S(1)}, f32[8,8,8,128]{3,2,1,0:T(8,128)S(1)}) custom-call(f32[32,16,128]{2,1,0:T(8,128)S(1)} %copy-done, f32[8,16,128]{2,1,0:T(8,128)S(1)} %collective-permute-done.xh_ref, f32[40,8,128]{2,1,0:T(8,128)S(1)} %collective-permute-done.1.ya_ref, ...), custom_call_target="tpu_custom_call" | custom-call | tf_op jit(solution)/shard_map/pallas_call | solution.py:738
  19.4 0.0 copy-start.1
  19.4 15.2 %all_to_all.5.refs_0_ = f32[8,8,8,128]{3,2,1,0:T(8,128)S(1)} all-to-all(f32[8,8,8,128]{3,2,1,0:T(8,128)S(1)} %get-tuple-element.13), channel_id=1, replica_groups=mesh['gx'=2,'gy'=4,'gz'=4] {'gx','gy'}, dimensions={0} | all-to-all | bytes 524288 | tf_op jit(solution)/shard_map/all_to_all | solution.py:746
  34.6 1.5 %collective-permute-start.5 = (f32[8,8,8,128]{3,2,1,0:T(8,128)S(1)}, f32[8,8,8,128]{3,2,1,0:T(8,128)S(1)}, u32[]{:S(2)}, u32[]{:S(2)}) collective-permute-start(f32[8,8,8,128]{3,2,1,0:T(8,128)S(1)} %all_to_all.5.refs_0_), channel_id=1, source_target_pairs={{0,2},{1,3},{2,0},{3,1},{4,6},{5,7},{6,4},{7,5},{8,10},{9,11},{10,... | collective-permute-start | bytes 786440 | tf_op jit(solution)/shard_map/ppermute | solution.py:747
  36.1 0.0 collective-permute-start.6
  36.1 5.2 %collective-permute-done.5.refs_1_ = f32[8,8,8,128]{3,2,1,0:T(8,128)S(1)} collective-permute-done((f32[8,8,8,128]{3,2,1,0:T(8,128)S(1)}, f32[8,8,8,128]{3,2,1,0:T(8,128)S(1)}, u32[]{:S(2)}, u32[]{:S(2)}) %collective-permute-start.5) | collective-permute-done | bytes 262176 | tf_op jit(solution)/shard_map/ppermute | solution.py:747
  41.3 0.0 collective-permute-start.7
  41.3 0.0 collective-permute-done.6.refs_2_
  41.3 1.5 %collective-permute-done.7.refs_3_ = f32[8,8,8,128]{3,2,1,0:T(8,128)S(1)} collective-permute-done((f32[8,8,8,128]{3,2,1,0:T(8,128)S(1)}, f32[8,8,8,128]{3,2,1,0:T(8,128)S(1)}, u32[]{:S(2)}, u32[]{:S(2)}) %collective-permute-start.7) | collective-permute-done | bytes 262176 | tf_op jit(solution)/shard_map/ppermute | solution.py:749
  42.8 0.0 copy-done.1
  42.8 6.9 %shard_map.30 = f32[32,16,128]{2,1,0:T(8,128)} custom-call(f32[8,8,8,128]{3,2,1,0:T(8,128)S(1)} %all_to_all.5.refs_0_, f32[8,8,8,128]{3,2,1,0:T(8,128)S(1)} %collective-permute-done.5.refs_1_, f32[8,8,8,128]{3,2,1,0:T(8,128)S(1)} %collective-permute-done.6.refs_2_, f32[8,8,8,128]{3,2,1,0:T(8,128)S(1)} %collective-permute-done.7.refs_3_, ...), custom_call_target="tpu_custom_call" | custom-call | tf_op jit(solution)/shard_map/pallas_call | solution.py:758
  (2 shorter events, 0.0 us)
Async XLA Ops:
  0.8 5.2 %collective-permute-start = (f32[8,16,128]{2,1,0:T(8,128)S(1)}, f32[8,16,128]{2,1,0:T(8,128)S(1)}, u32[]{:S(2)}, u32[]{:S(2)}) collective-permute-start(f32[8,16,128]{2,1,0:T(8,128)S(1)} %constant_dynamic-slice_fusion.2), channel_id=1, source_target_pairs={{0,16},{16,0},{1,17},{17,1},{2,18},{18,2},{3,19},{19,3},{4,20},{20... | collective-permute-start | bytes 196616 | tf_op jit(solution)/shard_map/ppermute | solution.py:714
  6.1 7.5 %copy-start = (f32[32,16,128]{2,1,0:T(8,128)S(1)}, f32[32,16,128]{2,1,0:T(8,128)}, u32[]{:S(2)}) copy-start(f32[32,16,128]{2,1,0:T(8,128)} %own_ref.3) | copy-start | bytes 786436
  6.1 5.4 %collective-permute-start.2 = (f32[40,8,128]{2,1,0:T(8,128)S(1)}, f32[40,8,128]{2,1,0:T(8,128)S(1)}, u32[]{:S(2)}, u32[]{:S(2)}) collective-permute-start(f32[40,8,128]{2,1,0:T(8,128)S(1)} %get-tuple-element.17), channel_id=1, source_target_pairs={{4,8},{8,4},{0,16},{12,28},{20,24},{24,20},{16,0},{28,12},{5,9},{9... | collective-permute-start | bytes 491528 | tf_op jit(solution)/shard_map/ppermute | solution.py:720
  8.2 5.3 %collective-permute-start.1 = (f32[40,8,128]{2,1,0:T(8,128)S(1)}, f32[40,8,128]{2,1,0:T(8,128)S(1)}, u32[]{:S(2)}, u32[]{:S(2)}) collective-permute-start(f32[40,8,128]{2,1,0:T(8,128)S(1)} %get-tuple-element.18), channel_id=1, source_target_pairs={{0,4},{4,0},{8,12},{12,8},{1,5},{5,1},{9,13},{13,9},{2,6},{6,2},{1... | collective-permute-start | bytes 491528 | tf_op jit(solution)/shard_map/ppermute | solution.py:719
  13.9 1.7 %collective-permute-start.3 = (f32[3,32,128]{2,1,0:T(8,128)S(1)}, f32[3,32,128]{2,1,0:T(8,128)S(1)}, u32[]{:S(2)}, u32[]{:S(2)}) collective-permute-start(f32[3,32,128]{2,1,0:T(8,128)S(1)} %get-tuple-element.11), channel_id=1, source_target_pairs={{0,1},{1,0},{2,3},{3,2},{4,5},{5,4},{6,7},{7,6},{8,9},{9,8},{10,11... | collective-permute-start | bytes 147464 | tf_op jit(solution)/shard_map/ppermute | solution.py:733
  14.0 3.6 %collective-permute-start.4 = (f32[3,32,128]{2,1,0:T(8,128)S(1)}, f32[3,32,128]{2,1,0:T(8,128)S(1)}, u32[]{:S(2)}, u32[]{:S(2)}) collective-permute-start(f32[3,32,128]{2,1,0:T(8,128)S(1)} %get-tuple-element.12), channel_id=1, source_target_pairs={{1,2},{2,1},{0,3},{3,0},{5,6},{6,5},{4,7},{7,4},{9,10},{10,9},{8,1... | collective-permute-start | bytes 147464 | tf_op jit(solution)/shard_map/ppermute | solution.py:734
  19.4 23.4 %copy-start.1 = (f32[128,128]{1,0:T(8,128)S(1)}, f32[128,128]{1,0:T(8,128)}, u32[]{:S(2)}) copy-start(f32[128,128]{1,0:T(8,128)} %constant.36.clone.refs_7_) | copy-start | bytes 196612
  34.6 6.7 %collective-permute-start.5 = (f32[8,8,8,128]{3,2,1,0:T(8,128)S(1)}, f32[8,8,8,128]{3,2,1,0:T(8,128)S(1)}, u32[]{:S(2)}, u32[]{:S(2)}) collective-permute-start(f32[8,8,8,128]{3,2,1,0:T(8,128)S(1)} %all_to_all.5.refs_0_), channel_id=1, source_target_pairs={{0,2},{1,3},{2,0},{3,1},{4,6},{5,7},{6,4},{7,5},{8,10},{9,11},{10,... | collective-permute-start | bytes 786440 | tf_op jit(solution)/shard_map/ppermute | solution.py:747
  36.1 5.2 %collective-permute-start.6 = (f32[8,8,8,128]{3,2,1,0:T(8,128)S(1)}, f32[8,8,8,128]{3,2,1,0:T(8,128)S(1)}, u32[]{:S(2)}, u32[]{:S(2)}) collective-permute-start(f32[8,8,8,128]{3,2,1,0:T(8,128)S(1)} %all_to_all.5.refs_0_), channel_id=1, source_target_pairs={{0,1},{1,0},{2,3},{3,2},{4,5},{5,4},{6,7},{7,6},{8,9},{9,8},{10,11... | collective-permute-start | bytes 786440 | tf_op jit(solution)/shard_map/ppermute | solution.py:748
  41.3 1.5 %collective-permute-start.7 = (f32[8,8,8,128]{3,2,1,0:T(8,128)S(1)}, f32[8,8,8,128]{3,2,1,0:T(8,128)S(1)}, u32[]{:S(2)}, u32[]{:S(2)}) collective-permute-start(f32[8,8,8,128]{3,2,1,0:T(8,128)S(1)} %collective-permute-done.5.refs_1_), channel_id=1, source_target_pairs={{0,1},{1,0},{2,3},{3,2},{4,5},{5,4},{6,7},{7,6},{8,9},{9,8},{10,11... | collective-permute-start | bytes 786440 | tf_op jit(solution)/shard_map/ppermute | solution.py:749

commit v6 on v5

--- a/solution.py
+++ b/solution.py
@@ -366,9 +366,12 @@
     pick = (((rows_of((half, nz)) + part) & 1) == 1) ^ (part >= 2)
     turn = quarter * lax.axis_index("gz")
     for at in range(own // 2):
-        packed = pltpu.roll(jnp.where(pick, coarse[2 * at + 1], coarse[2 * at]), turn, 1)
-        for member in range(send_ref.shape[0]):
-            send_ref[member, at] = packed
+        send_ref[at] = pltpu.roll(jnp.where(pick, coarse[2 * at + 1], coarse[2 * at]), turn, 1)
+
+
+def stack_kernel(*refs):
+    for which, ref in enumerate(refs[:-1]):
+        refs[-1][which] = ref[...]
 
 
 def small_shapes(whole):
@@ -415,9 +418,10 @@
 
 
 def solve_kernel(halo, whole, *refs):
-    here_ref, flip_ref, next_ref, both_ref, gr_ref, gb_ref, dark_ref, matrix_ref, out_ref = refs[:9]
-    fr1, fb1, red1, black1, rest1, tall_ref, red_ref, work_ref, passing = refs[9:18]
-    small = [refs[18 + 4 * i : 22 + 4 * i] for i in range(LEVELS - 4)]
+    gathered, refs = refs[:8], refs[8:]
+    gr_ref, gb_ref, dark_ref, matrix_ref, out_ref = refs[:5]
+    fr1, fb1, red1, black1, rest1, tall_ref, red_ref, work_ref, passing = refs[5:14]
+    small = [refs[14 + 4 * i : 18 + 4 * i] for i in range(LEVELS - 4)]
     gx, gy, gz = (lax.axis_index(axis) for axis in ("gx", "gy", "gz"))
     weight_z = 1.0 + rsd_beta
     share = 1.0 / centre
@@ -427,27 +431,25 @@
         for ref in level[2:]:
             clear_pads(ref)
 
-    members, slots, block_rows, _ = here_ref.shape
-    count_y = lax.axis_size("gy")
+    _, slots, block_rows, _ = gathered[0].shape
     count1, _, rows1, _ = fr1.shape
     quarter = LANES // 4
-    sources = [
-        (ref, jnp.bitwise_xor(gz, bits))
-        for ref, bits in ((here_ref, 0), (flip_ref, 2), (next_ref, 1), (both_ref, 3))
-    ]
     group = lanes_of((block_rows, LANES)) // quarter
-    held = [jnp.bitwise_and(group - which, 3) for _, which in sources]
-    for part, target in enumerate((fr1, fr1, fb1, fb1)):
-        theirs = [kind == part for kind in held]
-        for member in range(members):
-            i, j = member // count_y, member % count_y
+    held = [jnp.bitwise_and(group - jnp.bitwise_xor(gz, bits), 3) for bits in range(4)]
+    theirs = [[kind == part for kind in held] for part in range(4)]
+    for far in range(2):
+        for second in range(4):
+            x = jnp.bitwise_xor(gx, second & 1)
+            y = jnp.bitwise_xor(gy, 2 * far + (second >> 1))
+            rows = pl.ds(pl.multiple_of(y * block_rows, 8), block_rows)
             for at in range(slots):
-                value = sources[0][0][member, at]
-                for (ref, _), mine in zip(sources[1:], theirs[1:]):
-                    value = jnp.where(mine, ref[member, at], value)
-                rows = slice(j * block_rows, (j + 1) * block_rows)
-                turned = pltpu.roll(value, LANES - quarter * part, 1) if part else value
-                target[i * slots + at, part % 2, rows, :] = turned
+                blocks = [gathered[4 * (bits & 1) + second][far + (bits & 2), at] for bits in range(4)]
+                for part, target in enumerate((fr1, fr1, fb1, fb1)):
+                    value = blocks[0]
+                    for block, mine in zip(blocks[1:], theirs[part][1:]):
+                        value = jnp.where(mine, block, value)
+                    turned = pltpu.roll(value, LANES - quarter * part, 1) if part else value
+                    target[x * slots + at, part % 2, rows, :] = turned
 
     def fold_total(ref, at, e, start, count, low, high, odds, to_red):
         lane = lanes_of((count, LANES))
@@ -732,21 +734,33 @@
     )(density, side, ya, yb)
     za = lax.ppermute(za, "gz", pairs(count_z, 0))
     zb = lax.ppermute(zb, "gz", pairs(count_z, 1) + [(0, count_z - 1), (count_z - 1, 0)])
-    members = count_x * count_y
     slots = (planes // 2, 2, rows, LANES)
     padded = (planes // 2, 2, rows + 2 * PAD, LANES)
     gr, gb, black, send = pl.pallas_call(
         functools.partial(pre_kernel, halo),
-        out_shape=[struct(*slots)] * 3 + [struct(members, nx // 4, ny // 2, nz)],
+        out_shape=[struct(*slots)] * 3 + [struct(nx // 4, ny // 2, nz)],
         in_specs=vmem(6), out_specs=vmem(4), compiler_params=params(10),
         scratch_shapes=[scratch(nx // 2, ny, nz)] * 2
         + [scratch(*padded)] * 2
         + [scratch(nx // 2, ny, nz)],
     )(density, side, ya, yb, za, zb)
-    here = lax.all_to_all(send, ("gx", "gy"), 0, 0, tiled=True)
-    flip = lax.ppermute(here, "gz", flips(count_z, 2))
-    beside_here = lax.ppermute(here, "gz", flips(count_z, 1))
-    beside_flip = lax.ppermute(flip, "gz", flips(count_z, 1))
+    first = [
+        send,
+        lax.ppermute(send, "gy", flips(count_y, 2)),
+        lax.ppermute(send, "gz", flips(count_z, 2)),
+        lax.ppermute(send, ("gy", "gz"), flips(count_y * count_z, 2 * count_z + 2)),
+    ]
+    block = pl.pallas_call(
+        stack_kernel, out_shape=struct(4, *send.shape),
+        in_specs=vmem(4), out_specs=pl.BlockSpec(memory_space=pltpu.VMEM), compiler_params=params(2),
+    )(*first)
+    second = [
+        block,
+        lax.ppermute(block, "gx", flips(count_x, 1)),
+        lax.ppermute(block, "gy", flips(count_y, 1)),
+        lax.ppermute(block, ("gx", "gy"), flips(count_x * count_y, count_y + 1)),
+    ]
+    third = [lax.ppermute(blocks, "gz", flips(count_z, 1)) for blocks in second]
     count1, rows1, rows2 = whole[0] // 4, whole[1] // 2, whole[1] // 4
     room = [scratch(count1, 2, rows1, LANES)] * 2
     room += [scratch(count1, 2, rows1 + 2 * PAD, LANES)] * 2
@@ -758,9 +772,9 @@
     return pl.pallas_call(
         functools.partial(solve_kernel, halo, whole),
         out_shape=struct(nx, ny, nz),
-        in_specs=vmem(8), out_specs=pl.BlockSpec(memory_space=pltpu.VMEM),
+        in_specs=vmem(12), out_specs=pl.BlockSpec(memory_space=pltpu.VMEM),
         compiler_params=params(16), scratch_shapes=room,
-    )(here, flip, beside_here, beside_flip, gr, gb, black, cycle_matrix(whole))
+    )(*second, *third, gr, gb, black, cycle_matrix(whole))
 
 
 def fits_block_cycle(shape):
@@ -771,7 +785,7 @@
     exact = all(c << (LEVELS - 1) == size for c, size in zip(coarsest, whole))
     return (
         exact and coarsest[0] == coarsest[1] == 1 and nz == LANES and ny == 2 * HALO
-        and count_x == 2 and count_z == 4 and count_y % 2 == 0
+        and count_x == 2 and count_y == 4 and count_z == 4
     )
 
 

time: 49.9 us -> 44.5 us (0.89)
  blocking collectives: 15.2 us -> 0 us
  starting transfers between devices: 9.88 us -> 16.4 us
  waiting for transfers between devices: 13.7 us -> 17 us
    all_to_all x1 -> x0, blocking collectives: 15.2 us -> none  [block_cycle(): here = lax.all_to_all(send, ('gx', 'gy'), 0, 0, tiled=True)]
    ppermute x3 -> x10, starting transfers between devices: 1.5 us -> 8.02 us  [the longest x1 3.13 us: block_cycle(): lax.ppermute(send, ('gy', 'gz'), flips(count_y * count_z, 2 * count_z + 2))]
    ppermute x3 -> x10, waiting for transfers between devices: 6.74 us -> 10 us  [the longest x1 3.37 us: block_cycle(): lax.ppermute(block, ('gx', 'gy'), flips(count_x * count_y, count_y + 1))]
  transfers between devices with their start and end apart: 8 -> 15, of which waited for: 6 -> 12; matrix products, arithmetic and copies ran while one was open for 2% -> 2% of each run, Pallas kernels for 0% -> 0%
where the time goes in v6:
time: 44.5 us; the launch traced here: 44.3 us
  waiting for transfers between devices  17 us (38%)
  starting transfers between devices  16.4 us (37%)
  Pallas kernels  9.04 us (20%)
  local copies, waits for them, and re-layouts  1.86 us (4%)
    pallas_call x1, Pallas kernels, block_cycle(): pl.pallas_call(functools.partial(solve_kernel, halo, whole), out_shape=st...  6.86 us
    ppermute x1, waiting for transfers between devices, block_cycle(): lax.ppermute(block, ('gx', 'gy'), flips(count_x * count_y, count_y + 1))  3.37 us
    ppermute x1, starting transfers between devices, block_cycle(): lax.ppermute(send, ('gy', 'gz'), flips(count_y * count_z, 2 * count_z + 2))  3.13 us
    ppermute x1, starting transfers between devices, block_cycle(): side = lax.ppermute(face, 'gx', flips(count_x, 1))  3 us
    ppermute x1, starting transfers between devices, block_cycle(): yb = lax.ppermute(yb, ('gx', 'gy'), inner_pairs(count_x, count_y))  2.09 us
    ppermute x1, starting transfers between devices, block_cycle(): lax.ppermute(block, ('gx', 'gy'), flips(count_x * count_y, count_y + 1))  2.03 us
    ppermute x1, waiting for transfers between devices, block_cycle(): ya = lax.ppermute(ya, 'gy', pairs(count_y, 0))  2.02 us
    ppermute x1, waiting for transfers between devices, block_cycle(): lax.ppermute(zb, 'gz', pairs(count_z, 1) + [(0, count_z - 1), (count_z -...  1.98 us
  transfers between devices with their start and end apart: 15, of which 12 were waited for; matrix products, arithmetic and copies ran while one was open for 2% of the time, Pallas kernels for 0%

profile of v6, /device:TPU:0, one launch (start us, length us, event | category | flops | bytes accessed | tf_op | source)
XLA Modules:
  0.0 44.3 jit_solution(147535760641333856)
XLA Ops:
  0.0 0.8 %constant_dynamic-slice_fusion.2 = f32[8,16,128]{2,1,0:T(8,128)S(1)} fusion(f32[32,16,128]{2,1,0:T(8,128)} %own_ref.3, s32[]{:T(128)S(6)} %select_n.20), kind=kLoop, calls=%fused_computation.4 | loop fusion | bytes 131076 | tf_op jit(solution)/shard_map/dynamic_slice | solution.py:715
  0.8 3.0 %collective-permute-start = (f32[8,16,128]{2,1,0:T(8,128)S(1)}, f32[8,16,128]{2,1,0:T(8,128)S(1)}, u32[]{:S(2)}, u32[]{:S(2)}) collective-permute-start(f32[8,16,128]{2,1,0:T(8,128)S(1)} %constant_dynamic-slice_fusion.2), channel_id=1, source_target_pairs={{0,16},{16,0},{1,17},{17,1},{2,18},{18,2},{3,19},{19,3},{4,20},{20... | collective-permute-start | bytes 196616 | tf_op jit(solution)/shard_map/ppermute | solution.py:716
  3.8 1.0 %constant_dynamic-update-slice_fusion.1 = f32[40,16,128]{2,1,0:T(8,128)S(1)} fusion(f32[32,16,128]{2,1,0:T(8,128)} %own_ref.3), kind=kLoop, calls=%fused_computation.1 | loop fusion | bytes 524288
  4.8 1.3 %collective-permute-done.xh_ref = f32[8,16,128]{2,1,0:T(8,128)S(1)} collective-permute-done((f32[8,16,128]{2,1,0:T(8,128)S(1)}, f32[8,16,128]{2,1,0:T(8,128)S(1)}, u32[]{:S(2)}, u32[]{:S(2)}) %collective-permute-start) | collective-permute-done | bytes 65568 | tf_op jit(solution)/shard_map/ppermute | solution.py:716
  6.1 0.0 copy-start
  6.1 2.1 %collective-permute-start.2 = (f32[40,8,128]{2,1,0:T(8,128)S(1)}, f32[40,8,128]{2,1,0:T(8,128)S(1)}, u32[]{:S(2)}, u32[]{:S(2)}) collective-permute-start(f32[40,8,128]{2,1,0:T(8,128)S(1)} %get-tuple-element.17), channel_id=1, source_target_pairs={{4,8},{8,4},{0,16},{12,28},{20,24},{24,20},{16,0},{28,12},{5,9},{9... | collective-permute-start | bytes 491528 | tf_op jit(solution)/shard_map/ppermute | solution.py:722
  8.2 1.6 %collective-permute-start.1 = (f32[40,8,128]{2,1,0:T(8,128)S(1)}, f32[40,8,128]{2,1,0:T(8,128)S(1)}, u32[]{:S(2)}, u32[]{:S(2)}) collective-permute-start(f32[40,8,128]{2,1,0:T(8,128)S(1)} %get-tuple-element.18), channel_id=1, source_target_pairs={{0,4},{4,0},{8,12},{12,8},{1,5},{5,1},{9,13},{13,9},{2,6},{6,2},{1... | collective-permute-start | bytes 491528 | tf_op jit(solution)/shard_map/ppermute | solution.py:721
  9.9 1.7 %collective-permute-done.2.yb_ref = f32[40,8,128]{2,1,0:T(8,128)S(1)} collective-permute-done((f32[40,8,128]{2,1,0:T(8,128)S(1)}, f32[40,8,128]{2,1,0:T(8,128)S(1)}, u32[]{:S(2)}, u32[]{:S(2)}) %collective-permute-start.2) | collective-permute-done | bytes 163872 | tf_op jit(solution)/shard_map/ppermute | solution.py:722
  11.5 2.0 %collective-permute-done.1.ya_ref = f32[40,8,128]{2,1,0:T(8,128)S(1)} collective-permute-done((f32[40,8,128]{2,1,0:T(8,128)S(1)}, f32[40,8,128]{2,1,0:T(8,128)S(1)}, u32[]{:S(2)}, u32[]{:S(2)}) %collective-permute-start.1) | collective-permute-done | bytes 163872 | tf_op jit(solution)/shard_map/ppermute | solution.py:721
  13.5 0.0 copy-done
  13.5 0.4 shard_map.28
  13.9 0.1 collective-permute-start.3
  14.0 1.6 %collective-permute-start.4 = (f32[3,32,128]{2,1,0:T(8,128)S(1)}, f32[3,32,128]{2,1,0:T(8,128)S(1)}, u32[]{:S(2)}, u32[]{:S(2)}) collective-permute-start(f32[3,32,128]{2,1,0:T(8,128)S(1)} %get-tuple-element.12), channel_id=1, source_target_pairs={{1,2},{2,1},{0,3},{3,0},{5,6},{6,5},{4,7},{7,4},{9,10},{10,9},{8,1... | collective-permute-start | bytes 147464 | tf_op jit(solution)/shard_map/ppermute | solution.py:736
  15.6 0.0 collective-permute-done.3.za_ref
  15.6 2.0 %collective-permute-done.4.zb_ref = f32[3,32,128]{2,1,0:T(8,128)S(1)} collective-permute-done((f32[3,32,128]{2,1,0:T(8,128)S(1)}, f32[3,32,128]{2,1,0:T(8,128)S(1)}, u32[]{:S(2)}, u32[]{:S(2)}) %collective-permute-start.4) | collective-permute-done | bytes 49184 | tf_op jit(solution)/shard_map/ppermute | solution.py:736
  17.6 1.8 %shard_map.29 = (f32[20,2,32,128]{3,2,1,0:T(8,128)S(1)}, f32[20,2,32,128]{3,2,1,0:T(8,128)S(1)}, f32[20,2,32,128]{3,2,1,0:T(8,128)S(1)}, f32[8,8,128]{2,1,0:T(8,128)S(1)}) custom-call(f32[32,16,128]{2,1,0:T(8,128)S(1)} %copy-done, f32[8,16,128]{2,1,0:T(8,128)S(1)} %collective-permute-done.xh_ref, f32[40,8,128]{2,1,0:T(8,128)S(1)} %collective-permute-done.1.ya_ref, ...), custom_call_target="tpu_custom_call" | custom-call | tf_op jit(solution)/shard_map/pallas_call | solution.py:739
  19.4 0.0 copy-start.1
  19.4 3.1 %collective-permute-start.7 = (f32[8,8,128]{2,1,0:T(8,128)S(1)}, f32[8,8,128]{2,1,0:T(8,128)S(1)}, u32[]{:S(2)}, u32[]{:S(2)}) collective-permute-start(f32[8,8,128]{2,1,0:T(8,128)S(1)} %get-tuple-element.13.refs_0_), channel_id=1, source_target_pairs={{0,10},{1,11},{2,8},{3,9},{4,14},{5,15},{6,12},{7,13},{8,2},{9,3},... | collective-permute-start | bytes 98312 | tf_op jit(solution)/shard_map/ppermute | solution.py:751
  22.5 0.5 %collective-permute-start.6 = (f32[8,8,128]{2,1,0:T(8,128)S(1)}, f32[8,8,128]{2,1,0:T(8,128)S(1)}, u32[]{:S(2)}, u32[]{:S(2)}) collective-permute-start(f32[8,8,128]{2,1,0:T(8,128)S(1)} %get-tuple-element.13.refs_0_), channel_id=1, source_target_pairs={{0,2},{1,3},{2,0},{3,1},{4,6},{5,7},{6,4},{7,5},{8,10},{9,11},{10,... | collective-permute-start | bytes 98312 | tf_op jit(solution)/shard_map/ppermute | solution.py:750
  23.1 0.8 %collective-permute-start.5 = (f32[8,8,128]{2,1,0:T(8,128)S(1)}, f32[8,8,128]{2,1,0:T(8,128)S(1)}, u32[]{:S(2)}, u32[]{:S(2)}) collective-permute-start(f32[8,8,128]{2,1,0:T(8,128)S(1)} %get-tuple-element.13.refs_0_), channel_id=1, source_target_pairs={{0,8},{4,12},{8,0},{12,4},{1,9},{5,13},{9,1},{13,5},{2,10},{6,14},... | collective-permute-start | bytes 98312 | tf_op jit(solution)/shard_map/ppermute | solution.py:749
  23.8 1.3 %collective-permute-done.7.refs_3_ = f32[8,8,128]{2,1,0:T(8,128)S(1)} collective-permute-done((f32[8,8,128]{2,1,0:T(8,128)S(1)}, f32[8,8,128]{2,1,0:T(8,128)S(1)}, u32[]{:S(2)}, u32[]{:S(2)}) %collective-permute-start.7) | collective-permute-done | bytes 32800 | tf_op jit(solution)/shard_map/ppermute | solution.py:751
  25.2 1.3 %collective-permute-done.6.refs_2_ = f32[8,8,128]{2,1,0:T(8,128)S(1)} collective-permute-done((f32[8,8,128]{2,1,0:T(8,128)S(1)}, f32[8,8,128]{2,1,0:T(8,128)S(1)}, u32[]{:S(2)}, u32[]{:S(2)}) %collective-permute-start.6) | collective-permute-done | bytes 32800 | tf_op jit(solution)/shard_map/ppermute | solution.py:750
  26.4 1.4 %collective-permute-done.5.refs_1_ = f32[8,8,128]{2,1,0:T(8,128)S(1)} collective-permute-done((f32[8,8,128]{2,1,0:T(8,128)S(1)}, f32[8,8,128]{2,1,0:T(8,128)S(1)}, u32[]{:S(2)}, u32[]{:S(2)}) %collective-permute-start.5) | collective-permute-done | bytes 32800 | tf_op jit(solution)/shard_map/ppermute | solution.py:749
  27.9 2.0 %collective-permute-start.10 = (f32[4,8,8,128]{3,2,1,0:T(8,128)S(1)}, f32[4,8,8,128]{3,2,1,0:T(8,128)S(1)}, u32[]{:S(2)}, u32[]{:S(2)}) collective-permute-start(f32[4,8,8,128]{3,2,1,0:T(8,128)S(1)} %shard_map.30.refs_0_), channel_id=1, source_target_pairs={{0,20},{4,16},{8,28},{12,24},{16,4},{20,0},{24,12},{28,8},{1,21},{... | collective-permute-start | bytes 393224 | tf_op jit(solution)/shard_map/ppermute | solution.py:761
  29.9 0.7 %collective-permute-start.9 = (f32[4,8,8,128]{3,2,1,0:T(8,128)S(1)}, f32[4,8,8,128]{3,2,1,0:T(8,128)S(1)}, u32[]{:S(2)}, u32[]{:S(2)}) collective-permute-start(f32[4,8,8,128]{3,2,1,0:T(8,128)S(1)} %shard_map.30.refs_0_), channel_id=1, source_target_pairs={{0,4},{4,0},{8,12},{12,8},{1,5},{5,1},{9,13},{13,9},{2,6},{6,2},{1... | collective-permute-start | bytes 393224 | tf_op jit(solution)/shard_map/ppermute | solution.py:760
  30.6 0.8 %collective-permute-start.8 = (f32[4,8,8,128]{3,2,1,0:T(8,128)S(1)}, f32[4,8,8,128]{3,2,1,0:T(8,128)S(1)}, u32[]{:S(2)}, u32[]{:S(2)}) collective-permute-start(f32[4,8,8,128]{3,2,1,0:T(8,128)S(1)} %shard_map.30.refs_0_), channel_id=1, source_target_pairs={{0,16},{16,0},{1,17},{17,1},{2,18},{18,2},{3,19},{19,3},{4,20},{20... | collective-permute-start | bytes 393224 | tf_op jit(solution)/shard_map/ppermute | solution.py:759
  31.4 0.0 collective-permute-start.11
  31.4 3.4 %collective-permute-done.10.refs_3_ = f32[4,8,8,128]{3,2,1,0:T(8,128)S(1)} collective-permute-done((f32[4,8,8,128]{3,2,1,0:T(8,128)S(1)}, f32[4,8,8,128]{3,2,1,0:T(8,128)S(1)}, u32[]{:S(2)}, u32[]{:S(2)}) %collective-permute-start.10) | collective-permute-done | bytes 131104 | tf_op jit(solution)/shard_map/ppermute | solution.py:761
  34.8 0.0 collective-permute-start.14
  34.8 0.7 %collective-permute-done.9.refs_2_ = f32[4,8,8,128]{3,2,1,0:T(8,128)S(1)} collective-permute-done((f32[4,8,8,128]{3,2,1,0:T(8,128)S(1)}, f32[4,8,8,128]{3,2,1,0:T(8,128)S(1)}, u32[]{:S(2)}, u32[]{:S(2)}) %collective-permute-start.9) | collective-permute-done | bytes 131104 | tf_op jit(solution)/shard_map/ppermute | solution.py:760
  35.6 0.0 collective-permute-start.13
  35.6 0.5 %collective-permute-done.8.refs_1_ = f32[4,8,8,128]{3,2,1,0:T(8,128)S(1)} collective-permute-done((f32[4,8,8,128]{3,2,1,0:T(8,128)S(1)}, f32[4,8,8,128]{3,2,1,0:T(8,128)S(1)}, u32[]{:S(2)}, u32[]{:S(2)}) %collective-permute-start.8) | collective-permute-done | bytes 131104 | tf_op jit(solution)/shard_map/ppermute | solution.py:759
  36.1 0.0 collective-permute-start.12
  36.1 0.0 collective-permute-done.11.refs_4_
  36.1 0.0 collective-permute-done.14.refs_7_
  36.2 0.8 %collective-permute-done.13.refs_6_ = f32[4,8,8,128]{3,2,1,0:T(8,128)S(1)} collective-permute-done((f32[4,8,8,128]{3,2,1,0:T(8,128)S(1)}, f32[4,8,8,128]{3,2,1,0:T(8,128)S(1)}, u32[]{:S(2)}, u32[]{:S(2)}) %collective-permute-start.13) | collective-permute-done | bytes 131104 | tf_op jit(solution)/shard_map/ppermute | solution.py:763
  36.9 0.5 %collective-permute-done.12.refs_5_ = f32[4,8,8,128]{3,2,1,0:T(8,128)S(1)} collective-permute-done((f32[4,8,8,128]{3,2,1,0:T(8,128)S(1)}, f32[4,8,8,128]{3,2,1,0:T(8,128)S(1)}, u32[]{:S(2)}, u32[]{:S(2)}) %collective-permute-start.12) | collective-permute-done | bytes 131104 | tf_op jit(solution)/shard_map/ppermute | solution.py:763
  37.5 0.0 copy-done.1
  37.5 6.9 %shard_map.31 = f32[32,16,128]{2,1,0:T(8,128)} custom-call(f32[4,8,8,128]{3,2,1,0:T(8,128)S(1)} %shard_map.30.refs_0_, f32[4,8,8,128]{3,2,1,0:T(8,128)S(1)} %collective-permute-done.8.refs_1_, f32[4,8,8,128]{3,2,1,0:T(8,128)S(1)} %collective-permute-done.9.refs_2_, f32[4,8,8,128]{3,2,1,0:T(8,128)S(1)} %collective-permute-done.10.refs_3_, ...), custom_call_target="tpu_custom_call" | custom-call | tf_op jit(solution)/shard_map/pallas_call | solution.py:772
  (3 shorter events, 0.0 us)
Async XLA Ops:
  0.8 5.2 %collective-permute-start = (f32[8,16,128]{2,1,0:T(8,128)S(1)}, f32[8,16,128]{2,1,0:T(8,128)S(1)}, u32[]{:S(2)}, u32[]{:S(2)}) collective-permute-start(f32[8,16,128]{2,1,0:T(8,128)S(1)} %constant_dynamic-slice_fusion.2), channel_id=1, source_target_pairs={{0,16},{16,0},{1,17},{17,1},{2,18},{18,2},{3,19},{19,3},{4,20},{20... | collective-permute-start | bytes 196616 | tf_op jit(solution)/shard_map/ppermute | solution.py:716
  6.1 7.5 %copy-start = (f32[32,16,128]{2,1,0:T(8,128)S(1)}, f32[32,16,128]{2,1,0:T(8,128)}, u32[]{:S(2)}) copy-start(f32[32,16,128]{2,1,0:T(8,128)} %own_ref.3) | copy-start | bytes 786436
  6.1 5.4 %collective-permute-start.2 = (f32[40,8,128]{2,1,0:T(8,128)S(1)}, f32[40,8,128]{2,1,0:T(8,128)S(1)}, u32[]{:S(2)}, u32[]{:S(2)}) collective-permute-start(f32[40,8,128]{2,1,0:T(8,128)S(1)} %get-tuple-element.17), channel_id=1, source_target_pairs={{4,8},{8,4},{0,16},{12,28},{20,24},{24,20},{16,0},{28,12},{5,9},{9... | collective-permute-start | bytes 491528 | tf_op jit(solution)/shard_map/ppermute | solution.py:722
  8.2 5.3 %collective-permute-start.1 = (f32[40,8,128]{2,1,0:T(8,128)S(1)}, f32[40,8,128]{2,1,0:T(8,128)S(1)}, u32[]{:S(2)}, u32[]{:S(2)}) collective-permute-start(f32[40,8,128]{2,1,0:T(8,128)S(1)} %get-tuple-element.18), channel_id=1, source_target_pairs={{0,4},{4,0},{8,12},{12,8},{1,5},{5,1},{9,13},{13,9},{2,6},{6,2},{1... | collective-permute-start | bytes 491528 | tf_op jit(solution)/shard_map/ppermute | solution.py:721
  13.9 1.7 %collective-permute-start.3 = (f32[3,32,128]{2,1,0:T(8,128)S(1)}, f32[3,32,128]{2,1,0:T(8,128)S(1)}, u32[]{:S(2)}, u32[]{:S(2)}) collective-permute-start(f32[3,32,128]{2,1,0:T(8,128)S(1)} %get-tuple-element.11), channel_id=1, source_target_pairs={{0,1},{1,0},{2,3},{3,2},{4,5},{5,4},{6,7},{7,6},{8,9},{9,8},{10,11... | collective-permute-start | bytes 147464 | tf_op jit(solution)/shard_map/ppermute | solution.py:735
  14.0 3.6 %collective-permute-start.4 = (f32[3,32,128]{2,1,0:T(8,128)S(1)}, f32[3,32,128]{2,1,0:T(8,128)S(1)}, u32[]{:S(2)}, u32[]{:S(2)}) collective-permute-start(f32[3,32,128]{2,1,0:T(8,128)S(1)} %get-tuple-element.12), channel_id=1, source_target_pairs={{1,2},{2,1},{0,3},{3,0},{5,6},{6,5},{4,7},{7,4},{9,10},{10,9},{8,1... | collective-permute-start | bytes 147464 | tf_op jit(solution)/shard_map/ppermute | solution.py:736
  19.4 18.1 %copy-start.1 = (f32[128,128]{1,0:T(8,128)S(1)}, f32[128,128]{1,0:T(8,128)}, u32[]{:S(2)}) copy-start(f32[128,128]{1,0:T(8,128)} %constant.36.clone.refs_11_) | copy-start | bytes 196612
  19.4 5.8 %collective-permute-start.7 = (f32[8,8,128]{2,1,0:T(8,128)S(1)}, f32[8,8,128]{2,1,0:T(8,128)S(1)}, u32[]{:S(2)}, u32[]{:S(2)}) collective-permute-start(f32[8,8,128]{2,1,0:T(8,128)S(1)} %get-tuple-element.13.refs_0_), channel_id=1, source_target_pairs={{0,10},{1,11},{2,8},{3,9},{4,14},{5,15},{6,12},{7,13},{8,2},{9,3},... | collective-permute-start | bytes 98312 | tf_op jit(solution)/shard_map/ppermute | solution.py:751
  22.5 3.9 %collective-permute-start.6 = (f32[8,8,128]{2,1,0:T(8,128)S(1)}, f32[8,8,128]{2,1,0:T(8,128)S(1)}, u32[]{:S(2)}, u32[]{:S(2)}) collective-permute-start(f32[8,8,128]{2,1,0:T(8,128)S(1)} %get-tuple-element.13.refs_0_), channel_id=1, source_target_pairs={{0,2},{1,3},{2,0},{3,1},{4,6},{5,7},{6,4},{7,5},{8,10},{9,11},{10,... | collective-permute-start | bytes 98312 | tf_op jit(solution)/shard_map/ppermute | solution.py:750
  23.1 4.8 %collective-permute-start.5 = (f32[8,8,128]{2,1,0:T(8,128)S(1)}, f32[8,8,128]{2,1,0:T(8,128)S(1)}, u32[]{:S(2)}, u32[]{:S(2)}) collective-permute-start(f32[8,8,128]{2,1,0:T(8,128)S(1)} %get-tuple-element.13.refs_0_), channel_id=1, source_target_pairs={{0,8},{4,12},{8,0},{12,4},{1,9},{5,13},{9,1},{13,5},{2,10},{6,14},... | collective-permute-start | bytes 98312 | tf_op jit(solution)/shard_map/ppermute | solution.py:749
  27.9 6.9 %collective-permute-start.10 = (f32[4,8,8,128]{3,2,1,0:T(8,128)S(1)}, f32[4,8,8,128]{3,2,1,0:T(8,128)S(1)}, u32[]{:S(2)}, u32[]{:S(2)}) collective-permute-start(f32[4,8,8,128]{3,2,1,0:T(8,128)S(1)} %shard_map.30.refs_0_), channel_id=1, source_target_pairs={{0,20},{4,16},{8,28},{12,24},{16,4},{20,0},{24,12},{28,8},{1,21},{... | collective-permute-start | bytes 393224 | tf_op jit(solution)/shard_map/ppermute | solution.py:761
  29.9 5.7 %collective-permute-start.9 = (f32[4,8,8,128]{3,2,1,0:T(8,128)S(1)}, f32[4,8,8,128]{3,2,1,0:T(8,128)S(1)}, u32[]{:S(2)}, u32[]{:S(2)}) collective-permute-start(f32[4,8,8,128]{3,2,1,0:T(8,128)S(1)} %shard_map.30.refs_0_), channel_id=1, source_target_pairs={{0,4},{4,0},{8,12},{12,8},{1,5},{5,1},{9,13},{13,9},{2,6},{6,2},{1... | collective-permute-start | bytes 393224 | tf_op jit(solution)/shard_map/ppermute | solution.py:760
  30.6 5.5 %collective-permute-start.8 = (f32[4,8,8,128]{3,2,1,0:T(8,128)S(1)}, f32[4,8,8,128]{3,2,1,0:T(8,128)S(1)}, u32[]{:S(2)}, u32[]{:S(2)}) collective-permute-start(f32[4,8,8,128]{3,2,1,0:T(8,128)S(1)} %shard_map.30.refs_0_), channel_id=1, source_target_pairs={{0,16},{16,0},{1,17},{17,1},{2,18},{18,2},{3,19},{19,3},{4,20},{20... | collective-permute-start | bytes 393224 | tf_op jit(solution)/shard_map/ppermute | solution.py:759
  31.4 4.7 %collective-permute-start.11 = (f32[4,8,8,128]{3,2,1,0:T(8,128)S(1)}, f32[4,8,8,128]{3,2,1,0:T(8,128)S(1)}, u32[]{:S(2)}, u32[]{:S(2)}) collective-permute-start(f32[4,8,8,128]{3,2,1,0:T(8,128)S(1)} %shard_map.30.refs_0_), channel_id=1, source_target_pairs={{0,1},{1,0},{2,3},{3,2},{4,5},{5,4},{6,7},{7,6},{8,9},{9,8},{10,11... | collective-permute-start | bytes 393224 | tf_op jit(solution)/shard_map/ppermute | solution.py:763
  34.8 1.3 %collective-permute-start.14 = (f32[4,8,8,128]{3,2,1,0:T(8,128)S(1)}, f32[4,8,8,128]{3,2,1,0:T(8,128)S(1)}, u32[]{:S(2)}, u32[]{:S(2)}) collective-permute-start(f32[4,8,8,128]{3,2,1,0:T(8,128)S(1)} %collective-permute-done.10.refs_3_), channel_id=1, source_target_pairs={{0,1},{1,0},{2,3},{3,2},{4,5},{5,4},{6,7},{7,6},{8,9},{9,8},{10,11... | collective-permute-start | bytes 393224 | tf_op jit(solution)/shard_map/ppermute | solution.py:763
  35.6 1.3 %collective-permute-start.13 = (f32[4,8,8,128]{3,2,1,0:T(8,128)S(1)}, f32[4,8,8,128]{3,2,1,0:T(8,128)S(1)}, u32[]{:S(2)}, u32[]{:S(2)}) collective-permute-start(f32[4,8,8,128]{3,2,1,0:T(8,128)S(1)} %collective-permute-done.9.refs_2_), channel_id=1, source_target_pairs={{0,1},{1,0},{2,3},{3,2},{4,5},{5,4},{6,7},{7,6},{8,9},{9,8},{10,11... | collective-permute-start | bytes 393224 | tf_op jit(solution)/shard_map/ppermute | solution.py:763
  36.1 1.3 %collective-permute-start.12 = (f32[4,8,8,128]{3,2,1,0:T(8,128)S(1)}, f32[4,8,8,128]{3,2,1,0:T(8,128)S(1)}, u32[]{:S(2)}, u32[]{:S(2)}) collective-permute-start(f32[4,8,8,128]{3,2,1,0:T(8,128)S(1)} %collective-permute-done.8.refs_1_), channel_id=1, source_target_pairs={{0,1},{1,0},{2,3},{3,2},{4,5},{5,4},{6,7},{7,6},{8,9},{9,8},{10,11... | collective-permute-start | bytes 393224 | tf_op jit(solution)/shard_map/ppermute | solution.py:763

commit v7 on v6

--- a/solution.py
+++ b/solution.py
@@ -240,10 +240,10 @@
     for column, total in enumerate(block_sums(ref, at, rows)):
         before = window(ref, (at - 1) % slots, column, rows)
         after = window(ref, (at + 1) % slots, column, rows)
-        if at == 0:
-            before = jnp.where(at_low, 0.0, before)
-        if at == own - 1:
-            after = jnp.where(at_high, 0.0, after)
+        if at in (0, own):
+            before = jnp.where(at_low if at == 0 else at_high, 0.0, before)
+        if at in (own - 1, slots - 1):
+            after = jnp.where(at_low if at == slots - 1 else at_high, 0.0, after)
         totals.append(total + (jnp.where(odd, after, before) if to_red else jnp.where(odd, before, after)))
     return totals
 
@@ -264,15 +264,25 @@
     return masks
 
 
-def block_plane(at, nx, own_ref, xh_ref, ya_ref, yb_ref, even_y):
+def block_plane(at, own_ref, ya_ref, yb_ref, even_y):
     a, b = ya_ref[at], yb_ref[at]
-    middle = own_ref[at] if at < nx else xh_ref[at - nx]
     low = jnp.where(even_y, b, a)
     high = jnp.where(even_y, a, b)
-    return jnp.concatenate([low, middle, high], axis=0)
-
-
-def pack_kernel(halo, own_ref, xh_ref, ya_ref, yb_ref, za_ref, zb_ref):
+    return jnp.concatenate([low, own_ref[at], high], axis=0)
+
+
+def block_columns(halo, at, own_ref, ya_ref, yb_ref, za_ref, zb_ref, even_y, even_z):
+    _, _, nz = own_ref.shape
+    j, k = at // (nz // halo), at % (nz // halo)
+    a, b = za_ref[j], zb_ref[j]
+    left = pltpu.roll(jnp.where(even_z, b, a), (2 * nz - halo - halo * k) % nz, 1)
+    right = pltpu.roll(jnp.where(even_z, a, b), (nz - halo * k) % nz, 1)
+    lane = lanes_of(left.shape)
+    sides = jnp.where(lane < halo, right, jnp.where(lane >= nz - halo, left, 0.0))
+    return block_plane(at, own_ref, ya_ref, yb_ref, even_y), sides
+
+
+def pack_kernel(halo, own_ref, ya_ref, yb_ref, za_ref, zb_ref):
     even_y = lax.axis_index("gy") % 2 == 0
     even_z = lax.axis_index("gz") % 2 == 0
     nx, ny, nz = own_ref.shape
@@ -282,91 +292,150 @@
     for j in range(za_ref.shape[0]):
         last = jnp.zeros(shape, jnp.float32)
         first = jnp.zeros(shape, jnp.float32)
-        for k in range(groups):
-            at = j * groups + k
-            if at >= nx + halo:
-                break
-            plane = block_plane(at, nx, own_ref, xh_ref, ya_ref, yb_ref, even_y)
+        for k in range(min(groups, nx - j * groups)):
+            plane = block_plane(j * groups + k, own_ref, ya_ref, yb_ref, even_y)
             last = jnp.where(group == k, pltpu.roll(plane, (halo * k + halo) % nz, 1), last)
             first = jnp.where(group == k, pltpu.roll(plane, halo * k, 1), first)
         za_ref[j] = jnp.where(even_z, last, first)
         zb_ref[j] = jnp.where(even_z, first, last)
 
 
+def smooth(count, own, masks, odd, ends, gr_ref, gb_ref, red_ref, black_ref, done):
+    rows = odd.shape[0]
+    body = slice(PAD, PAD + rows)
+
+    def value_of(source, at, c, total):
+        value = masks[c] * total
+        return source[at, c] + value if at < source.shape[0] else value
+
+    for at in range(count):
+        for c in range(2):
+            red_ref[at, c, body, :] = gr_ref[at, c] if at < gr_ref.shape[0] else jnp.zeros_like(masks[c])
+    for step in range(3):
+        source, target, other = (gr_ref, red_ref, black_ref) if step == 1 else (gb_ref, black_ref, red_ref)
+        for at in range(count):
+            totals = block_totals(other, at, rows, own, odd, step == 1, *ends)
+            for c in range(2):
+                value = value_of(source, at, c, totals[c])
+                target[at, c, body, :] = value
+                if step == 2:
+                    done(at, c, totals[c], value)
+
+
+def x_ends():
+    here = lax.axis_index("gx")
+    return here == 0, here == lax.axis_size("gx") - 1
+
+
 def pre_kernel(
-    halo, own_ref, xh_ref, ya_ref, yb_ref, za_ref, zb_ref,
-    gr_ref, gb_ref, dark_ref, send_ref,
-    fr_ref, fb_ref, red_ref, black_ref, rest_ref,
+    halo, own_ref, ya_ref, yb_ref, za_ref, zb_ref,
+    send_ref, face_ref,
+    fr_ref, fb_ref, gr_ref, gb_ref, red_ref, black_ref, rest_ref,
+):
+    even_y = lax.axis_index("gy") % 2 == 0
+    even_z = lax.axis_index("gz") % 2 == 0
+    nx, ny, nz = own_ref.shape
+    count, _, rows, _ = red_ref.shape
+    rows = rows - 2 * PAD
+    own = nx // 2
+    shape = (rows, LANES)
+    odd = odd_of(shape)
+    masks = block_mask((ny, nz), halo)
+    inner = slice(halo, halo + ny)
+    ends = x_ends()
+    clear_pads(red_ref)
+    clear_pads(black_ref)
+    group = lanes_of(shape) // (2 * halo)
+    low_sides = jnp.zeros(shape, jnp.float32)
+    high_sides = jnp.zeros(shape, jnp.float32)
+    for at in range(own):
+        planes = []
+        for x in (2 * at, 2 * at + 1):
+            columns = block_columns(halo, x, own_ref, ya_ref, yb_ref, za_ref, zb_ref, even_y, even_z)
+            planes.append(columns)
+            if x < halo:
+                turned = pltpu.roll(columns[1], (halo + 2 * halo * x) % LANES, 1)
+                low_sides = jnp.where(group == x, turned, low_sides)
+
+                @pl.when(jnp.logical_not(ends[0]))
+                def _(x=x, plane=columns[0]):
+                    face_ref[x] = plane
+
+            if x >= nx - halo:
+                p = x - (nx - halo)
+                turned = pltpu.roll(columns[1], (halo + 2 * halo * p) % LANES, 1)
+                high_sides = jnp.where(group == p, turned, high_sides)
+
+                @pl.when(ends[0])
+                def _(p=p, plane=columns[0]):
+                    face_ref[p] = plane
+
+        for c in range(2):
+            red = jnp.where(odd, planes[1][c], planes[0][c])
+            black = jnp.where(odd, planes[0][c], planes[1][c])
+            if c == 0:
+                fr_ref[at], fb_ref[at] = red[inner], black[inner]
+            gr_ref[at, c], gb_ref[at, c] = masks[c] * red, masks[c] * black
+    face_ref[halo] = jnp.where(ends[0], high_sides, low_sides)
+
+    def keep(at, c, total, value):
+        if c == 0:
+            left_over = total[inner] - centre * value[inner]
+            rest_ref[at] = left_over + fb_ref[at] if at < own else left_over
+
+    smooth(count, own, masks, odd, ends, gr_ref, gb_ref, red_ref, black_ref, keep)
+    for at in range(count):
+        total = block_totals(black_ref, at, rows, own, odd, True, *ends)[0]
+        left_over = total[inner] - centre * red_ref[at, 0, PAD + halo : PAD + halo + ny, :]
+        if at < own:
+            left_over = left_over + fr_ref[at]
+        rest_ref[at] = rest_ref[at] + left_over
+    half, quarter = ny // 2, nz // 4
+    pairs_y = rest_ref[:, pl.ds(0, half, stride=2), :] + rest_ref[:, pl.ds(1, half, stride=2), :]
+    column = lanes_of((nz, nz))
+    target = 2 * (column % quarter) + (column // quarter) % 2
+    weight = jnp.where(rows_of((nz, nz)) // 2 == target, 0.5, 0.0)
+    coarse = exact_dot(pairs_y.reshape(count * half, nz), weight).reshape(count, half, nz)
+    part = lanes_of((half, nz)) // quarter
+    pick = (((rows_of((half, nz)) + part) & 1) == 1) ^ (part >= 2)
+    turn = quarter * lax.axis_index("gz")
+    for at in range(count // 2):
+        send_ref[at] = pltpu.roll(jnp.where(pick, coarse[2 * at + 1], coarse[2 * at]), turn, 1)
+
+
+def field_kernel(
+    halo, own_ref, ya_ref, yb_ref, za_ref, zb_ref, face_ref, after_ref,
+    gr_ref, gb_ref, dark_ref,
+    red_ref, black_ref,
 ):
     even_y = lax.axis_index("gy") % 2 == 0
     even_z = lax.axis_index("gz") % 2 == 0
     nx, ny, nz = own_ref.shape
     count, _, rows, _ = gr_ref.shape
     own = nx // 2
-    groups = nz // halo
     shape = (rows, LANES)
-    odd = odd_of(shape)
+    odd, lane = odd_of(shape), lanes_of(shape)
     masks = block_mask((ny, nz), halo)
-    lane = lanes_of(shape)
-    low, high = lane < halo, lane >= nz - halo
-    inner = slice(halo, halo + ny)
-    body = slice(PAD, PAD + rows)
-    here = lax.axis_index("gx")
-    ends = (here == 0, here == lax.axis_size("gx") - 1)
     clear_pads(red_ref)
     clear_pads(black_ref)
 
-    def columns(at):
-        j, k = at // groups, at % groups
-        a, b = za_ref[j], zb_ref[j]
-        left = jnp.where(even_z, b, a)
-        right = jnp.where(even_z, a, b)
-        right = pltpu.roll(right, (nz - halo * k) % nz, 1)
-        left = pltpu.roll(left, (2 * nz - halo - halo * k) % nz, 1)
-        sides = jnp.where(low, right, jnp.where(high, left, 0.0))
-        return block_plane(at, nx, own_ref, xh_ref, ya_ref, yb_ref, even_y), sides
+    def columns(x):
+        if x < nx:
+            return block_columns(halo, x, own_ref, ya_ref, yb_ref, za_ref, zb_ref, even_y, even_z)
+        p = x - nx
+        sides = pltpu.roll(face_ref[halo], (2 * LANES - halo - 2 * halo * p) % LANES, 1)
+        return face_ref[p], jnp.where((lane < halo) | (lane >= nz - halo), sides, 0.0)
 
     for at in range(count):
         first, second = columns(2 * at), columns(2 * at + 1)
         for c in range(2):
-            red = jnp.where(odd, second[c], first[c])
-            black = jnp.where(odd, first[c], second[c])
-            if c == 0 and at < own:
-                fr_ref[at], fb_ref[at] = red[inner], black[inner]
-            red = masks[c] * red
-            gr_ref[at, c], gb_ref[at, c] = red, masks[c] * black
-            red_ref[at, c, body, :] = red
-    for at in range(count):
-        totals = block_totals(red_ref, at, rows, own, odd, False, *ends)
-        for c in range(2):
-            black_ref[at, c, body, :] = gb_ref[at, c] + masks[c] * totals[c]
-    for at in range(count):
-        totals = block_totals(black_ref, at, rows, own, odd, True, *ends)
-        for c in range(2):
-            red_ref[at, c, body, :] = gr_ref[at, c] + masks[c] * totals[c]
-    for at in range(count):
-        totals = block_totals(red_ref, at, rows, own, odd, False, *ends)
-        for c in range(2):
-            value = gb_ref[at, c] + masks[c] * totals[c]
-            black_ref[at, c, body, :] = value
-            dark_ref[at, c] = value
-            if c == 0 and at < own:
-                rest_ref[at] = fb_ref[at] + totals[c][inner] - centre * value[inner]
-    for at in range(own):
-        total = block_totals(black_ref, at, rows, own, odd, True, *ends)[0]
-        left_over = fr_ref[at] + total[inner] - centre * red_ref[at, 0, PAD + halo : PAD + halo + ny, :]
-        rest_ref[at] = rest_ref[at] + left_over
-    half, quarter = ny // 2, nz // 4
-    pairs_y = rest_ref[:, pl.ds(0, half, stride=2), :] + rest_ref[:, pl.ds(1, half, stride=2), :]
-    column = lanes_of((nz, nz))
-    target = 2 * (column % quarter) + (column // quarter) % 2
-    weight = jnp.where(rows_of((nz, nz)) // 2 == target, 0.5, 0.0)
-    coarse = exact_dot(pairs_y.reshape(own * half, nz), weight).reshape(own, half, nz)
-    part = lanes_of((half, nz)) // quarter
-    pick = (((rows_of((half, nz)) + part) & 1) == 1) ^ (part >= 2)
-    turn = quarter * lax.axis_index("gz")
-    for at in range(own // 2):
-        send_ref[at] = pltpu.roll(jnp.where(pick, coarse[2 * at + 1], coarse[2 * at]), turn, 1)
+            gr_ref[at, c] = masks[c] * jnp.where(odd, second[c], first[c])
+            gb_ref[at, c] = masks[c] * jnp.where(odd, first[c], second[c])
+
+    def keep(at, c, total, value):
+        dark_ref[at, c] = value
+
+    smooth(count, own, masks, odd, x_ends(), gr_ref, gb_ref, red_ref, black_ref, keep)
 
 
 def stack_kernel(*refs):
@@ -432,24 +501,39 @@
             clear_pads(ref)
 
     _, slots, block_rows, _ = gathered[0].shape
+    slots = slots - 1
     count1, _, rows1, _ = fr1.shape
     quarter = LANES // 4
     group = lanes_of((block_rows, LANES)) // quarter
     held = [jnp.bitwise_and(group - jnp.bitwise_xor(gz, bits), 3) for bits in range(4)]
     theirs = [[kind == part for kind in held] for part in range(4)]
+    def unpack(far, second, at):
+        y = jnp.bitwise_xor(gy, 2 * far + (second >> 1))
+        rows = pl.ds(pl.multiple_of(y * block_rows, 8), block_rows)
+        blocks = [gathered[4 * (bits & 1) + second][far + (bits & 2), at] for bits in range(4)]
+        parts = []
+        for part in range(4):
+            value = blocks[0]
+            for block, mine in zip(blocks[1:], theirs[part][1:]):
+                value = jnp.where(mine, block, value)
+            parts.append(pltpu.roll(value, LANES - quarter * part, 1) if part else value)
+        return rows, parts
+
+    half1 = count1 // 2
     for far in range(2):
         for second in range(4):
             x = jnp.bitwise_xor(gx, second & 1)
-            y = jnp.bitwise_xor(gy, 2 * far + (second >> 1))
-            rows = pl.ds(pl.multiple_of(y * block_rows, 8), block_rows)
             for at in range(slots):
-                blocks = [gathered[4 * (bits & 1) + second][far + (bits & 2), at] for bits in range(4)]
+                rows, parts = unpack(far, second, at)
                 for part, target in enumerate((fr1, fr1, fb1, fb1)):
-                    value = blocks[0]
-                    for block, mine in zip(blocks[1:], theirs[part][1:]):
-                        value = jnp.where(mine, block, value)
-                    turned = pltpu.roll(value, LANES - quarter * part, 1) if part else value
-                    target[x * slots + at, part % 2, rows, :] = turned
+                    target[x * slots + at, part % 2, rows, :] = parts[part]
+    for far in range(2):
+        for second in range(4):
+            x = jnp.bitwise_xor(gx, second & 1)
+            next_slot = jnp.where(x == 0, half1, half1 - 1)
+            rows, parts = unpack(far, second, slots)
+            for part, target in enumerate((fr1, fr1, fb1, fb1)):
+                target[next_slot, part % 2, rows, :] = target[next_slot, part % 2, rows, :] + parts[part]
 
     def fold_total(ref, at, e, start, count, low, high, odds, to_red):
         lane = lanes_of((count, LANES))
@@ -711,18 +795,13 @@
     nx, ny, nz = density.shape
     count_x, count_y, count_z = (lax.axis_size(axis) for axis in ("gx", "gy", "gz"))
     whole = (nx * count_x, ny * count_y, nz * count_z)
-    gx, gy = lax.axis_index("gx"), lax.axis_index("gy")
-    face = lax.dynamic_slice_in_dim(density, jnp.where(gx == 0, nx - halo, 0), halo, 0)
-    side = lax.ppermute(face, "gx", flips(count_x, 1))
-    tall = jnp.concatenate([density, side], axis=0)
-    even = gy % 2 == 0
-    ya = lax.dynamic_slice_in_dim(tall, jnp.where(even, ny - halo, 0), halo, 1)
-    yb = lax.dynamic_slice_in_dim(tall, jnp.where(even, 0, ny - halo), halo, 1)
+    even = lax.axis_index("gy") % 2 == 0
+    ya = lax.dynamic_slice_in_dim(density, jnp.where(even, ny - halo, 0), halo, 1)
+    yb = lax.dynamic_slice_in_dim(density, jnp.where(even, 0, ny - halo), halo, 1)
     ya = lax.ppermute(ya, "gy", pairs(count_y, 0))
     yb = lax.ppermute(yb, ("gx", "gy"), inner_pairs(count_x, count_y))
     rows = ny + 2 * halo
-    planes = nx + halo
-    packs = -(-planes * halo // nz)
+    packs = -(-nx * halo // nz)
 
     def params(mib):
         return pltpu.CompilerParams(vmem_limit_bytes=mib * 1024 * 1024)
@@ -730,26 +809,31 @@
     za, zb = pl.pallas_call(
         functools.partial(pack_kernel, halo),
         out_shape=[struct(packs, rows, nz)] * 2,
-        in_specs=vmem(4), out_specs=vmem(2), compiler_params=params(4),
-    )(density, side, ya, yb)
+        in_specs=vmem(3), out_specs=vmem(2), compiler_params=params(4),
+    )(density, ya, yb)
     za = lax.ppermute(za, "gz", pairs(count_z, 0))
     zb = lax.ppermute(zb, "gz", pairs(count_z, 1) + [(0, count_z - 1), (count_z - 1, 0)])
+    own, near = nx // 2, nx // 2 + 2
+    send, face = pl.pallas_call(
+        functools.partial(pre_kernel, halo),
+        out_shape=[struct(near // 2, ny // 2, nz), struct(halo + 1, rows, LANES)],
+        in_specs=vmem(5), out_specs=vmem(2), compiler_params=params(10),
+        scratch_shapes=[scratch(own, ny, nz)] * 2
+        + [scratch(own, 2, rows, LANES)] * 2
+        + [scratch(near, 2, rows + 2 * PAD, LANES)] * 2
+        + [scratch(near, ny, nz)],
+    )(density, ya, yb, za, zb)
+    face = lax.ppermute(face, "gx", flips(count_x, 1))
+    planes = nx + halo
     slots = (planes // 2, 2, rows, LANES)
     padded = (planes // 2, 2, rows + 2 * PAD, LANES)
-    gr, gb, black, send = pl.pallas_call(
-        functools.partial(pre_kernel, halo),
-        out_shape=[struct(*slots)] * 3 + [struct(nx // 4, ny // 2, nz)],
-        in_specs=vmem(6), out_specs=vmem(4), compiler_params=params(10),
-        scratch_shapes=[scratch(nx // 2, ny, nz)] * 2
-        + [scratch(*padded)] * 2
-        + [scratch(nx // 2, ny, nz)],
-    )(density, side, ya, yb, za, zb)
     first = [
         send,
         lax.ppermute(send, "gy", flips(count_y, 2)),
         lax.ppermute(send, "gz", flips(count_z, 2)),
         lax.ppermute(send, ("gy", "gz"), flips(count_y * count_z, 2 * count_z + 2)),
     ]
+    first[3], face = lax.optimization_barrier((first[3], face))
     block = pl.pallas_call(
         stack_kernel, out_shape=struct(4, *send.shape),
         in_specs=vmem(4), out_specs=pl.BlockSpec(memory_space=pltpu.VMEM), compiler_params=params(2),
@@ -760,6 +844,14 @@
         lax.ppermute(block, "gy", flips(count_y, 1)),
         lax.ppermute(block, ("gx", "gy"), flips(count_x * count_y, count_y + 1)),
     ]
+    gr, gb, black = pl.pallas_call(
+        functools.partial(field_kernel, halo),
+        out_shape=[struct(*slots)] * 3,
+        in_specs=vmem(7), out_specs=vmem(3), compiler_params=params(8),
+        scratch_shapes=[scratch(*padded)] * 2,
+        cost_estimate=pl.CostEstimate(flops=20_000_000, bytes_accessed=2_000_000, transcendentals=0),
+    )(density, ya, yb, za, zb, face, block)
+    *second[1:], gr, gb, black = lax.optimization_barrier((*second[1:], gr, gb, black))
     third = [lax.ppermute(blocks, "gz", flips(count_z, 1)) for blocks in second]
     count1, rows1, rows2 = whole[0] // 4, whole[1] // 2, whole[1] // 4
     room = [scratch(count1, 2, rows1, LANES)] * 2

time: 44.5 us -> 43.4 us (0.975)
  waiting for transfers between devices: 17 us -> 13.4 us
  Pallas kernels: 9.04 us -> 12.5 us
  local copies, waits for them, and re-layouts: 1.86 us -> 1.04 us
    pallas_call x1 -> x2, Pallas kernels: 1.78 us -> 5.23 us  [the longest x1 3.77 us: block_cycle(): pl.pallas_call(functools.partial(pre_kernel, halo), out_shape=[struct(nea...]
    ppermute x1, waiting for transfers between devices: 3.37 us -> 1.63 us  [block_cycle(): lax.ppermute(block, ('gx', 'gy'), flips(count_x * count_y, count_y + 1))]
    ppermute x1, starting transfers between devices: 3 us -> 1.46 us  [block_cycle(): face = lax.ppermute(face, 'gx', flips(count_x, 1))]
    ppermute x1, waiting for transfers between devices: 1.27 us -> 0.01 us  [block_cycle(): face = lax.ppermute(face, 'gx', flips(count_x, 1))]
    ppermute x1, starting transfers between devices: 2.09 us -> 3.06 us  [block_cycle(): yb = lax.ppermute(yb, ('gx', 'gy'), inner_pairs(count_x, count_y))]
    unnamed x5 -> x4, local copies, waits for them, and re-layouts: 0.97 us -> 0.01 us
    ppermute x1, waiting for transfers between devices: 0.75 us -> 1.52 us  [block_cycle(): lax.ppermute(block, 'gy', flips(count_y, 1))]
    ppermute x1, waiting for transfers between devices: 1.27 us -> 0.7 us  [block_cycle(): lax.ppermute(send, 'gz', flips(count_z, 2))]
  transfers between devices with their start and end apart: 15 -> 15, of which waited for: 12 -> 12; matrix products, arithmetic and copies ran while one was open for 2% -> 0% of each run, Pallas kernels for 0% -> 3%
where the time goes in v7:
time: 43.4 us; the launch traced here: 43.3 us
  starting transfers between devices  16.3 us (38%)
  waiting for transfers between devices  13.4 us (31%)
  Pallas kernels  12.5 us (29%)
  local copies, waits for them, and re-layouts  1.04 us (2%)
    pallas_call x1, Pallas kernels, block_cycle(): pl.pallas_call(functools.partial(solve_kernel, halo, whole), out_shape=st...  6.96 us
    pallas_call x1, Pallas kernels, block_cycle(): pl.pallas_call(functools.partial(pre_kernel, halo), out_shape=[struct(nea...  3.77 us
    ppermute x1, starting transfers between devices, block_cycle(): yb = lax.ppermute(yb, ('gx', 'gy'), inner_pairs(count_x, count_y))  3.06 us
    ppermute x1, starting transfers between devices, block_cycle(): lax.ppermute(block, ('gx', 'gy'), flips(count_x * count_y, count_y + 1))  2.57 us
    ppermute x1, starting transfers between devices, block_cycle(): lax.ppermute(send, ('gy', 'gz'), flips(count_y * count_z, 2 * count_z + 2))  2.57 us
    ppermute x1, waiting for transfers between devices, block_cycle(): yb = lax.ppermute(yb, ('gx', 'gy'), inner_pairs(count_x, count_y))  1.86 us
    ppermute x1, waiting for transfers between devices, block_cycle(): lax.ppermute(zb, 'gz', pairs(count_z, 1) + [(0, count_z - 1), (count_z -...  1.81 us
    ppermute x1, starting transfers between devices, block_cycle(): ya = lax.ppermute(ya, 'gy', pairs(count_y, 0))  1.63 us
  transfers between devices with their start and end apart: 15, of which 12 were waited for; matrix products, arithmetic and copies ran while one was open for 0% of the time, Pallas kernels for 3%

profile of v7, /device:TPU:0, one launch (start us, length us, event | category | flops | bytes accessed | tf_op | source)
XLA Modules:
  0.0 43.3 jit_solution(3866638604164552545)
XLA Ops:
  0.0 0.0 copy-start
  0.0 1.0 %constant_dynamic-slice_fusion = (f32[32,8,128]{2,1,0:T(8,128)S(1)}, f32[32,8,128]{2,1,0:T(8,128)S(1)}) fusion(f32[32,16,128]{2,1,0:T(8,128)} %own_ref.5, s32[]{:T(128)S(6)} %select_n.18, s32[]{:T(128)S(6)} %select_n.17), kind=kLoop, calls=%fused_computation | loop fusion | bytes 524296 | tf_op jit(solution)/shard_map/dynamic_slice | solution.py:800
  1.0 3.1 %collective-permute-start.1 = (f32[32,8,128]{2,1,0:T(8,128)S(1)}, f32[32,8,128]{2,1,0:T(8,128)S(1)}, u32[]{:S(2)}, u32[]{:S(2)}) collective-permute-start(f32[32,8,128]{2,1,0:T(8,128)S(1)} %get-tuple-element.35), channel_id=1, source_target_pairs={{4,8},{8,4},{0,16},{12,28},{20,24},{24,20},{16,0},{28,12},{5,9},{9... | collective-permute-start | bytes 393224 | tf_op jit(solution)/shard_map/ppermute | solution.py:802
  4.1 1.6 %collective-permute-start = (f32[32,8,128]{2,1,0:T(8,128)S(1)}, f32[32,8,128]{2,1,0:T(8,128)S(1)}, u32[]{:S(2)}, u32[]{:S(2)}) collective-permute-start(f32[32,8,128]{2,1,0:T(8,128)S(1)} %get-tuple-element.36), channel_id=1, source_target_pairs={{0,4},{4,0},{8,12},{12,8},{1,5},{5,1},{9,13},{13,9},{2,6},{6,2},{1... | collective-permute-start | bytes 393224 | tf_op jit(solution)/shard_map/ppermute | solution.py:801
  5.7 1.9 %collective-permute-done.1.yb_ref = f32[32,8,128]{2,1,0:T(8,128)S(1)} collective-permute-done((f32[32,8,128]{2,1,0:T(8,128)S(1)}, f32[32,8,128]{2,1,0:T(8,128)S(1)}, u32[]{:S(2)}, u32[]{:S(2)}) %collective-permute-start.1) | collective-permute-done | bytes 131104 | tf_op jit(solution)/shard_map/ppermute | solution.py:802
  7.6 1.5 %collective-permute-done.ya_ref = f32[32,8,128]{2,1,0:T(8,128)S(1)} collective-permute-done((f32[32,8,128]{2,1,0:T(8,128)S(1)}, f32[32,8,128]{2,1,0:T(8,128)S(1)}, u32[]{:S(2)}, u32[]{:S(2)}) %collective-permute-start) | collective-permute-done | bytes 131104 | tf_op jit(solution)/shard_map/ppermute | solution.py:801
  9.1 0.0 copy-done
  9.1 0.3 shard_map.28
  9.4 0.1 collective-permute-start.2
  9.5 1.6 %collective-permute-start.3 = (f32[2,32,128]{2,1,0:T(8,128)S(1)}, f32[2,32,128]{2,1,0:T(8,128)S(1)}, u32[]{:S(2)}, u32[]{:S(2)}) collective-permute-start(f32[2,32,128]{2,1,0:T(8,128)S(1)} %get-tuple-element.21), channel_id=1, source_target_pairs={{1,2},{2,1},{0,3},{3,0},{5,6},{6,5},{4,7},{7,4},{9,10},{10,9},{8,1... | collective-permute-start | bytes 98312 | tf_op jit(solution)/shard_map/ppermute | solution.py:815
  11.1 0.0 collective-permute-done.2.za_ref
  11.1 1.8 %collective-permute-done.3.zb_ref = f32[2,32,128]{2,1,0:T(8,128)S(1)} collective-permute-done((f32[2,32,128]{2,1,0:T(8,128)S(1)}, f32[2,32,128]{2,1,0:T(8,128)S(1)}, u32[]{:S(2)}, u32[]{:S(2)}) %collective-permute-start.3) | collective-permute-done | bytes 32800 | tf_op jit(solution)/shard_map/ppermute | solution.py:815
  12.9 3.8 %shard_map.29 = (f32[9,8,128]{2,1,0:T(8,128)S(1)}, f32[9,32,128]{2,1,0:T(8,128)S(1)}) custom-call(f32[32,16,128]{2,1,0:T(8,128)S(1)} %copy-done, f32[32,8,128]{2,1,0:T(8,128)S(1)} %collective-permute-done.ya_ref, f32[32,8,128]{2,1,0:T(8,128)S(1)} %collective-permute-done.1.yb_ref, f32[2,32,128]{2,1,0:T(8,128)S(1)} %collective-permute-done.2.za_ref, ...), custom_call_target="tpu_custom_call" | custom-call | tf_op jit(solution)/shard_map/pallas_call | solution.py:817
  16.7 1.5 %collective-permute-start.7 = (f32[9,32,128]{2,1,0:T(8,128)S(1)}, f32[9,32,128]{2,1,0:T(8,128)S(1)}, u32[]{:S(2)}, u32[]{:S(2)}) collective-permute-start(f32[9,32,128]{2,1,0:T(8,128)S(1)} %get-tuple-element.23), channel_id=1, source_target_pairs={{0,16},{16,0},{1,17},{17,1},{2,18},{18,2},{3,19},{19,3},{4,20},{20... | collective-permute-start | bytes 442376 | tf_op jit(solution)/shard_map/ppermute | solution.py:826
  18.1 2.6 %collective-permute-start.6 = (f32[9,8,128]{2,1,0:T(8,128)S(1)}, f32[9,8,128]{2,1,0:T(8,128)S(1)}, u32[]{:S(2)}, u32[]{:S(2)}) collective-permute-start(f32[9,8,128]{2,1,0:T(8,128)S(1)} %get-tuple-element.22.refs_0_), channel_id=1, source_target_pairs={{0,10},{1,11},{2,8},{3,9},{4,14},{5,15},{6,12},{7,13},{8,2},{9,3},... | collective-permute-start | bytes 110600 | tf_op jit(solution)/shard_map/ppermute | solution.py:834
  20.7 0.5 %collective-permute-start.5 = (f32[9,8,128]{2,1,0:T(8,128)S(1)}, f32[9,8,128]{2,1,0:T(8,128)S(1)}, u32[]{:S(2)}, u32[]{:S(2)}) collective-permute-start(f32[9,8,128]{2,1,0:T(8,128)S(1)} %get-tuple-element.22.refs_0_), channel_id=1, source_target_pairs={{0,2},{1,3},{2,0},{3,1},{4,6},{5,7},{6,4},{7,5},{8,10},{9,11},{10,... | collective-permute-start | bytes 110600 | tf_op jit(solution)/shard_map/ppermute | solution.py:833
  21.2 1.3 %collective-permute-start.4 = (f32[9,8,128]{2,1,0:T(8,128)S(1)}, f32[9,8,128]{2,1,0:T(8,128)S(1)}, u32[]{:S(2)}, u32[]{:S(2)}) collective-permute-start(f32[9,8,128]{2,1,0:T(8,128)S(1)} %get-tuple-element.22.refs_0_), channel_id=1, source_target_pairs={{0,8},{4,12},{8,0},{12,4},{1,9},{5,13},{9,1},{13,5},{2,10},{6,14},... | collective-permute-start | bytes 110600 | tf_op jit(solution)/shard_map/ppermute | solution.py:832
  22.5 1.4 %collective-permute-done.6.refs_3_ = f32[9,8,128]{2,1,0:T(8,128)S(1)} collective-permute-done((f32[9,8,128]{2,1,0:T(8,128)S(1)}, f32[9,8,128]{2,1,0:T(8,128)S(1)}, u32[]{:S(2)}, u32[]{:S(2)}) %collective-permute-start.6) | collective-permute-done | bytes 36896 | tf_op jit(solution)/shard_map/ppermute | solution.py:834
  23.9 0.0 collective-permute-done.7.face_ref
  23.9 0.7 %collective-permute-done.5.refs_2_ = f32[9,8,128]{2,1,0:T(8,128)S(1)} collective-permute-done((f32[9,8,128]{2,1,0:T(8,128)S(1)}, f32[9,8,128]{2,1,0:T(8,128)S(1)}, u32[]{:S(2)}, u32[]{:S(2)}) %collective-permute-start.5) | collective-permute-done | bytes 36896 | tf_op jit(solution)/shard_map/ppermute | solution.py:833
  24.6 1.5 %collective-permute-done.4.refs_1_ = f32[9,8,128]{2,1,0:T(8,128)S(1)} collective-permute-done((f32[9,8,128]{2,1,0:T(8,128)S(1)}, f32[9,8,128]{2,1,0:T(8,128)S(1)}, u32[]{:S(2)}, u32[]{:S(2)}) %collective-permute-start.4) | collective-permute-done | bytes 36896 | tf_op jit(solution)/shard_map/ppermute | solution.py:832
  26.2 0.0 copy-start.1
  26.2 2.6 %collective-permute-start.10 = (f32[4,9,8,128]{3,2,1,0:T(8,128)S(1)}, f32[4,9,8,128]{3,2,1,0:T(8,128)S(1)}, u32[]{:S(2)}, u32[]{:S(2)}) collective-permute-start(f32[4,9,8,128]{3,2,1,0:T(8,128)S(1)} %shard_map.30.after_ref.refs_0_), channel_id=1, source_target_pairs={{0,20},{4,16},{8,28},{12,24},{16,4},{20,0},{24,12},{28,8},{1,21},{... | collective-permute-start | bytes 442376 | tf_op jit(solution)/shard_map/ppermute | solution.py:845
  28.8 0.5 %collective-permute-start.9 = (f32[4,9,8,128]{3,2,1,0:T(8,128)S(1)}, f32[4,9,8,128]{3,2,1,0:T(8,128)S(1)}, u32[]{:S(2)}, u32[]{:S(2)}) collective-permute-start(f32[4,9,8,128]{3,2,1,0:T(8,128)S(1)} %shard_map.30.after_ref.refs_0_), channel_id=1, source_target_pairs={{0,4},{4,0},{8,12},{12,8},{1,5},{5,1},{9,13},{13,9},{2,6},{6,2},{1... | collective-permute-start | bytes 442376 | tf_op jit(solution)/shard_map/ppermute | solution.py:844
  29.2 0.5 %collective-permute-start.8 = (f32[4,9,8,128]{3,2,1,0:T(8,128)S(1)}, f32[4,9,8,128]{3,2,1,0:T(8,128)S(1)}, u32[]{:S(2)}, u32[]{:S(2)}) collective-permute-start(f32[4,9,8,128]{3,2,1,0:T(8,128)S(1)} %shard_map.30.after_ref.refs_0_), channel_id=1, source_target_pairs={{0,16},{16,0},{1,17},{17,1},{2,18},{18,2},{3,19},{19,3},{4,20},{20... | collective-permute-start | bytes 442376 | tf_op jit(solution)/shard_map/ppermute | solution.py:843
  29.7 0.0 collective-permute-start.11
  29.7 1.5 %shard_map.31 = (f32[20,2,32,128]{3,2,1,0:T(8,128)S(1)}, f32[20,2,32,128]{3,2,1,0:T(8,128)S(1)}, f32[20,2,32,128]{3,2,1,0:T(8,128)S(1)}) custom-call(f32[32,16,128]{2,1,0:T(8,128)S(1)} %copy-done, f32[32,8,128]{2,1,0:T(8,128)S(1)} %collective-permute-done.ya_ref, f32[32,8,128]{2,1,0:T(8,128)S(1)} %collective-permute-done.1.yb_ref, ...), custom_call_target="tpu_custom_call" | custom-call | flops 20000000 | bytes 2000000 | tf_op jit(solution)/shard_map/pallas_call | solution.py:847
  31.2 1.6 %collective-permute-done.10.refs_3_ = f32[4,9,8,128]{3,2,1,0:T(8,128)S(1)} collective-permute-done((f32[4,9,8,128]{3,2,1,0:T(8,128)S(1)}, f32[4,9,8,128]{3,2,1,0:T(8,128)S(1)}, u32[]{:S(2)}, u32[]{:S(2)}) %collective-permute-start.10) | collective-permute-done | bytes 147488 | tf_op jit(solution)/shard_map/ppermute | solution.py:845
  32.8 1.5 %collective-permute-done.9.refs_2_ = f32[4,9,8,128]{3,2,1,0:T(8,128)S(1)} collective-permute-done((f32[4,9,8,128]{3,2,1,0:T(8,128)S(1)}, f32[4,9,8,128]{3,2,1,0:T(8,128)S(1)}, u32[]{:S(2)}, u32[]{:S(2)}) %collective-permute-start.9) | collective-permute-done | bytes 147488 | tf_op jit(solution)/shard_map/ppermute | solution.py:844
  34.4 0.1 collective-permute-done.8.refs_1_
  34.4 0.0 collective-permute-start.12
  34.4 0.5 %collective-permute-start.13 = (f32[4,9,8,128]{3,2,1,0:T(8,128)S(1)}, f32[4,9,8,128]{3,2,1,0:T(8,128)S(1)}, u32[]{:S(2)}, u32[]{:S(2)}) collective-permute-start(f32[4,9,8,128]{3,2,1,0:T(8,128)S(1)} %collective-permute-done.9.refs_2_), channel_id=1, source_target_pairs={{0,1},{1,0},{2,3},{3,2},{4,5},{5,4},{6,7},{7,6},{8,9},{9,8},{10,11... | collective-permute-start | bytes 442376 | tf_op jit(solution)/shard_map/ppermute | solution.py:855
  34.9 0.0 collective-permute-start.14
  34.9 0.0 collective-permute-done.11.refs_4_
  34.9 0.9 %collective-permute-done.12.refs_5_ = f32[4,9,8,128]{3,2,1,0:T(8,128)S(1)} collective-permute-done((f32[4,9,8,128]{3,2,1,0:T(8,128)S(1)}, f32[4,9,8,128]{3,2,1,0:T(8,128)S(1)}, u32[]{:S(2)}, u32[]{:S(2)}) %collective-permute-start.12) | collective-permute-done | bytes 147488 | tf_op jit(solution)/shard_map/ppermute | solution.py:855
  35.8 0.2 collective-permute-done.13.refs_6_
  36.0 0.3 collective-permute-done.14.refs_7_
  36.3 0.0 copy-done.1
  36.3 7.0 %shard_map.32 = f32[32,16,128]{2,1,0:T(8,128)} custom-call(f32[4,9,8,128]{3,2,1,0:T(8,128)S(1)} %shard_map.30.after_ref.refs_0_, f32[4,9,8,128]{3,2,1,0:T(8,128)S(1)} %collective-permute-done.8.refs_1_, f32[4,9,8,128]{3,2,1,0:T(8,128)S(1)} %collective-permute-done.9.refs_2_, f32[4,9,8,128]{3,2,1,0:T(8,128)S(1)} %collective-permute-done.10.refs_3_, ...), custom_call_target="tpu_custom_call" | custom-call | tf_op jit(solution)/shard_map/pallas_call | solution.py:864
  (1 shorter events, 0.0 us)
Async XLA Ops:
  0.0 9.1 %copy-start = (f32[32,16,128]{2,1,0:T(8,128)S(1)}, f32[32,16,128]{2,1,0:T(8,128)}, u32[]{:S(2)}) copy-start(f32[32,16,128]{2,1,0:T(8,128)} %own_ref.5) | copy-start | bytes 786436
  1.0 6.6 %collective-permute-start.1 = (f32[32,8,128]{2,1,0:T(8,128)S(1)}, f32[32,8,128]{2,1,0:T(8,128)S(1)}, u32[]{:S(2)}, u32[]{:S(2)}) collective-permute-start(f32[32,8,128]{2,1,0:T(8,128)S(1)} %get-tuple-element.35), channel_id=1, source_target_pairs={{4,8},{8,4},{0,16},{12,28},{20,24},{24,20},{16,0},{28,12},{5,9},{9... | collective-permute-start | bytes 393224 | tf_op jit(solution)/shard_map/ppermute | solution.py:802
  4.1 5.0 %collective-permute-start = (f32[32,8,128]{2,1,0:T(8,128)S(1)}, f32[32,8,128]{2,1,0:T(8,128)S(1)}, u32[]{:S(2)}, u32[]{:S(2)}) collective-permute-start(f32[32,8,128]{2,1,0:T(8,128)S(1)} %get-tuple-element.36), channel_id=1, source_target_pairs={{0,4},{4,0},{8,12},{12,8},{1,5},{5,1},{9,13},{13,9},{2,6},{6,2},{1... | collective-permute-start | bytes 393224 | tf_op jit(solution)/shard_map/ppermute | solution.py:801
  9.4 1.7 %collective-permute-start.2 = (f32[2,32,128]{2,1,0:T(8,128)S(1)}, f32[2,32,128]{2,1,0:T(8,128)S(1)}, u32[]{:S(2)}, u32[]{:S(2)}) collective-permute-start(f32[2,32,128]{2,1,0:T(8,128)S(1)} %get-tuple-element.20), channel_id=1, source_target_pairs={{0,1},{1,0},{2,3},{3,2},{4,5},{5,4},{6,7},{7,6},{8,9},{9,8},{10,11... | collective-permute-start | bytes 98312 | tf_op jit(solution)/shard_map/ppermute | solution.py:814
  9.5 3.4 %collective-permute-start.3 = (f32[2,32,128]{2,1,0:T(8,128)S(1)}, f32[2,32,128]{2,1,0:T(8,128)S(1)}, u32[]{:S(2)}, u32[]{:S(2)}) collective-permute-start(f32[2,32,128]{2,1,0:T(8,128)S(1)} %get-tuple-element.21), channel_id=1, source_target_pairs={{1,2},{2,1},{0,3},{3,0},{5,6},{6,5},{4,7},{7,4},{9,10},{10,9},{8,1... | collective-permute-start | bytes 98312 | tf_op jit(solution)/shard_map/ppermute | solution.py:815
  16.7 7.3 %collective-permute-start.7 = (f32[9,32,128]{2,1,0:T(8,128)S(1)}, f32[9,32,128]{2,1,0:T(8,128)S(1)}, u32[]{:S(2)}, u32[]{:S(2)}) collective-permute-start(f32[9,32,128]{2,1,0:T(8,128)S(1)} %get-tuple-element.23), channel_id=1, source_target_pairs={{0,16},{16,0},{1,17},{17,1},{2,18},{18,2},{3,19},{19,3},{4,20},{20... | collective-permute-start | bytes 442376 | tf_op jit(solution)/shard_map/ppermute | solution.py:826
  18.1 5.8 %collective-permute-start.6 = (f32[9,8,128]{2,1,0:T(8,128)S(1)}, f32[9,8,128]{2,1,0:T(8,128)S(1)}, u32[]{:S(2)}, u32[]{:S(2)}) collective-permute-start(f32[9,8,128]{2,1,0:T(8,128)S(1)} %get-tuple-element.22.refs_0_), channel_id=1, source_target_pairs={{0,10},{1,11},{2,8},{3,9},{4,14},{5,15},{6,12},{7,13},{8,2},{9,3},... | collective-permute-start | bytes 110600 | tf_op jit(solution)/shard_map/ppermute | solution.py:834
  20.7 4.0 %collective-permute-start.5 = (f32[9,8,128]{2,1,0:T(8,128)S(1)}, f32[9,8,128]{2,1,0:T(8,128)S(1)}, u32[]{:S(2)}, u32[]{:S(2)}) collective-permute-start(f32[9,8,128]{2,1,0:T(8,128)S(1)} %get-tuple-element.22.refs_0_), channel_id=1, source_target_pairs={{0,2},{1,3},{2,0},{3,1},{4,6},{5,7},{6,4},{7,5},{8,10},{9,11},{10,... | collective-permute-start | bytes 110600 | tf_op jit(solution)/shard_map/ppermute | solution.py:833
  21.2 4.9 %collective-permute-start.4 = (f32[9,8,128]{2,1,0:T(8,128)S(1)}, f32[9,8,128]{2,1,0:T(8,128)S(1)}, u32[]{:S(2)}, u32[]{:S(2)}) collective-permute-start(f32[9,8,128]{2,1,0:T(8,128)S(1)} %get-tuple-element.22.refs_0_), channel_id=1, source_target_pairs={{0,8},{4,12},{8,0},{12,4},{1,9},{5,13},{9,1},{13,5},{2,10},{6,14},... | collective-permute-start | bytes 110600 | tf_op jit(solution)/shard_map/ppermute | solution.py:832
  26.2 10.1 %copy-start.1 = (f32[128,128]{1,0:T(8,128)S(1)}, f32[128,128]{1,0:T(8,128)}, u32[]{:S(2)}) copy-start(f32[128,128]{1,0:T(8,128)} %constant.26.clone.refs_11_) | copy-start | bytes 196612
  26.2 6.7 %collective-permute-start.10 = (f32[4,9,8,128]{3,2,1,0:T(8,128)S(1)}, f32[4,9,8,128]{3,2,1,0:T(8,128)S(1)}, u32[]{:S(2)}, u32[]{:S(2)}) collective-permute-start(f32[4,9,8,128]{3,2,1,0:T(8,128)S(1)} %shard_map.30.after_ref.refs_0_), channel_id=1, source_target_pairs={{0,20},{4,16},{8,28},{12,24},{16,4},{20,0},{24,12},{28,8},{1,21},{... | collective-permute-start | bytes 442376 | tf_op jit(solution)/shard_map/ppermute | solution.py:845
  28.8 5.6 %collective-permute-start.9 = (f32[4,9,8,128]{3,2,1,0:T(8,128)S(1)}, f32[4,9,8,128]{3,2,1,0:T(8,128)S(1)}, u32[]{:S(2)}, u32[]{:S(2)}) collective-permute-start(f32[4,9,8,128]{3,2,1,0:T(8,128)S(1)} %shard_map.30.after_ref.refs_0_), channel_id=1, source_target_pairs={{0,4},{4,0},{8,12},{12,8},{1,5},{5,1},{9,13},{13,9},{2,6},{6,2},{1... | collective-permute-start | bytes 442376 | tf_op jit(solution)/shard_map/ppermute | solution.py:844
  29.2 5.2 %collective-permute-start.8 = (f32[4,9,8,128]{3,2,1,0:T(8,128)S(1)}, f32[4,9,8,128]{3,2,1,0:T(8,128)S(1)}, u32[]{:S(2)}, u32[]{:S(2)}) collective-permute-start(f32[4,9,8,128]{3,2,1,0:T(8,128)S(1)} %shard_map.30.after_ref.refs_0_), channel_id=1, source_target_pairs={{0,16},{16,0},{1,17},{17,1},{2,18},{18,2},{3,19},{19,3},{4,20},{20... | collective-permute-start | bytes 442376 | tf_op jit(solution)/shard_map/ppermute | solution.py:843
  29.7 5.2 %collective-permute-start.11 = (f32[4,9,8,128]{3,2,1,0:T(8,128)S(1)}, f32[4,9,8,128]{3,2,1,0:T(8,128)S(1)}, u32[]{:S(2)}, u32[]{:S(2)}) collective-permute-start(f32[4,9,8,128]{3,2,1,0:T(8,128)S(1)} %shard_map.30.after_ref.refs_0_), channel_id=1, source_target_pairs={{0,1},{1,0},{2,3},{3,2},{4,5},{5,4},{6,7},{7,6},{8,9},{9,8},{10,11... | collective-permute-start | bytes 442376 | tf_op jit(solution)/shard_map/ppermute | solution.py:855
  34.4 1.4 %collective-permute-start.12 = (f32[4,9,8,128]{3,2,1,0:T(8,128)S(1)}, f32[4,9,8,128]{3,2,1,0:T(8,128)S(1)}, u32[]{:S(2)}, u32[]{:S(2)}) collective-permute-start(f32[4,9,8,128]{3,2,1,0:T(8,128)S(1)} %collective-permute-done.8.refs_1_), channel_id=1, source_target_pairs={{0,1},{1,0},{2,3},{3,2},{4,5},{5,4},{6,7},{7,6},{8,9},{9,8},{10,11... | collective-permute-start | bytes 442376 | tf_op jit(solution)/shard_map/ppermute | solution.py:855
  34.4 1.6 %collective-permute-start.13 = (f32[4,9,8,128]{3,2,1,0:T(8,128)S(1)}, f32[4,9,8,128]{3,2,1,0:T(8,128)S(1)}, u32[]{:S(2)}, u32[]{:S(2)}) collective-permute-start(f32[4,9,8,128]{3,2,1,0:T(8,128)S(1)} %collective-permute-done.9.refs_2_), channel_id=1, source_target_pairs={{0,1},{1,0},{2,3},{3,2},{4,5},{5,4},{6,7},{7,6},{8,9},{9,8},{10,11... | collective-permute-start | bytes 442376 | tf_op jit(solution)/shard_map/ppermute | solution.py:855
  34.9 1.4 %collective-permute-start.14 = (f32[4,9,8,128]{3,2,1,0:T(8,128)S(1)}, f32[4,9,8,128]{3,2,1,0:T(8,128)S(1)}, u32[]{:S(2)}, u32[]{:S(2)}) collective-permute-start(f32[4,9,8,128]{3,2,1,0:T(8,128)S(1)} %collective-permute-done.10.refs_3_), channel_id=1, source_target_pairs={{0,1},{1,0},{2,3},{3,2},{4,5},{5,4},{6,7},{7,6},{8,9},{9,8},{10,11... | collective-permute-start | bytes 442376 | tf_op jit(solution)/shard_map/ppermute | solution.py:855

commit v8 on v7

--- a/solution.py
+++ b/solution.py
@@ -356,26 +356,19 @@
             if x < halo:
                 turned = pltpu.roll(columns[1], (halo + 2 * halo * x) % LANES, 1)
                 low_sides = jnp.where(group == x, turned, low_sides)
-
-                @pl.when(jnp.logical_not(ends[0]))
-                def _(x=x, plane=columns[0]):
-                    face_ref[x] = plane
-
             if x >= nx - halo:
                 p = x - (nx - halo)
                 turned = pltpu.roll(columns[1], (halo + 2 * halo * p) % LANES, 1)
                 high_sides = jnp.where(group == p, turned, high_sides)
-
-                @pl.when(ends[0])
-                def _(p=p, plane=columns[0]):
-                    face_ref[p] = plane
-
         for c in range(2):
             red = jnp.where(odd, planes[1][c], planes[0][c])
             black = jnp.where(odd, planes[0][c], planes[1][c])
             if c == 0:
                 fr_ref[at], fb_ref[at] = red[inner], black[inner]
             gr_ref[at, c], gb_ref[at, c] = masks[c] * red, masks[c] * black
+    for p in range(halo):
+        high = block_plane(nx - halo + p, own_ref, ya_ref, yb_ref, even_y)
+        face_ref[p] = jnp.where(ends[0], high, block_plane(p, own_ref, ya_ref, yb_ref, even_y))
     face_ref[halo] = jnp.where(ends[0], high_sides, low_sides)
 
     def keep(at, c, total, value):

time: 43.4 us -> 42 us (0.968)
  Pallas kernels: 12.5 us -> 11.1 us
    pallas_call x1, Pallas kernels: 3.77 us -> 2.4 us  [block_cycle(): pl.pallas_call(functools.partial(pre_kernel, halo), out_shape=[struct(nea...]
where the time goes in v8:
time: 42 us; the launch traced here: 41.9 us
  starting transfers between devices  16.3 us (39%)
  waiting for transfers between devices  13.4 us (32%)
  Pallas kernels  11.1 us (26%)
  local copies, waits for them, and re-layouts  1.04 us (2%)
    pallas_call x1, Pallas kernels, block_cycle(): pl.pallas_call(functools.partial(solve_kernel, halo, whole), out_shape=st...  6.95 us
    ppermute x1, starting transfers between devices, block_cycle(): yb = lax.ppermute(yb, ('gx', 'gy'), inner_pairs(count_x, count_y))  3.06 us
    ppermute x1, starting transfers between devices, block_cycle(): lax.ppermute(block, ('gx', 'gy'), flips(count_x * count_y, count_y + 1))  2.57 us
    ppermute x1, starting transfers between devices, block_cycle(): lax.ppermute(send, ('gy', 'gz'), flips(count_y * count_z, 2 * count_z + 2))  2.57 us
    pallas_call x1, Pallas kernels, block_cycle(): pl.pallas_call(functools.partial(pre_kernel, halo), out_shape=[struct(nea...  2.4 us
    ppermute x1, waiting for transfers between devices, block_cycle(): yb = lax.ppermute(yb, ('gx', 'gy'), inner_pairs(count_x, count_y))  1.86 us
    ppermute x1, waiting for transfers between devices, block_cycle(): lax.ppermute(zb, 'gz', pairs(count_z, 1) + [(0, count_z - 1), (count_z -...  1.81 us
    ppermute x1, starting transfers between devices, block_cycle(): ya = lax.ppermute(ya, 'gy', pairs(count_y, 0))  1.63 us
  transfers between devices with their start and end apart: 15, of which 12 were waited for; matrix products, arithmetic and copies ran while one was open for 0% of the time, Pallas kernels for 3%

profile of v8, /device:TPU:0, one launch (start us, length us, event | category | flops | bytes accessed | tf_op | source)
XLA Modules:
  0.0 41.9 jit_solution(9845589889953262623)
XLA Ops:
  0.0 0.0 copy-start
  0.0 1.0 %constant_dynamic-slice_fusion = (f32[32,8,128]{2,1,0:T(8,128)S(1)}, f32[32,8,128]{2,1,0:T(8,128)S(1)}) fusion(f32[32,16,128]{2,1,0:T(8,128)} %own_ref.5, s32[]{:T(128)S(6)} %select_n.18, s32[]{:T(128)S(6)} %select_n.17), kind=kLoop, calls=%fused_computation | loop fusion | bytes 524296 | tf_op jit(solution)/shard_map/dynamic_slice | solution.py:793
  1.0 3.1 %collective-permute-start.1 = (f32[32,8,128]{2,1,0:T(8,128)S(1)}, f32[32,8,128]{2,1,0:T(8,128)S(1)}, u32[]{:S(2)}, u32[]{:S(2)}) collective-permute-start(f32[32,8,128]{2,1,0:T(8,128)S(1)} %get-tuple-element.35), channel_id=1, source_target_pairs={{4,8},{8,4},{0,16},{12,28},{20,24},{24,20},{16,0},{28,12},{5,9},{9... | collective-permute-start | bytes 393224 | tf_op jit(solution)/shard_map/ppermute | solution.py:795
  4.1 1.6 %collective-permute-start = (f32[32,8,128]{2,1,0:T(8,128)S(1)}, f32[32,8,128]{2,1,0:T(8,128)S(1)}, u32[]{:S(2)}, u32[]{:S(2)}) collective-permute-start(f32[32,8,128]{2,1,0:T(8,128)S(1)} %get-tuple-element.36), channel_id=1, source_target_pairs={{0,4},{4,0},{8,12},{12,8},{1,5},{5,1},{9,13},{13,9},{2,6},{6,2},{1... | collective-permute-start | bytes 393224 | tf_op jit(solution)/shard_map/ppermute | solution.py:794
  5.7 1.9 %collective-permute-done.1.yb_ref = f32[32,8,128]{2,1,0:T(8,128)S(1)} collective-permute-done((f32[32,8,128]{2,1,0:T(8,128)S(1)}, f32[32,8,128]{2,1,0:T(8,128)S(1)}, u32[]{:S(2)}, u32[]{:S(2)}) %collective-permute-start.1) | collective-permute-done | bytes 131104 | tf_op jit(solution)/shard_map/ppermute | solution.py:795
  7.6 1.5 %collective-permute-done.ya_ref = f32[32,8,128]{2,1,0:T(8,128)S(1)} collective-permute-done((f32[32,8,128]{2,1,0:T(8,128)S(1)}, f32[32,8,128]{2,1,0:T(8,128)S(1)}, u32[]{:S(2)}, u32[]{:S(2)}) %collective-permute-start) | collective-permute-done | bytes 131104 | tf_op jit(solution)/shard_map/ppermute | solution.py:794
  9.1 0.0 copy-done
  9.1 0.3 shard_map.28
  9.4 0.1 collective-permute-start.2
  9.5 1.6 %collective-permute-start.3 = (f32[2,32,128]{2,1,0:T(8,128)S(1)}, f32[2,32,128]{2,1,0:T(8,128)S(1)}, u32[]{:S(2)}, u32[]{:S(2)}) collective-permute-start(f32[2,32,128]{2,1,0:T(8,128)S(1)} %get-tuple-element.21), channel_id=1, source_target_pairs={{1,2},{2,1},{0,3},{3,0},{5,6},{6,5},{4,7},{7,4},{9,10},{10,9},{8,1... | collective-permute-start | bytes 98312 | tf_op jit(solution)/shard_map/ppermute | solution.py:808
  11.1 0.0 collective-permute-done.2.za_ref
  11.1 1.8 %collective-permute-done.3.zb_ref = f32[2,32,128]{2,1,0:T(8,128)S(1)} collective-permute-done((f32[2,32,128]{2,1,0:T(8,128)S(1)}, f32[2,32,128]{2,1,0:T(8,128)S(1)}, u32[]{:S(2)}, u32[]{:S(2)}) %collective-permute-start.3) | collective-permute-done | bytes 32800 | tf_op jit(solution)/shard_map/ppermute | solution.py:808
  12.9 2.4 %shard_map.29 = (f32[9,8,128]{2,1,0:T(8,128)S(1)}, f32[9,32,128]{2,1,0:T(8,128)S(1)}) custom-call(f32[32,16,128]{2,1,0:T(8,128)S(1)} %copy-done, f32[32,8,128]{2,1,0:T(8,128)S(1)} %collective-permute-done.ya_ref, f32[32,8,128]{2,1,0:T(8,128)S(1)} %collective-permute-done.1.yb_ref, f32[2,32,128]{2,1,0:T(8,128)S(1)} %collective-permute-done.2.za_ref, ...), custom_call_target="tpu_custom_call" | custom-call | tf_op jit(solution)/shard_map/pallas_call | solution.py:810
  15.3 1.5 %collective-permute-start.7 = (f32[9,32,128]{2,1,0:T(8,128)S(1)}, f32[9,32,128]{2,1,0:T(8,128)S(1)}, u32[]{:S(2)}, u32[]{:S(2)}) collective-permute-start(f32[9,32,128]{2,1,0:T(8,128)S(1)} %get-tuple-element.23), channel_id=1, source_target_pairs={{0,16},{16,0},{1,17},{17,1},{2,18},{18,2},{3,19},{19,3},{4,20},{20... | collective-permute-start | bytes 442376 | tf_op jit(solution)/shard_map/ppermute | solution.py:819
  16.7 2.6 %collective-permute-start.6 = (f32[9,8,128]{2,1,0:T(8,128)S(1)}, f32[9,8,128]{2,1,0:T(8,128)S(1)}, u32[]{:S(2)}, u32[]{:S(2)}) collective-permute-start(f32[9,8,128]{2,1,0:T(8,128)S(1)} %get-tuple-element.22.refs_0_), channel_id=1, source_target_pairs={{0,10},{1,11},{2,8},{3,9},{4,14},{5,15},{6,12},{7,13},{8,2},{9,3},... | collective-permute-start | bytes 110600 | tf_op jit(solution)/shard_map/ppermute | solution.py:827
  19.3 0.5 %collective-permute-start.5 = (f32[9,8,128]{2,1,0:T(8,128)S(1)}, f32[9,8,128]{2,1,0:T(8,128)S(1)}, u32[]{:S(2)}, u32[]{:S(2)}) collective-permute-start(f32[9,8,128]{2,1,0:T(8,128)S(1)} %get-tuple-element.22.refs_0_), channel_id=1, source_target_pairs={{0,2},{1,3},{2,0},{3,1},{4,6},{5,7},{6,4},{7,5},{8,10},{9,11},{10,... | collective-permute-start | bytes 110600 | tf_op jit(solution)/shard_map/ppermute | solution.py:826
  19.8 1.3 %collective-permute-start.4 = (f32[9,8,128]{2,1,0:T(8,128)S(1)}, f32[9,8,128]{2,1,0:T(8,128)S(1)}, u32[]{:S(2)}, u32[]{:S(2)}) collective-permute-start(f32[9,8,128]{2,1,0:T(8,128)S(1)} %get-tuple-element.22.refs_0_), channel_id=1, source_target_pairs={{0,8},{4,12},{8,0},{12,4},{1,9},{5,13},{9,1},{13,5},{2,10},{6,14},... | collective-permute-start | bytes 110600 | tf_op jit(solution)/shard_map/ppermute | solution.py:825
  21.1 1.4 %collective-permute-done.6.refs_3_ = f32[9,8,128]{2,1,0:T(8,128)S(1)} collective-permute-done((f32[9,8,128]{2,1,0:T(8,128)S(1)}, f32[9,8,128]{2,1,0:T(8,128)S(1)}, u32[]{:S(2)}, u32[]{:S(2)}) %collective-permute-start.6) | collective-permute-done | bytes 36896 | tf_op jit(solution)/shard_map/ppermute | solution.py:827
  22.6 0.0 collective-permute-done.7.face_ref
  22.6 0.7 %collective-permute-done.5.refs_2_ = f32[9,8,128]{2,1,0:T(8,128)S(1)} collective-permute-done((f32[9,8,128]{2,1,0:T(8,128)S(1)}, f32[9,8,128]{2,1,0:T(8,128)S(1)}, u32[]{:S(2)}, u32[]{:S(2)}) %collective-permute-start.5) | collective-permute-done | bytes 36896 | tf_op jit(solution)/shard_map/ppermute | solution.py:826
  23.3 1.5 %collective-permute-done.4.refs_1_ = f32[9,8,128]{2,1,0:T(8,128)S(1)} collective-permute-done((f32[9,8,128]{2,1,0:T(8,128)S(1)}, f32[9,8,128]{2,1,0:T(8,128)S(1)}, u32[]{:S(2)}, u32[]{:S(2)}) %collective-permute-start.4) | collective-permute-done | bytes 36896 | tf_op jit(solution)/shard_map/ppermute | solution.py:825
  24.8 0.0 copy-start.1
  24.8 2.6 %collective-permute-start.10 = (f32[4,9,8,128]{3,2,1,0:T(8,128)S(1)}, f32[4,9,8,128]{3,2,1,0:T(8,128)S(1)}, u32[]{:S(2)}, u32[]{:S(2)}) collective-permute-start(f32[4,9,8,128]{3,2,1,0:T(8,128)S(1)} %shard_map.30.after_ref.refs_0_), channel_id=1, source_target_pairs={{0,20},{4,16},{8,28},{12,24},{16,4},{20,0},{24,12},{28,8},{1,21},{... | collective-permute-start | bytes 442376 | tf_op jit(solution)/shard_map/ppermute | solution.py:838
  27.4 0.5 %collective-permute-start.9 = (f32[4,9,8,128]{3,2,1,0:T(8,128)S(1)}, f32[4,9,8,128]{3,2,1,0:T(8,128)S(1)}, u32[]{:S(2)}, u32[]{:S(2)}) collective-permute-start(f32[4,9,8,128]{3,2,1,0:T(8,128)S(1)} %shard_map.30.after_ref.refs_0_), channel_id=1, source_target_pairs={{0,4},{4,0},{8,12},{12,8},{1,5},{5,1},{9,13},{13,9},{2,6},{6,2},{1... | collective-permute-start | bytes 442376 | tf_op jit(solution)/shard_map/ppermute | solution.py:837
  27.9 0.5 %collective-permute-start.8 = (f32[4,9,8,128]{3,2,1,0:T(8,128)S(1)}, f32[4,9,8,128]{3,2,1,0:T(8,128)S(1)}, u32[]{:S(2)}, u32[]{:S(2)}) collective-permute-start(f32[4,9,8,128]{3,2,1,0:T(8,128)S(1)} %shard_map.30.after_ref.refs_0_), channel_id=1, source_target_pairs={{0,16},{16,0},{1,17},{17,1},{2,18},{18,2},{3,19},{19,3},{4,20},{20... | collective-permute-start | bytes 442376 | tf_op jit(solution)/shard_map/ppermute | solution.py:836
  28.4 0.0 collective-permute-start.11
  28.4 1.5 %shard_map.31 = (f32[20,2,32,128]{3,2,1,0:T(8,128)S(1)}, f32[20,2,32,128]{3,2,1,0:T(8,128)S(1)}, f32[20,2,32,128]{3,2,1,0:T(8,128)S(1)}) custom-call(f32[32,16,128]{2,1,0:T(8,128)S(1)} %copy-done, f32[32,8,128]{2,1,0:T(8,128)S(1)} %collective-permute-done.ya_ref, f32[32,8,128]{2,1,0:T(8,128)S(1)} %collective-permute-done.1.yb_ref, ...), custom_call_target="tpu_custom_call" | custom-call | flops 20000000 | bytes 2000000 | tf_op jit(solution)/shard_map/pallas_call | solution.py:840
  29.8 1.6 %collective-permute-done.10.refs_3_ = f32[4,9,8,128]{3,2,1,0:T(8,128)S(1)} collective-permute-done((f32[4,9,8,128]{3,2,1,0:T(8,128)S(1)}, f32[4,9,8,128]{3,2,1,0:T(8,128)S(1)}, u32[]{:S(2)}, u32[]{:S(2)}) %collective-permute-start.10) | collective-permute-done | bytes 147488 | tf_op jit(solution)/shard_map/ppermute | solution.py:838
  31.5 1.5 %collective-permute-done.9.refs_2_ = f32[4,9,8,128]{3,2,1,0:T(8,128)S(1)} collective-permute-done((f32[4,9,8,128]{3,2,1,0:T(8,128)S(1)}, f32[4,9,8,128]{3,2,1,0:T(8,128)S(1)}, u32[]{:S(2)}, u32[]{:S(2)}) %collective-permute-start.9) | collective-permute-done | bytes 147488 | tf_op jit(solution)/shard_map/ppermute | solution.py:837
  33.0 0.1 collective-permute-done.8.refs_1_
  33.0 0.0 collective-permute-start.12
  33.0 0.5 %collective-permute-start.13 = (f32[4,9,8,128]{3,2,1,0:T(8,128)S(1)}, f32[4,9,8,128]{3,2,1,0:T(8,128)S(1)}, u32[]{:S(2)}, u32[]{:S(2)}) collective-permute-start(f32[4,9,8,128]{3,2,1,0:T(8,128)S(1)} %collective-permute-done.9.refs_2_), channel_id=1, source_target_pairs={{0,1},{1,0},{2,3},{3,2},{4,5},{5,4},{6,7},{7,6},{8,9},{9,8},{10,11... | collective-permute-start | bytes 442376 | tf_op jit(solution)/shard_map/ppermute | solution.py:848
  33.6 0.0 collective-permute-start.14
  33.6 0.0 collective-permute-done.11.refs_4_
  33.6 0.9 %collective-permute-done.12.refs_5_ = f32[4,9,8,128]{3,2,1,0:T(8,128)S(1)} collective-permute-done((f32[4,9,8,128]{3,2,1,0:T(8,128)S(1)}, f32[4,9,8,128]{3,2,1,0:T(8,128)S(1)}, u32[]{:S(2)}, u32[]{:S(2)}) %collective-permute-start.12) | collective-permute-done | bytes 147488 | tf_op jit(solution)/shard_map/ppermute | solution.py:848
  34.4 0.2 collective-permute-done.13.refs_6_
  34.6 0.3 collective-permute-done.14.refs_7_
  34.9 0.0 copy-done.1
  34.9 7.0 %shard_map.32 = f32[32,16,128]{2,1,0:T(8,128)} custom-call(f32[4,9,8,128]{3,2,1,0:T(8,128)S(1)} %shard_map.30.after_ref.refs_0_, f32[4,9,8,128]{3,2,1,0:T(8,128)S(1)} %collective-permute-done.8.refs_1_, f32[4,9,8,128]{3,2,1,0:T(8,128)S(1)} %collective-permute-done.9.refs_2_, f32[4,9,8,128]{3,2,1,0:T(8,128)S(1)} %collective-permute-done.10.refs_3_, ...), custom_call_target="tpu_custom_call" | custom-call | tf_op jit(solution)/shard_map/pallas_call | solution.py:857
  (1 shorter events, 0.0 us)
Async XLA Ops:
  0.0 9.1 %copy-start = (f32[32,16,128]{2,1,0:T(8,128)S(1)}, f32[32,16,128]{2,1,0:T(8,128)}, u32[]{:S(2)}) copy-start(f32[32,16,128]{2,1,0:T(8,128)} %own_ref.5) | copy-start | bytes 786436
  1.0 6.6 %collective-permute-start.1 = (f32[32,8,128]{2,1,0:T(8,128)S(1)}, f32[32,8,128]{2,1,0:T(8,128)S(1)}, u32[]{:S(2)}, u32[]{:S(2)}) collective-permute-start(f32[32,8,128]{2,1,0:T(8,128)S(1)} %get-tuple-element.35), channel_id=1, source_target_pairs={{4,8},{8,4},{0,16},{12,28},{20,24},{24,20},{16,0},{28,12},{5,9},{9... | collective-permute-start | bytes 393224 | tf_op jit(solution)/shard_map/ppermute | solution.py:795
  4.1 5.0 %collective-permute-start = (f32[32,8,128]{2,1,0:T(8,128)S(1)}, f32[32,8,128]{2,1,0:T(8,128)S(1)}, u32[]{:S(2)}, u32[]{:S(2)}) collective-permute-start(f32[32,8,128]{2,1,0:T(8,128)S(1)} %get-tuple-element.36), channel_id=1, source_target_pairs={{0,4},{4,0},{8,12},{12,8},{1,5},{5,1},{9,13},{13,9},{2,6},{6,2},{1... | collective-permute-start | bytes 393224 | tf_op jit(solution)/shard_map/ppermute | solution.py:794
  9.4 1.7 %collective-permute-start.2 = (f32[2,32,128]{2,1,0:T(8,128)S(1)}, f32[2,32,128]{2,1,0:T(8,128)S(1)}, u32[]{:S(2)}, u32[]{:S(2)}) collective-permute-start(f32[2,32,128]{2,1,0:T(8,128)S(1)} %get-tuple-element.20), channel_id=1, source_target_pairs={{0,1},{1,0},{2,3},{3,2},{4,5},{5,4},{6,7},{7,6},{8,9},{9,8},{10,11... | collective-permute-start | bytes 98312 | tf_op jit(solution)/shard_map/ppermute | solution.py:807
  9.5 3.4 %collective-permute-start.3 = (f32[2,32,128]{2,1,0:T(8,128)S(1)}, f32[2,32,128]{2,1,0:T(8,128)S(1)}, u32[]{:S(2)}, u32[]{:S(2)}) collective-permute-start(f32[2,32,128]{2,1,0:T(8,128)S(1)} %get-tuple-element.21), channel_id=1, source_target_pairs={{1,2},{2,1},{0,3},{3,0},{5,6},{6,5},{4,7},{7,4},{9,10},{10,9},{8,1... | collective-permute-start | bytes 98312 | tf_op jit(solution)/shard_map/ppermute | solution.py:808
  15.3 7.3 %collective-permute-start.7 = (f32[9,32,128]{2,1,0:T(8,128)S(1)}, f32[9,32,128]{2,1,0:T(8,128)S(1)}, u32[]{:S(2)}, u32[]{:S(2)}) collective-permute-start(f32[9,32,128]{2,1,0:T(8,128)S(1)} %get-tuple-element.23), channel_id=1, source_target_pairs={{0,16},{16,0},{1,17},{17,1},{2,18},{18,2},{3,19},{19,3},{4,20},{20... | collective-permute-start | bytes 442376 | tf_op jit(solution)/shard_map/ppermute | solution.py:819
  16.7 5.8 %collective-permute-start.6 = (f32[9,8,128]{2,1,0:T(8,128)S(1)}, f32[9,8,128]{2,1,0:T(8,128)S(1)}, u32[]{:S(2)}, u32[]{:S(2)}) collective-permute-start(f32[9,8,128]{2,1,0:T(8,128)S(1)} %get-tuple-element.22.refs_0_), channel_id=1, source_target_pairs={{0,10},{1,11},{2,8},{3,9},{4,14},{5,15},{6,12},{7,13},{8,2},{9,3},... | collective-permute-start | bytes 110600 | tf_op jit(solution)/shard_map/ppermute | solution.py:827
  19.3 4.0 %collective-permute-start.5 = (f32[9,8,128]{2,1,0:T(8,128)S(1)}, f32[9,8,128]{2,1,0:T(8,128)S(1)}, u32[]{:S(2)}, u32[]{:S(2)}) collective-permute-start(f32[9,8,128]{2,1,0:T(8,128)S(1)} %get-tuple-element.22.refs_0_), channel_id=1, source_target_pairs={{0,2},{1,3},{2,0},{3,1},{4,6},{5,7},{6,4},{7,5},{8,10},{9,11},{10,... | collective-permute-start | bytes 110600 | tf_op jit(solution)/shard_map/ppermute | solution.py:826
  19.8 4.9 %collective-permute-start.4 = (f32[9,8,128]{2,1,0:T(8,128)S(1)}, f32[9,8,128]{2,1,0:T(8,128)S(1)}, u32[]{:S(2)}, u32[]{:S(2)}) collective-permute-start(f32[9,8,128]{2,1,0:T(8,128)S(1)} %get-tuple-element.22.refs_0_), channel_id=1, source_target_pairs={{0,8},{4,12},{8,0},{12,4},{1,9},{5,13},{9,1},{13,5},{2,10},{6,14},... | collective-permute-start | bytes 110600 | tf_op jit(solution)/shard_map/ppermute | solution.py:825
  24.8 10.1 %copy-start.1 = (f32[128,128]{1,0:T(8,128)S(1)}, f32[128,128]{1,0:T(8,128)}, u32[]{:S(2)}) copy-start(f32[128,128]{1,0:T(8,128)} %constant.26.clone.refs_11_) | copy-start | bytes 196612
  24.8 6.7 %collective-permute-start.10 = (f32[4,9,8,128]{3,2,1,0:T(8,128)S(1)}, f32[4,9,8,128]{3,2,1,0:T(8,128)S(1)}, u32[]{:S(2)}, u32[]{:S(2)}) collective-permute-start(f32[4,9,8,128]{3,2,1,0:T(8,128)S(1)} %shard_map.30.after_ref.refs_0_), channel_id=1, source_target_pairs={{0,20},{4,16},{8,28},{12,24},{16,4},{20,0},{24,12},{28,8},{1,21},{... | collective-permute-start | bytes 442376 | tf_op jit(solution)/shard_map/ppermute | solution.py:838
  27.4 5.6 %collective-permute-start.9 = (f32[4,9,8,128]{3,2,1,0:T(8,128)S(1)}, f32[4,9,8,128]{3,2,1,0:T(8,128)S(1)}, u32[]{:S(2)}, u32[]{:S(2)}) collective-permute-start(f32[4,9,8,128]{3,2,1,0:T(8,128)S(1)} %shard_map.30.after_ref.refs_0_), channel_id=1, source_target_pairs={{0,4},{4,0},{8,12},{12,8},{1,5},{5,1},{9,13},{13,9},{2,6},{6,2},{1... | collective-permute-start | bytes 442376 | tf_op jit(solution)/shard_map/ppermute | solution.py:837
  27.9 5.2 %collective-permute-start.8 = (f32[4,9,8,128]{3,2,1,0:T(8,128)S(1)}, f32[4,9,8,128]{3,2,1,0:T(8,128)S(1)}, u32[]{:S(2)}, u32[]{:S(2)}) collective-permute-start(f32[4,9,8,128]{3,2,1,0:T(8,128)S(1)} %shard_map.30.after_ref.refs_0_), channel_id=1, source_target_pairs={{0,16},{16,0},{1,17},{17,1},{2,18},{18,2},{3,19},{19,3},{4,20},{20... | collective-permute-start | bytes 442376 | tf_op jit(solution)/shard_map/ppermute | solution.py:836
  28.4 5.2 %collective-permute-start.11 = (f32[4,9,8,128]{3,2,1,0:T(8,128)S(1)}, f32[4,9,8,128]{3,2,1,0:T(8,128)S(1)}, u32[]{:S(2)}, u32[]{:S(2)}) collective-permute-start(f32[4,9,8,128]{3,2,1,0:T(8,128)S(1)} %shard_map.30.after_ref.refs_0_), channel_id=1, source_target_pairs={{0,1},{1,0},{2,3},{3,2},{4,5},{5,4},{6,7},{7,6},{8,9},{9,8},{10,11... | collective-permute-start | bytes 442376 | tf_op jit(solution)/shard_map/ppermute | solution.py:848
  33.0 1.4 %collective-permute-start.12 = (f32[4,9,8,128]{3,2,1,0:T(8,128)S(1)}, f32[4,9,8,128]{3,2,1,0:T(8,128)S(1)}, u32[]{:S(2)}, u32[]{:S(2)}) collective-permute-start(f32[4,9,8,128]{3,2,1,0:T(8,128)S(1)} %collective-permute-done.8.refs_1_), channel_id=1, source_target_pairs={{0,1},{1,0},{2,3},{3,2},{4,5},{5,4},{6,7},{7,6},{8,9},{9,8},{10,11... | collective-permute-start | bytes 442376 | tf_op jit(solution)/shard_map/ppermute | solution.py:848
  33.0 1.6 %collective-permute-start.13 = (f32[4,9,8,128]{3,2,1,0:T(8,128)S(1)}, f32[4,9,8,128]{3,2,1,0:T(8,128)S(1)}, u32[]{:S(2)}, u32[]{:S(2)}) collective-permute-start(f32[4,9,8,128]{3,2,1,0:T(8,128)S(1)} %collective-permute-done.9.refs_2_), channel_id=1, source_target_pairs={{0,1},{1,0},{2,3},{3,2},{4,5},{5,4},{6,7},{7,6},{8,9},{9,8},{10,11... | collective-permute-start | bytes 442376 | tf_op jit(solution)/shard_map/ppermute | solution.py:848
  33.6 1.4 %collective-permute-start.14 = (f32[4,9,8,128]{3,2,1,0:T(8,128)S(1)}, f32[4,9,8,128]{3,2,1,0:T(8,128)S(1)}, u32[]{:S(2)}, u32[]{:S(2)}) collective-permute-start(f32[4,9,8,128]{3,2,1,0:T(8,128)S(1)} %collective-permute-done.10.refs_3_), channel_id=1, source_target_pairs={{0,1},{1,0},{2,3},{3,2},{4,5},{5,4},{6,7},{7,6},{8,9},{9,8},{10,11... | collective-permute-start | bytes 442376 | tf_op jit(solution)/shard_map/ppermute | solution.py:848

commit v9 on v8

--- a/solution.py
+++ b/solution.py
@@ -282,6 +282,18 @@
     return block_plane(at, own_ref, ya_ref, yb_ref, even_y), sides
 
 
+def faces_kernel(halo, own_ref, ya_ref, yb_ref, sems):
+    even = lax.axis_index("gy") % 2 == 0
+    far = own_ref.shape[1] - halo
+    copies = []
+    for which, (ref, start) in enumerate(((ya_ref, jnp.where(even, far, 0)), (yb_ref, jnp.where(even, 0, far)))):
+        face = own_ref.at[:, pl.ds(pl.multiple_of(start, 8), halo), :]
+        copies.append(pltpu.make_async_copy(face, ref, sems.at[which]))
+        copies[-1].start()
+    for copy in copies:
+        copy.wait()
+
+
 def pack_kernel(halo, own_ref, ya_ref, yb_ref, za_ref, zb_ref):
     even_y = lax.axis_index("gy") % 2 == 0
     even_z = lax.axis_index("gz") % 2 == 0
@@ -345,31 +357,27 @@
     ends = x_ends()
     clear_pads(red_ref)
     clear_pads(black_ref)
-    group = lanes_of(shape) // (2 * halo)
-    low_sides = jnp.zeros(shape, jnp.float32)
-    high_sides = jnp.zeros(shape, jnp.float32)
+    for p in range(halo):
+        high = block_plane(nx - halo + p, own_ref, ya_ref, yb_ref, even_y)
+        face_ref[p] = jnp.where(ends[0], high, block_plane(p, own_ref, ya_ref, yb_ref, even_y))
+    middle = halo * halo
+    top = za_ref.shape[0] - 1
+    left = [jnp.where(even_z, zb_ref[j], za_ref[j]) for j in (0, top)]
+    right = [jnp.where(even_z, za_ref[j], zb_ref[j]) for j in (0, top)]
+    left = jnp.where(ends[0], pltpu.roll(left[1], middle, 1), left[0])
+    right = jnp.where(ends[0], right[1], pltpu.roll(right[0], middle, 1))
+    face_ref[halo] = jnp.where(lanes_of(shape) < middle, left, right)
     for at in range(own):
-        planes = []
-        for x in (2 * at, 2 * at + 1):
-            columns = block_columns(halo, x, own_ref, ya_ref, yb_ref, za_ref, zb_ref, even_y, even_z)
-            planes.append(columns)
-            if x < halo:
-                turned = pltpu.roll(columns[1], (halo + 2 * halo * x) % LANES, 1)
-                low_sides = jnp.where(group == x, turned, low_sides)
-            if x >= nx - halo:
-                p = x - (nx - halo)
-                turned = pltpu.roll(columns[1], (halo + 2 * halo * p) % LANES, 1)
-                high_sides = jnp.where(group == p, turned, high_sides)
+        planes = [
+            block_columns(halo, x, own_ref, ya_ref, yb_ref, za_ref, zb_ref, even_y, even_z)
+            for x in (2 * at, 2 * at + 1)
+        ]
         for c in range(2):
             red = jnp.where(odd, planes[1][c], planes[0][c])
             black = jnp.where(odd, planes[0][c], planes[1][c])
             if c == 0:
                 fr_ref[at], fb_ref[at] = red[inner], black[inner]
             gr_ref[at, c], gb_ref[at, c] = masks[c] * red, masks[c] * black
-    for p in range(halo):
-        high = block_plane(nx - halo + p, own_ref, ya_ref, yb_ref, even_y)
-        face_ref[p] = jnp.where(ends[0], high, block_plane(p, own_ref, ya_ref, yb_ref, even_y))
-    face_ref[halo] = jnp.where(ends[0], high_sides, low_sides)
 
     def keep(at, c, total, value):
         if c == 0:
@@ -385,15 +393,15 @@
         rest_ref[at] = rest_ref[at] + left_over
     half, quarter = ny // 2, nz // 4
     pairs_y = rest_ref[:, pl.ds(0, half, stride=2), :] + rest_ref[:, pl.ds(1, half, stride=2), :]
-    column = lanes_of((nz, nz))
+    turn = quarter * lax.axis_index("gz")
+    column = (lanes_of((nz, nz)) - turn) & (nz - 1)
     target = 2 * (column % quarter) + (column // quarter) % 2
     weight = jnp.where(rows_of((nz, nz)) // 2 == target, 0.5, 0.0)
     coarse = exact_dot(pairs_y.reshape(count * half, nz), weight).reshape(count, half, nz)
-    part = lanes_of((half, nz)) // quarter
+    part = ((lanes_of((half, nz)) - turn) & (nz - 1)) // quarter
     pick = (((rows_of((half, nz)) + part) & 1) == 1) ^ (part >= 2)
-    turn = quarter * lax.axis_index("gz")
     for at in range(count // 2):
-        send_ref[at] = pltpu.roll(jnp.where(pick, coarse[2 * at + 1], coarse[2 * at]), turn, 1)
+        send_ref[at] = jnp.where(pick, coarse[2 * at + 1], coarse[2 * at])
 
 
 def field_kernel(
@@ -416,8 +424,9 @@
         if x < nx:
             return block_columns(halo, x, own_ref, ya_ref, yb_ref, za_ref, zb_ref, even_y, even_z)
         p = x - nx
-        sides = pltpu.roll(face_ref[halo], (2 * LANES - halo - 2 * halo * p) % LANES, 1)
-        return face_ref[p], jnp.where((lane < halo) | (lane >= nz - halo), sides, 0.0)
+        left = pltpu.roll(face_ref[halo], (2 * LANES - halo - halo * p) % LANES, 1)
+        right = pltpu.roll(face_ref[halo], (2 * LANES - halo * halo - halo * p) % LANES, 1)
+        return face_ref[p], jnp.where(lane < halo, right, jnp.where(lane >= nz - halo, left, 0.0))
 
     for at in range(count):
         first, second = columns(2 * at), columns(2 * at + 1)
@@ -788,17 +797,20 @@
     nx, ny, nz = density.shape
     count_x, count_y, count_z = (lax.axis_size(axis) for axis in ("gx", "gy", "gz"))
     whole = (nx * count_x, ny * count_y, nz * count_z)
-    even = lax.axis_index("gy") % 2 == 0
-    ya = lax.dynamic_slice_in_dim(density, jnp.where(even, ny - halo, 0), halo, 1)
-    yb = lax.dynamic_slice_in_dim(density, jnp.where(even, 0, ny - halo), halo, 1)
+
+    def params(mib):
+        return pltpu.CompilerParams(vmem_limit_bytes=mib * 1024 * 1024)
+
+    ya, yb = pl.pallas_call(
+        functools.partial(faces_kernel, halo),
+        out_shape=[struct(nx, halo, nz)] * 2,
+        in_specs=[pl.BlockSpec(memory_space=pltpu.HBM)], out_specs=vmem(2),
+        compiler_params=params(2), scratch_shapes=[pltpu.SemaphoreType.DMA((2,))],
+    )(density)
     ya = lax.ppermute(ya, "gy", pairs(count_y, 0))
     yb = lax.ppermute(yb, ("gx", "gy"), inner_pairs(count_x, count_y))
     rows = ny + 2 * halo
     packs = -(-nx * halo // nz)
-
-    def params(mib):
-        return pltpu.CompilerParams(vmem_limit_bytes=mib * 1024 * 1024)
-
     za, zb = pl.pallas_call(
         functools.partial(pack_kernel, halo),
         out_shape=[struct(packs, rows, nz)] * 2,
@@ -816,7 +828,6 @@
         + [scratch(near, 2, rows + 2 * PAD, LANES)] * 2
         + [scratch(near, ny, nz)],
     )(density, ya, yb, za, zb)
-    face = lax.ppermute(face, "gx", flips(count_x, 1))
     planes = nx + halo
     slots = (planes // 2, 2, rows, LANES)
     padded = (planes // 2, 2, rows + 2 * PAD, LANES)
@@ -826,6 +837,7 @@
         lax.ppermute(send, "gz", flips(count_z, 2)),
         lax.ppermute(send, ("gy", "gz"), flips(count_y * count_z, 2 * count_z + 2)),
     ]
+    face = lax.ppermute(face, "gx", flips(count_x, 1))
     first[3], face = lax.optimization_barrier((first[3], face))
     block = pl.pallas_call(
         stack_kernel, out_shape=struct(4, *send.shape),

time: 42 us -> 42.7 us (1.017)
  waiting for transfers between devices: 13.4 us -> 14.7 us
  Pallas kernels: 11.1 us -> 10.5 us
    ppermute x1, starting transfers between devices: 2.57 us -> 0.2 us  [block_cycle(): lax.ppermute(block, ('gx', 'gy'), flips(count_x * count_y, count_y + 1))]
    ppermute x1, starting transfers between devices: 3.06 us -> 1.52 us  [block_cycle(): yb = lax.ppermute(yb, ('gx', 'gy'), inner_pairs(count_x, count_y))]
    ppermute x1, starting transfers between devices: 1.63 us -> 3.12 us  [block_cycle(): ya = lax.ppermute(ya, 'gy', pairs(count_y, 0))]
    ppermute x1, starting transfers between devices: 0.48 us -> 1.83 us  [block_cycle(): lax.ppermute(block, 'gy', flips(count_y, 1))]
    dynamic_slice x1 -> x0, local copies, waits for them, and re-layouts: 1.03 us -> none  [block_cycle(): lax.dynamic_slice_in_dim(density, jnp.where(even, 0, ny - halo), halo, 1)]
    ppermute x1, starting transfers between devices: 0.51 us -> 1.52 us  [block_cycle(): lax.ppermute(block, 'gx', flips(count_x, 1))]
    ppermute x1, waiting for transfers between devices: 1.52 us -> 0.52 us  [block_cycle(): lax.ppermute(block, 'gy', flips(count_y, 1))]
    ppermute x1, starting transfers between devices: 2.57 us -> 3.52 us  [block_cycle(): lax.ppermute(send, ('gy', 'gz'), flips(count_y * count_z, 2 * count_z + 2))]
  transfers between devices with their start and end apart: 15 -> 15, of which waited for: 12 -> 12; matrix products, arithmetic and copies ran while one was open for 0% -> 0% of each run, Pallas kernels for 3% -> 4%
where the time goes in v9:
time: 42.7 us; the launch traced here: 42.5 us
  starting transfers between devices  16.3 us (38%)
  waiting for transfers between devices  14.7 us (34%)
  Pallas kernels  10.5 us (25%)
  local copies, waits for them, and re-layouts  0.96 us (2%)
    pallas_call x1, Pallas kernels, block_cycle(): pl.pallas_call(functools.partial(solve_kernel, halo, whole), out_shape=st...  6.96 us
    ppermute x1, starting transfers between devices, block_cycle(): lax.ppermute(send, ('gy', 'gz'), flips(count_y * count_z, 2 * count_z + 2))  3.52 us
    ppermute x1, starting transfers between devices, block_cycle(): ya = lax.ppermute(ya, 'gy', pairs(count_y, 0))  3.12 us
    ppermute x1, waiting for transfers between devices, block_cycle(): ya = lax.ppermute(ya, 'gy', pairs(count_y, 0))  1.98 us
    ppermute x1, starting transfers between devices, block_cycle(): lax.ppermute(block, 'gy', flips(count_y, 1))  1.83 us
    ppermute x1, waiting for transfers between devices, block_cycle(): lax.ppermute(zb, 'gz', pairs(count_z, 1) + [(0, count_z - 1), (count_z -...  1.81 us
    ppermute x1, waiting for transfers between devices, block_cycle(): lax.ppermute(block, ('gx', 'gy'), flips(count_x * count_y, count_y + 1))  1.78 us
    ppermute x1, waiting for transfers between devices, block_cycle(): lax.ppermute(send, ('gy', 'gz'), flips(count_y * count_z, 2 * count_z + 2))  1.78 us
  transfers between devices with their start and end apart: 15, of which 12 were waited for; matrix products, arithmetic and copies ran while one was open for 0% of the time, Pallas kernels for 4%

profile of v9, /device:TPU:0, one launch (start us, length us, event | category | flops | bytes accessed | tf_op | source)
XLA Modules:
  0.0 42.5 jit_solution(6418134381748438531)
XLA Ops:
  0.0 0.0 copy-start
  0.0 0.9 %copy-done = f32[32,16,128]{2,1,0:T(8,128)S(1)} copy-done((f32[32,16,128]{2,1,0:T(8,128)S(1)}, f32[32,16,128]{2,1,0:T(8,128)}, u32[]{:S(2)}) %copy-start) | copy-done | bytes 262168
  1.0 0.0 copy-start.1
  1.0 3.1 %collective-permute-start = (f32[32,8,128]{2,1,0:T(8,128)S(1)}, f32[32,8,128]{2,1,0:T(8,128)S(1)}, u32[]{:S(2)}, u32[]{:S(2)}) collective-permute-start(f32[32,8,128]{2,1,0:T(8,128)S(1)} %get-tuple-element.22), channel_id=1, source_target_pairs={{0,4},{4,0},{8,12},{12,8},{1,5},{5,1},{9,13},{13,9},{2,6},{6,2},{1... | collective-permute-start | bytes 393224 | tf_op jit(solution)/shard_map/ppermute | solution.py:810
  4.1 1.5 %collective-permute-start.1 = (f32[32,8,128]{2,1,0:T(8,128)S(1)}, f32[32,8,128]{2,1,0:T(8,128)S(1)}, u32[]{:S(2)}, u32[]{:S(2)}) collective-permute-start(f32[32,8,128]{2,1,0:T(8,128)S(1)} %get-tuple-element.23), channel_id=1, source_target_pairs={{4,8},{8,4},{0,16},{12,28},{20,24},{24,20},{16,0},{28,12},{5,9},{9... | collective-permute-start | bytes 393224 | tf_op jit(solution)/shard_map/ppermute | solution.py:811
  5.6 2.0 %collective-permute-done.ya_ref = f32[32,8,128]{2,1,0:T(8,128)S(1)} collective-permute-done((f32[32,8,128]{2,1,0:T(8,128)S(1)}, f32[32,8,128]{2,1,0:T(8,128)S(1)}, u32[]{:S(2)}, u32[]{:S(2)}) %collective-permute-start) | collective-permute-done | bytes 131104 | tf_op jit(solution)/shard_map/ppermute | solution.py:810
  7.6 1.5 %collective-permute-done.1.yb_ref = f32[32,8,128]{2,1,0:T(8,128)S(1)} collective-permute-done((f32[32,8,128]{2,1,0:T(8,128)S(1)}, f32[32,8,128]{2,1,0:T(8,128)S(1)}, u32[]{:S(2)}, u32[]{:S(2)}) %collective-permute-start.1) | collective-permute-done | bytes 131104 | tf_op jit(solution)/shard_map/ppermute | solution.py:811
  9.1 0.0 copy-done.1
  9.1 0.3 shard_map.29
  9.4 0.1 collective-permute-start.2
  9.5 1.6 %collective-permute-start.3 = (f32[2,32,128]{2,1,0:T(8,128)S(1)}, f32[2,32,128]{2,1,0:T(8,128)S(1)}, u32[]{:S(2)}, u32[]{:S(2)}) collective-permute-start(f32[2,32,128]{2,1,0:T(8,128)S(1)} %get-tuple-element.25), channel_id=1, source_target_pairs={{1,2},{2,1},{0,3},{3,0},{5,6},{6,5},{4,7},{7,4},{9,10},{10,9},{8,1... | collective-permute-start | bytes 98312 | tf_op jit(solution)/shard_map/ppermute | solution.py:820
  11.1 0.0 collective-permute-done.2.za_ref
  11.1 1.8 %collective-permute-done.3.zb_ref = f32[2,32,128]{2,1,0:T(8,128)S(1)} collective-permute-done((f32[2,32,128]{2,1,0:T(8,128)S(1)}, f32[2,32,128]{2,1,0:T(8,128)S(1)}, u32[]{:S(2)}, u32[]{:S(2)}) %collective-permute-start.3) | collective-permute-done | bytes 32800 | tf_op jit(solution)/shard_map/ppermute | solution.py:820
  12.9 1.7 %shard_map.30 = (f32[9,8,128]{2,1,0:T(8,128)S(1)}, f32[9,32,128]{2,1,0:T(8,128)S(1)}) custom-call(f32[32,16,128]{2,1,0:T(8,128)S(1)} %copy-done.1, f32[32,8,128]{2,1,0:T(8,128)S(1)} %collective-permute-done.ya_ref, f32[32,8,128]{2,1,0:T(8,128)S(1)} %collective-permute-done.1.yb_ref, f32[2,32,128]{2,1,0:T(8,128)S(1)} %collective-permute-done.2.za_ref, ...), custom_call_target="tpu_custom_call" | custom-call | tf_op jit(solution)/shard_map/pallas_call | solution.py:822
  14.6 1.6 %collective-permute-start.7 = (f32[9,32,128]{2,1,0:T(8,128)S(1)}, f32[9,32,128]{2,1,0:T(8,128)S(1)}, u32[]{:S(2)}, u32[]{:S(2)}) collective-permute-start(f32[9,32,128]{2,1,0:T(8,128)S(1)} %get-tuple-element.27), channel_id=1, source_target_pairs={{0,16},{16,0},{1,17},{17,1},{2,18},{18,2},{3,19},{19,3},{4,20},{20... | collective-permute-start | bytes 442376 | tf_op jit(solution)/shard_map/ppermute | solution.py:840
  16.2 3.5 %collective-permute-start.6 = (f32[9,8,128]{2,1,0:T(8,128)S(1)}, f32[9,8,128]{2,1,0:T(8,128)S(1)}, u32[]{:S(2)}, u32[]{:S(2)}) collective-permute-start(f32[9,8,128]{2,1,0:T(8,128)S(1)} %get-tuple-element.26.refs_0_), channel_id=1, source_target_pairs={{0,10},{1,11},{2,8},{3,9},{4,14},{5,15},{6,12},{7,13},{8,2},{9,3},... | collective-permute-start | bytes 110600 | tf_op jit(solution)/shard_map/ppermute | solution.py:838
  19.7 0.5 %collective-permute-start.5 = (f32[9,8,128]{2,1,0:T(8,128)S(1)}, f32[9,8,128]{2,1,0:T(8,128)S(1)}, u32[]{:S(2)}, u32[]{:S(2)}) collective-permute-start(f32[9,8,128]{2,1,0:T(8,128)S(1)} %get-tuple-element.26.refs_0_), channel_id=1, source_target_pairs={{0,2},{1,3},{2,0},{3,1},{4,6},{5,7},{6,4},{7,5},{8,10},{9,11},{10,... | collective-permute-start | bytes 110600 | tf_op jit(solution)/shard_map/ppermute | solution.py:837
  20.2 0.3 collective-permute-start.4
  20.6 1.8 %collective-permute-done.6.refs_3_ = f32[9,8,128]{2,1,0:T(8,128)S(1)} collective-permute-done((f32[9,8,128]{2,1,0:T(8,128)S(1)}, f32[9,8,128]{2,1,0:T(8,128)S(1)}, u32[]{:S(2)}, u32[]{:S(2)}) %collective-permute-start.6) | collective-permute-done | bytes 36896 | tf_op jit(solution)/shard_map/ppermute | solution.py:838
  22.3 0.0 collective-permute-done.7.face_ref
  22.3 1.3 %collective-permute-done.5.refs_2_ = f32[9,8,128]{2,1,0:T(8,128)S(1)} collective-permute-done((f32[9,8,128]{2,1,0:T(8,128)S(1)}, f32[9,8,128]{2,1,0:T(8,128)S(1)}, u32[]{:S(2)}, u32[]{:S(2)}) %collective-permute-start.5) | collective-permute-done | bytes 36896 | tf_op jit(solution)/shard_map/ppermute | solution.py:837
  23.6 1.7 %collective-permute-done.4.refs_1_ = f32[9,8,128]{2,1,0:T(8,128)S(1)} collective-permute-done((f32[9,8,128]{2,1,0:T(8,128)S(1)}, f32[9,8,128]{2,1,0:T(8,128)S(1)}, u32[]{:S(2)}, u32[]{:S(2)}) %collective-permute-start.4) | collective-permute-done | bytes 36896 | tf_op jit(solution)/shard_map/ppermute | solution.py:836
  25.4 0.0 copy-start.2
  25.4 0.2 collective-permute-start.10
  25.6 1.8 %collective-permute-start.9 = (f32[4,9,8,128]{3,2,1,0:T(8,128)S(1)}, f32[4,9,8,128]{3,2,1,0:T(8,128)S(1)}, u32[]{:S(2)}, u32[]{:S(2)}) collective-permute-start(f32[4,9,8,128]{3,2,1,0:T(8,128)S(1)} %shard_map.31.after_ref.refs_0_), channel_id=1, source_target_pairs={{0,4},{4,0},{8,12},{12,8},{1,5},{5,1},{9,13},{13,9},{2,6},{6,2},{1... | collective-permute-start | bytes 442376 | tf_op jit(solution)/shard_map/ppermute | solution.py:849
  27.4 1.5 %collective-permute-start.8 = (f32[4,9,8,128]{3,2,1,0:T(8,128)S(1)}, f32[4,9,8,128]{3,2,1,0:T(8,128)S(1)}, u32[]{:S(2)}, u32[]{:S(2)}) collective-permute-start(f32[4,9,8,128]{3,2,1,0:T(8,128)S(1)} %shard_map.31.after_ref.refs_0_), channel_id=1, source_target_pairs={{0,16},{16,0},{1,17},{17,1},{2,18},{18,2},{3,19},{19,3},{4,20},{20... | collective-permute-start | bytes 442376 | tf_op jit(solution)/shard_map/ppermute | solution.py:848
  28.9 0.0 collective-permute-start.11
  28.9 1.5 %shard_map.32 = (f32[20,2,32,128]{3,2,1,0:T(8,128)S(1)}, f32[20,2,32,128]{3,2,1,0:T(8,128)S(1)}, f32[20,2,32,128]{3,2,1,0:T(8,128)S(1)}) custom-call(f32[32,16,128]{2,1,0:T(8,128)S(1)} %copy-done.1, f32[32,8,128]{2,1,0:T(8,128)S(1)} %collective-permute-done.ya_ref, f32[32,8,128]{2,1,0:T(8,128)S(1)} %collective-permute-done.1.yb_ref, ...), custom_call_target="tpu_custom_call" | custom-call | flops 20000000 | bytes 2000000 | tf_op jit(solution)/shard_map/pallas_call | solution.py:852
  30.4 1.8 %collective-permute-done.10.refs_3_ = f32[4,9,8,128]{3,2,1,0:T(8,128)S(1)} collective-permute-done((f32[4,9,8,128]{3,2,1,0:T(8,128)S(1)}, f32[4,9,8,128]{3,2,1,0:T(8,128)S(1)}, u32[]{:S(2)}, u32[]{:S(2)}) %collective-permute-start.10) | collective-permute-done | bytes 147488 | tf_op jit(solution)/shard_map/ppermute | solution.py:850
  32.2 0.5 %collective-permute-done.9.refs_2_ = f32[4,9,8,128]{3,2,1,0:T(8,128)S(1)} collective-permute-done((f32[4,9,8,128]{3,2,1,0:T(8,128)S(1)}, f32[4,9,8,128]{3,2,1,0:T(8,128)S(1)}, u32[]{:S(2)}, u32[]{:S(2)}) %collective-permute-start.9) | collective-permute-done | bytes 147488 | tf_op jit(solution)/shard_map/ppermute | solution.py:849
  32.7 1.0 %collective-permute-done.8.refs_1_ = f32[4,9,8,128]{3,2,1,0:T(8,128)S(1)} collective-permute-done((f32[4,9,8,128]{3,2,1,0:T(8,128)S(1)}, f32[4,9,8,128]{3,2,1,0:T(8,128)S(1)}, u32[]{:S(2)}, u32[]{:S(2)}) %collective-permute-start.8) | collective-permute-done | bytes 147488 | tf_op jit(solution)/shard_map/ppermute | solution.py:848
  33.7 0.0 collective-permute-start.12
  33.7 0.5 %collective-permute-start.13 = (f32[4,9,8,128]{3,2,1,0:T(8,128)S(1)}, f32[4,9,8,128]{3,2,1,0:T(8,128)S(1)}, u32[]{:S(2)}, u32[]{:S(2)}) collective-permute-start(f32[4,9,8,128]{3,2,1,0:T(8,128)S(1)} %collective-permute-done.9.refs_2_), channel_id=1, source_target_pairs={{0,1},{1,0},{2,3},{3,2},{4,5},{5,4},{6,7},{7,6},{8,9},{9,8},{10,11... | collective-permute-start | bytes 442376 | tf_op jit(solution)/shard_map/ppermute | solution.py:860
  34.2 0.0 collective-permute-start.14
  34.2 0.0 collective-permute-done.11.refs_4_
  34.2 0.9 %collective-permute-done.12.refs_5_ = f32[4,9,8,128]{3,2,1,0:T(8,128)S(1)} collective-permute-done((f32[4,9,8,128]{3,2,1,0:T(8,128)S(1)}, f32[4,9,8,128]{3,2,1,0:T(8,128)S(1)}, u32[]{:S(2)}, u32[]{:S(2)}) %collective-permute-start.12) | collective-permute-done | bytes 147488 | tf_op jit(solution)/shard_map/ppermute | solution.py:860
  35.1 0.2 collective-permute-done.13.refs_6_
  35.3 0.3 collective-permute-done.14.refs_7_
  35.6 0.0 copy-done.2
  35.6 7.0 %shard_map.33 = f32[32,16,128]{2,1,0:T(8,128)} custom-call(f32[4,9,8,128]{3,2,1,0:T(8,128)S(1)} %shard_map.31.after_ref.refs_0_, f32[4,9,8,128]{3,2,1,0:T(8,128)S(1)} %collective-permute-done.8.refs_1_, f32[4,9,8,128]{3,2,1,0:T(8,128)S(1)} %collective-permute-done.9.refs_2_, f32[4,9,8,128]{3,2,1,0:T(8,128)S(1)} %collective-permute-done.10.refs_3_, ...), custom_call_target="tpu_custom_call" | custom-call | tf_op jit(solution)/shard_map/pallas_call | solution.py:869
  (2 shorter events, 0.1 us)
Async XLA Ops:
  0.0 0.9 %copy-start = (f32[32,16,128]{2,1,0:T(8,128)S(1)}, f32[32,16,128]{2,1,0:T(8,128)}, u32[]{:S(2)}) copy-start(f32[32,16,128]{2,1,0:T(8,128)} %own_ref.7) | copy-start | bytes 786436
  1.0 8.1 %copy-start.1 = (f32[32,16,128]{2,1,0:T(8,128)S(1)}, f32[32,16,128]{2,1,0:T(8,128)}, u32[]{:S(2)}) copy-start(f32[32,16,128]{2,1,0:T(8,128)} %own_ref.7) | copy-start | bytes 786436
  1.0 6.6 %collective-permute-start = (f32[32,8,128]{2,1,0:T(8,128)S(1)}, f32[32,8,128]{2,1,0:T(8,128)S(1)}, u32[]{:S(2)}, u32[]{:S(2)}) collective-permute-start(f32[32,8,128]{2,1,0:T(8,128)S(1)} %get-tuple-element.22), channel_id=1, source_target_pairs={{0,4},{4,0},{8,12},{12,8},{1,5},{5,1},{9,13},{13,9},{2,6},{6,2},{1... | collective-permute-start | bytes 393224 | tf_op jit(solution)/shard_map/ppermute | solution.py:810
  4.1 5.0 %collective-permute-start.1 = (f32[32,8,128]{2,1,0:T(8,128)S(1)}, f32[32,8,128]{2,1,0:T(8,128)S(1)}, u32[]{:S(2)}, u32[]{:S(2)}) collective-permute-start(f32[32,8,128]{2,1,0:T(8,128)S(1)} %get-tuple-element.23), channel_id=1, source_target_pairs={{4,8},{8,4},{0,16},{12,28},{20,24},{24,20},{16,0},{28,12},{5,9},{9... | collective-permute-start | bytes 393224 | tf_op jit(solution)/shard_map/ppermute | solution.py:811
  9.4 1.7 %collective-permute-start.2 = (f32[2,32,128]{2,1,0:T(8,128)S(1)}, f32[2,32,128]{2,1,0:T(8,128)S(1)}, u32[]{:S(2)}, u32[]{:S(2)}) collective-permute-start(f32[2,32,128]{2,1,0:T(8,128)S(1)} %get-tuple-element.24), channel_id=1, source_target_pairs={{0,1},{1,0},{2,3},{3,2},{4,5},{5,4},{6,7},{7,6},{8,9},{9,8},{10,11... | collective-permute-start | bytes 98312 | tf_op jit(solution)/shard_map/ppermute | solution.py:819
  9.5 3.4 %collective-permute-start.3 = (f32[2,32,128]{2,1,0:T(8,128)S(1)}, f32[2,32,128]{2,1,0:T(8,128)S(1)}, u32[]{:S(2)}, u32[]{:S(2)}) collective-permute-start(f32[2,32,128]{2,1,0:T(8,128)S(1)} %get-tuple-element.25), channel_id=1, source_target_pairs={{1,2},{2,1},{0,3},{3,0},{5,6},{6,5},{4,7},{7,4},{9,10},{10,9},{8,1... | collective-permute-start | bytes 98312 | tf_op jit(solution)/shard_map/ppermute | solution.py:820
  14.6 7.8 %collective-permute-start.7 = (f32[9,32,128]{2,1,0:T(8,128)S(1)}, f32[9,32,128]{2,1,0:T(8,128)S(1)}, u32[]{:S(2)}, u32[]{:S(2)}) collective-permute-start(f32[9,32,128]{2,1,0:T(8,128)S(1)} %get-tuple-element.27), channel_id=1, source_target_pairs={{0,16},{16,0},{1,17},{17,1},{2,18},{18,2},{3,19},{19,3},{4,20},{20... | collective-permute-start | bytes 442376 | tf_op jit(solution)/shard_map/ppermute | solution.py:840
  16.2 6.2 %collective-permute-start.6 = (f32[9,8,128]{2,1,0:T(8,128)S(1)}, f32[9,8,128]{2,1,0:T(8,128)S(1)}, u32[]{:S(2)}, u32[]{:S(2)}) collective-permute-start(f32[9,8,128]{2,1,0:T(8,128)S(1)} %get-tuple-element.26.refs_0_), channel_id=1, source_target_pairs={{0,10},{1,11},{2,8},{3,9},{4,14},{5,15},{6,12},{7,13},{8,2},{9,3},... | collective-permute-start | bytes 110600 | tf_op jit(solution)/shard_map/ppermute | solution.py:838
  19.7 4.0 %collective-permute-start.5 = (f32[9,8,128]{2,1,0:T(8,128)S(1)}, f32[9,8,128]{2,1,0:T(8,128)S(1)}, u32[]{:S(2)}, u32[]{:S(2)}) collective-permute-start(f32[9,8,128]{2,1,0:T(8,128)S(1)} %get-tuple-element.26.refs_0_), channel_id=1, source_target_pairs={{0,2},{1,3},{2,0},{3,1},{4,6},{5,7},{6,4},{7,5},{8,10},{9,11},{10,... | collective-permute-start | bytes 110600 | tf_op jit(solution)/shard_map/ppermute | solution.py:837
  20.2 5.1 %collective-permute-start.4 = (f32[9,8,128]{2,1,0:T(8,128)S(1)}, f32[9,8,128]{2,1,0:T(8,128)S(1)}, u32[]{:S(2)}, u32[]{:S(2)}) collective-permute-start(f32[9,8,128]{2,1,0:T(8,128)S(1)} %get-tuple-element.26.refs_0_), channel_id=1, source_target_pairs={{0,8},{4,12},{8,0},{12,4},{1,9},{5,13},{9,1},{13,5},{2,10},{6,14},... | collective-permute-start | bytes 110600 | tf_op jit(solution)/shard_map/ppermute | solution.py:836
  25.4 10.2 %copy-start.2 = (f32[128,128]{1,0:T(8,128)S(1)}, f32[128,128]{1,0:T(8,128)}, u32[]{:S(2)}) copy-start(f32[128,128]{1,0:T(8,128)} %constant.2.clone.refs_11_) | copy-start | bytes 196612
  25.4 6.8 %collective-permute-start.10 = (f32[4,9,8,128]{3,2,1,0:T(8,128)S(1)}, f32[4,9,8,128]{3,2,1,0:T(8,128)S(1)}, u32[]{:S(2)}, u32[]{:S(2)}) collective-permute-start(f32[4,9,8,128]{3,2,1,0:T(8,128)S(1)} %shard_map.31.after_ref.refs_0_), channel_id=1, source_target_pairs={{0,20},{4,16},{8,28},{12,24},{16,4},{20,0},{24,12},{28,8},{1,21},{... | collective-permute-start | bytes 442376 | tf_op jit(solution)/shard_map/ppermute | solution.py:850
  25.6 7.2 %collective-permute-start.9 = (f32[4,9,8,128]{3,2,1,0:T(8,128)S(1)}, f32[4,9,8,128]{3,2,1,0:T(8,128)S(1)}, u32[]{:S(2)}, u32[]{:S(2)}) collective-permute-start(f32[4,9,8,128]{3,2,1,0:T(8,128)S(1)} %shard_map.31.after_ref.refs_0_), channel_id=1, source_target_pairs={{0,4},{4,0},{8,12},{12,8},{1,5},{5,1},{9,13},{13,9},{2,6},{6,2},{1... | collective-permute-start | bytes 442376 | tf_op jit(solution)/shard_map/ppermute | solution.py:849
  27.4 6.3 %collective-permute-start.8 = (f32[4,9,8,128]{3,2,1,0:T(8,128)S(1)}, f32[4,9,8,128]{3,2,1,0:T(8,128)S(1)}, u32[]{:S(2)}, u32[]{:S(2)}) collective-permute-start(f32[4,9,8,128]{3,2,1,0:T(8,128)S(1)} %shard_map.31.after_ref.refs_0_), channel_id=1, source_target_pairs={{0,16},{16,0},{1,17},{17,1},{2,18},{18,2},{3,19},{19,3},{4,20},{20... | collective-permute-start | bytes 442376 | tf_op jit(solution)/shard_map/ppermute | solution.py:848
  28.9 5.3 %collective-permute-start.11 = (f32[4,9,8,128]{3,2,1,0:T(8,128)S(1)}, f32[4,9,8,128]{3,2,1,0:T(8,128)S(1)}, u32[]{:S(2)}, u32[]{:S(2)}) collective-permute-start(f32[4,9,8,128]{3,2,1,0:T(8,128)S(1)} %shard_map.31.after_ref.refs_0_), channel_id=1, source_target_pairs={{0,1},{1,0},{2,3},{3,2},{4,5},{5,4},{6,7},{7,6},{8,9},{9,8},{10,11... | collective-permute-start | bytes 442376 | tf_op jit(solution)/shard_map/ppermute | solution.py:860
  33.7 1.4 %collective-permute-start.12 = (f32[4,9,8,128]{3,2,1,0:T(8,128)S(1)}, f32[4,9,8,128]{3,2,1,0:T(8,128)S(1)}, u32[]{:S(2)}, u32[]{:S(2)}) collective-permute-start(f32[4,9,8,128]{3,2,1,0:T(8,128)S(1)} %collective-permute-done.8.refs_1_), channel_id=1, source_target_pairs={{0,1},{1,0},{2,3},{3,2},{4,5},{5,4},{6,7},{7,6},{8,9},{9,8},{10,11... | collective-permute-start | bytes 442376 | tf_op jit(solution)/shard_map/ppermute | solution.py:860
  33.7 1.6 %collective-permute-start.13 = (f32[4,9,8,128]{3,2,1,0:T(8,128)S(1)}, f32[4,9,8,128]{3,2,1,0:T(8,128)S(1)}, u32[]{:S(2)}, u32[]{:S(2)}) collective-permute-start(f32[4,9,8,128]{3,2,1,0:T(8,128)S(1)} %collective-permute-done.9.refs_2_), channel_id=1, source_target_pairs={{0,1},{1,0},{2,3},{3,2},{4,5},{5,4},{6,7},{7,6},{8,9},{9,8},{10,11... | collective-permute-start | bytes 442376 | tf_op jit(solution)/shard_map/ppermute | solution.py:860
  34.2 1.4 %collective-permute-start.14 = (f32[4,9,8,128]{3,2,1,0:T(8,128)S(1)}, f32[4,9,8,128]{3,2,1,0:T(8,128)S(1)}, u32[]{:S(2)}, u32[]{:S(2)}) collective-permute-start(f32[4,9,8,128]{3,2,1,0:T(8,128)S(1)} %collective-permute-done.10.refs_3_), channel_id=1, source_target_pairs={{0,1},{1,0},{2,3},{3,2},{4,5},{5,4},{6,7},{7,6},{8,9},{9,8},{10,11... | collective-permute-start | bytes 442376 | tf_op jit(solution)/shard_map/ppermute | solution.py:860

commit v10 on v9

--- a/solution.py
+++ b/solution.py
@@ -280,18 +280,6 @@
     lane = lanes_of(left.shape)
     sides = jnp.where(lane < halo, right, jnp.where(lane >= nz - halo, left, 0.0))
     return block_plane(at, own_ref, ya_ref, yb_ref, even_y), sides
-
-
-def faces_kernel(halo, own_ref, ya_ref, yb_ref, sems):
-    even = lax.axis_index("gy") % 2 == 0
-    far = own_ref.shape[1] - halo
-    copies = []
-    for which, (ref, start) in enumerate(((ya_ref, jnp.where(even, far, 0)), (yb_ref, jnp.where(even, 0, far)))):
-        face = own_ref.at[:, pl.ds(pl.multiple_of(start, 8), halo), :]
-        copies.append(pltpu.make_async_copy(face, ref, sems.at[which]))
-        copies[-1].start()
-    for copy in copies:
-        copy.wait()
 
 
 def pack_kernel(halo, own_ref, ya_ref, yb_ref, za_ref, zb_ref):
@@ -492,14 +480,14 @@
     gathered, refs = refs[:8], refs[8:]
     gr_ref, gb_ref, dark_ref, matrix_ref, out_ref = refs[:5]
     fr1, fb1, red1, black1, rest1, tall_ref, red_ref, work_ref, passing = refs[5:14]
-    small = [refs[14 + 4 * i : 18 + 4 * i] for i in range(LEVELS - 4)]
+    small = [refs[14 + 6 * i : 20 + 6 * i] for i in range(LEVELS - 4)]
     gx, gy, gz = (lax.axis_index(axis) for axis in ("gx", "gy", "gz"))
     weight_z = 1.0 + rsd_beta
     share = 1.0 / centre
     for ref in (red1, black1, red_ref, work_ref, passing):
         clear_pads(ref)
     for level in small:
-        for ref in level[2:]:
+        for ref in level[2:4]:
             clear_pads(ref)
 
     _, slots, block_rows, _ = gathered[0].shape
@@ -606,16 +594,13 @@
     def odd_at(index):
         return (((row2 >> index) + (lane2 >> index)) & 1) == 1
 
-    def along(value, step):
-        left = jnp.where(lane2 < step, 0.0, pltpu.roll(value, step, 1))
-        right = jnp.where(lane2 >= LANES - step, 0.0, pltpu.roll(value, LANES - step, 1))
-        return weight_z * (left + right)
-
-    def small_total(index, ref, at, odd, to_red):
+    def turned(value, step):
+        inside = lane2 >= step if step > 0 else lane2 < LANES + step
+        return jnp.where(inside, pltpu.roll(value, step % LANES, 1), 0.0)
+
+    def small_plane(index, ref, at, odd, to_red):
         step = 1 << index
-        value = ref[at, 0, body2, :]
-        total = value + along(value, step)
-        total = total + (
+        total = ref[at, 0, body2, :] + (
             ref[at, 0, PAD - step : PAD - step + rows2, :] + ref[at, 0, PAD + step : PAD + step + rows2, :]
         )
         slots = ref.shape[0]
@@ -626,17 +611,35 @@
         return total + (jnp.where(odd, after, before) if to_red else jnp.where(odd, before, after))
 
     def small_sweeps(index, start):
-        fr, fb, red, black = small[index]
-        mask, odd = jnp.where(grid_of(index), share, 0.0), odd_at(index)
+        fr, fb, red, black, fr_low, fr_high = small[index]
+        odd, width = odd_at(index), 1 << index
+        mask = jnp.where(grid_of(index), share, 0.0)
+        mask_low = jnp.where(lane2 < width, 0.0, mask)
+        mask_high = jnp.where(lane2 >= LANES - width, 0.0, mask)
         slots = fr.shape[0]
+        if start:
+            for at in range(slots):
+                fr_low[at] = pltpu.roll(fr[at], width, 1)
+                fr_high[at] = pltpu.roll(fr[at], LANES - width, 1)
         for step in range(2):
+            sides = []
             for at in range(slots):
-                source = fr[at]
+                here, low, high = fr[at], fr_low[at], fr_high[at]
                 if not (start and step == 0):
-                    source = source + small_total(index, black, at, odd, True)
-                red[at, 0, body2, :] = mask * source
+                    value = black[at, 0, body2, :]
+                    plane = small_plane(index, black, at, odd, True)
+                    here = here + plane + weight_z * (turned(value, width) + turned(value, -width))
+                    low = low + pltpu.roll(plane, width, 1) + weight_z * (turned(value, 2 * width) + value)
+                    high = high + pltpu.roll(plane, LANES - width, 1)
+                    high = high + weight_z * (value + turned(value, -2 * width))
+                red[at, 0, body2, :] = mask * here
+                sides.append(weight_z * (mask_low * low + mask_high * high))
+            totals = []
             for at in range(slots):
-                black[at, 0, body2, :] = mask * (fb[at] + small_total(index, red, at, odd, False))
+                total = fb[at] + small_plane(index, red, at, odd, False) + sides[at]
+                black[at, 0, body2, :] = mask * total
+                totals.append(total)
+        return totals
 
     def spread_rows(value, step, ref, at):
         ref[at, 0, body2, :] = value
@@ -644,23 +647,32 @@
 
     last = len(small) - 1
     for index in range(len(small)):
-        fr, fb, red, black = small[index]
+        fr, fb, red, black, _, fr_high = small[index]
         slots, odd, step = fr.shape[0], odd_at(index), 1 << index
         for at in range(slots):
             p, q = planes[2 * at], planes[2 * at + 1]
             fr[at], fb[at] = jnp.where(odd, q, p), jnp.where(odd, p, q)
-        small_sweeps(index, True)
+        black_totals = small_sweeps(index, True)
         totals = []
         for at in range(slots):
-            first = fb[at] + small_total(index, red, at, odd, False) - centre * black[at, 0, body2, :]
-            second = fr[at] + small_total(index, black, at, odd, True) - centre * red[at, 0, body2, :]
-            totals.append(first + second)
-        for at in range(slots):
-            passing[at, 0, body2, :] = totals[at]
+            value, field = black[at, 0, body2, :], red[at, 0, body2, :]
+            plane = small_plane(index, black, at, odd, True)
+            total = black_totals[at] - centre * value
+            next_total = pltpu.roll(total, LANES - step, 1)
+            total = total + (
+                fr[at] + plane + weight_z * (turned(value, step) + turned(value, -step)) - centre * field
+            )
+            if index < last:
+                next_total = next_total + (
+                    fr_high[at] + pltpu.roll(plane, LANES - step, 1)
+                    + weight_z * (value + turned(value, -2 * step))
+                    - centre * pltpu.roll(field, LANES - step, 1)
+                )
+                total = total + next_total
+            totals.append(total)
+            passing[at, 0, body2, :] = total
         lower = [passing[at, 0, PAD + step : PAD + step + rows2, :] for at in range(slots)]
-        if index < last:
-            totals = [total + below for total, below in zip(totals, lower)]
-            planes = [0.5 * (total + pltpu.roll(total, LANES - step, 1)) for total in totals]
+        planes = [0.5 * (total + below) for total, below in zip(totals, lower)]
 
     half_rows = rows2 // 2
     upper = [passing[at, 0, PAD - step : PAD - step + rows2, :] for at in range(slots)]
@@ -682,7 +694,7 @@
     spreads = [jnp.concatenate(parts[2 * at : 2 * at + 2], axis=0) for at in range(slots)]
 
     for index in reversed(range(len(small))):
-        _, _, red, black = small[index]
+        _, _, red, black, _, _ = small[index]
         slots, odd, step = red.shape[0], odd_at(index), 1 << index
         if index < last:
             spreads = [
@@ -801,12 +813,9 @@
     def params(mib):
         return pltpu.CompilerParams(vmem_limit_bytes=mib * 1024 * 1024)
 
-    ya, yb = pl.pallas_call(
-        functools.partial(faces_kernel, halo),
-        out_shape=[struct(nx, halo, nz)] * 2,
-        in_specs=[pl.BlockSpec(memory_space=pltpu.HBM)], out_specs=vmem(2),
-        compiler_params=params(2), scratch_shapes=[pltpu.SemaphoreType.DMA((2,))],
-    )(density)
+    even = lax.axis_index("gy") % 2 == 0
+    ya = lax.dynamic_slice_in_dim(density, jnp.where(even, ny - halo, 0), halo, 1)
+    yb = lax.dynamic_slice_in_dim(density, jnp.where(even, 0, ny - halo), halo, 1)
     ya = lax.ppermute(ya, "gy", pairs(count_y, 0))
     yb = lax.ppermute(yb, ("gx", "gy"), inner_pairs(count_x, count_y))
     rows = ny + 2 * halo
@@ -866,6 +875,7 @@
     for count in small_shapes(whole):
         room += [scratch(count, rows2, LANES)] * 2
         room += [scratch(count, 1, rows2 + 2 * PAD, LANES)] * 2
+        room += [scratch(count, rows2, LANES)] * 2
     return pl.pallas_call(
         functools.partial(solve_kernel, halo, whole),
         out_shape=struct(nx, ny, nz),

time: 42.7 us -> 40.9 us (0.958)
  waiting for transfers between devices: 14.7 us -> 13.3 us
  Pallas kernels: 10.5 us -> 9.99 us
    ppermute x1, starting transfers between devices: 0.2 us -> 2.57 us  [block_cycle(): lax.ppermute(block, ('gx', 'gy'), flips(count_x * count_y, count_y + 1))]
    ppermute x1, starting transfers between devices: 1.52 us -> 3.06 us  [block_cycle(): yb = lax.ppermute(yb, ('gx', 'gy'), inner_pairs(count_x, count_y))]
    ppermute x1, starting transfers between devices: 3.12 us -> 1.63 us  [block_cycle(): ya = lax.ppermute(ya, 'gy', pairs(count_y, 0))]
    ppermute x1, starting transfers between devices: 1.83 us -> 0.48 us  [block_cycle(): lax.ppermute(block, 'gy', flips(count_y, 1))]
    dynamic_slice x0 -> x1, local copies, waits for them, and re-layouts: none -> 1.03 us  [block_cycle(): lax.dynamic_slice_in_dim(density, jnp.where(even, 0, ny - halo), halo, 1)]
    ppermute x1, starting transfers between devices: 1.52 us -> 0.51 us  [block_cycle(): lax.ppermute(block, 'gx', flips(count_x, 1))]
    ppermute x1, waiting for transfers between devices: 0.52 us -> 1.52 us  [block_cycle(): lax.ppermute(block, 'gy', flips(count_y, 1))]
    ppermute x1, starting transfers between devices: 3.52 us -> 2.57 us  [block_cycle(): lax.ppermute(send, ('gy', 'gz'), flips(count_y * count_z, 2 * count_z + 2))]
where the time goes in v10:
time: 40.9 us; the launch traced here: 40.7 us
  starting transfers between devices  16.3 us (40%)
  waiting for transfers between devices  13.3 us (33%)
  Pallas kernels  9.99 us (24%)
  local copies, waits for them, and re-layouts  1.04 us (3%)
    pallas_call x1, Pallas kernels, block_cycle(): pl.pallas_call(functools.partial(solve_kernel, halo, whole), out_shape=st...  6.5 us
    ppermute x1, starting transfers between devices, block_cycle(): yb = lax.ppermute(yb, ('gx', 'gy'), inner_pairs(count_x, count_y))  3.06 us
    ppermute x1, starting transfers between devices, block_cycle(): lax.ppermute(block, ('gx', 'gy'), flips(count_x * count_y, count_y + 1))  2.57 us
    ppermute x1, starting transfers between devices, block_cycle(): lax.ppermute(send, ('gy', 'gz'), flips(count_y * count_z, 2 * count_z + 2))  2.57 us
    ppermute x1, waiting for transfers between devices, block_cycle(): yb = lax.ppermute(yb, ('gx', 'gy'), inner_pairs(count_x, count_y))  1.86 us
    ppermute x1, waiting for transfers between devices, block_cycle(): lax.ppermute(zb, 'gz', pairs(count_z, 1) + [(0, count_z - 1), (count_z -...  1.81 us
    pallas_call x1, Pallas kernels, block_cycle(): pl.pallas_call(functools.partial(pre_kernel, halo), out_shape=[struct(nea...  1.66 us
    ppermute x1, starting transfers between devices, block_cycle(): ya = lax.ppermute(ya, 'gy', pairs(count_y, 0))  1.63 us
  transfers between devices with their start and end apart: 15, of which 12 were waited for; matrix products, arithmetic and copies ran while one was open for 0% of the time, Pallas kernels for 4%

profile of v10, /device:TPU:0, one launch (start us, length us, event | category | flops | bytes accessed | tf_op | source)
XLA Modules:
  0.0 40.7 jit_solution(14004874188174657926)
XLA Ops:
  0.0 0.0 copy-start
  0.0 1.0 %constant_dynamic-slice_fusion = (f32[32,8,128]{2,1,0:T(8,128)S(1)}, f32[32,8,128]{2,1,0:T(8,128)S(1)}) fusion(f32[32,16,128]{2,1,0:T(8,128)} %own_ref.5, s32[]{:T(128)S(6)} %select_n.18, s32[]{:T(128)S(6)} %select_n.17), kind=kLoop, calls=%fused_computation | loop fusion | bytes 524296 | tf_op jit(solution)/shard_map/dynamic_slice | solution.py:818
  1.0 3.1 %collective-permute-start.1 = (f32[32,8,128]{2,1,0:T(8,128)S(1)}, f32[32,8,128]{2,1,0:T(8,128)S(1)}, u32[]{:S(2)}, u32[]{:S(2)}) collective-permute-start(f32[32,8,128]{2,1,0:T(8,128)S(1)} %get-tuple-element.35), channel_id=1, source_target_pairs={{4,8},{8,4},{0,16},{12,28},{20,24},{24,20},{16,0},{28,12},{5,9},{9... | collective-permute-start | bytes 393224 | tf_op jit(solution)/shard_map/ppermute | solution.py:820
  4.1 1.6 %collective-permute-start = (f32[32,8,128]{2,1,0:T(8,128)S(1)}, f32[32,8,128]{2,1,0:T(8,128)S(1)}, u32[]{:S(2)}, u32[]{:S(2)}) collective-permute-start(f32[32,8,128]{2,1,0:T(8,128)S(1)} %get-tuple-element.36), channel_id=1, source_target_pairs={{0,4},{4,0},{8,12},{12,8},{1,5},{5,1},{9,13},{13,9},{2,6},{6,2},{1... | collective-permute-start | bytes 393224 | tf_op jit(solution)/shard_map/ppermute | solution.py:819
  5.7 1.9 %collective-permute-done.1.yb_ref = f32[32,8,128]{2,1,0:T(8,128)S(1)} collective-permute-done((f32[32,8,128]{2,1,0:T(8,128)S(1)}, f32[32,8,128]{2,1,0:T(8,128)S(1)}, u32[]{:S(2)}, u32[]{:S(2)}) %collective-permute-start.1) | collective-permute-done | bytes 131104 | tf_op jit(solution)/shard_map/ppermute | solution.py:820
  7.6 1.5 %collective-permute-done.ya_ref = f32[32,8,128]{2,1,0:T(8,128)S(1)} collective-permute-done((f32[32,8,128]{2,1,0:T(8,128)S(1)}, f32[32,8,128]{2,1,0:T(8,128)S(1)}, u32[]{:S(2)}, u32[]{:S(2)}) %collective-permute-start) | collective-permute-done | bytes 131104 | tf_op jit(solution)/shard_map/ppermute | solution.py:819
  9.1 0.0 copy-done
  9.1 0.3 shard_map.28
  9.4 0.1 collective-permute-start.2
  9.5 1.6 %collective-permute-start.3 = (f32[2,32,128]{2,1,0:T(8,128)S(1)}, f32[2,32,128]{2,1,0:T(8,128)S(1)}, u32[]{:S(2)}, u32[]{:S(2)}) collective-permute-start(f32[2,32,128]{2,1,0:T(8,128)S(1)} %get-tuple-element.21), channel_id=1, source_target_pairs={{1,2},{2,1},{0,3},{3,0},{5,6},{6,5},{4,7},{7,4},{9,10},{10,9},{8,1... | collective-permute-start | bytes 98312 | tf_op jit(solution)/shard_map/ppermute | solution.py:829
  11.1 0.0 collective-permute-done.2.za_ref
  11.1 1.8 %collective-permute-done.3.zb_ref = f32[2,32,128]{2,1,0:T(8,128)S(1)} collective-permute-done((f32[2,32,128]{2,1,0:T(8,128)S(1)}, f32[2,32,128]{2,1,0:T(8,128)S(1)}, u32[]{:S(2)}, u32[]{:S(2)}) %collective-permute-start.3) | collective-permute-done | bytes 32800 | tf_op jit(solution)/shard_map/ppermute | solution.py:829
  12.9 1.7 %shard_map.29 = (f32[9,8,128]{2,1,0:T(8,128)S(1)}, f32[9,32,128]{2,1,0:T(8,128)S(1)}) custom-call(f32[32,16,128]{2,1,0:T(8,128)S(1)} %copy-done, f32[32,8,128]{2,1,0:T(8,128)S(1)} %collective-permute-done.ya_ref, f32[32,8,128]{2,1,0:T(8,128)S(1)} %collective-permute-done.1.yb_ref, f32[2,32,128]{2,1,0:T(8,128)S(1)} %collective-permute-done.2.za_ref, ...), custom_call_target="tpu_custom_call" | custom-call | tf_op jit(solution)/shard_map/pallas_call | solution.py:831
  14.6 1.5 %collective-permute-start.7 = (f32[9,32,128]{2,1,0:T(8,128)S(1)}, f32[9,32,128]{2,1,0:T(8,128)S(1)}, u32[]{:S(2)}, u32[]{:S(2)}) collective-permute-start(f32[9,32,128]{2,1,0:T(8,128)S(1)} %get-tuple-element.23), channel_id=1, source_target_pairs={{0,16},{16,0},{1,17},{17,1},{2,18},{18,2},{3,19},{19,3},{4,20},{20... | collective-permute-start | bytes 442376 | tf_op jit(solution)/shard_map/ppermute | solution.py:849
  16.0 2.6 %collective-permute-start.6 = (f32[9,8,128]{2,1,0:T(8,128)S(1)}, f32[9,8,128]{2,1,0:T(8,128)S(1)}, u32[]{:S(2)}, u32[]{:S(2)}) collective-permute-start(f32[9,8,128]{2,1,0:T(8,128)S(1)} %get-tuple-element.22.refs_0_), channel_id=1, source_target_pairs={{0,10},{1,11},{2,8},{3,9},{4,14},{5,15},{6,12},{7,13},{8,2},{9,3},... | collective-permute-start | bytes 110600 | tf_op jit(solution)/shard_map/ppermute | solution.py:847
  18.6 0.5 %collective-permute-start.5 = (f32[9,8,128]{2,1,0:T(8,128)S(1)}, f32[9,8,128]{2,1,0:T(8,128)S(1)}, u32[]{:S(2)}, u32[]{:S(2)}) collective-permute-start(f32[9,8,128]{2,1,0:T(8,128)S(1)} %get-tuple-element.22.refs_0_), channel_id=1, source_target_pairs={{0,2},{1,3},{2,0},{3,1},{4,6},{5,7},{6,4},{7,5},{8,10},{9,11},{10,... | collective-permute-start | bytes 110600 | tf_op jit(solution)/shard_map/ppermute | solution.py:846
  19.1 1.3 %collective-permute-start.4 = (f32[9,8,128]{2,1,0:T(8,128)S(1)}, f32[9,8,128]{2,1,0:T(8,128)S(1)}, u32[]{:S(2)}, u32[]{:S(2)}) collective-permute-start(f32[9,8,128]{2,1,0:T(8,128)S(1)} %get-tuple-element.22.refs_0_), channel_id=1, source_target_pairs={{0,8},{4,12},{8,0},{12,4},{1,9},{5,13},{9,1},{13,5},{2,10},{6,14},... | collective-permute-start | bytes 110600 | tf_op jit(solution)/shard_map/ppermute | solution.py:845
  20.4 1.4 %collective-permute-done.6.refs_3_ = f32[9,8,128]{2,1,0:T(8,128)S(1)} collective-permute-done((f32[9,8,128]{2,1,0:T(8,128)S(1)}, f32[9,8,128]{2,1,0:T(8,128)S(1)}, u32[]{:S(2)}, u32[]{:S(2)}) %collective-permute-start.6) | collective-permute-done | bytes 36896 | tf_op jit(solution)/shard_map/ppermute | solution.py:847
  21.8 0.0 collective-permute-done.7.face_ref
  21.8 0.7 %collective-permute-done.5.refs_2_ = f32[9,8,128]{2,1,0:T(8,128)S(1)} collective-permute-done((f32[9,8,128]{2,1,0:T(8,128)S(1)}, f32[9,8,128]{2,1,0:T(8,128)S(1)}, u32[]{:S(2)}, u32[]{:S(2)}) %collective-permute-start.5) | collective-permute-done | bytes 36896 | tf_op jit(solution)/shard_map/ppermute | solution.py:846
  22.5 1.5 %collective-permute-done.4.refs_1_ = f32[9,8,128]{2,1,0:T(8,128)S(1)} collective-permute-done((f32[9,8,128]{2,1,0:T(8,128)S(1)}, f32[9,8,128]{2,1,0:T(8,128)S(1)}, u32[]{:S(2)}, u32[]{:S(2)}) %collective-permute-start.4) | collective-permute-done | bytes 36896 | tf_op jit(solution)/shard_map/ppermute | solution.py:845
  24.1 0.0 copy-start.1
  24.1 2.6 %collective-permute-start.10 = (f32[4,9,8,128]{3,2,1,0:T(8,128)S(1)}, f32[4,9,8,128]{3,2,1,0:T(8,128)S(1)}, u32[]{:S(2)}, u32[]{:S(2)}) collective-permute-start(f32[4,9,8,128]{3,2,1,0:T(8,128)S(1)} %shard_map.30.after_ref.refs_0_), channel_id=1, source_target_pairs={{0,20},{4,16},{8,28},{12,24},{16,4},{20,0},{24,12},{28,8},{1,21},{... | collective-permute-start | bytes 442376 | tf_op jit(solution)/shard_map/ppermute | solution.py:859
  26.7 0.5 %collective-permute-start.9 = (f32[4,9,8,128]{3,2,1,0:T(8,128)S(1)}, f32[4,9,8,128]{3,2,1,0:T(8,128)S(1)}, u32[]{:S(2)}, u32[]{:S(2)}) collective-permute-start(f32[4,9,8,128]{3,2,1,0:T(8,128)S(1)} %shard_map.30.after_ref.refs_0_), channel_id=1, source_target_pairs={{0,4},{4,0},{8,12},{12,8},{1,5},{5,1},{9,13},{13,9},{2,6},{6,2},{1... | collective-permute-start | bytes 442376 | tf_op jit(solution)/shard_map/ppermute | solution.py:858
  27.1 0.5 %collective-permute-start.8 = (f32[4,9,8,128]{3,2,1,0:T(8,128)S(1)}, f32[4,9,8,128]{3,2,1,0:T(8,128)S(1)}, u32[]{:S(2)}, u32[]{:S(2)}) collective-permute-start(f32[4,9,8,128]{3,2,1,0:T(8,128)S(1)} %shard_map.30.after_ref.refs_0_), channel_id=1, source_target_pairs={{0,16},{16,0},{1,17},{17,1},{2,18},{18,2},{3,19},{19,3},{4,20},{20... | collective-permute-start | bytes 442376 | tf_op jit(solution)/shard_map/ppermute | solution.py:857
  27.6 0.0 collective-permute-start.11
  27.6 1.5 %shard_map.31 = (f32[20,2,32,128]{3,2,1,0:T(8,128)S(1)}, f32[20,2,32,128]{3,2,1,0:T(8,128)S(1)}, f32[20,2,32,128]{3,2,1,0:T(8,128)S(1)}) custom-call(f32[32,16,128]{2,1,0:T(8,128)S(1)} %copy-done, f32[32,8,128]{2,1,0:T(8,128)S(1)} %collective-permute-done.ya_ref, f32[32,8,128]{2,1,0:T(8,128)S(1)} %collective-permute-done.1.yb_ref, ...), custom_call_target="tpu_custom_call" | custom-call | flops 20000000 | bytes 2000000 | tf_op jit(solution)/shard_map/pallas_call | solution.py:861
  29.1 1.6 %collective-permute-done.10.refs_3_ = f32[4,9,8,128]{3,2,1,0:T(8,128)S(1)} collective-permute-done((f32[4,9,8,128]{3,2,1,0:T(8,128)S(1)}, f32[4,9,8,128]{3,2,1,0:T(8,128)S(1)}, u32[]{:S(2)}, u32[]{:S(2)}) %collective-permute-start.10) | collective-permute-done | bytes 147488 | tf_op jit(solution)/shard_map/ppermute | solution.py:859
  30.7 1.5 %collective-permute-done.9.refs_2_ = f32[4,9,8,128]{3,2,1,0:T(8,128)S(1)} collective-permute-done((f32[4,9,8,128]{3,2,1,0:T(8,128)S(1)}, f32[4,9,8,128]{3,2,1,0:T(8,128)S(1)}, u32[]{:S(2)}, u32[]{:S(2)}) %collective-permute-start.9) | collective-permute-done | bytes 147488 | tf_op jit(solution)/shard_map/ppermute | solution.py:858
  32.3 0.1 collective-permute-done.8.refs_1_
  32.3 0.0 collective-permute-start.12
  32.3 0.5 %collective-permute-start.13 = (f32[4,9,8,128]{3,2,1,0:T(8,128)S(1)}, f32[4,9,8,128]{3,2,1,0:T(8,128)S(1)}, u32[]{:S(2)}, u32[]{:S(2)}) collective-permute-start(f32[4,9,8,128]{3,2,1,0:T(8,128)S(1)} %collective-permute-done.9.refs_2_), channel_id=1, source_target_pairs={{0,1},{1,0},{2,3},{3,2},{4,5},{5,4},{6,7},{7,6},{8,9},{9,8},{10,11... | collective-permute-start | bytes 442376 | tf_op jit(solution)/shard_map/ppermute | solution.py:869
  32.8 0.0 collective-permute-start.14
  32.8 0.0 collective-permute-done.11.refs_4_
  32.8 0.9 %collective-permute-done.12.refs_5_ = f32[4,9,8,128]{3,2,1,0:T(8,128)S(1)} collective-permute-done((f32[4,9,8,128]{3,2,1,0:T(8,128)S(1)}, f32[4,9,8,128]{3,2,1,0:T(8,128)S(1)}, u32[]{:S(2)}, u32[]{:S(2)}) %collective-permute-start.12) | collective-permute-done | bytes 147488 | tf_op jit(solution)/shard_map/ppermute | solution.py:869
  33.7 0.2 collective-permute-done.13.refs_6_
  33.9 0.3 collective-permute-done.14.refs_7_
  34.2 0.0 copy-done.1
  34.2 6.5 %shard_map.32 = f32[32,16,128]{2,1,0:T(8,128)} custom-call(f32[4,9,8,128]{3,2,1,0:T(8,128)S(1)} %shard_map.30.after_ref.refs_0_, f32[4,9,8,128]{3,2,1,0:T(8,128)S(1)} %collective-permute-done.8.refs_1_, f32[4,9,8,128]{3,2,1,0:T(8,128)S(1)} %collective-permute-done.9.refs_2_, f32[4,9,8,128]{3,2,1,0:T(8,128)S(1)} %collective-permute-done.10.refs_3_, ...), custom_call_target="tpu_custom_call" | custom-call | tf_op jit(solution)/shard_map/pallas_call | solution.py:879
  (1 shorter events, 0.0 us)
Async XLA Ops:
  0.0 9.1 %copy-start = (f32[32,16,128]{2,1,0:T(8,128)S(1)}, f32[32,16,128]{2,1,0:T(8,128)}, u32[]{:S(2)}) copy-start(f32[32,16,128]{2,1,0:T(8,128)} %own_ref.5) | copy-start | bytes 786436
  1.0 6.6 %collective-permute-start.1 = (f32[32,8,128]{2,1,0:T(8,128)S(1)}, f32[32,8,128]{2,1,0:T(8,128)S(1)}, u32[]{:S(2)}, u32[]{:S(2)}) collective-permute-start(f32[32,8,128]{2,1,0:T(8,128)S(1)} %get-tuple-element.35), channel_id=1, source_target_pairs={{4,8},{8,4},{0,16},{12,28},{20,24},{24,20},{16,0},{28,12},{5,9},{9... | collective-permute-start | bytes 393224 | tf_op jit(solution)/shard_map/ppermute | solution.py:820
  4.1 5.0 %collective-permute-start = (f32[32,8,128]{2,1,0:T(8,128)S(1)}, f32[32,8,128]{2,1,0:T(8,128)S(1)}, u32[]{:S(2)}, u32[]{:S(2)}) collective-permute-start(f32[32,8,128]{2,1,0:T(8,128)S(1)} %get-tuple-element.36), channel_id=1, source_target_pairs={{0,4},{4,0},{8,12},{12,8},{1,5},{5,1},{9,13},{13,9},{2,6},{6,2},{1... | collective-permute-start | bytes 393224 | tf_op jit(solution)/shard_map/ppermute | solution.py:819
  9.4 1.7 %collective-permute-start.2 = (f32[2,32,128]{2,1,0:T(8,128)S(1)}, f32[2,32,128]{2,1,0:T(8,128)S(1)}, u32[]{:S(2)}, u32[]{:S(2)}) collective-permute-start(f32[2,32,128]{2,1,0:T(8,128)S(1)} %get-tuple-element.20), channel_id=1, source_target_pairs={{0,1},{1,0},{2,3},{3,2},{4,5},{5,4},{6,7},{7,6},{8,9},{9,8},{10,11... | collective-permute-start | bytes 98312 | tf_op jit(solution)/shard_map/ppermute | solution.py:828
  9.5 3.4 %collective-permute-start.3 = (f32[2,32,128]{2,1,0:T(8,128)S(1)}, f32[2,32,128]{2,1,0:T(8,128)S(1)}, u32[]{:S(2)}, u32[]{:S(2)}) collective-permute-start(f32[2,32,128]{2,1,0:T(8,128)S(1)} %get-tuple-element.21), channel_id=1, source_target_pairs={{1,2},{2,1},{0,3},{3,0},{5,6},{6,5},{4,7},{7,4},{9,10},{10,9},{8,1... | collective-permute-start | bytes 98312 | tf_op jit(solution)/shard_map/ppermute | solution.py:829
  14.6 7.3 %collective-permute-start.7 = (f32[9,32,128]{2,1,0:T(8,128)S(1)}, f32[9,32,128]{2,1,0:T(8,128)S(1)}, u32[]{:S(2)}, u32[]{:S(2)}) collective-permute-start(f32[9,32,128]{2,1,0:T(8,128)S(1)} %get-tuple-element.23), channel_id=1, source_target_pairs={{0,16},{16,0},{1,17},{17,1},{2,18},{18,2},{3,19},{19,3},{4,20},{20... | collective-permute-start | bytes 442376 | tf_op jit(solution)/shard_map/ppermute | solution.py:849
  16.0 5.8 %collective-permute-start.6 = (f32[9,8,128]{2,1,0:T(8,128)S(1)}, f32[9,8,128]{2,1,0:T(8,128)S(1)}, u32[]{:S(2)}, u32[]{:S(2)}) collective-permute-start(f32[9,8,128]{2,1,0:T(8,128)S(1)} %get-tuple-element.22.refs_0_), channel_id=1, source_target_pairs={{0,10},{1,11},{2,8},{3,9},{4,14},{5,15},{6,12},{7,13},{8,2},{9,3},... | collective-permute-start | bytes 110600 | tf_op jit(solution)/shard_map/ppermute | solution.py:847
  18.6 4.0 %collective-permute-start.5 = (f32[9,8,128]{2,1,0:T(8,128)S(1)}, f32[9,8,128]{2,1,0:T(8,128)S(1)}, u32[]{:S(2)}, u32[]{:S(2)}) collective-permute-start(f32[9,8,128]{2,1,0:T(8,128)S(1)} %get-tuple-element.22.refs_0_), channel_id=1, source_target_pairs={{0,2},{1,3},{2,0},{3,1},{4,6},{5,7},{6,4},{7,5},{8,10},{9,11},{10,... | collective-permute-start | bytes 110600 | tf_op jit(solution)/shard_map/ppermute | solution.py:846
  19.1 4.9 %collective-permute-start.4 = (f32[9,8,128]{2,1,0:T(8,128)S(1)}, f32[9,8,128]{2,1,0:T(8,128)S(1)}, u32[]{:S(2)}, u32[]{:S(2)}) collective-permute-start(f32[9,8,128]{2,1,0:T(8,128)S(1)} %get-tuple-element.22.refs_0_), channel_id=1, source_target_pairs={{0,8},{4,12},{8,0},{12,4},{1,9},{5,13},{9,1},{13,5},{2,10},{6,14},... | collective-permute-start | bytes 110600 | tf_op jit(solution)/shard_map/ppermute | solution.py:845
  24.1 10.1 %copy-start.1 = (f32[128,128]{1,0:T(8,128)S(1)}, f32[128,128]{1,0:T(8,128)}, u32[]{:S(2)}) copy-start(f32[128,128]{1,0:T(8,128)} %constant.26.clone.refs_11_) | copy-start | bytes 196612
  24.1 6.7 %collective-permute-start.10 = (f32[4,9,8,128]{3,2,1,0:T(8,128)S(1)}, f32[4,9,8,128]{3,2,1,0:T(8,128)S(1)}, u32[]{:S(2)}, u32[]{:S(2)}) collective-permute-start(f32[4,9,8,128]{3,2,1,0:T(8,128)S(1)} %shard_map.30.after_ref.refs_0_), channel_id=1, source_target_pairs={{0,20},{4,16},{8,28},{12,24},{16,4},{20,0},{24,12},{28,8},{1,21},{... | collective-permute-start | bytes 442376 | tf_op jit(solution)/shard_map/ppermute | solution.py:859
  26.7 5.6 %collective-permute-start.9 = (f32[4,9,8,128]{3,2,1,0:T(8,128)S(1)}, f32[4,9,8,128]{3,2,1,0:T(8,128)S(1)}, u32[]{:S(2)}, u32[]{:S(2)}) collective-permute-start(f32[4,9,8,128]{3,2,1,0:T(8,128)S(1)} %shard_map.30.after_ref.refs_0_), channel_id=1, source_target_pairs={{0,4},{4,0},{8,12},{12,8},{1,5},{5,1},{9,13},{13,9},{2,6},{6,2},{1... | collective-permute-start | bytes 442376 | tf_op jit(solution)/shard_map/ppermute | solution.py:858
  27.1 5.2 %collective-permute-start.8 = (f32[4,9,8,128]{3,2,1,0:T(8,128)S(1)}, f32[4,9,8,128]{3,2,1,0:T(8,128)S(1)}, u32[]{:S(2)}, u32[]{:S(2)}) collective-permute-start(f32[4,9,8,128]{3,2,1,0:T(8,128)S(1)} %shard_map.30.after_ref.refs_0_), channel_id=1, source_target_pairs={{0,16},{16,0},{1,17},{17,1},{2,18},{18,2},{3,19},{19,3},{4,20},{20... | collective-permute-start | bytes 442376 | tf_op jit(solution)/shard_map/ppermute | solution.py:857
  27.6 5.2 %collective-permute-start.11 = (f32[4,9,8,128]{3,2,1,0:T(8,128)S(1)}, f32[4,9,8,128]{3,2,1,0:T(8,128)S(1)}, u32[]{:S(2)}, u32[]{:S(2)}) collective-permute-start(f32[4,9,8,128]{3,2,1,0:T(8,128)S(1)} %shard_map.30.after_ref.refs_0_), channel_id=1, source_target_pairs={{0,1},{1,0},{2,3},{3,2},{4,5},{5,4},{6,7},{7,6},{8,9},{9,8},{10,11... | collective-permute-start | bytes 442376 | tf_op jit(solution)/shard_map/ppermute | solution.py:869
  32.3 1.4 %collective-permute-start.12 = (f32[4,9,8,128]{3,2,1,0:T(8,128)S(1)}, f32[4,9,8,128]{3,2,1,0:T(8,128)S(1)}, u32[]{:S(2)}, u32[]{:S(2)}) collective-permute-start(f32[4,9,8,128]{3,2,1,0:T(8,128)S(1)} %collective-permute-done.8.refs_1_), channel_id=1, source_target_pairs={{0,1},{1,0},{2,3},{3,2},{4,5},{5,4},{6,7},{7,6},{8,9},{9,8},{10,11... | collective-permute-start | bytes 442376 | tf_op jit(solution)/shard_map/ppermute | solution.py:869
  32.3 1.6 %collective-permute-start.13 = (f32[4,9,8,128]{3,2,1,0:T(8,128)S(1)}, f32[4,9,8,128]{3,2,1,0:T(8,128)S(1)}, u32[]{:S(2)}, u32[]{:S(2)}) collective-permute-start(f32[4,9,8,128]{3,2,1,0:T(8,128)S(1)} %collective-permute-done.9.refs_2_), channel_id=1, source_target_pairs={{0,1},{1,0},{2,3},{3,2},{4,5},{5,4},{6,7},{7,6},{8,9},{9,8},{10,11... | collective-permute-start | bytes 442376 | tf_op jit(solution)/shard_map/ppermute | solution.py:869
  32.8 1.4 %collective-permute-start.14 = (f32[4,9,8,128]{3,2,1,0:T(8,128)S(1)}, f32[4,9,8,128]{3,2,1,0:T(8,128)S(1)}, u32[]{:S(2)}, u32[]{:S(2)}) collective-permute-start(f32[4,9,8,128]{3,2,1,0:T(8,128)S(1)} %collective-permute-done.10.refs_3_), channel_id=1, source_target_pairs={{0,1},{1,0},{2,3},{3,2},{4,5},{5,4},{6,7},{7,6},{8,9},{9,8},{10,11... | collective-permute-start | bytes 442376 | tf_op jit(solution)/shard_map/ppermute | solution.py:869

commit v11 on v10

--- a/solution.py
+++ b/solution.py
@@ -82,14 +82,14 @@
     parity = parity_of(source.shape, (0, 0, 0))
     field = jnp.zeros_like(source)
     if level == LEVELS - 1:
-        for number in range(CSWEEPS):
+        for _ in range(CSWEEPS):
             field = full_sweep(field, source, scale, parity)
         return field
-    for number in range(2):
+    for _ in range(2):
         field = full_sweep(field, source, scale, parity)
     residue = source - scale * (centre * field - stencil_sum(jnp.pad(field, 1)))
     field = field + prolong(local_cycle(restrict(residue), level + 1))
-    for number in range(2):
+    for _ in range(2):
         field = full_sweep(field, source, scale, parity)
     return field
 
@@ -159,7 +159,7 @@
     field = wide_sweep(wide(field), wide_source, scale, red_wide, source, black)
     residue = source - scale * (centre * field - stencil_sum(faces(field)))
     field = field + prolong(shared_cycle(restrict(residue), level + 1, top))
-    for number in range(2):
+    for _ in range(2):
         field = wide_sweep(wide(field), wide_source, scale, red_wide, source, black)
     return field
 
@@ -201,6 +201,17 @@
 
 def exact_dot(a, b):
     return jnp.dot(a, b, precision=lax.Precision.HIGHEST, preferred_element_type=jnp.float32)
+
+
+def pick_dot(a, b):
+    b = b.astype(jnp.bfloat16)
+    total = None
+    for _ in range(3):
+        high = a.astype(jnp.bfloat16)
+        term = jnp.dot(high, b, preferred_element_type=jnp.float32)
+        total = term if total is None else total + term
+        a = a - high.astype(jnp.float32)
+    return total
 
 
 def window(ref, at, column, count, start=0, shift=0):
@@ -385,7 +396,7 @@
     column = (lanes_of((nz, nz)) - turn) & (nz - 1)
     target = 2 * (column % quarter) + (column // quarter) % 2
     weight = jnp.where(rows_of((nz, nz)) // 2 == target, 0.5, 0.0)
-    coarse = exact_dot(pairs_y.reshape(count * half, nz), weight).reshape(count, half, nz)
+    coarse = pick_dot(pairs_y.reshape(count * half, nz), weight).reshape(count, half, nz)
     part = ((lanes_of((half, nz)) - turn) & (nz - 1)) // quarter
     pick = (((rows_of((half, nz)) + part) & 1) == 1) ^ (part >= 2)
     for at in range(count // 2):
@@ -476,7 +487,7 @@
     return jnp.asarray(result.transpose(0, 3, 1, 2).reshape(size, size), jnp.float32)
 
 
-def solve_kernel(halo, whole, *refs):
+def solve_kernel(halo, *refs):
     gathered, refs = refs[:8], refs[8:]
     gr_ref, gb_ref, dark_ref, matrix_ref, out_ref = refs[:5]
     fr1, fb1, red1, black1, rest1, tall_ref, red_ref, work_ref, passing = refs[5:14]
@@ -497,6 +508,7 @@
     group = lanes_of((block_rows, LANES)) // quarter
     held = [jnp.bitwise_and(group - jnp.bitwise_xor(gz, bits), 3) for bits in range(4)]
     theirs = [[kind == part for kind in held] for part in range(4)]
+
     def unpack(far, second, at):
         y = jnp.bitwise_xor(gy, 2 * far + (second >> 1))
         rows = pl.ds(pl.multiple_of(y * block_rows, 8), block_rows)
@@ -735,7 +747,7 @@
                 value = share * (source + up_total(other, at, e, to_red))
                 target[slot0 + at, e, pl.ds(pl.multiple_of(row0 + PAD, 8), part_rows), :] = value
 
-    for sweep in range(2):
+    for _ in range(2):
         up_half(red1, black1, fr1, True)
         up_half(black1, red1, fb1, False)
 
@@ -758,7 +770,7 @@
     line = rows_of(shape)
     line = jnp.where(line < LANES, 2 * line, 2 * (line - LANES) + 1)
     weight = jnp.where(line == lax.shift_right_arithmetic(z, 1), 1.0, 0.0)
-    spread = exact_dot(tall_ref[...].reshape(count * half, 2 * LANES), weight)
+    spread = pick_dot(tall_ref[...].reshape(count * half, 2 * LANES), weight)
     spread = spread.reshape(count, half, 2 * LANES)
     for at in range(count):
         for c in range(2):
@@ -772,12 +784,13 @@
     odd = odd_of((rows, LANES))
     masks = block_mask((ny, nz), halo)
     ends = (gx == 0, gx == lax.axis_size("gx") - 1)
+    beside_own = [*range(own), own, count - 1]
     for sweep in range(2):
-        for at in range(count):
+        for at in range(count) if sweep == 0 else beside_own:
             totals = block_totals(work_ref, at, rows, own, odd, True, *ends)
             for c in range(2):
                 red_ref[at, c, body, :] = gr_ref[at, c] + masks[c] * totals[c]
-        for at in range(count if sweep == 0 else own):
+        for at in beside_own if sweep == 0 else range(own):
             totals = block_totals(red_ref, at, rows, own, odd, False, *ends)
             for c in range(2 if sweep == 0 else 1):
                 work_ref[at, c, body, :] = gb_ref[at, c] + masks[c] * totals[c]
@@ -847,7 +860,6 @@
         lax.ppermute(send, ("gy", "gz"), flips(count_y * count_z, 2 * count_z + 2)),
     ]
     face = lax.ppermute(face, "gx", flips(count_x, 1))
-    first[3], face = lax.optimization_barrier((first[3], face))
     block = pl.pallas_call(
         stack_kernel, out_shape=struct(4, *send.shape),
         in_specs=vmem(4), out_specs=pl.BlockSpec(memory_space=pltpu.VMEM), compiler_params=params(2),
@@ -877,7 +889,7 @@
         room += [scratch(count, 1, rows2 + 2 * PAD, LANES)] * 2
         room += [scratch(count, rows2, LANES)] * 2
     return pl.pallas_call(
-        functools.partial(solve_kernel, halo, whole),
+        functools.partial(solve_kernel, halo),
         out_shape=struct(nx, ny, nz),
         in_specs=vmem(12), out_specs=pl.BlockSpec(memory_space=pltpu.VMEM),
         compiler_params=params(16), scratch_shapes=room,

time: 40.9 us -> 40.2 us (0.983)
    ppermute x1, waiting for transfers between devices: 1.43 us -> 0.01 us  [block_cycle(): lax.ppermute(send, ('gy', 'gz'), flips(count_y * count_z, 2 * count_z + 2))]
    ppermute x1, starting transfers between devices: 2.57 us -> 1.37 us  [block_cycle(): lax.ppermute(block, ('gx', 'gy'), flips(count_x * count_y, count_y + 1))]
    ppermute x1, starting transfers between devices: 0.51 us -> 1.43 us  [block_cycle(): lax.ppermute(block, 'gx', flips(count_x, 1))]
    ppermute x1, starting transfers between devices: 2.57 us -> 3.4 us  [block_cycle(): lax.ppermute(send, ('gy', 'gz'), flips(count_y * count_z, 2 * count_z + 2))]
    ppermute x1, waiting for transfers between devices: 0.7 us -> 1.51 us  [block_cycle(): lax.ppermute(send, 'gz', flips(count_z, 2))]
    ppermute x1, starting transfers between devices: 1.28 us -> 0.51 us  [block_cycle(): lax.ppermute(send, 'gy', flips(count_y, 2))]
    ppermute x1, waiting for transfers between devices: 1.52 us -> 1.04 us  [block_cycle(): lax.ppermute(block, 'gy', flips(count_y, 1))]
  transfers between devices with their start and end apart: 15 -> 15, of which waited for: 12 -> 11; matrix products, arithmetic and copies ran while one was open for 0% -> 0% of each run, Pallas kernels for 4% -> 4%
where the time goes in v11:
time: 40.2 us; the launch traced here: 40.1 us
  starting transfers between devices  16.3 us (41%)
  waiting for transfers between devices  13 us (32%)
  Pallas kernels  9.72 us (24%)
  local copies, waits for them, and re-layouts  1.04 us (3%)
    pallas_call x1, Pallas kernels, block_cycle(): pl.pallas_call(functools.partial(solve_kernel, halo), out_shape=struct(nx...  6.27 us
    ppermute x1, starting transfers between devices, block_cycle(): lax.ppermute(send, ('gy', 'gz'), flips(count_y * count_z, 2 * count_z + 2))  3.4 us
    ppermute x1, starting transfers between devices, block_cycle(): yb = lax.ppermute(yb, ('gx', 'gy'), inner_pairs(count_x, count_y))  3.06 us
    ppermute x1, waiting for transfers between devices, block_cycle(): yb = lax.ppermute(yb, ('gx', 'gy'), inner_pairs(count_x, count_y))  1.86 us
    ppermute x1, waiting for transfers between devices, block_cycle(): lax.ppermute(send, 'gy', flips(count_y, 2))  1.83 us
    ppermute x1, waiting for transfers between devices, block_cycle(): lax.ppermute(zb, 'gz', pairs(count_z, 1) + [(0, count_z - 1), (count_z -...  1.81 us
    ppermute x1, waiting for transfers between devices, block_cycle(): lax.ppermute(block, ('gx', 'gy'), flips(count_x * count_y, count_y + 1))  1.66 us
    ppermute x1, starting transfers between devices, block_cycle(): ya = lax.ppermute(ya, 'gy', pairs(count_y, 0))  1.63 us
  transfers between devices with their start and end apart: 15, of which 11 were waited for; matrix products, arithmetic and copies ran while one was open for 0% of the time, Pallas kernels for 4%

profile of v11, /device:TPU:0, one launch (start us, length us, event | category | flops | bytes accessed | tf_op | source)
XLA Modules:
  0.0 40.1 jit_solution(10959661263841702235)
XLA Ops:
  0.0 0.0 copy-start
  0.0 1.0 %constant_dynamic-slice_fusion = (f32[32,8,128]{2,1,0:T(8,128)S(1)}, f32[32,8,128]{2,1,0:T(8,128)S(1)}) fusion(f32[32,16,128]{2,1,0:T(8,128)} %own_ref.5, s32[]{:T(128)S(6)} %select_n.18, s32[]{:T(128)S(6)} %select_n.17), kind=kLoop, calls=%fused_computation | loop fusion | bytes 524296 | tf_op jit(solution)/shard_map/dynamic_slice | solution.py:831
  1.0 3.1 %collective-permute-start.1 = (f32[32,8,128]{2,1,0:T(8,128)S(1)}, f32[32,8,128]{2,1,0:T(8,128)S(1)}, u32[]{:S(2)}, u32[]{:S(2)}) collective-permute-start(f32[32,8,128]{2,1,0:T(8,128)S(1)} %get-tuple-element.31), channel_id=1, source_target_pairs={{4,8},{8,4},{0,16},{12,28},{20,24},{24,20},{16,0},{28,12},{5,9},{9... | collective-permute-start | bytes 393224 | tf_op jit(solution)/shard_map/ppermute | solution.py:833
  4.1 1.6 %collective-permute-start = (f32[32,8,128]{2,1,0:T(8,128)S(1)}, f32[32,8,128]{2,1,0:T(8,128)S(1)}, u32[]{:S(2)}, u32[]{:S(2)}) collective-permute-start(f32[32,8,128]{2,1,0:T(8,128)S(1)} %get-tuple-element.32), channel_id=1, source_target_pairs={{0,4},{4,0},{8,12},{12,8},{1,5},{5,1},{9,13},{13,9},{2,6},{6,2},{1... | collective-permute-start | bytes 393224 | tf_op jit(solution)/shard_map/ppermute | solution.py:832
  5.7 1.9 %collective-permute-done.1.yb_ref = f32[32,8,128]{2,1,0:T(8,128)S(1)} collective-permute-done((f32[32,8,128]{2,1,0:T(8,128)S(1)}, f32[32,8,128]{2,1,0:T(8,128)S(1)}, u32[]{:S(2)}, u32[]{:S(2)}) %collective-permute-start.1) | collective-permute-done | bytes 131104 | tf_op jit(solution)/shard_map/ppermute | solution.py:833
  7.6 1.5 %collective-permute-done.ya_ref = f32[32,8,128]{2,1,0:T(8,128)S(1)} collective-permute-done((f32[32,8,128]{2,1,0:T(8,128)S(1)}, f32[32,8,128]{2,1,0:T(8,128)S(1)}, u32[]{:S(2)}, u32[]{:S(2)}) %collective-permute-start) | collective-permute-done | bytes 131104 | tf_op jit(solution)/shard_map/ppermute | solution.py:832
  9.1 0.0 copy-done
  9.1 0.3 shard_map.28
  9.4 0.1 collective-permute-start.2
  9.5 1.6 %collective-permute-start.3 = (f32[2,32,128]{2,1,0:T(8,128)S(1)}, f32[2,32,128]{2,1,0:T(8,128)S(1)}, u32[]{:S(2)}, u32[]{:S(2)}) collective-permute-start(f32[2,32,128]{2,1,0:T(8,128)S(1)} %get-tuple-element.19), channel_id=1, source_target_pairs={{1,2},{2,1},{0,3},{3,0},{5,6},{6,5},{4,7},{7,4},{9,10},{10,9},{8,1... | collective-permute-start | bytes 98312 | tf_op jit(solution)/shard_map/ppermute | solution.py:842
  11.1 0.0 collective-permute-done.2.za_ref
  11.1 1.8 %collective-permute-done.3.zb_ref = f32[2,32,128]{2,1,0:T(8,128)S(1)} collective-permute-done((f32[2,32,128]{2,1,0:T(8,128)S(1)}, f32[2,32,128]{2,1,0:T(8,128)S(1)}, u32[]{:S(2)}, u32[]{:S(2)}) %collective-permute-start.3) | collective-permute-done | bytes 32800 | tf_op jit(solution)/shard_map/ppermute | solution.py:842
  12.9 1.6 %shard_map.29 = (f32[9,8,128]{2,1,0:T(8,128)S(1)}, f32[9,32,128]{2,1,0:T(8,128)S(1)}) custom-call(f32[32,16,128]{2,1,0:T(8,128)S(1)} %copy-done, f32[32,8,128]{2,1,0:T(8,128)S(1)} %collective-permute-done.ya_ref, f32[32,8,128]{2,1,0:T(8,128)S(1)} %collective-permute-done.1.yb_ref, f32[2,32,128]{2,1,0:T(8,128)S(1)} %collective-permute-done.2.za_ref, ...), custom_call_target="tpu_custom_call" | custom-call | tf_op jit(solution)/shard_map/pallas_call | solution.py:844
  14.5 3.4 %collective-permute-start.6 = (f32[9,8,128]{2,1,0:T(8,128)S(1)}, f32[9,8,128]{2,1,0:T(8,128)S(1)}, u32[]{:S(2)}, u32[]{:S(2)}) collective-permute-start(f32[9,8,128]{2,1,0:T(8,128)S(1)} %get-tuple-element.20.refs_0_), channel_id=1, source_target_pairs={{0,10},{1,11},{2,8},{3,9},{4,14},{5,15},{6,12},{7,13},{8,2},{9,3},... | collective-permute-start | bytes 110600 | tf_op jit(solution)/shard_map/ppermute | solution.py:860
  17.9 0.5 %collective-permute-start.5 = (f32[9,8,128]{2,1,0:T(8,128)S(1)}, f32[9,8,128]{2,1,0:T(8,128)S(1)}, u32[]{:S(2)}, u32[]{:S(2)}) collective-permute-start(f32[9,8,128]{2,1,0:T(8,128)S(1)} %get-tuple-element.20.refs_0_), channel_id=1, source_target_pairs={{0,2},{1,3},{2,0},{3,1},{4,6},{5,7},{6,4},{7,5},{8,10},{9,11},{10,... | collective-permute-start | bytes 110600 | tf_op jit(solution)/shard_map/ppermute | solution.py:859
  18.5 0.5 %collective-permute-start.4 = (f32[9,8,128]{2,1,0:T(8,128)S(1)}, f32[9,8,128]{2,1,0:T(8,128)S(1)}, u32[]{:S(2)}, u32[]{:S(2)}) collective-permute-start(f32[9,8,128]{2,1,0:T(8,128)S(1)} %get-tuple-element.20.refs_0_), channel_id=1, source_target_pairs={{0,8},{4,12},{8,0},{12,4},{1,9},{5,13},{9,1},{13,5},{2,10},{6,14},... | collective-permute-start | bytes 110600 | tf_op jit(solution)/shard_map/ppermute | solution.py:858
  19.0 1.4 %collective-permute-start.10 = (f32[9,32,128]{2,1,0:T(8,128)S(1)}, f32[9,32,128]{2,1,0:T(8,128)S(1)}, u32[]{:S(2)}, u32[]{:S(2)}) collective-permute-start(f32[9,32,128]{2,1,0:T(8,128)S(1)} %get-tuple-element.21), channel_id=1, source_target_pairs={{0,16},{16,0},{1,17},{17,1},{2,18},{18,2},{3,19},{19,3},{4,20},{20... | collective-permute-start | bytes 442376 | tf_op jit(solution)/shard_map/ppermute | solution.py:862
  20.4 0.0 collective-permute-done.6.refs_3_
  20.4 1.5 %collective-permute-done.5.refs_2_ = f32[9,8,128]{2,1,0:T(8,128)S(1)} collective-permute-done((f32[9,8,128]{2,1,0:T(8,128)S(1)}, f32[9,8,128]{2,1,0:T(8,128)S(1)}, u32[]{:S(2)}, u32[]{:S(2)}) %collective-permute-start.5) | collective-permute-done | bytes 36896 | tf_op jit(solution)/shard_map/ppermute | solution.py:859
  21.9 1.8 %collective-permute-done.4.refs_1_ = f32[9,8,128]{2,1,0:T(8,128)S(1)} collective-permute-done((f32[9,8,128]{2,1,0:T(8,128)S(1)}, f32[9,8,128]{2,1,0:T(8,128)S(1)}, u32[]{:S(2)}, u32[]{:S(2)}) %collective-permute-start.4) | collective-permute-done | bytes 36896 | tf_op jit(solution)/shard_map/ppermute | solution.py:858
  23.7 0.0 copy-start.1
  23.7 1.4 %collective-permute-start.9 = (f32[4,9,8,128]{3,2,1,0:T(8,128)S(1)}, f32[4,9,8,128]{3,2,1,0:T(8,128)S(1)}, u32[]{:S(2)}, u32[]{:S(2)}) collective-permute-start(f32[4,9,8,128]{3,2,1,0:T(8,128)S(1)} %shard_map.30.after_ref.refs_0_), channel_id=1, source_target_pairs={{0,20},{4,16},{8,28},{12,24},{16,4},{20,0},{24,12},{28,8},{1,21},{... | collective-permute-start | bytes 442376 | tf_op jit(solution)/shard_map/ppermute | solution.py:871
  25.1 0.8 %collective-permute-start.8 = (f32[4,9,8,128]{3,2,1,0:T(8,128)S(1)}, f32[4,9,8,128]{3,2,1,0:T(8,128)S(1)}, u32[]{:S(2)}, u32[]{:S(2)}) collective-permute-start(f32[4,9,8,128]{3,2,1,0:T(8,128)S(1)} %shard_map.30.after_ref.refs_0_), channel_id=1, source_target_pairs={{0,4},{4,0},{8,12},{12,8},{1,5},{5,1},{9,13},{13,9},{2,6},{6,2},{1... | collective-permute-start | bytes 442376 | tf_op jit(solution)/shard_map/ppermute | solution.py:870
  25.9 1.4 %collective-permute-start.7 = (f32[4,9,8,128]{3,2,1,0:T(8,128)S(1)}, f32[4,9,8,128]{3,2,1,0:T(8,128)S(1)}, u32[]{:S(2)}, u32[]{:S(2)}) collective-permute-start(f32[4,9,8,128]{3,2,1,0:T(8,128)S(1)} %shard_map.30.after_ref.refs_0_), channel_id=1, source_target_pairs={{0,16},{16,0},{1,17},{17,1},{2,18},{18,2},{3,19},{19,3},{4,20},{20... | collective-permute-start | bytes 442376 | tf_op jit(solution)/shard_map/ppermute | solution.py:869
  27.3 0.0 collective-permute-start.11
  27.3 0.0 collective-permute-done.10.face_ref
  27.3 1.5 %shard_map.31 = (f32[20,2,32,128]{3,2,1,0:T(8,128)S(1)}, f32[20,2,32,128]{3,2,1,0:T(8,128)S(1)}, f32[20,2,32,128]{3,2,1,0:T(8,128)S(1)}) custom-call(f32[32,16,128]{2,1,0:T(8,128)S(1)} %copy-done, f32[32,8,128]{2,1,0:T(8,128)S(1)} %collective-permute-done.ya_ref, f32[32,8,128]{2,1,0:T(8,128)S(1)} %collective-permute-done.1.yb_ref, ...), custom_call_target="tpu_custom_call" | custom-call | flops 20000000 | bytes 2000000 | tf_op jit(solution)/shard_map/pallas_call | solution.py:873
  28.8 1.7 %collective-permute-done.9.refs_3_ = f32[4,9,8,128]{3,2,1,0:T(8,128)S(1)} collective-permute-done((f32[4,9,8,128]{3,2,1,0:T(8,128)S(1)}, f32[4,9,8,128]{3,2,1,0:T(8,128)S(1)}, u32[]{:S(2)}, u32[]{:S(2)}) %collective-permute-start.9) | collective-permute-done | bytes 147488 | tf_op jit(solution)/shard_map/ppermute | solution.py:871
  30.5 1.0 %collective-permute-done.8.refs_2_ = f32[4,9,8,128]{3,2,1,0:T(8,128)S(1)} collective-permute-done((f32[4,9,8,128]{3,2,1,0:T(8,128)S(1)}, f32[4,9,8,128]{3,2,1,0:T(8,128)S(1)}, u32[]{:S(2)}, u32[]{:S(2)}) %collective-permute-start.8) | collective-permute-done | bytes 147488 | tf_op jit(solution)/shard_map/ppermute | solution.py:870
  31.5 0.4 %collective-permute-done.7.refs_1_ = f32[4,9,8,128]{3,2,1,0:T(8,128)S(1)} collective-permute-done((f32[4,9,8,128]{3,2,1,0:T(8,128)S(1)}, f32[4,9,8,128]{3,2,1,0:T(8,128)S(1)}, u32[]{:S(2)}, u32[]{:S(2)}) %collective-permute-start.7) | collective-permute-done | bytes 147488 | tf_op jit(solution)/shard_map/ppermute | solution.py:869
  31.9 0.0 collective-permute-start.12
  31.9 0.5 %collective-permute-start.13 = (f32[4,9,8,128]{3,2,1,0:T(8,128)S(1)}, f32[4,9,8,128]{3,2,1,0:T(8,128)S(1)}, u32[]{:S(2)}, u32[]{:S(2)}) collective-permute-start(f32[4,9,8,128]{3,2,1,0:T(8,128)S(1)} %collective-permute-done.8.refs_2_), channel_id=1, source_target_pairs={{0,1},{1,0},{2,3},{3,2},{4,5},{5,4},{6,7},{7,6},{8,9},{9,8},{10,11... | collective-permute-start | bytes 442376 | tf_op jit(solution)/shard_map/ppermute | solution.py:881
  32.5 0.0 collective-permute-start.14
  32.5 0.0 collective-permute-done.11.refs_4_
  32.5 0.9 %collective-permute-done.12.refs_5_ = f32[4,9,8,128]{3,2,1,0:T(8,128)S(1)} collective-permute-done((f32[4,9,8,128]{3,2,1,0:T(8,128)S(1)}, f32[4,9,8,128]{3,2,1,0:T(8,128)S(1)}, u32[]{:S(2)}, u32[]{:S(2)}) %collective-permute-start.12) | collective-permute-done | bytes 147488 | tf_op jit(solution)/shard_map/ppermute | solution.py:881
  33.3 0.2 collective-permute-done.13.refs_6_
  33.5 0.3 collective-permute-done.14.refs_7_
  33.8 0.0 copy-done.1
  33.8 6.3 %shard_map.32 = f32[32,16,128]{2,1,0:T(8,128)} custom-call(f32[4,9,8,128]{3,2,1,0:T(8,128)S(1)} %shard_map.30.after_ref.refs_0_, f32[4,9,8,128]{3,2,1,0:T(8,128)S(1)} %collective-permute-done.7.refs_1_, f32[4,9,8,128]{3,2,1,0:T(8,128)S(1)} %collective-permute-done.8.refs_2_, f32[4,9,8,128]{3,2,1,0:T(8,128)S(1)} %collective-permute-done.9.refs_3_, ...), custom_call_target="tpu_custom_call" | custom-call | tf_op jit(solution)/shard_map/pallas_call | solution.py:891
  (1 shorter events, 0.0 us)
Async XLA Ops:
  0.0 9.1 %copy-start = (f32[32,16,128]{2,1,0:T(8,128)S(1)}, f32[32,16,128]{2,1,0:T(8,128)}, u32[]{:S(2)}) copy-start(f32[32,16,128]{2,1,0:T(8,128)} %own_ref.5) | copy-start | bytes 786436
  1.0 6.6 %collective-permute-start.1 = (f32[32,8,128]{2,1,0:T(8,128)S(1)}, f32[32,8,128]{2,1,0:T(8,128)S(1)}, u32[]{:S(2)}, u32[]{:S(2)}) collective-permute-start(f32[32,8,128]{2,1,0:T(8,128)S(1)} %get-tuple-element.31), channel_id=1, source_target_pairs={{4,8},{8,4},{0,16},{12,28},{20,24},{24,20},{16,0},{28,12},{5,9},{9... | collective-permute-start | bytes 393224 | tf_op jit(solution)/shard_map/ppermute | solution.py:833
  4.1 5.0 %collective-permute-start = (f32[32,8,128]{2,1,0:T(8,128)S(1)}, f32[32,8,128]{2,1,0:T(8,128)S(1)}, u32[]{:S(2)}, u32[]{:S(2)}) collective-permute-start(f32[32,8,128]{2,1,0:T(8,128)S(1)} %get-tuple-element.32), channel_id=1, source_target_pairs={{0,4},{4,0},{8,12},{12,8},{1,5},{5,1},{9,13},{13,9},{2,6},{6,2},{1... | collective-permute-start | bytes 393224 | tf_op jit(solution)/shard_map/ppermute | solution.py:832
  9.4 1.7 %collective-permute-start.2 = (f32[2,32,128]{2,1,0:T(8,128)S(1)}, f32[2,32,128]{2,1,0:T(8,128)S(1)}, u32[]{:S(2)}, u32[]{:S(2)}) collective-permute-start(f32[2,32,128]{2,1,0:T(8,128)S(1)} %get-tuple-element.18), channel_id=1, source_target_pairs={{0,1},{1,0},{2,3},{3,2},{4,5},{5,4},{6,7},{7,6},{8,9},{9,8},{10,11... | collective-permute-start | bytes 98312 | tf_op jit(solution)/shard_map/ppermute | solution.py:841
  9.5 3.4 %collective-permute-start.3 = (f32[2,32,128]{2,1,0:T(8,128)S(1)}, f32[2,32,128]{2,1,0:T(8,128)S(1)}, u32[]{:S(2)}, u32[]{:S(2)}) collective-permute-start(f32[2,32,128]{2,1,0:T(8,128)S(1)} %get-tuple-element.19), channel_id=1, source_target_pairs={{1,2},{2,1},{0,3},{3,0},{5,6},{6,5},{4,7},{7,4},{9,10},{10,9},{8,1... | collective-permute-start | bytes 98312 | tf_op jit(solution)/shard_map/ppermute | solution.py:842
  14.5 5.9 %collective-permute-start.6 = (f32[9,8,128]{2,1,0:T(8,128)S(1)}, f32[9,8,128]{2,1,0:T(8,128)S(1)}, u32[]{:S(2)}, u32[]{:S(2)}) collective-permute-start(f32[9,8,128]{2,1,0:T(8,128)S(1)} %get-tuple-element.20.refs_0_), channel_id=1, source_target_pairs={{0,10},{1,11},{2,8},{3,9},{4,14},{5,15},{6,12},{7,13},{8,2},{9,3},... | collective-permute-start | bytes 110600 | tf_op jit(solution)/shard_map/ppermute | solution.py:860
  17.9 4.0 %collective-permute-start.5 = (f32[9,8,128]{2,1,0:T(8,128)S(1)}, f32[9,8,128]{2,1,0:T(8,128)S(1)}, u32[]{:S(2)}, u32[]{:S(2)}) collective-permute-start(f32[9,8,128]{2,1,0:T(8,128)S(1)} %get-tuple-element.20.refs_0_), channel_id=1, source_target_pairs={{0,2},{1,3},{2,0},{3,1},{4,6},{5,7},{6,4},{7,5},{8,10},{9,11},{10,... | collective-permute-start | bytes 110600 | tf_op jit(solution)/shard_map/ppermute | solution.py:859
  18.5 5.3 %collective-permute-start.4 = (f32[9,8,128]{2,1,0:T(8,128)S(1)}, f32[9,8,128]{2,1,0:T(8,128)S(1)}, u32[]{:S(2)}, u32[]{:S(2)}) collective-permute-start(f32[9,8,128]{2,1,0:T(8,128)S(1)} %get-tuple-element.20.refs_0_), channel_id=1, source_target_pairs={{0,8},{4,12},{8,0},{12,4},{1,9},{5,13},{9,1},{13,5},{2,10},{6,14},... | collective-permute-start | bytes 110600 | tf_op jit(solution)/shard_map/ppermute | solution.py:858
  19.0 8.3 %collective-permute-start.10 = (f32[9,32,128]{2,1,0:T(8,128)S(1)}, f32[9,32,128]{2,1,0:T(8,128)S(1)}, u32[]{:S(2)}, u32[]{:S(2)}) collective-permute-start(f32[9,32,128]{2,1,0:T(8,128)S(1)} %get-tuple-element.21), channel_id=1, source_target_pairs={{0,16},{16,0},{1,17},{17,1},{2,18},{18,2},{3,19},{19,3},{4,20},{20... | collective-permute-start | bytes 442376 | tf_op jit(solution)/shard_map/ppermute | solution.py:862
  23.7 10.1 %copy-start.1 = (f32[128,128]{1,0:T(8,128)S(1)}, f32[128,128]{1,0:T(8,128)}, u32[]{:S(2)}) copy-start(f32[128,128]{1,0:T(8,128)} %constant.26.clone.refs_11_) | copy-start | bytes 196612
  23.7 6.7 %collective-permute-start.9 = (f32[4,9,8,128]{3,2,1,0:T(8,128)S(1)}, f32[4,9,8,128]{3,2,1,0:T(8,128)S(1)}, u32[]{:S(2)}, u32[]{:S(2)}) collective-permute-start(f32[4,9,8,128]{3,2,1,0:T(8,128)S(1)} %shard_map.30.after_ref.refs_0_), channel_id=1, source_target_pairs={{0,20},{4,16},{8,28},{12,24},{16,4},{20,0},{24,12},{28,8},{1,21},{... | collective-permute-start | bytes 442376 | tf_op jit(solution)/shard_map/ppermute | solution.py:871
  25.1 6.4 %collective-permute-start.8 = (f32[4,9,8,128]{3,2,1,0:T(8,128)S(1)}, f32[4,9,8,128]{3,2,1,0:T(8,128)S(1)}, u32[]{:S(2)}, u32[]{:S(2)}) collective-permute-start(f32[4,9,8,128]{3,2,1,0:T(8,128)S(1)} %shard_map.30.after_ref.refs_0_), channel_id=1, source_target_pairs={{0,4},{4,0},{8,12},{12,8},{1,5},{5,1},{9,13},{13,9},{2,6},{6,2},{1... | collective-permute-start | bytes 442376 | tf_op jit(solution)/shard_map/ppermute | solution.py:870
  25.9 6.1 %collective-permute-start.7 = (f32[4,9,8,128]{3,2,1,0:T(8,128)S(1)}, f32[4,9,8,128]{3,2,1,0:T(8,128)S(1)}, u32[]{:S(2)}, u32[]{:S(2)}) collective-permute-start(f32[4,9,8,128]{3,2,1,0:T(8,128)S(1)} %shard_map.30.after_ref.refs_0_), channel_id=1, source_target_pairs={{0,16},{16,0},{1,17},{17,1},{2,18},{18,2},{3,19},{19,3},{4,20},{20... | collective-permute-start | bytes 442376 | tf_op jit(solution)/shard_map/ppermute | solution.py:869
  27.3 5.2 %collective-permute-start.11 = (f32[4,9,8,128]{3,2,1,0:T(8,128)S(1)}, f32[4,9,8,128]{3,2,1,0:T(8,128)S(1)}, u32[]{:S(2)}, u32[]{:S(2)}) collective-permute-start(f32[4,9,8,128]{3,2,1,0:T(8,128)S(1)} %shard_map.30.after_ref.refs_0_), channel_id=1, source_target_pairs={{0,1},{1,0},{2,3},{3,2},{4,5},{5,4},{6,7},{7,6},{8,9},{9,8},{10,11... | collective-permute-start | bytes 442376 | tf_op jit(solution)/shard_map/ppermute | solution.py:881
  31.9 1.4 %collective-permute-start.12 = (f32[4,9,8,128]{3,2,1,0:T(8,128)S(1)}, f32[4,9,8,128]{3,2,1,0:T(8,128)S(1)}, u32[]{:S(2)}, u32[]{:S(2)}) collective-permute-start(f32[4,9,8,128]{3,2,1,0:T(8,128)S(1)} %collective-permute-done.7.refs_1_), channel_id=1, source_target_pairs={{0,1},{1,0},{2,3},{3,2},{4,5},{5,4},{6,7},{7,6},{8,9},{9,8},{10,11... | collective-permute-start | bytes 442376 | tf_op jit(solution)/shard_map/ppermute | solution.py:881
  31.9 1.6 %collective-permute-start.13 = (f32[4,9,8,128]{3,2,1,0:T(8,128)S(1)}, f32[4,9,8,128]{3,2,1,0:T(8,128)S(1)}, u32[]{:S(2)}, u32[]{:S(2)}) collective-permute-start(f32[4,9,8,128]{3,2,1,0:T(8,128)S(1)} %collective-permute-done.8.refs_2_), channel_id=1, source_target_pairs={{0,1},{1,0},{2,3},{3,2},{4,5},{5,4},{6,7},{7,6},{8,9},{9,8},{10,11... | collective-permute-start | bytes 442376 | tf_op jit(solution)/shard_map/ppermute | solution.py:881
  32.5 1.4 %collective-permute-start.14 = (f32[4,9,8,128]{3,2,1,0:T(8,128)S(1)}, f32[4,9,8,128]{3,2,1,0:T(8,128)S(1)}, u32[]{:S(2)}, u32[]{:S(2)}) collective-permute-start(f32[4,9,8,128]{3,2,1,0:T(8,128)S(1)} %collective-permute-done.9.refs_3_), channel_id=1, source_target_pairs={{0,1},{1,0},{2,3},{3,2},{4,5},{5,4},{6,7},{7,6},{8,9},{9,8},{10,11... | collective-permute-start | bytes 442376 | tf_op jit(solution)/shard_map/ppermute | solution.py:881

commit v12 on v11

--- a/solution.py
+++ b/solution.py
@@ -853,12 +853,11 @@
     planes = nx + halo
     slots = (planes // 2, 2, rows, LANES)
     padded = (planes // 2, 2, rows + 2 * PAD, LANES)
-    first = [
-        send,
-        lax.ppermute(send, "gy", flips(count_y, 2)),
-        lax.ppermute(send, "gz", flips(count_z, 2)),
-        lax.ppermute(send, ("gy", "gz"), flips(count_y * count_z, 2 * count_z + 2)),
-    ]
+    first = [send]
+    first.append(lax.ppermute(send, "gy", flips(count_y, 2)))
+    first.append(lax.ppermute(send, "gz", flips(count_z, 2)))
+    swaps = flips(count_y * count_z, 2 * count_z + 2)
+    first.append(lax.ppermute(send, ("gy", "gz"), swaps))
     face = lax.ppermute(face, "gx", flips(count_x, 1))
     block = pl.pallas_call(
         stack_kernel, out_shape=struct(4, *send.shape),
@@ -877,7 +876,7 @@
         scratch_shapes=[scratch(*padded)] * 2,
         cost_estimate=pl.CostEstimate(flops=20_000_000, bytes_accessed=2_000_000, transcendentals=0),
     )(density, ya, yb, za, zb, face, block)
-    *second[1:], gr, gb, black = lax.optimization_barrier((*second[1:], gr, gb, black))
+    second[3], gr, gb, black = lax.optimization_barrier((second[3], gr, gb, black))
     third = [lax.ppermute(blocks, "gz", flips(count_z, 1)) for blocks in second]
     count1, rows1, rows2 = whole[0] // 4, whole[1] // 2, whole[1] // 4
     room = [scratch(count1, 2, rows1, LANES)] * 2

time: 40.2 us -> 41.4 us (1.030)
  waiting for transfers between devices: 13 us -> 14.2 us
    ppermute x1, starting transfers between devices: 3.06 us -> 1.52 us  [block_cycle(): yb = lax.ppermute(yb, ('gx', 'gy'), inner_pairs(count_x, count_y))]
    ppermute x1, starting transfers between devices: 1.63 us -> 3.12 us  [block_cycle(): ya = lax.ppermute(ya, 'gy', pairs(count_y, 0))]
    ppermute x1, starting transfers between devices: 0.76 us -> 1.83 us  [block_cycle(): lax.ppermute(block, 'gy', flips(count_y, 1))]
    ppermute x1, waiting for transfers between devices: 0.44 us -> 1.41 us  [block_cycle(): lax.ppermute(block, 'gx', flips(count_x, 1))]
    ppermute x1, starting transfers between devices: 1.43 us -> 0.51 us  [block_cycle(): lax.ppermute(block, 'gx', flips(count_x, 1))]
    ppermute x1, waiting for transfers between devices: 1.04 us -> 0.13 us  [block_cycle(): lax.ppermute(block, 'gy', flips(count_y, 1))]
    ppermute x3, waiting for transfers between devices: 3.34 us -> 4.21 us  [the longest x1 3.57 us: block_cycle(): first.append(lax.ppermute(send, ('gy', 'gz'), swaps))]
    ppermute x1, waiting for transfers between devices: 1.47 us -> 1.98 us  [block_cycle(): ya = lax.ppermute(ya, 'gy', pairs(count_y, 0))]
  transfers between devices with their start and end apart: 15 -> 15, of which waited for: 11 -> 10; matrix products, arithmetic and copies ran while one was open for 0% -> 0% of each run, Pallas kernels for 4% -> 4%
where the time goes in v12:
time: 41.4 us; the launch traced here: 41.2 us
  starting transfers between devices  16.2 us (39%)
  waiting for transfers between devices  14.2 us (34%)
  Pallas kernels  9.72 us (23%)
  local copies, waits for them, and re-layouts  1.04 us (3%)
    pallas_call x1, Pallas kernels, block_cycle(): pl.pallas_call(functools.partial(solve_kernel, halo), out_shape=struct(nx...  6.27 us
    ppermute x1, waiting for transfers between devices, block_cycle(): first.append(lax.ppermute(send, ('gy', 'gz'), swaps))  3.57 us
    ppermute x1, starting transfers between devices, block_cycle(): ya = lax.ppermute(ya, 'gy', pairs(count_y, 0))  3.12 us
    ppermute x1, starting transfers between devices, block_cycle(): first.append(lax.ppermute(send, 'gy', flips(count_y, 2)))  2.65 us
    ppermute x1, waiting for transfers between devices, block_cycle(): lax.ppermute(block, ('gx', 'gy'), flips(count_x * count_y, count_y + 1))  2.1 us
    ppermute x1, waiting for transfers between devices, block_cycle(): ya = lax.ppermute(ya, 'gy', pairs(count_y, 0))  1.98 us
    ppermute x1, starting transfers between devices, block_cycle(): lax.ppermute(block, 'gy', flips(count_y, 1))  1.83 us
    ppermute x1, waiting for transfers between devices, block_cycle(): lax.ppermute(zb, 'gz', pairs(count_z, 1) + [(0, count_z - 1), (count_z -...  1.81 us
  transfers between devices with their start and end apart: 15, of which 10 were waited for; matrix products, arithmetic and copies ran while one was open for 0% of the time, Pallas kernels for 4%

profile of v12, /device:TPU:0, one launch (start us, length us, event | category | flops | bytes accessed | tf_op | source)
XLA Modules:
  0.0 41.2 jit_solution(15029609483564946537)
XLA Ops:
  0.0 0.0 copy-start
  0.0 1.0 %constant_dynamic-slice_fusion = (f32[32,8,128]{2,1,0:T(8,128)S(1)}, f32[32,8,128]{2,1,0:T(8,128)S(1)}) fusion(f32[32,16,128]{2,1,0:T(8,128)} %own_ref.5, s32[]{:T(128)S(6)} %select_n.18, s32[]{:T(128)S(6)} %select_n.17), kind=kLoop, calls=%fused_computation | loop fusion | bytes 524296 | tf_op jit(solution)/shard_map/dynamic_slice | solution.py:831
  1.0 3.1 %collective-permute-start = (f32[32,8,128]{2,1,0:T(8,128)S(1)}, f32[32,8,128]{2,1,0:T(8,128)S(1)}, u32[]{:S(2)}, u32[]{:S(2)}) collective-permute-start(f32[32,8,128]{2,1,0:T(8,128)S(1)} %get-tuple-element.28), channel_id=1, source_target_pairs={{0,4},{4,0},{8,12},{12,8},{1,5},{5,1},{9,13},{13,9},{2,6},{6,2},{1... | collective-permute-start | bytes 393224 | tf_op jit(solution)/shard_map/ppermute | solution.py:832
  4.2 1.5 %collective-permute-start.1 = (f32[32,8,128]{2,1,0:T(8,128)S(1)}, f32[32,8,128]{2,1,0:T(8,128)S(1)}, u32[]{:S(2)}, u32[]{:S(2)}) collective-permute-start(f32[32,8,128]{2,1,0:T(8,128)S(1)} %get-tuple-element.27), channel_id=1, source_target_pairs={{4,8},{8,4},{0,16},{12,28},{20,24},{24,20},{16,0},{28,12},{5,9},{9... | collective-permute-start | bytes 393224 | tf_op jit(solution)/shard_map/ppermute | solution.py:833
  5.7 2.0 %collective-permute-done.ya_ref = f32[32,8,128]{2,1,0:T(8,128)S(1)} collective-permute-done((f32[32,8,128]{2,1,0:T(8,128)S(1)}, f32[32,8,128]{2,1,0:T(8,128)S(1)}, u32[]{:S(2)}, u32[]{:S(2)}) %collective-permute-start) | collective-permute-done | bytes 131104 | tf_op jit(solution)/shard_map/ppermute | solution.py:832
  7.6 1.5 %collective-permute-done.1.yb_ref = f32[32,8,128]{2,1,0:T(8,128)S(1)} collective-permute-done((f32[32,8,128]{2,1,0:T(8,128)S(1)}, f32[32,8,128]{2,1,0:T(8,128)S(1)}, u32[]{:S(2)}, u32[]{:S(2)}) %collective-permute-start.1) | collective-permute-done | bytes 131104 | tf_op jit(solution)/shard_map/ppermute | solution.py:833
  9.1 0.0 copy-done
  9.1 0.3 shard_map.28
  9.5 0.1 collective-permute-start.2
  9.5 1.6 %collective-permute-start.3 = (f32[2,32,128]{2,1,0:T(8,128)S(1)}, f32[2,32,128]{2,1,0:T(8,128)S(1)}, u32[]{:S(2)}, u32[]{:S(2)}) collective-permute-start(f32[2,32,128]{2,1,0:T(8,128)S(1)} %get-tuple-element.17), channel_id=1, source_target_pairs={{1,2},{2,1},{0,3},{3,0},{5,6},{6,5},{4,7},{7,4},{9,10},{10,9},{8,1... | collective-permute-start | bytes 98312 | tf_op jit(solution)/shard_map/ppermute | solution.py:842
  11.1 0.0 collective-permute-done.2.za_ref
  11.1 1.8 %collective-permute-done.3.zb_ref = f32[2,32,128]{2,1,0:T(8,128)S(1)} collective-permute-done((f32[2,32,128]{2,1,0:T(8,128)S(1)}, f32[2,32,128]{2,1,0:T(8,128)S(1)}, u32[]{:S(2)}, u32[]{:S(2)}) %collective-permute-start.3) | collective-permute-done | bytes 32800 | tf_op jit(solution)/shard_map/ppermute | solution.py:842
  12.9 1.6 %shard_map.29 = (f32[9,8,128]{2,1,0:T(8,128)S(1)}, f32[9,32,128]{2,1,0:T(8,128)S(1)}) custom-call(f32[32,16,128]{2,1,0:T(8,128)S(1)} %copy-done, f32[32,8,128]{2,1,0:T(8,128)S(1)} %collective-permute-done.ya_ref, f32[32,8,128]{2,1,0:T(8,128)S(1)} %collective-permute-done.1.yb_ref, f32[2,32,128]{2,1,0:T(8,128)S(1)} %collective-permute-done.2.za_ref, ...), custom_call_target="tpu_custom_call" | custom-call | tf_op jit(solution)/shard_map/pallas_call | solution.py:844
  14.6 2.7 %collective-permute-start.4 = (f32[9,8,128]{2,1,0:T(8,128)S(1)}, f32[9,8,128]{2,1,0:T(8,128)S(1)}, u32[]{:S(2)}, u32[]{:S(2)}) collective-permute-start(f32[9,8,128]{2,1,0:T(8,128)S(1)} %get-tuple-element.18.refs_0_), channel_id=1, source_target_pairs={{0,8},{4,12},{8,0},{12,4},{1,9},{5,13},{9,1},{13,5},{2,10},{6,14},... | collective-permute-start | bytes 110600 | tf_op jit(solution)/shard_map/ppermute | solution.py:857
  17.2 1.5 %collective-permute-start.5 = (f32[9,8,128]{2,1,0:T(8,128)S(1)}, f32[9,8,128]{2,1,0:T(8,128)S(1)}, u32[]{:S(2)}, u32[]{:S(2)}) collective-permute-start(f32[9,8,128]{2,1,0:T(8,128)S(1)} %get-tuple-element.18.refs_0_), channel_id=1, source_target_pairs={{0,2},{1,3},{2,0},{3,1},{4,6},{5,7},{6,4},{7,5},{8,10},{9,11},{10,... | collective-permute-start | bytes 110600 | tf_op jit(solution)/shard_map/ppermute | solution.py:858
  18.7 0.3 collective-permute-start.6
  19.0 1.5 %collective-permute-start.10 = (f32[9,32,128]{2,1,0:T(8,128)S(1)}, f32[9,32,128]{2,1,0:T(8,128)S(1)}, u32[]{:S(2)}, u32[]{:S(2)}) collective-permute-start(f32[9,32,128]{2,1,0:T(8,128)S(1)} %get-tuple-element.19), channel_id=1, source_target_pairs={{0,16},{16,0},{1,17},{17,1},{2,18},{18,2},{3,19},{19,3},{4,20},{20... | collective-permute-start | bytes 442376 | tf_op jit(solution)/shard_map/ppermute | solution.py:861
  20.5 0.0 collective-permute-done.4.refs_1_
  20.5 0.6 %collective-permute-done.5.refs_2_ = f32[9,8,128]{2,1,0:T(8,128)S(1)} collective-permute-done((f32[9,8,128]{2,1,0:T(8,128)S(1)}, f32[9,8,128]{2,1,0:T(8,128)S(1)}, u32[]{:S(2)}, u32[]{:S(2)}) %collective-permute-start.5) | collective-permute-done | bytes 36896 | tf_op jit(solution)/shard_map/ppermute | solution.py:858
  21.2 3.6 %collective-permute-done.6.refs_3_ = f32[9,8,128]{2,1,0:T(8,128)S(1)} collective-permute-done((f32[9,8,128]{2,1,0:T(8,128)S(1)}, f32[9,8,128]{2,1,0:T(8,128)S(1)}, u32[]{:S(2)}, u32[]{:S(2)}) %collective-permute-start.6) | collective-permute-done | bytes 36896 | tf_op jit(solution)/shard_map/ppermute | solution.py:860
  24.8 0.0 copy-start.1
  24.8 1.2 %collective-permute-start.9 = (f32[4,9,8,128]{3,2,1,0:T(8,128)S(1)}, f32[4,9,8,128]{3,2,1,0:T(8,128)S(1)}, u32[]{:S(2)}, u32[]{:S(2)}) collective-permute-start(f32[4,9,8,128]{3,2,1,0:T(8,128)S(1)} %shard_map.30.after_ref.refs_0_), channel_id=1, source_target_pairs={{0,20},{4,16},{8,28},{12,24},{16,4},{20,0},{24,12},{28,8},{1,21},{... | collective-permute-start | bytes 442376 | tf_op jit(solution)/shard_map/ppermute | solution.py:870
  26.0 0.5 %collective-permute-start.7 = (f32[4,9,8,128]{3,2,1,0:T(8,128)S(1)}, f32[4,9,8,128]{3,2,1,0:T(8,128)S(1)}, u32[]{:S(2)}, u32[]{:S(2)}) collective-permute-start(f32[4,9,8,128]{3,2,1,0:T(8,128)S(1)} %shard_map.30.after_ref.refs_0_), channel_id=1, source_target_pairs={{0,16},{16,0},{1,17},{17,1},{2,18},{18,2},{3,19},{19,3},{4,20},{20... | collective-permute-start | bytes 442376 | tf_op jit(solution)/shard_map/ppermute | solution.py:868
  26.5 1.8 %collective-permute-start.8 = (f32[4,9,8,128]{3,2,1,0:T(8,128)S(1)}, f32[4,9,8,128]{3,2,1,0:T(8,128)S(1)}, u32[]{:S(2)}, u32[]{:S(2)}) collective-permute-start(f32[4,9,8,128]{3,2,1,0:T(8,128)S(1)} %shard_map.30.after_ref.refs_0_), channel_id=1, source_target_pairs={{0,4},{4,0},{8,12},{12,8},{1,5},{5,1},{9,13},{13,9},{2,6},{6,2},{1... | collective-permute-start | bytes 442376 | tf_op jit(solution)/shard_map/ppermute | solution.py:869
  28.3 0.0 collective-permute-start.11
  28.3 0.0 collective-permute-done.10.face_ref
  28.3 1.5 %shard_map.31 = (f32[20,2,32,128]{3,2,1,0:T(8,128)S(1)}, f32[20,2,32,128]{3,2,1,0:T(8,128)S(1)}, f32[20,2,32,128]{3,2,1,0:T(8,128)S(1)}) custom-call(f32[32,16,128]{2,1,0:T(8,128)S(1)} %copy-done, f32[32,8,128]{2,1,0:T(8,128)S(1)} %collective-permute-done.ya_ref, f32[32,8,128]{2,1,0:T(8,128)S(1)} %collective-permute-done.1.yb_ref, ...), custom_call_target="tpu_custom_call" | custom-call | flops 20000000 | bytes 2000000 | tf_op jit(solution)/shard_map/pallas_call | solution.py:872
  29.8 2.1 %collective-permute-done.9.refs_3_ = f32[4,9,8,128]{3,2,1,0:T(8,128)S(1)} collective-permute-done((f32[4,9,8,128]{3,2,1,0:T(8,128)S(1)}, f32[4,9,8,128]{3,2,1,0:T(8,128)S(1)}, u32[]{:S(2)}, u32[]{:S(2)}) %collective-permute-start.9) | collective-permute-done | bytes 147488 | tf_op jit(solution)/shard_map/ppermute | solution.py:870
  31.9 0.0 collective-permute-start.14
  31.9 1.4 %collective-permute-done.7.refs_1_ = f32[4,9,8,128]{3,2,1,0:T(8,128)S(1)} collective-permute-done((f32[4,9,8,128]{3,2,1,0:T(8,128)S(1)}, f32[4,9,8,128]{3,2,1,0:T(8,128)S(1)}, u32[]{:S(2)}, u32[]{:S(2)}) %collective-permute-start.7) | collective-permute-done | bytes 147488 | tf_op jit(solution)/shard_map/ppermute | solution.py:868
  33.4 0.0 collective-permute-start.12
  33.4 0.1 collective-permute-done.8.refs_2_
  33.5 0.4 collective-permute-start.13
  33.9 0.0 collective-permute-done.11.refs_4_
  33.9 0.0 collective-permute-done.14.refs_7_
  33.9 0.9 %collective-permute-done.12.refs_5_ = f32[4,9,8,128]{3,2,1,0:T(8,128)S(1)} collective-permute-done((f32[4,9,8,128]{3,2,1,0:T(8,128)S(1)}, f32[4,9,8,128]{3,2,1,0:T(8,128)S(1)}, u32[]{:S(2)}, u32[]{:S(2)}) %collective-permute-start.12) | collective-permute-done | bytes 147488 | tf_op jit(solution)/shard_map/ppermute | solution.py:880
  34.7 0.2 collective-permute-done.13.refs_6_
  34.9 0.0 copy-done.1
  34.9 6.3 %shard_map.32 = f32[32,16,128]{2,1,0:T(8,128)} custom-call(f32[4,9,8,128]{3,2,1,0:T(8,128)S(1)} %shard_map.30.after_ref.refs_0_, f32[4,9,8,128]{3,2,1,0:T(8,128)S(1)} %collective-permute-done.7.refs_1_, f32[4,9,8,128]{3,2,1,0:T(8,128)S(1)} %collective-permute-done.8.refs_2_, f32[4,9,8,128]{3,2,1,0:T(8,128)S(1)} %collective-permute-done.9.refs_3_, ...), custom_call_target="tpu_custom_call" | custom-call | tf_op jit(solution)/shard_map/pallas_call | solution.py:890
  (1 shorter events, 0.0 us)
Async XLA Ops:
  0.0 9.1 %copy-start = (f32[32,16,128]{2,1,0:T(8,128)S(1)}, f32[32,16,128]{2,1,0:T(8,128)}, u32[]{:S(2)}) copy-start(f32[32,16,128]{2,1,0:T(8,128)} %own_ref.5) | copy-start | bytes 786436
  1.0 6.6 %collective-permute-start = (f32[32,8,128]{2,1,0:T(8,128)S(1)}, f32[32,8,128]{2,1,0:T(8,128)S(1)}, u32[]{:S(2)}, u32[]{:S(2)}) collective-permute-start(f32[32,8,128]{2,1,0:T(8,128)S(1)} %get-tuple-element.28), channel_id=1, source_target_pairs={{0,4},{4,0},{8,12},{12,8},{1,5},{5,1},{9,13},{13,9},{2,6},{6,2},{1... | collective-permute-start | bytes 393224 | tf_op jit(solution)/shard_map/ppermute | solution.py:832
  4.2 5.0 %collective-permute-start.1 = (f32[32,8,128]{2,1,0:T(8,128)S(1)}, f32[32,8,128]{2,1,0:T(8,128)S(1)}, u32[]{:S(2)}, u32[]{:S(2)}) collective-permute-start(f32[32,8,128]{2,1,0:T(8,128)S(1)} %get-tuple-element.27), channel_id=1, source_target_pairs={{4,8},{8,4},{0,16},{12,28},{20,24},{24,20},{16,0},{28,12},{5,9},{9... | collective-permute-start | bytes 393224 | tf_op jit(solution)/shard_map/ppermute | solution.py:833
  9.5 1.7 %collective-permute-start.2 = (f32[2,32,128]{2,1,0:T(8,128)S(1)}, f32[2,32,128]{2,1,0:T(8,128)S(1)}, u32[]{:S(2)}, u32[]{:S(2)}) collective-permute-start(f32[2,32,128]{2,1,0:T(8,128)S(1)} %get-tuple-element.16), channel_id=1, source_target_pairs={{0,1},{1,0},{2,3},{3,2},{4,5},{5,4},{6,7},{7,6},{8,9},{9,8},{10,11... | collective-permute-start | bytes 98312 | tf_op jit(solution)/shard_map/ppermute | solution.py:841
  9.5 3.4 %collective-permute-start.3 = (f32[2,32,128]{2,1,0:T(8,128)S(1)}, f32[2,32,128]{2,1,0:T(8,128)S(1)}, u32[]{:S(2)}, u32[]{:S(2)}) collective-permute-start(f32[2,32,128]{2,1,0:T(8,128)S(1)} %get-tuple-element.17), channel_id=1, source_target_pairs={{1,2},{2,1},{0,3},{3,0},{5,6},{6,5},{4,7},{7,4},{9,10},{10,9},{8,1... | collective-permute-start | bytes 98312 | tf_op jit(solution)/shard_map/ppermute | solution.py:842
  14.6 6.0 %collective-permute-start.4 = (f32[9,8,128]{2,1,0:T(8,128)S(1)}, f32[9,8,128]{2,1,0:T(8,128)S(1)}, u32[]{:S(2)}, u32[]{:S(2)}) collective-permute-start(f32[9,8,128]{2,1,0:T(8,128)S(1)} %get-tuple-element.18.refs_0_), channel_id=1, source_target_pairs={{0,8},{4,12},{8,0},{12,4},{1,9},{5,13},{9,1},{13,5},{2,10},{6,14},... | collective-permute-start | bytes 110600 | tf_op jit(solution)/shard_map/ppermute | solution.py:857
  17.2 4.0 %collective-permute-start.5 = (f32[9,8,128]{2,1,0:T(8,128)S(1)}, f32[9,8,128]{2,1,0:T(8,128)S(1)}, u32[]{:S(2)}, u32[]{:S(2)}) collective-permute-start(f32[9,8,128]{2,1,0:T(8,128)S(1)} %get-tuple-element.18.refs_0_), channel_id=1, source_target_pairs={{0,2},{1,3},{2,0},{3,1},{4,6},{5,7},{6,4},{7,5},{8,10},{9,11},{10,... | collective-permute-start | bytes 110600 | tf_op jit(solution)/shard_map/ppermute | solution.py:858
  18.7 6.0 %collective-permute-start.6 = (f32[9,8,128]{2,1,0:T(8,128)S(1)}, f32[9,8,128]{2,1,0:T(8,128)S(1)}, u32[]{:S(2)}, u32[]{:S(2)}) collective-permute-start(f32[9,8,128]{2,1,0:T(8,128)S(1)} %get-tuple-element.18.refs_0_), channel_id=1, source_target_pairs={{0,10},{1,11},{2,8},{3,9},{4,14},{5,15},{6,12},{7,13},{8,2},{9,3},... | collective-permute-start | bytes 110600 | tf_op jit(solution)/shard_map/ppermute | solution.py:860
  19.0 9.3 %collective-permute-start.10 = (f32[9,32,128]{2,1,0:T(8,128)S(1)}, f32[9,32,128]{2,1,0:T(8,128)S(1)}, u32[]{:S(2)}, u32[]{:S(2)}) collective-permute-start(f32[9,32,128]{2,1,0:T(8,128)S(1)} %get-tuple-element.19), channel_id=1, source_target_pairs={{0,16},{16,0},{1,17},{17,1},{2,18},{18,2},{3,19},{19,3},{4,20},{20... | collective-permute-start | bytes 442376 | tf_op jit(solution)/shard_map/ppermute | solution.py:861
  24.8 10.2 %copy-start.1 = (f32[128,128]{1,0:T(8,128)S(1)}, f32[128,128]{1,0:T(8,128)}, u32[]{:S(2)}) copy-start(f32[128,128]{1,0:T(8,128)} %constant.26.clone.refs_11_) | copy-start | bytes 196612
  24.8 7.2 %collective-permute-start.9 = (f32[4,9,8,128]{3,2,1,0:T(8,128)S(1)}, f32[4,9,8,128]{3,2,1,0:T(8,128)S(1)}, u32[]{:S(2)}, u32[]{:S(2)}) collective-permute-start(f32[4,9,8,128]{3,2,1,0:T(8,128)S(1)} %shard_map.30.after_ref.refs_0_), channel_id=1, source_target_pairs={{0,20},{4,16},{8,28},{12,24},{16,4},{20,0},{24,12},{28,8},{1,21},{... | collective-permute-start | bytes 442376 | tf_op jit(solution)/shard_map/ppermute | solution.py:870
  26.0 7.4 %collective-permute-start.7 = (f32[4,9,8,128]{3,2,1,0:T(8,128)S(1)}, f32[4,9,8,128]{3,2,1,0:T(8,128)S(1)}, u32[]{:S(2)}, u32[]{:S(2)}) collective-permute-start(f32[4,9,8,128]{3,2,1,0:T(8,128)S(1)} %shard_map.30.after_ref.refs_0_), channel_id=1, source_target_pairs={{0,16},{16,0},{1,17},{17,1},{2,18},{18,2},{3,19},{19,3},{4,20},{20... | collective-permute-start | bytes 442376 | tf_op jit(solution)/shard_map/ppermute | solution.py:868
  26.5 7.0 %collective-permute-start.8 = (f32[4,9,8,128]{3,2,1,0:T(8,128)S(1)}, f32[4,9,8,128]{3,2,1,0:T(8,128)S(1)}, u32[]{:S(2)}, u32[]{:S(2)}) collective-permute-start(f32[4,9,8,128]{3,2,1,0:T(8,128)S(1)} %shard_map.30.after_ref.refs_0_), channel_id=1, source_target_pairs={{0,4},{4,0},{8,12},{12,8},{1,5},{5,1},{9,13},{13,9},{2,6},{6,2},{1... | collective-permute-start | bytes 442376 | tf_op jit(solution)/shard_map/ppermute | solution.py:869
  28.3 5.5 %collective-permute-start.11 = (f32[4,9,8,128]{3,2,1,0:T(8,128)S(1)}, f32[4,9,8,128]{3,2,1,0:T(8,128)S(1)}, u32[]{:S(2)}, u32[]{:S(2)}) collective-permute-start(f32[4,9,8,128]{3,2,1,0:T(8,128)S(1)} %shard_map.30.after_ref.refs_0_), channel_id=1, source_target_pairs={{0,1},{1,0},{2,3},{3,2},{4,5},{5,4},{6,7},{7,6},{8,9},{9,8},{10,11... | collective-permute-start | bytes 442376 | tf_op jit(solution)/shard_map/ppermute | solution.py:880
  31.9 1.9 %collective-permute-start.14 = (f32[4,9,8,128]{3,2,1,0:T(8,128)S(1)}, f32[4,9,8,128]{3,2,1,0:T(8,128)S(1)}, u32[]{:S(2)}, u32[]{:S(2)}) collective-permute-start(f32[4,9,8,128]{3,2,1,0:T(8,128)S(1)} %collective-permute-done.9.refs_3_), channel_id=1, source_target_pairs={{0,1},{1,0},{2,3},{3,2},{4,5},{5,4},{6,7},{7,6},{8,9},{9,8},{10,11... | collective-permute-start | bytes 442376 | tf_op jit(solution)/shard_map/ppermute | solution.py:880
  33.4 1.4 %collective-permute-start.12 = (f32[4,9,8,128]{3,2,1,0:T(8,128)S(1)}, f32[4,9,8,128]{3,2,1,0:T(8,128)S(1)}, u32[]{:S(2)}, u32[]{:S(2)}) collective-permute-start(f32[4,9,8,128]{3,2,1,0:T(8,128)S(1)} %collective-permute-done.7.refs_1_), channel_id=1, source_target_pairs={{0,1},{1,0},{2,3},{3,2},{4,5},{5,4},{6,7},{7,6},{8,9},{9,8},{10,11... | collective-permute-start | bytes 442376 | tf_op jit(solution)/shard_map/ppermute | solution.py:880
  33.5 1.5 %collective-permute-start.13 = (f32[4,9,8,128]{3,2,1,0:T(8,128)S(1)}, f32[4,9,8,128]{3,2,1,0:T(8,128)S(1)}, u32[]{:S(2)}, u32[]{:S(2)}) collective-permute-start(f32[4,9,8,128]{3,2,1,0:T(8,128)S(1)} %collective-permute-done.8.refs_2_), channel_id=1, source_target_pairs={{0,1},{1,0},{2,3},{3,2},{4,5},{5,4},{6,7},{7,6},{8,9},{9,8},{10,11... | collective-permute-start | bytes 442376 | tf_op jit(solution)/shard_map/ppermute | solution.py:880

commit v13 on v12

--- a/solution.py
+++ b/solution.py
@@ -490,8 +490,8 @@
 def solve_kernel(halo, *refs):
     gathered, refs = refs[:8], refs[8:]
     gr_ref, gb_ref, dark_ref, matrix_ref, out_ref = refs[:5]
-    fr1, fb1, red1, black1, rest1, tall_ref, red_ref, work_ref, passing = refs[5:14]
-    small = [refs[14 + 6 * i : 20 + 6 * i] for i in range(LEVELS - 4)]
+    fr1, fb1, red1, black1, rest1, tall_ref, red_ref, work_ref, passing, result_ref, sems = refs[5:16]
+    small = [refs[16 + 6 * i : 22 + 6 * i] for i in range(LEVELS - 4)]
     gx, gy, gz = (lax.axis_index(axis) for axis in ("gx", "gy", "gz"))
     weight_z = 1.0 + rsd_beta
     share = 1.0 / centre
@@ -785,21 +785,41 @@
     masks = block_mask((ny, nz), halo)
     ends = (gx == 0, gx == lax.axis_size("gx") - 1)
     beside_own = [*range(own), own, count - 1]
-    for sweep in range(2):
-        for at in range(count) if sweep == 0 else beside_own:
+
+    def red_half(slots):
+        for at in slots:
             totals = block_totals(work_ref, at, rows, own, odd, True, *ends)
             for c in range(2):
                 red_ref[at, c, body, :] = gr_ref[at, c] + masks[c] * totals[c]
-        for at in beside_own if sweep == 0 else range(own):
-            totals = block_totals(red_ref, at, rows, own, odd, False, *ends)
-            for c in range(2 if sweep == 0 else 1):
-                work_ref[at, c, body, :] = gb_ref[at, c] + masks[c] * totals[c]
-    inner = slice(PAD + halo, PAD + halo + ny)
-    odd = odd_of((ny, nz))
+
+    red_half(range(count))
+    for at in beside_own:
+        totals = block_totals(red_ref, at, rows, own, odd, False, *ends)
+        for c in range(2):
+            work_ref[at, c, body, :] = gb_ref[at, c] + masks[c] * totals[c]
+    red_half(beside_own)
+    inner = slice(halo, halo + ny)
+    odd_inner = odd_of((ny, nz))
+    groups = sems.shape[0]
+    size = nx // groups
+    copies = [
+        pltpu.make_async_copy(
+            result_ref.at[pl.ds(q * size, size)], out_ref.at[pl.ds(q * size, size)], sems.at[q]
+        )
+        for q in range(groups)
+    ]
     for at in range(own):
-        r, b = red_ref[at, 0, inner, :], work_ref[at, 0, inner, :]
-        out_ref[2 * at] = jnp.where(odd, b, r)
-        out_ref[2 * at + 1] = jnp.where(odd, r, b)
+        total = block_totals(red_ref, at, rows, own, odd, False, *ends)[0]
+        b = (gb_ref[at, 0] + masks[0] * total)[inner]
+        r = red_ref[at, 0, PAD + halo : PAD + halo + ny, :]
+        result_ref[2 * at] = jnp.where(odd_inner, b, r)
+        result_ref[2 * at + 1] = jnp.where(odd_inner, r, b)
+        done = (2 * at + 2) // size
+        if (2 * at + 2) % size == 0 and done > 1:
+            copies[done - 2].start()
+    copies[-1].start()
+    for copy in copies:
+        copy.wait()
 
 
 def vmem(number):
@@ -883,6 +903,7 @@
     room += [scratch(count1, 2, rows1 + 2 * PAD, LANES)] * 2
     room += [scratch(count1, rows1, LANES), scratch(planes // 2, rows // 2, 2 * LANES)]
     room += [scratch(*padded)] * 2 + [scratch(count1 // 2, 1, rows2 + 2 * PAD, LANES)]
+    room += [scratch(nx, ny, nz), pltpu.SemaphoreType.DMA((4,))]
     for count in small_shapes(whole):
         room += [scratch(count, rows2, LANES)] * 2
         room += [scratch(count, 1, rows2 + 2 * PAD, LANES)] * 2
@@ -890,7 +911,7 @@
     return pl.pallas_call(
         functools.partial(solve_kernel, halo),
         out_shape=struct(nx, ny, nz),
-        in_specs=vmem(12), out_specs=pl.BlockSpec(memory_space=pltpu.VMEM),
+        in_specs=vmem(12), out_specs=pl.BlockSpec(memory_space=pl.ANY),
         compiler_params=params(16), scratch_shapes=room,
     )(*second, *third, gr, gb, black, cycle_matrix(whole))
 

time: 41.4 us -> 41.2 us (level)
  no operation moved by 1% of the time
where the time goes in v13:
time: 41.2 us; the launch traced here: 41.1 us
  starting transfers between devices  16.2 us (39%)
  waiting for transfers between devices  14.2 us (34%)
  Pallas kernels  9.58 us (23%)
  local copies, waits for them, and re-layouts  1.04 us (3%)
    pallas_call x1, Pallas kernels, block_cycle(): pl.pallas_call(functools.partial(solve_kernel, halo), out_shape=struct(nx...  6.13 us
    ppermute x1, waiting for transfers between devices, block_cycle(): first.append(lax.ppermute(send, ('gy', 'gz'), swaps))  3.57 us
    ppermute x1, starting transfers between devices, block_cycle(): ya = lax.ppermute(ya, 'gy', pairs(count_y, 0))  3.12 us
    ppermute x1, starting transfers between devices, block_cycle(): first.append(lax.ppermute(send, 'gy', flips(count_y, 2)))  2.65 us
    ppermute x1, waiting for transfers between devices, block_cycle(): lax.ppermute(block, ('gx', 'gy'), flips(count_x * count_y, count_y + 1))  2.1 us
    ppermute x1, waiting for transfers between devices, block_cycle(): ya = lax.ppermute(ya, 'gy', pairs(count_y, 0))  1.98 us
    ppermute x1, starting transfers between devices, block_cycle(): lax.ppermute(block, 'gy', flips(count_y, 1))  1.83 us
    ppermute x1, waiting for transfers between devices, block_cycle(): lax.ppermute(zb, 'gz', pairs(count_z, 1) + [(0, count_z - 1), (count_z -...  1.81 us
  transfers between devices with their start and end apart: 15, of which 10 were waited for; matrix products, arithmetic and copies ran while one was open for 0% of the time, Pallas kernels for 4%

profile of v13, /device:TPU:0, one launch (start us, length us, event | category | flops | bytes accessed | tf_op | source)
XLA Modules:
  0.0 41.1 jit_solution(17951229242154995065)
XLA Ops:
  0.0 0.0 copy-start
  0.0 1.0 %constant_dynamic-slice_fusion = (f32[32,8,128]{2,1,0:T(8,128)S(1)}, f32[32,8,128]{2,1,0:T(8,128)S(1)}) fusion(f32[32,16,128]{2,1,0:T(8,128)} %own_ref.5, s32[]{:T(128)S(6)} %select_n.18, s32[]{:T(128)S(6)} %select_n.17), kind=kLoop, calls=%fused_computation | loop fusion | bytes 524296 | tf_op jit(solution)/shard_map/dynamic_slice | solution.py:851
  1.0 3.1 %collective-permute-start = (f32[32,8,128]{2,1,0:T(8,128)S(1)}, f32[32,8,128]{2,1,0:T(8,128)S(1)}, u32[]{:S(2)}, u32[]{:S(2)}) collective-permute-start(f32[32,8,128]{2,1,0:T(8,128)S(1)} %get-tuple-element.28), channel_id=1, source_target_pairs={{0,4},{4,0},{8,12},{12,8},{1,5},{5,1},{9,13},{13,9},{2,6},{6,2},{1... | collective-permute-start | bytes 393224 | tf_op jit(solution)/shard_map/ppermute | solution.py:852
  4.2 1.5 %collective-permute-start.1 = (f32[32,8,128]{2,1,0:T(8,128)S(1)}, f32[32,8,128]{2,1,0:T(8,128)S(1)}, u32[]{:S(2)}, u32[]{:S(2)}) collective-permute-start(f32[32,8,128]{2,1,0:T(8,128)S(1)} %get-tuple-element.27), channel_id=1, source_target_pairs={{4,8},{8,4},{0,16},{12,28},{20,24},{24,20},{16,0},{28,12},{5,9},{9... | collective-permute-start | bytes 393224 | tf_op jit(solution)/shard_map/ppermute | solution.py:853
  5.7 2.0 %collective-permute-done.ya_ref = f32[32,8,128]{2,1,0:T(8,128)S(1)} collective-permute-done((f32[32,8,128]{2,1,0:T(8,128)S(1)}, f32[32,8,128]{2,1,0:T(8,128)S(1)}, u32[]{:S(2)}, u32[]{:S(2)}) %collective-permute-start) | collective-permute-done | bytes 131104 | tf_op jit(solution)/shard_map/ppermute | solution.py:852
  7.6 1.5 %collective-permute-done.1.yb_ref = f32[32,8,128]{2,1,0:T(8,128)S(1)} collective-permute-done((f32[32,8,128]{2,1,0:T(8,128)S(1)}, f32[32,8,128]{2,1,0:T(8,128)S(1)}, u32[]{:S(2)}, u32[]{:S(2)}) %collective-permute-start.1) | collective-permute-done | bytes 131104 | tf_op jit(solution)/shard_map/ppermute | solution.py:853
  9.1 0.0 copy-done
  9.1 0.3 shard_map.28
  9.5 0.1 collective-permute-start.2
  9.5 1.6 %collective-permute-start.3 = (f32[2,32,128]{2,1,0:T(8,128)S(1)}, f32[2,32,128]{2,1,0:T(8,128)S(1)}, u32[]{:S(2)}, u32[]{:S(2)}) collective-permute-start(f32[2,32,128]{2,1,0:T(8,128)S(1)} %get-tuple-element.17), channel_id=1, source_target_pairs={{1,2},{2,1},{0,3},{3,0},{5,6},{6,5},{4,7},{7,4},{9,10},{10,9},{8,1... | collective-permute-start | bytes 98312 | tf_op jit(solution)/shard_map/ppermute | solution.py:862
  11.1 0.0 collective-permute-done.2.za_ref
  11.1 1.8 %collective-permute-done.3.zb_ref = f32[2,32,128]{2,1,0:T(8,128)S(1)} collective-permute-done((f32[2,32,128]{2,1,0:T(8,128)S(1)}, f32[2,32,128]{2,1,0:T(8,128)S(1)}, u32[]{:S(2)}, u32[]{:S(2)}) %collective-permute-start.3) | collective-permute-done | bytes 32800 | tf_op jit(solution)/shard_map/ppermute | solution.py:862
  12.9 1.6 %shard_map.29 = (f32[9,8,128]{2,1,0:T(8,128)S(1)}, f32[9,32,128]{2,1,0:T(8,128)S(1)}) custom-call(f32[32,16,128]{2,1,0:T(8,128)S(1)} %copy-done, f32[32,8,128]{2,1,0:T(8,128)S(1)} %collective-permute-done.ya_ref, f32[32,8,128]{2,1,0:T(8,128)S(1)} %collective-permute-done.1.yb_ref, f32[2,32,128]{2,1,0:T(8,128)S(1)} %collective-permute-done.2.za_ref, ...), custom_call_target="tpu_custom_call" | custom-call | tf_op jit(solution)/shard_map/pallas_call | solution.py:864
  14.6 2.7 %collective-permute-start.4 = (f32[9,8,128]{2,1,0:T(8,128)S(1)}, f32[9,8,128]{2,1,0:T(8,128)S(1)}, u32[]{:S(2)}, u32[]{:S(2)}) collective-permute-start(f32[9,8,128]{2,1,0:T(8,128)S(1)} %get-tuple-element.18.refs_0_), channel_id=1, source_target_pairs={{0,8},{4,12},{8,0},{12,4},{1,9},{5,13},{9,1},{13,5},{2,10},{6,14},... | collective-permute-start | bytes 110600 | tf_op jit(solution)/shard_map/ppermute | solution.py:877
  17.2 1.5 %collective-permute-start.5 = (f32[9,8,128]{2,1,0:T(8,128)S(1)}, f32[9,8,128]{2,1,0:T(8,128)S(1)}, u32[]{:S(2)}, u32[]{:S(2)}) collective-permute-start(f32[9,8,128]{2,1,0:T(8,128)S(1)} %get-tuple-element.18.refs_0_), channel_id=1, source_target_pairs={{0,2},{1,3},{2,0},{3,1},{4,6},{5,7},{6,4},{7,5},{8,10},{9,11},{10,... | collective-permute-start | bytes 110600 | tf_op jit(solution)/shard_map/ppermute | solution.py:878
  18.7 0.3 collective-permute-start.6
  19.0 1.5 %collective-permute-start.10 = (f32[9,32,128]{2,1,0:T(8,128)S(1)}, f32[9,32,128]{2,1,0:T(8,128)S(1)}, u32[]{:S(2)}, u32[]{:S(2)}) collective-permute-start(f32[9,32,128]{2,1,0:T(8,128)S(1)} %get-tuple-element.19), channel_id=1, source_target_pairs={{0,16},{16,0},{1,17},{17,1},{2,18},{18,2},{3,19},{19,3},{4,20},{20... | collective-permute-start | bytes 442376 | tf_op jit(solution)/shard_map/ppermute | solution.py:881
  20.5 0.0 collective-permute-done.4.refs_1_
  20.5 0.6 %collective-permute-done.5.refs_2_ = f32[9,8,128]{2,1,0:T(8,128)S(1)} collective-permute-done((f32[9,8,128]{2,1,0:T(8,128)S(1)}, f32[9,8,128]{2,1,0:T(8,128)S(1)}, u32[]{:S(2)}, u32[]{:S(2)}) %collective-permute-start.5) | collective-permute-done | bytes 36896 | tf_op jit(solution)/shard_map/ppermute | solution.py:878
  21.2 3.6 %collective-permute-done.6.refs_3_ = f32[9,8,128]{2,1,0:T(8,128)S(1)} collective-permute-done((f32[9,8,128]{2,1,0:T(8,128)S(1)}, f32[9,8,128]{2,1,0:T(8,128)S(1)}, u32[]{:S(2)}, u32[]{:S(2)}) %collective-permute-start.6) | collective-permute-done | bytes 36896 | tf_op jit(solution)/shard_map/ppermute | solution.py:880
  24.8 0.0 copy-start.1
  24.8 1.2 %collective-permute-start.9 = (f32[4,9,8,128]{3,2,1,0:T(8,128)S(1)}, f32[4,9,8,128]{3,2,1,0:T(8,128)S(1)}, u32[]{:S(2)}, u32[]{:S(2)}) collective-permute-start(f32[4,9,8,128]{3,2,1,0:T(8,128)S(1)} %shard_map.30.after_ref.refs_0_), channel_id=1, source_target_pairs={{0,20},{4,16},{8,28},{12,24},{16,4},{20,0},{24,12},{28,8},{1,21},{... | collective-permute-start | bytes 442376 | tf_op jit(solution)/shard_map/ppermute | solution.py:890
  26.0 0.5 %collective-permute-start.7 = (f32[4,9,8,128]{3,2,1,0:T(8,128)S(1)}, f32[4,9,8,128]{3,2,1,0:T(8,128)S(1)}, u32[]{:S(2)}, u32[]{:S(2)}) collective-permute-start(f32[4,9,8,128]{3,2,1,0:T(8,128)S(1)} %shard_map.30.after_ref.refs_0_), channel_id=1, source_target_pairs={{0,16},{16,0},{1,17},{17,1},{2,18},{18,2},{3,19},{19,3},{4,20},{20... | collective-permute-start | bytes 442376 | tf_op jit(solution)/shard_map/ppermute | solution.py:888
  26.5 1.8 %collective-permute-start.8 = (f32[4,9,8,128]{3,2,1,0:T(8,128)S(1)}, f32[4,9,8,128]{3,2,1,0:T(8,128)S(1)}, u32[]{:S(2)}, u32[]{:S(2)}) collective-permute-start(f32[4,9,8,128]{3,2,1,0:T(8,128)S(1)} %shard_map.30.after_ref.refs_0_), channel_id=1, source_target_pairs={{0,4},{4,0},{8,12},{12,8},{1,5},{5,1},{9,13},{13,9},{2,6},{6,2},{1... | collective-permute-start | bytes 442376 | tf_op jit(solution)/shard_map/ppermute | solution.py:889
  28.3 0.0 collective-permute-start.11
  28.3 0.0 collective-permute-done.10.face_ref
  28.3 1.5 %shard_map.31 = (f32[20,2,32,128]{3,2,1,0:T(8,128)S(1)}, f32[20,2,32,128]{3,2,1,0:T(8,128)S(1)}, f32[20,2,32,128]{3,2,1,0:T(8,128)S(1)}) custom-call(f32[32,16,128]{2,1,0:T(8,128)S(1)} %copy-done, f32[32,8,128]{2,1,0:T(8,128)S(1)} %collective-permute-done.ya_ref, f32[32,8,128]{2,1,0:T(8,128)S(1)} %collective-permute-done.1.yb_ref, ...), custom_call_target="tpu_custom_call" | custom-call | flops 20000000 | bytes 2000000 | tf_op jit(solution)/shard_map/pallas_call | solution.py:892
  29.8 2.1 %collective-permute-done.9.refs_3_ = f32[4,9,8,128]{3,2,1,0:T(8,128)S(1)} collective-permute-done((f32[4,9,8,128]{3,2,1,0:T(8,128)S(1)}, f32[4,9,8,128]{3,2,1,0:T(8,128)S(1)}, u32[]{:S(2)}, u32[]{:S(2)}) %collective-permute-start.9) | collective-permute-done | bytes 147488 | tf_op jit(solution)/shard_map/ppermute | solution.py:890
  31.9 0.0 collective-permute-start.14
  31.9 1.4 %collective-permute-done.7.refs_1_ = f32[4,9,8,128]{3,2,1,0:T(8,128)S(1)} collective-permute-done((f32[4,9,8,128]{3,2,1,0:T(8,128)S(1)}, f32[4,9,8,128]{3,2,1,0:T(8,128)S(1)}, u32[]{:S(2)}, u32[]{:S(2)}) %collective-permute-start.7) | collective-permute-done | bytes 147488 | tf_op jit(solution)/shard_map/ppermute | solution.py:888
  33.4 0.0 collective-permute-start.12
  33.4 0.1 collective-permute-done.8.refs_2_
  33.5 0.4 collective-permute-start.13
  33.9 0.0 collective-permute-done.11.refs_4_
  33.9 0.0 collective-permute-done.14.refs_7_
  33.9 0.9 %collective-permute-done.12.refs_5_ = f32[4,9,8,128]{3,2,1,0:T(8,128)S(1)} collective-permute-done((f32[4,9,8,128]{3,2,1,0:T(8,128)S(1)}, f32[4,9,8,128]{3,2,1,0:T(8,128)S(1)}, u32[]{:S(2)}, u32[]{:S(2)}) %collective-permute-start.12) | collective-permute-done | bytes 147488 | tf_op jit(solution)/shard_map/ppermute | solution.py:900
  34.7 0.2 collective-permute-done.13.refs_6_
  34.9 0.0 copy-done.1
  34.9 6.1 %shard_map.32 = f32[32,16,128]{2,1,0:T(8,128)} custom-call(f32[4,9,8,128]{3,2,1,0:T(8,128)S(1)} %shard_map.30.after_ref.refs_0_, f32[4,9,8,128]{3,2,1,0:T(8,128)S(1)} %collective-permute-done.7.refs_1_, f32[4,9,8,128]{3,2,1,0:T(8,128)S(1)} %collective-permute-done.8.refs_2_, f32[4,9,8,128]{3,2,1,0:T(8,128)S(1)} %collective-permute-done.9.refs_3_, ...), custom_call_target="tpu_custom_call" | custom-call | tf_op jit(solution)/shard_map/pallas_call | solution.py:911
  (1 shorter events, 0.0 us)
Async XLA Ops:
  0.0 9.1 %copy-start = (f32[32,16,128]{2,1,0:T(8,128)S(1)}, f32[32,16,128]{2,1,0:T(8,128)}, u32[]{:S(2)}) copy-start(f32[32,16,128]{2,1,0:T(8,128)} %own_ref.5) | copy-start | bytes 786436
  1.0 6.6 %collective-permute-start = (f32[32,8,128]{2,1,0:T(8,128)S(1)}, f32[32,8,128]{2,1,0:T(8,128)S(1)}, u32[]{:S(2)}, u32[]{:S(2)}) collective-permute-start(f32[32,8,128]{2,1,0:T(8,128)S(1)} %get-tuple-element.28), channel_id=1, source_target_pairs={{0,4},{4,0},{8,12},{12,8},{1,5},{5,1},{9,13},{13,9},{2,6},{6,2},{1... | collective-permute-start | bytes 393224 | tf_op jit(solution)/shard_map/ppermute | solution.py:852
  4.2 5.0 %collective-permute-start.1 = (f32[32,8,128]{2,1,0:T(8,128)S(1)}, f32[32,8,128]{2,1,0:T(8,128)S(1)}, u32[]{:S(2)}, u32[]{:S(2)}) collective-permute-start(f32[32,8,128]{2,1,0:T(8,128)S(1)} %get-tuple-element.27), channel_id=1, source_target_pairs={{4,8},{8,4},{0,16},{12,28},{20,24},{24,20},{16,0},{28,12},{5,9},{9... | collective-permute-start | bytes 393224 | tf_op jit(solution)/shard_map/ppermute | solution.py:853
  9.5 1.7 %collective-permute-start.2 = (f32[2,32,128]{2,1,0:T(8,128)S(1)}, f32[2,32,128]{2,1,0:T(8,128)S(1)}, u32[]{:S(2)}, u32[]{:S(2)}) collective-permute-start(f32[2,32,128]{2,1,0:T(8,128)S(1)} %get-tuple-element.16), channel_id=1, source_target_pairs={{0,1},{1,0},{2,3},{3,2},{4,5},{5,4},{6,7},{7,6},{8,9},{9,8},{10,11... | collective-permute-start | bytes 98312 | tf_op jit(solution)/shard_map/ppermute | solution.py:861
  9.5 3.4 %collective-permute-start.3 = (f32[2,32,128]{2,1,0:T(8,128)S(1)}, f32[2,32,128]{2,1,0:T(8,128)S(1)}, u32[]{:S(2)}, u32[]{:S(2)}) collective-permute-start(f32[2,32,128]{2,1,0:T(8,128)S(1)} %get-tuple-element.17), channel_id=1, source_target_pairs={{1,2},{2,1},{0,3},{3,0},{5,6},{6,5},{4,7},{7,4},{9,10},{10,9},{8,1... | collective-permute-start | bytes 98312 | tf_op jit(solution)/shard_map/ppermute | solution.py:862
  14.6 6.0 %collective-permute-start.4 = (f32[9,8,128]{2,1,0:T(8,128)S(1)}, f32[9,8,128]{2,1,0:T(8,128)S(1)}, u32[]{:S(2)}, u32[]{:S(2)}) collective-permute-start(f32[9,8,128]{2,1,0:T(8,128)S(1)} %get-tuple-element.18.refs_0_), channel_id=1, source_target_pairs={{0,8},{4,12},{8,0},{12,4},{1,9},{5,13},{9,1},{13,5},{2,10},{6,14},... | collective-permute-start | bytes 110600 | tf_op jit(solution)/shard_map/ppermute | solution.py:877
  17.2 4.0 %collective-permute-start.5 = (f32[9,8,128]{2,1,0:T(8,128)S(1)}, f32[9,8,128]{2,1,0:T(8,128)S(1)}, u32[]{:S(2)}, u32[]{:S(2)}) collective-permute-start(f32[9,8,128]{2,1,0:T(8,128)S(1)} %get-tuple-element.18.refs_0_), channel_id=1, source_target_pairs={{0,2},{1,3},{2,0},{3,1},{4,6},{5,7},{6,4},{7,5},{8,10},{9,11},{10,... | collective-permute-start | bytes 110600 | tf_op jit(solution)/shard_map/ppermute | solution.py:878
  18.7 6.0 %collective-permute-start.6 = (f32[9,8,128]{2,1,0:T(8,128)S(1)}, f32[9,8,128]{2,1,0:T(8,128)S(1)}, u32[]{:S(2)}, u32[]{:S(2)}) collective-permute-start(f32[9,8,128]{2,1,0:T(8,128)S(1)} %get-tuple-element.18.refs_0_), channel_id=1, source_target_pairs={{0,10},{1,11},{2,8},{3,9},{4,14},{5,15},{6,12},{7,13},{8,2},{9,3},... | collective-permute-start | bytes 110600 | tf_op jit(solution)/shard_map/ppermute | solution.py:880
  19.0 9.3 %collective-permute-start.10 = (f32[9,32,128]{2,1,0:T(8,128)S(1)}, f32[9,32,128]{2,1,0:T(8,128)S(1)}, u32[]{:S(2)}, u32[]{:S(2)}) collective-permute-start(f32[9,32,128]{2,1,0:T(8,128)S(1)} %get-tuple-element.19), channel_id=1, source_target_pairs={{0,16},{16,0},{1,17},{17,1},{2,18},{18,2},{3,19},{19,3},{4,20},{20... | collective-permute-start | bytes 442376 | tf_op jit(solution)/shard_map/ppermute | solution.py:881
  24.8 10.2 %copy-start.1 = (f32[128,128]{1,0:T(8,128)S(1)}, f32[128,128]{1,0:T(8,128)}, u32[]{:S(2)}) copy-start(f32[128,128]{1,0:T(8,128)} %constant.26.clone.refs_11_) | copy-start | bytes 196612
  24.8 7.2 %collective-permute-start.9 = (f32[4,9,8,128]{3,2,1,0:T(8,128)S(1)}, f32[4,9,8,128]{3,2,1,0:T(8,128)S(1)}, u32[]{:S(2)}, u32[]{:S(2)}) collective-permute-start(f32[4,9,8,128]{3,2,1,0:T(8,128)S(1)} %shard_map.30.after_ref.refs_0_), channel_id=1, source_target_pairs={{0,20},{4,16},{8,28},{12,24},{16,4},{20,0},{24,12},{28,8},{1,21},{... | collective-permute-start | bytes 442376 | tf_op jit(solution)/shard_map/ppermute | solution.py:890
  26.0 7.4 %collective-permute-start.7 = (f32[4,9,8,128]{3,2,1,0:T(8,128)S(1)}, f32[4,9,8,128]{3,2,1,0:T(8,128)S(1)}, u32[]{:S(2)}, u32[]{:S(2)}) collective-permute-start(f32[4,9,8,128]{3,2,1,0:T(8,128)S(1)} %shard_map.30.after_ref.refs_0_), channel_id=1, source_target_pairs={{0,16},{16,0},{1,17},{17,1},{2,18},{18,2},{3,19},{19,3},{4,20},{20... | collective-permute-start | bytes 442376 | tf_op jit(solution)/shard_map/ppermute | solution.py:888
  26.5 7.0 %collective-permute-start.8 = (f32[4,9,8,128]{3,2,1,0:T(8,128)S(1)}, f32[4,9,8,128]{3,2,1,0:T(8,128)S(1)}, u32[]{:S(2)}, u32[]{:S(2)}) collective-permute-start(f32[4,9,8,128]{3,2,1,0:T(8,128)S(1)} %shard_map.30.after_ref.refs_0_), channel_id=1, source_target_pairs={{0,4},{4,0},{8,12},{12,8},{1,5},{5,1},{9,13},{13,9},{2,6},{6,2},{1... | collective-permute-start | bytes 442376 | tf_op jit(solution)/shard_map/ppermute | solution.py:889
  28.3 5.5 %collective-permute-start.11 = (f32[4,9,8,128]{3,2,1,0:T(8,128)S(1)}, f32[4,9,8,128]{3,2,1,0:T(8,128)S(1)}, u32[]{:S(2)}, u32[]{:S(2)}) collective-permute-start(f32[4,9,8,128]{3,2,1,0:T(8,128)S(1)} %shard_map.30.after_ref.refs_0_), channel_id=1, source_target_pairs={{0,1},{1,0},{2,3},{3,2},{4,5},{5,4},{6,7},{7,6},{8,9},{9,8},{10,11... | collective-permute-start | bytes 442376 | tf_op jit(solution)/shard_map/ppermute | solution.py:900
  31.9 1.9 %collective-permute-start.14 = (f32[4,9,8,128]{3,2,1,0:T(8,128)S(1)}, f32[4,9,8,128]{3,2,1,0:T(8,128)S(1)}, u32[]{:S(2)}, u32[]{:S(2)}) collective-permute-start(f32[4,9,8,128]{3,2,1,0:T(8,128)S(1)} %collective-permute-done.9.refs_3_), channel_id=1, source_target_pairs={{0,1},{1,0},{2,3},{3,2},{4,5},{5,4},{6,7},{7,6},{8,9},{9,8},{10,11... | collective-permute-start | bytes 442376 | tf_op jit(solution)/shard_map/ppermute | solution.py:900
  33.4 1.4 %collective-permute-start.12 = (f32[4,9,8,128]{3,2,1,0:T(8,128)S(1)}, f32[4,9,8,128]{3,2,1,0:T(8,128)S(1)}, u32[]{:S(2)}, u32[]{:S(2)}) collective-permute-start(f32[4,9,8,128]{3,2,1,0:T(8,128)S(1)} %collective-permute-done.7.refs_1_), channel_id=1, source_target_pairs={{0,1},{1,0},{2,3},{3,2},{4,5},{5,4},{6,7},{7,6},{8,9},{9,8},{10,11... | collective-permute-start | bytes 442376 | tf_op jit(solution)/shard_map/ppermute | solution.py:900
  33.5 1.5 %collective-permute-start.13 = (f32[4,9,8,128]{3,2,1,0:T(8,128)S(1)}, f32[4,9,8,128]{3,2,1,0:T(8,128)S(1)}, u32[]{:S(2)}, u32[]{:S(2)}) collective-permute-start(f32[4,9,8,128]{3,2,1,0:T(8,128)S(1)} %collective-permute-done.8.refs_2_), channel_id=1, source_target_pairs={{0,1},{1,0},{2,3},{3,2},{4,5},{5,4},{6,7},{7,6},{8,9},{9,8},{10,11... | collective-permute-start | bytes 442376 | tf_op jit(solution)/shard_map/ppermute | solution.py:900

commit v14 on v13

--- a/solution.py
+++ b/solution.py
@@ -490,8 +490,8 @@
 def solve_kernel(halo, *refs):
     gathered, refs = refs[:8], refs[8:]
     gr_ref, gb_ref, dark_ref, matrix_ref, out_ref = refs[:5]
-    fr1, fb1, red1, black1, rest1, tall_ref, red_ref, work_ref, passing, result_ref, sems = refs[5:16]
-    small = [refs[16 + 6 * i : 22 + 6 * i] for i in range(LEVELS - 4)]
+    fr1, fb1, red1, black1, rest1, tall_ref, red_ref, work_ref, passing = refs[5:14]
+    small = [refs[14 + 6 * i : 20 + 6 * i] for i in range(LEVELS - 4)]
     gx, gy, gz = (lax.axis_index(axis) for axis in ("gx", "gy", "gz"))
     weight_z = 1.0 + rsd_beta
     share = 1.0 / centre
@@ -800,26 +800,12 @@
     red_half(beside_own)
     inner = slice(halo, halo + ny)
     odd_inner = odd_of((ny, nz))
-    groups = sems.shape[0]
-    size = nx // groups
-    copies = [
-        pltpu.make_async_copy(
-            result_ref.at[pl.ds(q * size, size)], out_ref.at[pl.ds(q * size, size)], sems.at[q]
-        )
-        for q in range(groups)
-    ]
     for at in range(own):
         total = block_totals(red_ref, at, rows, own, odd, False, *ends)[0]
         b = (gb_ref[at, 0] + masks[0] * total)[inner]
         r = red_ref[at, 0, PAD + halo : PAD + halo + ny, :]
-        result_ref[2 * at] = jnp.where(odd_inner, b, r)
-        result_ref[2 * at + 1] = jnp.where(odd_inner, r, b)
-        done = (2 * at + 2) // size
-        if (2 * at + 2) % size == 0 and done > 1:
-            copies[done - 2].start()
-    copies[-1].start()
-    for copy in copies:
-        copy.wait()
+        out_ref[2 * at] = jnp.where(odd_inner, b, r)
+        out_ref[2 * at + 1] = jnp.where(odd_inner, r, b)
 
 
 def vmem(number):
@@ -903,7 +889,6 @@
     room += [scratch(count1, 2, rows1 + 2 * PAD, LANES)] * 2
     room += [scratch(count1, rows1, LANES), scratch(planes // 2, rows // 2, 2 * LANES)]
     room += [scratch(*padded)] * 2 + [scratch(count1 // 2, 1, rows2 + 2 * PAD, LANES)]
-    room += [scratch(nx, ny, nz), pltpu.SemaphoreType.DMA((4,))]
     for count in small_shapes(whole):
         room += [scratch(count, rows2, LANES)] * 2
         room += [scratch(count, 1, rows2 + 2 * PAD, LANES)] * 2
@@ -911,7 +896,7 @@
     return pl.pallas_call(
         functools.partial(solve_kernel, halo),
         out_shape=struct(nx, ny, nz),
-        in_specs=vmem(12), out_specs=pl.BlockSpec(memory_space=pl.ANY),
+        in_specs=vmem(12), out_specs=pl.BlockSpec(memory_space=pltpu.VMEM),
         compiler_params=params(16), scratch_shapes=room,
     )(*second, *third, gr, gb, black, cycle_matrix(whole))
 

time: 41.2 us -> 41.2 us (level)
  no operation moved by 1% of the time
where the time goes in v14:
time: 41.2 us; the launch traced here: 41.1 us
  starting transfers between devices  16.2 us (39%)
  waiting for transfers between devices  14.2 us (34%)
  Pallas kernels  9.6 us (23%)
  local copies, waits for them, and re-layouts  1.04 us (3%)
    pallas_call x1, Pallas kernels, block_cycle(): pl.pallas_call(functools.partial(solve_kernel, halo), out_shape=struct(nx...  6.14 us
    ppermute x1, waiting for transfers between devices, block_cycle(): first.append(lax.ppermute(send, ('gy', 'gz'), swaps))  3.57 us
    ppermute x1, starting transfers between devices, block_cycle(): ya = lax.ppermute(ya, 'gy', pairs(count_y, 0))  3.12 us
    ppermute x1, starting transfers between devices, block_cycle(): first.append(lax.ppermute(send, 'gy', flips(count_y, 2)))  2.65 us
    ppermute x1, waiting for transfers between devices, block_cycle(): lax.ppermute(block, ('gx', 'gy'), flips(count_x * count_y, count_y + 1))  2.1 us
    ppermute x1, waiting for transfers between devices, block_cycle(): ya = lax.ppermute(ya, 'gy', pairs(count_y, 0))  1.98 us
    ppermute x1, starting transfers between devices, block_cycle(): lax.ppermute(block, 'gy', flips(count_y, 1))  1.83 us
    ppermute x1, waiting for transfers between devices, block_cycle(): lax.ppermute(zb, 'gz', pairs(count_z, 1) + [(0, count_z - 1), (count_z -...  1.81 us
  transfers between devices with their start and end apart: 15, of which 10 were waited for; matrix products, arithmetic and copies ran while one was open for 0% of the time, Pallas kernels for 4%

profile of v14, /device:TPU:0, one launch (start us, length us, event | category | flops | bytes accessed | tf_op | source)
XLA Modules:
  0.0 41.1 jit_solution(1760454383661313866)
XLA Ops:
  0.0 0.0 copy-start
  0.0 1.0 %constant_dynamic-slice_fusion = (f32[32,8,128]{2,1,0:T(8,128)S(1)}, f32[32,8,128]{2,1,0:T(8,128)S(1)}) fusion(f32[32,16,128]{2,1,0:T(8,128)} %own_ref.5, s32[]{:T(128)S(6)} %select_n.18, s32[]{:T(128)S(6)} %select_n.17), kind=kLoop, calls=%fused_computation | loop fusion | bytes 524296 | tf_op jit(solution)/shard_map/dynamic_slice | solution.py:837
  1.0 3.1 %collective-permute-start = (f32[32,8,128]{2,1,0:T(8,128)S(1)}, f32[32,8,128]{2,1,0:T(8,128)S(1)}, u32[]{:S(2)}, u32[]{:S(2)}) collective-permute-start(f32[32,8,128]{2,1,0:T(8,128)S(1)} %get-tuple-element.28), channel_id=1, source_target_pairs={{0,4},{4,0},{8,12},{12,8},{1,5},{5,1},{9,13},{13,9},{2,6},{6,2},{1... | collective-permute-start | bytes 393224 | tf_op jit(solution)/shard_map/ppermute | solution.py:838
  4.2 1.5 %collective-permute-start.1 = (f32[32,8,128]{2,1,0:T(8,128)S(1)}, f32[32,8,128]{2,1,0:T(8,128)S(1)}, u32[]{:S(2)}, u32[]{:S(2)}) collective-permute-start(f32[32,8,128]{2,1,0:T(8,128)S(1)} %get-tuple-element.27), channel_id=1, source_target_pairs={{4,8},{8,4},{0,16},{12,28},{20,24},{24,20},{16,0},{28,12},{5,9},{9... | collective-permute-start | bytes 393224 | tf_op jit(solution)/shard_map/ppermute | solution.py:839
  5.7 2.0 %collective-permute-done.ya_ref = f32[32,8,128]{2,1,0:T(8,128)S(1)} collective-permute-done((f32[32,8,128]{2,1,0:T(8,128)S(1)}, f32[32,8,128]{2,1,0:T(8,128)S(1)}, u32[]{:S(2)}, u32[]{:S(2)}) %collective-permute-start) | collective-permute-done | bytes 131104 | tf_op jit(solution)/shard_map/ppermute | solution.py:838
  7.6 1.5 %collective-permute-done.1.yb_ref = f32[32,8,128]{2,1,0:T(8,128)S(1)} collective-permute-done((f32[32,8,128]{2,1,0:T(8,128)S(1)}, f32[32,8,128]{2,1,0:T(8,128)S(1)}, u32[]{:S(2)}, u32[]{:S(2)}) %collective-permute-start.1) | collective-permute-done | bytes 131104 | tf_op jit(solution)/shard_map/ppermute | solution.py:839
  9.1 0.0 copy-done
  9.1 0.3 shard_map.28
  9.5 0.1 collective-permute-start.2
  9.5 1.6 %collective-permute-start.3 = (f32[2,32,128]{2,1,0:T(8,128)S(1)}, f32[2,32,128]{2,1,0:T(8,128)S(1)}, u32[]{:S(2)}, u32[]{:S(2)}) collective-permute-start(f32[2,32,128]{2,1,0:T(8,128)S(1)} %get-tuple-element.17), channel_id=1, source_target_pairs={{1,2},{2,1},{0,3},{3,0},{5,6},{6,5},{4,7},{7,4},{9,10},{10,9},{8,1... | collective-permute-start | bytes 98312 | tf_op jit(solution)/shard_map/ppermute | solution.py:848
  11.1 0.0 collective-permute-done.2.za_ref
  11.1 1.8 %collective-permute-done.3.zb_ref = f32[2,32,128]{2,1,0:T(8,128)S(1)} collective-permute-done((f32[2,32,128]{2,1,0:T(8,128)S(1)}, f32[2,32,128]{2,1,0:T(8,128)S(1)}, u32[]{:S(2)}, u32[]{:S(2)}) %collective-permute-start.3) | collective-permute-done | bytes 32800 | tf_op jit(solution)/shard_map/ppermute | solution.py:848
  12.9 1.6 %shard_map.29 = (f32[9,8,128]{2,1,0:T(8,128)S(1)}, f32[9,32,128]{2,1,0:T(8,128)S(1)}) custom-call(f32[32,16,128]{2,1,0:T(8,128)S(1)} %copy-done, f32[32,8,128]{2,1,0:T(8,128)S(1)} %collective-permute-done.ya_ref, f32[32,8,128]{2,1,0:T(8,128)S(1)} %collective-permute-done.1.yb_ref, f32[2,32,128]{2,1,0:T(8,128)S(1)} %collective-permute-done.2.za_ref, ...), custom_call_target="tpu_custom_call" | custom-call | tf_op jit(solution)/shard_map/pallas_call | solution.py:850
  14.6 2.7 %collective-permute-start.4 = (f32[9,8,128]{2,1,0:T(8,128)S(1)}, f32[9,8,128]{2,1,0:T(8,128)S(1)}, u32[]{:S(2)}, u32[]{:S(2)}) collective-permute-start(f32[9,8,128]{2,1,0:T(8,128)S(1)} %get-tuple-element.18.refs_0_), channel_id=1, source_target_pairs={{0,8},{4,12},{8,0},{12,4},{1,9},{5,13},{9,1},{13,5},{2,10},{6,14},... | collective-permute-start | bytes 110600 | tf_op jit(solution)/shard_map/ppermute | solution.py:863
  17.2 1.5 %collective-permute-start.5 = (f32[9,8,128]{2,1,0:T(8,128)S(1)}, f32[9,8,128]{2,1,0:T(8,128)S(1)}, u32[]{:S(2)}, u32[]{:S(2)}) collective-permute-start(f32[9,8,128]{2,1,0:T(8,128)S(1)} %get-tuple-element.18.refs_0_), channel_id=1, source_target_pairs={{0,2},{1,3},{2,0},{3,1},{4,6},{5,7},{6,4},{7,5},{8,10},{9,11},{10,... | collective-permute-start | bytes 110600 | tf_op jit(solution)/shard_map/ppermute | solution.py:864
  18.7 0.3 collective-permute-start.6
  19.0 1.5 %collective-permute-start.10 = (f32[9,32,128]{2,1,0:T(8,128)S(1)}, f32[9,32,128]{2,1,0:T(8,128)S(1)}, u32[]{:S(2)}, u32[]{:S(2)}) collective-permute-start(f32[9,32,128]{2,1,0:T(8,128)S(1)} %get-tuple-element.19), channel_id=1, source_target_pairs={{0,16},{16,0},{1,17},{17,1},{2,18},{18,2},{3,19},{19,3},{4,20},{20... | collective-permute-start | bytes 442376 | tf_op jit(solution)/shard_map/ppermute | solution.py:867
  20.5 0.0 collective-permute-done.4.refs_1_
  20.5 0.6 %collective-permute-done.5.refs_2_ = f32[9,8,128]{2,1,0:T(8,128)S(1)} collective-permute-done((f32[9,8,128]{2,1,0:T(8,128)S(1)}, f32[9,8,128]{2,1,0:T(8,128)S(1)}, u32[]{:S(2)}, u32[]{:S(2)}) %collective-permute-start.5) | collective-permute-done | bytes 36896 | tf_op jit(solution)/shard_map/ppermute | solution.py:864
  21.2 3.6 %collective-permute-done.6.refs_3_ = f32[9,8,128]{2,1,0:T(8,128)S(1)} collective-permute-done((f32[9,8,128]{2,1,0:T(8,128)S(1)}, f32[9,8,128]{2,1,0:T(8,128)S(1)}, u32[]{:S(2)}, u32[]{:S(2)}) %collective-permute-start.6) | collective-permute-done | bytes 36896 | tf_op jit(solution)/shard_map/ppermute | solution.py:866
  24.8 0.0 copy-start.1
  24.8 1.2 %collective-permute-start.9 = (f32[4,9,8,128]{3,2,1,0:T(8,128)S(1)}, f32[4,9,8,128]{3,2,1,0:T(8,128)S(1)}, u32[]{:S(2)}, u32[]{:S(2)}) collective-permute-start(f32[4,9,8,128]{3,2,1,0:T(8,128)S(1)} %shard_map.30.after_ref.refs_0_), channel_id=1, source_target_pairs={{0,20},{4,16},{8,28},{12,24},{16,4},{20,0},{24,12},{28,8},{1,21},{... | collective-permute-start | bytes 442376 | tf_op jit(solution)/shard_map/ppermute | solution.py:876
  26.0 0.5 %collective-permute-start.7 = (f32[4,9,8,128]{3,2,1,0:T(8,128)S(1)}, f32[4,9,8,128]{3,2,1,0:T(8,128)S(1)}, u32[]{:S(2)}, u32[]{:S(2)}) collective-permute-start(f32[4,9,8,128]{3,2,1,0:T(8,128)S(1)} %shard_map.30.after_ref.refs_0_), channel_id=1, source_target_pairs={{0,16},{16,0},{1,17},{17,1},{2,18},{18,2},{3,19},{19,3},{4,20},{20... | collective-permute-start | bytes 442376 | tf_op jit(solution)/shard_map/ppermute | solution.py:874
  26.5 1.8 %collective-permute-start.8 = (f32[4,9,8,128]{3,2,1,0:T(8,128)S(1)}, f32[4,9,8,128]{3,2,1,0:T(8,128)S(1)}, u32[]{:S(2)}, u32[]{:S(2)}) collective-permute-start(f32[4,9,8,128]{3,2,1,0:T(8,128)S(1)} %shard_map.30.after_ref.refs_0_), channel_id=1, source_target_pairs={{0,4},{4,0},{8,12},{12,8},{1,5},{5,1},{9,13},{13,9},{2,6},{6,2},{1... | collective-permute-start | bytes 442376 | tf_op jit(solution)/shard_map/ppermute | solution.py:875
  28.3 0.0 collective-permute-start.11
  28.3 0.0 collective-permute-done.10.face_ref
  28.3 1.5 %shard_map.31 = (f32[20,2,32,128]{3,2,1,0:T(8,128)S(1)}, f32[20,2,32,128]{3,2,1,0:T(8,128)S(1)}, f32[20,2,32,128]{3,2,1,0:T(8,128)S(1)}) custom-call(f32[32,16,128]{2,1,0:T(8,128)S(1)} %copy-done, f32[32,8,128]{2,1,0:T(8,128)S(1)} %collective-permute-done.ya_ref, f32[32,8,128]{2,1,0:T(8,128)S(1)} %collective-permute-done.1.yb_ref, ...), custom_call_target="tpu_custom_call" | custom-call | flops 20000000 | bytes 2000000 | tf_op jit(solution)/shard_map/pallas_call | solution.py:878
  29.8 2.1 %collective-permute-done.9.refs_3_ = f32[4,9,8,128]{3,2,1,0:T(8,128)S(1)} collective-permute-done((f32[4,9,8,128]{3,2,1,0:T(8,128)S(1)}, f32[4,9,8,128]{3,2,1,0:T(8,128)S(1)}, u32[]{:S(2)}, u32[]{:S(2)}) %collective-permute-start.9) | collective-permute-done | bytes 147488 | tf_op jit(solution)/shard_map/ppermute | solution.py:876
  31.9 0.0 collective-permute-start.14
  31.9 1.4 %collective-permute-done.7.refs_1_ = f32[4,9,8,128]{3,2,1,0:T(8,128)S(1)} collective-permute-done((f32[4,9,8,128]{3,2,1,0:T(8,128)S(1)}, f32[4,9,8,128]{3,2,1,0:T(8,128)S(1)}, u32[]{:S(2)}, u32[]{:S(2)}) %collective-permute-start.7) | collective-permute-done | bytes 147488 | tf_op jit(solution)/shard_map/ppermute | solution.py:874
  33.4 0.0 collective-permute-start.12
  33.4 0.1 collective-permute-done.8.refs_2_
  33.5 0.4 collective-permute-start.13
  33.9 0.0 collective-permute-done.11.refs_4_
  33.9 0.0 collective-permute-done.14.refs_7_
  33.9 0.9 %collective-permute-done.12.refs_5_ = f32[4,9,8,128]{3,2,1,0:T(8,128)S(1)} collective-permute-done((f32[4,9,8,128]{3,2,1,0:T(8,128)S(1)}, f32[4,9,8,128]{3,2,1,0:T(8,128)S(1)}, u32[]{:S(2)}, u32[]{:S(2)}) %collective-permute-start.12) | collective-permute-done | bytes 147488 | tf_op jit(solution)/shard_map/ppermute | solution.py:886
  34.7 0.2 collective-permute-done.13.refs_6_
  34.9 0.0 copy-done.1
  34.9 6.1 %shard_map.32 = f32[32,16,128]{2,1,0:T(8,128)} custom-call(f32[4,9,8,128]{3,2,1,0:T(8,128)S(1)} %shard_map.30.after_ref.refs_0_, f32[4,9,8,128]{3,2,1,0:T(8,128)S(1)} %collective-permute-done.7.refs_1_, f32[4,9,8,128]{3,2,1,0:T(8,128)S(1)} %collective-permute-done.8.refs_2_, f32[4,9,8,128]{3,2,1,0:T(8,128)S(1)} %collective-permute-done.9.refs_3_, ...), custom_call_target="tpu_custom_call" | custom-call | tf_op jit(solution)/shard_map/pallas_call | solution.py:896
  (1 shorter events, 0.0 us)
Async XLA Ops:
  0.0 9.1 %copy-start = (f32[32,16,128]{2,1,0:T(8,128)S(1)}, f32[32,16,128]{2,1,0:T(8,128)}, u32[]{:S(2)}) copy-start(f32[32,16,128]{2,1,0:T(8,128)} %own_ref.5) | copy-start | bytes 786436
  1.0 6.6 %collective-permute-start = (f32[32,8,128]{2,1,0:T(8,128)S(1)}, f32[32,8,128]{2,1,0:T(8,128)S(1)}, u32[]{:S(2)}, u32[]{:S(2)}) collective-permute-start(f32[32,8,128]{2,1,0:T(8,128)S(1)} %get-tuple-element.28), channel_id=1, source_target_pairs={{0,4},{4,0},{8,12},{12,8},{1,5},{5,1},{9,13},{13,9},{2,6},{6,2},{1... | collective-permute-start | bytes 393224 | tf_op jit(solution)/shard_map/ppermute | solution.py:838
  4.2 5.0 %collective-permute-start.1 = (f32[32,8,128]{2,1,0:T(8,128)S(1)}, f32[32,8,128]{2,1,0:T(8,128)S(1)}, u32[]{:S(2)}, u32[]{:S(2)}) collective-permute-start(f32[32,8,128]{2,1,0:T(8,128)S(1)} %get-tuple-element.27), channel_id=1, source_target_pairs={{4,8},{8,4},{0,16},{12,28},{20,24},{24,20},{16,0},{28,12},{5,9},{9... | collective-permute-start | bytes 393224 | tf_op jit(solution)/shard_map/ppermute | solution.py:839
  9.5 1.7 %collective-permute-start.2 = (f32[2,32,128]{2,1,0:T(8,128)S(1)}, f32[2,32,128]{2,1,0:T(8,128)S(1)}, u32[]{:S(2)}, u32[]{:S(2)}) collective-permute-start(f32[2,32,128]{2,1,0:T(8,128)S(1)} %get-tuple-element.16), channel_id=1, source_target_pairs={{0,1},{1,0},{2,3},{3,2},{4,5},{5,4},{6,7},{7,6},{8,9},{9,8},{10,11... | collective-permute-start | bytes 98312 | tf_op jit(solution)/shard_map/ppermute | solution.py:847
  9.5 3.4 %collective-permute-start.3 = (f32[2,32,128]{2,1,0:T(8,128)S(1)}, f32[2,32,128]{2,1,0:T(8,128)S(1)}, u32[]{:S(2)}, u32[]{:S(2)}) collective-permute-start(f32[2,32,128]{2,1,0:T(8,128)S(1)} %get-tuple-element.17), channel_id=1, source_target_pairs={{1,2},{2,1},{0,3},{3,0},{5,6},{6,5},{4,7},{7,4},{9,10},{10,9},{8,1... | collective-permute-start | bytes 98312 | tf_op jit(solution)/shard_map/ppermute | solution.py:848
  14.6 6.0 %collective-permute-start.4 = (f32[9,8,128]{2,1,0:T(8,128)S(1)}, f32[9,8,128]{2,1,0:T(8,128)S(1)}, u32[]{:S(2)}, u32[]{:S(2)}) collective-permute-start(f32[9,8,128]{2,1,0:T(8,128)S(1)} %get-tuple-element.18.refs_0_), channel_id=1, source_target_pairs={{0,8},{4,12},{8,0},{12,4},{1,9},{5,13},{9,1},{13,5},{2,10},{6,14},... | collective-permute-start | bytes 110600 | tf_op jit(solution)/shard_map/ppermute | solution.py:863
  17.2 4.0 %collective-permute-start.5 = (f32[9,8,128]{2,1,0:T(8,128)S(1)}, f32[9,8,128]{2,1,0:T(8,128)S(1)}, u32[]{:S(2)}, u32[]{:S(2)}) collective-permute-start(f32[9,8,128]{2,1,0:T(8,128)S(1)} %get-tuple-element.18.refs_0_), channel_id=1, source_target_pairs={{0,2},{1,3},{2,0},{3,1},{4,6},{5,7},{6,4},{7,5},{8,10},{9,11},{10,... | collective-permute-start | bytes 110600 | tf_op jit(solution)/shard_map/ppermute | solution.py:864
  18.7 6.0 %collective-permute-start.6 = (f32[9,8,128]{2,1,0:T(8,128)S(1)}, f32[9,8,128]{2,1,0:T(8,128)S(1)}, u32[]{:S(2)}, u32[]{:S(2)}) collective-permute-start(f32[9,8,128]{2,1,0:T(8,128)S(1)} %get-tuple-element.18.refs_0_), channel_id=1, source_target_pairs={{0,10},{1,11},{2,8},{3,9},{4,14},{5,15},{6,12},{7,13},{8,2},{9,3},... | collective-permute-start | bytes 110600 | tf_op jit(solution)/shard_map/ppermute | solution.py:866
  19.0 9.3 %collective-permute-start.10 = (f32[9,32,128]{2,1,0:T(8,128)S(1)}, f32[9,32,128]{2,1,0:T(8,128)S(1)}, u32[]{:S(2)}, u32[]{:S(2)}) collective-permute-start(f32[9,32,128]{2,1,0:T(8,128)S(1)} %get-tuple-element.19), channel_id=1, source_target_pairs={{0,16},{16,0},{1,17},{17,1},{2,18},{18,2},{3,19},{19,3},{4,20},{20... | collective-permute-start | bytes 442376 | tf_op jit(solution)/shard_map/ppermute | solution.py:867
  24.8 10.2 %copy-start.1 = (f32[128,128]{1,0:T(8,128)S(1)}, f32[128,128]{1,0:T(8,128)}, u32[]{:S(2)}) copy-start(f32[128,128]{1,0:T(8,128)} %constant.26.clone.refs_11_) | copy-start | bytes 196612
  24.8 7.2 %collective-permute-start.9 = (f32[4,9,8,128]{3,2,1,0:T(8,128)S(1)}, f32[4,9,8,128]{3,2,1,0:T(8,128)S(1)}, u32[]{:S(2)}, u32[]{:S(2)}) collective-permute-start(f32[4,9,8,128]{3,2,1,0:T(8,128)S(1)} %shard_map.30.after_ref.refs_0_), channel_id=1, source_target_pairs={{0,20},{4,16},{8,28},{12,24},{16,4},{20,0},{24,12},{28,8},{1,21},{... | collective-permute-start | bytes 442376 | tf_op jit(solution)/shard_map/ppermute | solution.py:876
  26.0 7.4 %collective-permute-start.7 = (f32[4,9,8,128]{3,2,1,0:T(8,128)S(1)}, f32[4,9,8,128]{3,2,1,0:T(8,128)S(1)}, u32[]{:S(2)}, u32[]{:S(2)}) collective-permute-start(f32[4,9,8,128]{3,2,1,0:T(8,128)S(1)} %shard_map.30.after_ref.refs_0_), channel_id=1, source_target_pairs={{0,16},{16,0},{1,17},{17,1},{2,18},{18,2},{3,19},{19,3},{4,20},{20... | collective-permute-start | bytes 442376 | tf_op jit(solution)/shard_map/ppermute | solution.py:874
  26.5 7.0 %collective-permute-start.8 = (f32[4,9,8,128]{3,2,1,0:T(8,128)S(1)}, f32[4,9,8,128]{3,2,1,0:T(8,128)S(1)}, u32[]{:S(2)}, u32[]{:S(2)}) collective-permute-start(f32[4,9,8,128]{3,2,1,0:T(8,128)S(1)} %shard_map.30.after_ref.refs_0_), channel_id=1, source_target_pairs={{0,4},{4,0},{8,12},{12,8},{1,5},{5,1},{9,13},{13,9},{2,6},{6,2},{1... | collective-permute-start | bytes 442376 | tf_op jit(solution)/shard_map/ppermute | solution.py:875
  28.3 5.5 %collective-permute-start.11 = (f32[4,9,8,128]{3,2,1,0:T(8,128)S(1)}, f32[4,9,8,128]{3,2,1,0:T(8,128)S(1)}, u32[]{:S(2)}, u32[]{:S(2)}) collective-permute-start(f32[4,9,8,128]{3,2,1,0:T(8,128)S(1)} %shard_map.30.after_ref.refs_0_), channel_id=1, source_target_pairs={{0,1},{1,0},{2,3},{3,2},{4,5},{5,4},{6,7},{7,6},{8,9},{9,8},{10,11... | collective-permute-start | bytes 442376 | tf_op jit(solution)/shard_map/ppermute | solution.py:886
  31.9 1.9 %collective-permute-start.14 = (f32[4,9,8,128]{3,2,1,0:T(8,128)S(1)}, f32[4,9,8,128]{3,2,1,0:T(8,128)S(1)}, u32[]{:S(2)}, u32[]{:S(2)}) collective-permute-start(f32[4,9,8,128]{3,2,1,0:T(8,128)S(1)} %collective-permute-done.9.refs_3_), channel_id=1, source_target_pairs={{0,1},{1,0},{2,3},{3,2},{4,5},{5,4},{6,7},{7,6},{8,9},{9,8},{10,11... | collective-permute-start | bytes 442376 | tf_op jit(solution)/shard_map/ppermute | solution.py:886
  33.4 1.4 %collective-permute-start.12 = (f32[4,9,8,128]{3,2,1,0:T(8,128)S(1)}, f32[4,9,8,128]{3,2,1,0:T(8,128)S(1)}, u32[]{:S(2)}, u32[]{:S(2)}) collective-permute-start(f32[4,9,8,128]{3,2,1,0:T(8,128)S(1)} %collective-permute-done.7.refs_1_), channel_id=1, source_target_pairs={{0,1},{1,0},{2,3},{3,2},{4,5},{5,4},{6,7},{7,6},{8,9},{9,8},{10,11... | collective-permute-start | bytes 442376 | tf_op jit(solution)/shard_map/ppermute | solution.py:886
  33.5 1.5 %collective-permute-start.13 = (f32[4,9,8,128]{3,2,1,0:T(8,128)S(1)}, f32[4,9,8,128]{3,2,1,0:T(8,128)S(1)}, u32[]{:S(2)}, u32[]{:S(2)}) collective-permute-start(f32[4,9,8,128]{3,2,1,0:T(8,128)S(1)} %collective-permute-done.8.refs_2_), channel_id=1, source_target_pairs={{0,1},{1,0},{2,3},{3,2},{4,5},{5,4},{6,7},{7,6},{8,9},{9,8},{10,11... | collective-permute-start | bytes 442376 | tf_op jit(solution)/shard_map/ppermute | solution.py:886
